TPU v7x, 16 devices: a whole 2x2x2 slice. The times are simulated.
16 devices in a mesh: tp: 2 (over z), ep: 8 (over y, x, core).
Axes of the slice: x: 2, y: 2, z: 2, core: 2. Of those that a mesh axis runs over, the one named last changes fastest.
Arguments:
- act_in: bfloat16 [16384, 1024], P('ep')
- w_router: float32 [1024, 32], replicated
- choice_one: int32 [16384], P('ep')
- choice_two: int32 [16384], P('ep')
- w_gelu: bfloat16 [32, 1024, 512], P('ep', None, 'tp')
- w_lin: bfloat16 [32, 1024, 512], P('ep', None, 'tp')
- w_out: bfloat16 [32, 512, 1024], P('ep', 'tp')
- grad_out: bfloat16 [16384, 1024], P('ep')
Outputs:
- output 1: bfloat16 [16384, 1024], P('ep')
- output 2: bfloat16 [16384, 1024], P('ep')
- output 3: float32 [32, 1024, 512], P('ep', None, 'tp')
- output 4: float32 [32, 1024, 512], P('ep', None, 'tp')
- output 5: float32 [32, 512, 1024], P('ep', 'tp')
- output 6: float32 [1024, 32], replicated
All inputs are finite; a program needn't handle non-finite values.
Results may differ from a plain program's by a relative error of at most 0.00998415.
Values are sent between devices in bfloat16 or wider.
A program may use at most 1 GiB of HBM per device.

v0:
```python
import functools

import jax
import jax.numpy as jnp
from jax import lax
from jax.experimental import pallas as pl
from jax.experimental.pallas import tpu as pltpu
from jax.sharding import PartitionSpec as P


GELU_COEF = 0.7978845608028654
F32 = jnp.float32
BF16 = jnp.bfloat16
NT = (((1,), (1,)), ((), ()))
TN = (((0,), (0,)), ((), ()))
TILE = 256


def gelu_parts(pre_act):
    inner_arg = GELU_COEF * (pre_act + 0.044715 * pre_act * pre_act * pre_act)
    tanh_val = jnp.tanh(inner_arg)
    gelu_val = 0.5 * pre_act * (1.0 + tanh_val)
    gelu_slope = 0.5 * (1.0 + tanh_val) + 0.5 * pre_act * (1.0 - tanh_val * tanh_val) * GELU_COEF * (1.0 + 0.134145 * pre_act * pre_act)
    return gelu_val, gelu_slope


def split3(val):
    high = val.astype(BF16)
    rest = val - high.astype(F32)
    mid = rest.astype(BF16)
    return high, mid, (rest - mid.astype(F32)).astype(BF16)


def route_kernel(me_ref, x_ref, wt_ref, ids_ref, rows_ref, prob_ref, *, slot_cap, own_experts):
    n_experts, n_tokens = prob_ref.shape
    pieces = jnp.concatenate(split3(wt_ref[...]), axis=0)
    raw = lax.dot_general(pieces, x_ref[...], NT, preferred_element_type=F32)
    logits = raw[:n_experts] + raw[n_experts:2 * n_experts] + raw[2 * n_experts:]
    expo = jnp.exp(logits - jnp.max(logits, axis=0, keepdims=True))
    prob = expo / jnp.sum(expo, axis=0, keepdims=True)
    prob_ref[...] = prob
    expert = lax.broadcasted_iota(jnp.int32, (n_experts, n_tokens), 0)
    id_one, id_two = ids_ref[0:1, :], ids_ref[1:2, :]
    hot_one = jnp.where(id_one == expert, 1.0, 0.0)
    hot_two = jnp.where(id_two == expert, 1.0, 0.0)
    hots = jnp.concatenate([hot_one, hot_two], axis=0)
    before = lax.broadcasted_iota(jnp.int32, (TILE, TILE), 0) < lax.broadcasted_iota(jnp.int32, (TILE, TILE), 1)
    tri = jnp.where(before, 1.0, 0.0).astype(BF16)
    run = jnp.zeros((2 * n_experts, 1), F32)
    counts = []
    for b in range(n_tokens // TILE):
        part = hots[:, b * TILE:(b + 1) * TILE]
        counts.append(jnp.dot(part.astype(BF16), tri, preferred_element_type=F32) + run)
        run = run + jnp.sum(part, axis=1, keepdims=True)
    count = jnp.concatenate(counts, axis=1)
    pos_one = jnp.sum(count[:n_experts] * hot_one, axis=0, keepdims=True)
    pos_two = jnp.sum((count[n_experts:] + run[:n_experts]) * hot_two, axis=0, keepdims=True)
    prob_one = jnp.sum(prob * hot_one, axis=0, keepdims=True)
    prob_two = jnp.sum(prob * hot_two, axis=0, keepdims=True)
    turn = me_ref[0] * (own_experts * slot_cap)

    def slot_of(ids, pos):
        place = pos.astype(jnp.int32)
        slot = jnp.where(place < slot_cap, ids * slot_cap + place, n_experts * slot_cap)
        return jnp.bitwise_xor(slot, turn).astype(F32)

    gate_sum = prob_one + prob_two
    rows_ref[...] = jnp.concatenate(
        [slot_of(id_one, pos_one), slot_of(id_two, pos_two), prob_one / gate_sum, prob_two / gate_sum, prob_one, prob_two, jnp.zeros((10, n_tokens), F32)],
        axis=0)


def gather_kernel(z_ref, rows_ref, src_ref, *outs, peers, per, scaled):
    step = pl.program_id(0)
    n_tokens = src_ref.shape[0]
    peer = sum(jnp.where(step // per == i, d, 0) for i, d in enumerate(peers))
    slot = (peer * per + step % per) * TILE + lax.broadcasted_iota(jnp.int32, (TILE, n_tokens), 0)
    slot = slot.astype(F32)
    hit_one = rows_ref[0:1, :] == slot
    hit_two = rows_ref[1:2, :] == slot
    pick = jnp.where(jnp.logical_or(hit_one, hit_two), 1.0, 0.0).astype(BF16)
    val = jnp.dot(pick, src_ref[...], preferred_element_type=F32)
    if scaled:
        gate = jnp.where(hit_one, rows_ref[2:3, :], 0.0) + jnp.where(hit_two, rows_ref[3:4, :], 0.0)
        val = jnp.sum(gate, axis=1, keepdims=True) * val
    val = val.astype(BF16)
    for i, out in enumerate(outs):
        @pl.when(step // per == i)
        def _(out=out):
            out[...] = val


def forward_own_kernel(z_ref, *refs, n_src, cols):
    xs = refs[:n_src]
    wa, wb, wc, gv_ref, sv_ref, h_ref, part_ref = refs[n_src:]
    cap = xs[0].shape[1]
    col = pl.ds(pl.multiple_of(z_ref[0] * cols, cols), cols)
    for j in range(n_src // 2):
        x = jnp.concatenate([xs[2 * j][0], xs[2 * j + 1][0]], axis=0)
        rows = slice(2 * j * cap, 2 * (j + 1) * cap)
        pre_a = jnp.dot(x, wa[0], preferred_element_type=F32)
        pre_b = jnp.dot(x, wb[0], preferred_element_type=F32)
        gelu_val, gelu_slope = gelu_parts(pre_a)
        hidden = (gelu_val * pre_b).astype(BF16)
        gv_ref[0, rows, :] = gelu_val
        sv_ref[0, rows, :] = pre_b * gelu_slope
        h_ref[0, rows, :] = hidden
        part_ref[0, rows, :] = jnp.dot(hidden, wc[0, :, col], preferred_element_type=F32).astype(BF16)


def forward_other_kernel(*refs, n_src, n_chunk):
    xs = refs[:n_src]
    part_ref, wa, wb, wc = refs[n_src:n_src + 4]
    outs = refs[n_src + 4:n_src + 4 + n_chunk * n_src]
    gv_ref, sv_ref = refs[n_src + 4 + n_chunk * n_src:]
    cap = xs[0].shape[1]
    wide = outs[0].shape[2]
    for j in range(n_src // 2):
        x = jnp.concatenate([xs[2 * j][0], xs[2 * j + 1][0]], axis=0)
        rows = slice(2 * j * cap, 2 * (j + 1) * cap)
        pre_a = jnp.dot(x, wa[0], preferred_element_type=F32)
        pre_b = jnp.dot(x, wb[0], preferred_element_type=F32)
        gelu_val, gelu_slope = gelu_parts(pre_a)
        hidden = (gelu_val * pre_b).astype(BF16)
        gv_ref[0, rows, :] = gelu_val
        sv_ref[0, rows, :] = pre_b * gelu_slope
        part = jnp.dot(hidden, wc[0], preferred_element_type=F32).astype(BF16).astype(F32)
        total = (part_ref[0, rows, :].astype(F32) + part).astype(BF16)
        for c in range(n_chunk):
            outs[c * n_src + 2 * j][0] = total[:cap, c * wide:(c + 1) * wide]
            outs[c * n_src + 2 * j + 1][0] = total[cap:, c * wide:(c + 1) * wide]


def put_rows(z, rows, ref, dest):
    if len(ref) == 1:
        dest[rows, :] = ref[0][0]
        return
    cols = ref[0].shape[2]
    dest[rows, pl.ds(pl.multiple_of(z * cols, cols), cols)] = ref[0][0]
    dest[rows, pl.ds(pl.multiple_of((1 - z) * cols, cols), cols)] = ref[1][0]


def group_refs(refs, widths):
    groups, at = [], 0
    for w in widths:
        groups.append(refs[at:at + w])
        at += w
    return groups, refs[at:]


def backward_kernel(z_ref, *refs, widths, cols, n_chunk):
    dos, refs = group_refs(refs, widths)
    n_src = len(widths)
    gv_ref, sv_ref, gv2_ref, sv2_ref, wa, wb, wc, wa2, wb2, wcz, wcn = refs[:11]
    outs = refs[11:11 + n_chunk * n_src]
    da_ref, db_ref, do_ref = refs[11 + n_chunk * n_src:]
    cap = dos[0][0].shape[1]
    z = z_ref[0]
    near = pl.ds(pl.multiple_of(z * cols, cols), cols)
    far = pl.ds(pl.multiple_of((1 - z) * cols, cols), cols)
    wide = cols // n_chunk
    for j in range(n_src // 2):
        rows = slice(2 * j * cap, 2 * (j + 1) * cap)
        put_rows(z, slice(2 * j * cap, (2 * j + 1) * cap), dos[2 * j], do_ref)
        put_rows(z, slice((2 * j + 1) * cap, 2 * (j + 1) * cap), dos[2 * j + 1], do_ref)
        total = None
        for k, (a_ref, b_ref, s_ref, g_ref) in enumerate(((wa, wb, sv_ref, gv_ref), (wa2, wb2, sv2_ref, gv2_ref))):
            if k == 0:
                dhid = lax.dot_general(do_ref[rows, :], wc[0], NT, preferred_element_type=F32)
            else:
                dhid = lax.dot_general(do_ref[rows, near], wcz[0], NT, preferred_element_type=F32)
                dhid = dhid + lax.dot_general(do_ref[rows, far], wcn[0], NT, preferred_element_type=F32)
            grad_a = (dhid * s_ref[0, rows, :]).astype(BF16)
            grad_b = (dhid * g_ref[0, rows, :]).astype(BF16)
            if k == 0:
                da_ref[0, rows, :] = grad_a
                db_ref[0, rows, :] = grad_b
            part = lax.dot_general(grad_a, a_ref[0, near, :], NT, preferred_element_type=F32)
            part = part + lax.dot_general(grad_b, b_ref[0, near, :], NT, preferred_element_type=F32)
            part = part.astype(BF16).astype(F32)
            total = part if total is None else total + part
        total = total.astype(BF16)
        for c in range(n_chunk):
            outs[c * n_src + 2 * j][0] = total[:cap, c * wide:(c + 1) * wide]
            outs[c * n_src + 2 * j + 1][0] = total[cap:, c * wide:(c + 1) * wide]


def weight_grad_kernel(z_ref, *refs, n_src, widths):
    xs = refs[:n_src]
    dos, refs = group_refs(refs[n_src:], widths)
    h_ref, da_ref, da2_ref, db_ref, db2_ref, ga_ref, gb_ref, gc_ref, do_ref = refs
    cap = xs[0].shape[1]
    for i, ref in enumerate(dos):
        put_rows(z_ref[0], slice(i * cap, (i + 1) * cap), ref, do_ref)
    x = jnp.concatenate([r[0] for r in xs], axis=0)
    grad_a = jnp.concatenate([da_ref[0], da2_ref[0]], axis=0)
    grad_b = jnp.concatenate([db_ref[0], db2_ref[0]], axis=0)
    ga_ref[0] = lax.dot_general(x, grad_a, TN, preferred_element_type=F32)
    gb_ref[0] = lax.dot_general(x, grad_b, TN, preferred_element_type=F32)
    gc_ref[0] = lax.dot_general(h_ref[0], do_ref[...], TN, preferred_element_type=F32)


def slot_picks(cols_ref):
    lane = lax.broadcasted_iota(jnp.int32, (TILE, 128), 1).astype(F32)
    picks = []
    for k in range(2):
        slot = cols_ref[:, k:k + 1]
        blk = jnp.floor(slot * (1.0 / 128.0))
        hot = jnp.where(slot - 128.0 * blk == lane, 1.0, 0.0).astype(BF16)
        picks.append((jnp.broadcast_to(blk, (TILE, 128)).astype(BF16), hot))
    return picks


def stack_rows(srcs, all_ref):
    per = srcs[0].shape[0]

    @pl.when(pl.program_id(0) == 0)
    def _():
        for d, src in enumerate(srcs):
            all_ref[d * per:(d + 1) * per, :] = src[...]


def combine_out_kernel(z_ref, cols_ref, dy_ref, *refs, n_src):
    srcs = refs[:n_src]
    y_ref, dg_ref, all_ref = refs[n_src:]
    stack_rows(srcs, all_ref)
    n_slots = all_ref.shape[0]
    zero = jnp.zeros((TILE, 128), BF16)
    pick = jnp.concatenate(
        [jnp.concatenate([jnp.where(blk == jnp.asarray(b, BF16), hot, zero) for b in range(n_slots // 128)], axis=1) for blk, hot in slot_picks(cols_ref)],
        axis=0)
    both = jnp.dot(pick, all_ref[...], preferred_element_type=F32)
    dy = dy_ref[...].astype(F32)
    one, two = both[:TILE], both[TILE:]
    y_ref[...] = (cols_ref[:, 2:3] * one + cols_ref[:, 3:4] * two).astype(BF16)
    dg_one = jnp.sum(dy * one, axis=1, keepdims=True)
    dg_two = jnp.sum(dy * two, axis=1, keepdims=True)
    wide = jnp.concatenate([dg_one, dg_two, jnp.zeros((TILE, 126), F32)], axis=1)
    dg_ref[...] = wide.T[:8, :]


def logit_grad_kernel(z_ref, rows_ref, prob_ref, ids_ref, x_ref, *refs, n_chunk):
    dgs, (dl_ref, dw_ref) = refs[:2 * n_chunk], refs[2 * n_chunk:]
    n_experts, n_tokens = prob_ref.shape
    mine = sum(r[0:2, :] for r in dgs[:n_chunk])
    other = sum(r[0:2, :] for r in dgs[n_chunk:])
    dgate = mine + other
    dg_one, dg_two = dgate[0:1], dgate[1:2]
    gate_one, gate_two = rows_ref[2:3, :], rows_ref[3:4, :]
    prob_one, prob_two = rows_ref[4:5, :], rows_ref[5:6, :]
    shared = dg_one * gate_one + dg_two * gate_two
    gate_sum = prob_one + prob_two
    dp_one = (dg_one - shared) / gate_sum
    dp_two = (dg_two - shared) / gate_sum
    centre = dp_one * prob_one + dp_two * prob_two
    expert = lax.broadcasted_iota(jnp.int32, (n_experts, n_tokens), 0)
    inner = jnp.where(ids_ref[0:1, :] == expert, dp_one, 0.0) + jnp.where(ids_ref[1:2, :] == expert, dp_two, 0.0) - centre
    high, mid, low = split3(prob_ref[...] * inner)
    dl_ref[...] = jnp.concatenate([high, high, mid, high, low, mid], axis=0)
    raw = jnp.dot(jnp.concatenate([high, mid, low], axis=0), x_ref[...], preferred_element_type=F32)
    dw_ref[...] = raw[:n_experts] + raw[n_experts:2 * n_experts] + raw[2 * n_experts:]


def combine_in_kernel(z_ref, cols_ref, dl_ref, wt_ref, *refs, n_src):
    srcs = refs[:n_src]
    dx_ref, all_ref = refs[n_src:]
    stack_rows(srcs, all_ref)
    n_slots = all_ref.shape[0]
    (blk_one, hot_one), (blk_two, hot_two) = slot_picks(cols_ref)
    zero = jnp.zeros((TILE, 128), BF16)
    parts = []
    for b in range(n_slots // 128):
        this = jnp.asarray(b, BF16)
        parts.append(jnp.where(blk_one == this, hot_one, jnp.where(blk_two == this, hot_two, zero)))
    acc = jnp.dot(jnp.concatenate(parts, axis=1), all_ref[...], preferred_element_type=F32)
    high, mid, low = split3(wt_ref[...])
    weights = jnp.concatenate([high, mid, high, low, high, mid], axis=0)
    back = lax.dot_general(dl_ref[...], weights, TN, preferred_element_type=F32)
    dx_ref[...] = (acc + back).astype(BF16)


def place_kernel(z_ref, *refs):
    pieces, out = refs[:-1], refs[-1]
    n_chunk = len(pieces) // 2
    wide = pieces[0].shape[1]
    for side in range(2):
        base = jnp.where(side == 0, z_ref[0], 1 - z_ref[0]) * (n_chunk * wide)
        for c in range(n_chunk):
            out[:, pl.ds(pl.multiple_of(base + c * wide, wide), wide)] = pieces[side * n_chunk + c][...]


def cost(flops, nbytes, trans=0):
    return pl.CostEstimate(flops=int(flops), bytes_accessed=int(nbytes), transcendentals=int(trans))


def solution(mesh):
    tp_size = mesh.shape["tp"]
    n_src = mesh.shape["ep"]
    n_chunk = 2
    diag = [n_src - 2, n_src - 1]
    early = diag + [2, 4, 0, 1]
    late = [3, 5]
    src_order = early + late

    def local_step(x_rows, w_router, first_ids, second_ids, w_gelu, w_lin, w_out, dy_rows):
        n_tokens, model = x_rows.shape
        n_experts = w_router.shape[1]
        own, width = w_gelu.shape[0], w_gelu.shape[2]
        slot_cap = 2 * n_tokens // n_experts
        block = own * slot_cap
        cols = model // tp_size
        wide = cols // n_chunk
        rows_all = n_src * slot_cap
        rows_early = len(early) * slot_cap
        rows_late = len(late) * slot_cap
        sds = jax.ShapeDtypeStruct
        me = lax.axis_index("ep").astype(jnp.int32).reshape(1)
        z = lax.axis_index("tp").astype(jnp.int32).reshape(1)
        swap = [(i, tp_size - 1 - i) for i in range(tp_size)]

        def across(val):
            return lax.ppermute(val, "tp", swap)

        def to_peer(val, d):
            if d == 0:
                return val
            return lax.ppermute(val, "ep", [(i, i ^ d) for i in range(n_src)])

        def call(kernel, grid, in_specs, out_specs, out_shape, estimate, args, scratch=()):
            return pl.pallas_call(
                kernel,
                grid_spec=pltpu.PrefetchScalarGridSpec(num_scalar_prefetch=1, grid=grid, in_specs=in_specs, out_specs=out_specs, scratch_shapes=list(scratch)),
                out_shape=out_shape, cost_estimate=estimate)(z, *args)

        wa2, wb2 = across(w_gelu), across(w_lin)
        wt = w_router.T
        ids = jnp.stack([first_ids, second_ids])
        rows, prob = pl.pallas_call(
            functools.partial(route_kernel, slot_cap=slot_cap, own_experts=own),
            in_specs=[pl.BlockSpec(memory_space=pltpu.SMEM)] + [pl.BlockSpec(memory_space=pltpu.VMEM)] * 3,
            out_shape=(sds((16, n_tokens), F32), sds((n_experts, n_tokens), F32)),
            cost_estimate=cost(2 * 96 * n_tokens * model, 2 * n_tokens * model, n_experts * n_tokens),
            name="route",
        )(me, x_rows, wt, ids)
        token_cols = rows.T
        wcz = across(lax.dynamic_slice_in_dim(w_out, (1 - z[0]) * cols, cols, 2))
        wcn = across(lax.dynamic_slice_in_dim(w_out, z[0] * cols, cols, 2))

        per = block // TILE

        def gather(src, peers, scaled, part=False):
            width_out = cols if part else model

            def out_map(g, z, i):
                return (jnp.clip(g - i * per, 0, per - 1), 0)

            def src_map(g, z):
                return (0, z[0] if part else 0)

            return call(
                functools.partial(gather_kernel, peers=peers, per=per, scaled=scaled), (len(peers) * per,),
                [pl.BlockSpec((16, n_tokens), lambda g, z: (0, 0)), pl.BlockSpec((n_tokens, width_out), src_map)],
                [pl.BlockSpec((TILE, width_out), functools.partial(out_map, i=i)) for i in range(len(peers))],
                [sds((block, width_out), BF16)] * len(peers),
                cost(2 * len(peers) * block * n_tokens * width_out, 2 * (n_tokens + len(peers) * block) * width_out),
                (rows, src))

        xs, dos = [None] * n_src, [None] * n_src
        for peers in ([6], [4, 2], [7, 5, 3], [1, 0]):
            for d, val in zip(peers, gather(x_rows, peers, False)):
                xs[d] = to_peer(val, d).reshape(own, slot_cap, model)
        for d, val in zip(diag, gather(dy_rows, diag, True, part=True)):
            mine = to_peer(val, d)
            dos[d] = tuple(v.reshape(own, slot_cap, cols) for v in (mine, across(mine)))
        for peers in ([4, 2], [1, 0], [5, 3]):
            for d, val in zip(peers, gather(dy_rows, peers, True)):
                dos[d] = (to_peer(val, d).reshape(own, slot_cap, model),)
        xs = [xs[d] for d in src_order]

        def whole(a, b, at=0):
            return pl.BlockSpec((1, a, b), lambda e, *_: (e, at, 0))

        act_specs = [whole(rows_all, width)] * 3
        act_shapes = [sds((own, rows_all, width), F32)] * 2 + [sds((own, rows_all, width), BF16)]
        gv, sv, hidden, part = call(
            functools.partial(forward_own_kernel, n_src=n_src, cols=cols), (own,),
            [whole(slot_cap, model)] * n_src + [whole(model, width)] * 2 + [whole(width, model)],
            act_specs + [whole(rows_all, cols)], act_shapes + [sds((own, rows_all, cols), BF16)],
            cost(2 * own * rows_all * width * (2 * model + cols), 32e6, own * rows_all * width),
            (*xs, w_gelu, w_lin, w_out))
        fwd = pl.pallas_call(
            functools.partial(forward_other_kernel, n_src=n_src, n_chunk=n_chunk), grid=(own,),
            in_specs=[whole(slot_cap, model)] * n_src + [whole(rows_all, cols)] + [whole(model, width)] * 2 + [whole(width, cols)],
            out_specs=[whole(slot_cap, wide)] * (n_src * n_chunk) + act_specs[:2],
            out_shape=[sds((own, slot_cap, wide), BF16)] * (n_src * n_chunk) + act_shapes[:2],
            cost_estimate=cost(2 * own * rows_all * width * (2 * model + cols), 32e6, own * rows_all * width),
            name="k_fwd_other")(*xs, part, wa2, wb2, wcz)
        gv2, sv2 = fwd[n_chunk * n_src:]
        back_out = []
        for c in range(n_chunk):
            got = [None] * n_src
            for i, d in enumerate(src_order):
                got[d] = to_peer(fwd[c * n_src + i], d).reshape(block, wide)
            back_out.append(got)

        def backward(peers, at):
            n_rows = len(peers) * slot_cap
            args = [v for d in peers for v in dos[d]]
            saved = [whole(n_rows, width, at)] * 4
            return call(
                functools.partial(backward_kernel, widths=[len(dos[d]) for d in peers], cols=cols, n_chunk=n_chunk), (own,),
                [whole(slot_cap, v.shape[2]) for v in args] + saved + [whole(model, width)] * 2 + [whole(width, model)] + [whole(model, width)] * 2 + [whole(width, cols)] * 2,
                [whole(slot_cap, wide)] * (len(peers) * n_chunk) + [whole(n_rows, width)] * 2,
                [sds((own, slot_cap, wide), BF16)] * (len(peers) * n_chunk) + [sds((own, n_rows, width), BF16)] * 2,
                cost(4 * own * n_rows * width * (model + 2 * cols), 6e3 * own * n_rows),
                (*args, gv, sv, gv2, sv2, w_gelu, w_lin, w_out, wa2, wb2, wcz, wcn),
                [pltpu.VMEM((n_rows, model), BF16)])

        bwd_a = backward(early, 0)
        bwd_b = backward(late, rows_early // rows_late)
        back_in = []
        for c in range(n_chunk):
            got = [None] * n_src
            for peers, vals in ((early, bwd_a), (late, bwd_b)):
                for i, d in enumerate(peers):
                    got[d] = to_peer(vals[c * len(peers) + i], d).reshape(block, wide)
            back_in.append(got)

        all_dos = [v for d in src_order for v in dos[d]]
        grad_wa, grad_wb, grad_wc = call(
            functools.partial(weight_grad_kernel, n_src=n_src, widths=[len(dos[d]) for d in src_order]), (own,),
            [whole(slot_cap, model)] * n_src + [whole(slot_cap, v.shape[2]) for v in all_dos] + [whole(rows_all, width)] + [whole(rows_early, width), whole(rows_late, width)] * 2,
            [whole(model, width), whole(model, width), whole(width, model)],
            [sds((own, model, width), F32)] * 2 + [sds((own, width, model), F32)],
            cost(6 * own * rows_all * width * model, 40e6),
            (*xs, *all_dos, hidden, bwd_a[-2], bwd_b[-2], bwd_a[-1], bwd_b[-1]),
            [pltpu.VMEM((rows_all, model), BF16)])

        def resident(a, b):
            return pl.BlockSpec((a, b), lambda i, *_: (0, 0))

        def tiles(b, col=None):
            return pl.BlockSpec((TILE, b), lambda i, z: (i, 0 if col is None else z[0] * n_chunk + col))

        n_tiles = (n_tokens // TILE,)
        stacked = [pltpu.VMEM((n_src * block, wide), BF16)]
        y_mine, y_other, dg_mine, dg_other = [], [], [], []
        for c in range(n_chunk):
            y, dg = call(
                functools.partial(combine_out_kernel, n_src=n_src), n_tiles,
                [tiles(16), tiles(wide, c)] + [resident(block, wide)] * n_src,
                [tiles(wide), pl.BlockSpec((8, TILE), lambda i, z: (0, i))],
                [sds((n_tokens, wide), BF16), sds((8, n_tokens), F32)],
                cost(4 * n_tokens * n_src * block * wide, 6e6),
                (token_cols, dy_rows, *back_out[c]), stacked)
            y_mine.append(y)
            dg_mine.append(dg)
            dg_other.append(across(dg))
            y_other.append(across(y))

        dl, dw = call(
            functools.partial(logit_grad_kernel, n_chunk=n_chunk), (1,),
            [resident(16, n_tokens), resident(n_experts, n_tokens), resident(2, n_tokens), pl.BlockSpec((n_tokens, cols), lambda i, z: (0, z[0]))] + [resident(8, n_tokens)] * (2 * n_chunk),
            [resident(6 * n_experts, n_tokens), resident(n_experts, cols)],
            [sds((6 * n_experts, n_tokens), BF16), sds((n_experts, cols), F32)],
            cost(2 * 96 * n_tokens * cols, 4e6),
            (rows, prob, ids, x_rows, *dg_mine, *dg_other))

        dx_mine, dx_other = [], []
        for c in range(n_chunk):
            dx = call(
                functools.partial(combine_in_kernel, n_src=n_src), n_tiles,
                [tiles(16), pl.BlockSpec((6 * n_experts, TILE), lambda i, z: (0, i)), pl.BlockSpec((n_experts, wide), lambda i, z: (0, z[0] * n_chunk + c))] + [resident(block, wide)] * n_src,
                tiles(wide), sds((n_tokens, wide), BF16),
                cost(2 * n_tokens * n_src * block * wide, 6e6),
                (token_cols, dl, wt, *back_in[c]), stacked)
            dx_mine.append(dx)
            dx_other.append(across(dx))
        bit = 1
        while bit < n_src:
            dw = dw + to_peer(dw, bit)
            bit *= 2
        dw_other = across(dw)

        def place(pieces):
            return call(place_kernel, n_tiles, [tiles(wide)] * len(pieces), tiles(model), sds((n_tokens, model), BF16), cost(1e6, 8e6), pieces)

        act_out = place(y_mine + y_other)
        grad_in = place(dx_mine + dx_other)
        grad_router = jnp.where(z[0] == 0, jnp.concatenate([dw, dw_other], axis=1), jnp.concatenate([dw_other, dw], axis=1)).T
        return act_out, grad_in, grad_wa, grad_wb, grad_wc, grad_router

    return jax.shard_map(local_step, mesh=mesh, in_specs=(P("ep", None), P(), P("ep"), P("ep"), P("ep", None, "tp"), P("ep", None, "tp"), P("ep", "tp", None), P("ep", None)), out_specs=(P("ep", None), P("ep", None), P("ep", None, "tp"), P("ep", None, "tp"), P("ep", "tp", None), P()), check_vma=False)
```

profile of v0, /device:TPU:0, one launch (start us, length us, event | category | flops | bytes accessed | tf_op | source)
XLA Modules:
  0.0 499.8 jit_solution(11935707895738662206)
XLA Ops:
  0.6 1.3 pad_add_fusion.ids_ref
  2.0 4.7 route.1
  6.6 11.5 %shard_map.128 = (bf16[512,1024]{1,0:T(8,128)(2,1)}, bf16[512,1024]{1,0:T(8,128)(2,1)}, bf16[512,1024]{1,0:T(8,128)(2,1)}) custom-call(s32[1]{0:T(128)} %bitcast.z_ref, f32[16,2048]{1,0:T(8,128)} %get-tuple-element.74.rows_ref, bf16[2048,1024]{1,0:T(8,128)(2,1)} %x_ref.3), custom_call_target="tpu_custom_call" | custom-call | flops 6442450944 | bytes 7340032 | tf_op jit(solution)/shard_map/pallas_call | solution.py:330
  18.2 2.6 collective-permute-start.5
  20.8 1.8 collective-permute-start.6
  22.6 5.8 %shard_map.136 = (bf16[512,512]{1,0:T(8,128)(2,1)}, bf16[512,512]{1,0:T(8,128)(2,1)}) custom-call(s32[1]{0:T(128)} %bitcast.z_ref, f32[16,2048]{1,0:T(8,128)} %get-tuple-element.74.rows_ref, bf16[2048,1024]{1,0:T(8,128)(2,1)} %src_ref.15), custom_call_target="tpu_custom_call" | custom-call | flops 2147483648 | bytes 3145728 | tf_op jit(solution)/shard_map/pallas_call | solution.py:330
  28.4 2.4 collective-permute-start.28
  31.0 8.6 %shard_map.130 = (bf16[512,1024]{1,0:T(8,128)(2,1)}, bf16[512,1024]{1,0:T(8,128)(2,1)}) custom-call(s32[1]{0:T(128)} %bitcast.z_ref, f32[16,2048]{1,0:T(8,128)} %get-tuple-element.74.rows_ref, bf16[2048,1024]{1,0:T(8,128)(2,1)} %x_ref.3), custom_call_target="tpu_custom_call" | custom-call | flops 4294967296 | bytes 6291456 | tf_op jit(solution)/shard_map/pallas_call | solution.py:330
  39.6 8.6 %shard_map.129 = (bf16[512,1024]{1,0:T(8,128)(2,1)}, bf16[512,1024]{1,0:T(8,128)(2,1)}) custom-call(s32[1]{0:T(128)} %bitcast.z_ref, f32[16,2048]{1,0:T(8,128)} %get-tuple-element.74.rows_ref, bf16[2048,1024]{1,0:T(8,128)(2,1)} %x_ref.3), custom_call_target="tpu_custom_call" | custom-call | flops 4294967296 | bytes 6291456 | tf_op jit(solution)/shard_map/pallas_call | solution.py:330
  48.2 32.0 %collective-permute-done.28 = bf16[512,512]{1,0:T(8,128)(2,1)S(1)} collective-permute-done((bf16[512,512]{1,0:T(8,128)(2,1)}, bf16[512,512]{1,0:T(8,128)(2,1)S(1)}, u32[]{:S(2)}, u32[]{:S(2)}) %collective-permute-start.28) | collective-permute-done | bytes 524320 | tf_op jit(solution)/shard_map/ppermute | solution.py:327
  80.2 11.1 %collective-permute-done.30 = bf16[512,512]{1,0:T(8,128)(2,1)S(1)} collective-permute-done((bf16[512,512]{1,0:T(8,128)(2,1)}, bf16[512,512]{1,0:T(8,128)(2,1)S(1)}, u32[]{:S(2)}, u32[]{:S(2)}) %collective-permute-start.30) | collective-permute-done | bytes 524320 | tf_op jit(solution)/shard_map/ppermute | solution.py:327
  91.4 1.5 collective-permute-start.2
  93.4 5.7 %shard_map.127 = bf16[512,1024]{1,0:T(8,128)(2,1)} custom-call(s32[1]{0:T(128)} %bitcast.z_ref, f32[16,2048]{1,0:T(8,128)} %get-tuple-element.74.rows_ref, bf16[2048,1024]{1,0:T(8,128)(2,1)} %x_ref.3), custom_call_target="tpu_custom_call" | custom-call | flops 2147483648 | bytes 5242880 | tf_op jit(solution)/shard_map/pallas_call | solution.py:330
  99.1 1.4 collective-permute-start
  100.6 1.5 constant_dynamic-slice_fusion
  102.1 1.6 collective-permute-start.9
  104.2 13.5 %collective-permute-done.2 = bf16[512,1024]{1,0:T(8,128)(2,1)} collective-permute-done((bf16[512,1024]{1,0:T(8,128)(2,1)}, bf16[512,1024]{1,0:T(8,128)(2,1)}, u32[]{:S(2)}, u32[]{:S(2)}) %collective-permute-start.2) | collective-permute-done | bytes 1048608 | tf_op jit(solution)/shard_map/ppermute | solution.py:327
  117.7 1.6 collective-permute-start.8
  119.3 9.3 %shard_map.140 = (bf16[512,1024]{1,0:T(8,128)(2,1)}, bf16[512,1024]{1,0:T(8,128)(2,1)}) custom-call(s32[1]{0:T(128)} %bitcast.z_ref, f32[16,2048]{1,0:T(8,128)} %get-tuple-element.74.rows_ref, bf16[2048,1024]{1,0:T(8,128)(2,1)} %src_ref.15), custom_call_target="tpu_custom_call" | custom-call | flops 4294967296 | bytes 6291456 | tf_op jit(solution)/shard_map/pallas_call | solution.py:330
  128.6 12.0 %collective-permute-done.3 = bf16[512,1024]{1,0:T(8,128)(2,1)} collective-permute-done((bf16[512,1024]{1,0:T(8,128)(2,1)}, bf16[512,1024]{1,0:T(8,128)(2,1)}, u32[]{:S(2)}, u32[]{:S(2)}) %collective-permute-start.3) | collective-permute-done | bytes 1048608 | tf_op jit(solution)/shard_map/ppermute | solution.py:327
  140.6 1.6 collective-permute-start.35
  142.2 9.4 %shard_map.137 = (bf16[512,1024]{1,0:T(8,128)(2,1)}, bf16[512,1024]{1,0:T(8,128)(2,1)}) custom-call(s32[1]{0:T(128)} %bitcast.z_ref, f32[16,2048]{1,0:T(8,128)} %get-tuple-element.74.rows_ref, bf16[2048,1024]{1,0:T(8,128)(2,1)} %src_ref.15), custom_call_target="tpu_custom_call" | custom-call | flops 4294967296 | bytes 6291456 | tf_op jit(solution)/shard_map/pallas_call | solution.py:330
  151.7 13.8 %collective-permute-done.38 = bf16[512,1024]{1,0:T(8,128)(2,1)} collective-permute-done((bf16[512,1024]{1,0:T(8,128)(2,1)}, bf16[512,1024]{1,0:T(8,128)(2,1)}, u32[]{:S(2)}, u32[]{:S(2)}) %collective-permute-start.38) | collective-permute-done | bytes 1048608 | tf_op jit(solution)/shard_map/ppermute | solution.py:327
  166.8 9.3 %shard_map.138 = (bf16[512,1024]{1,0:T(8,128)(2,1)}, bf16[512,1024]{1,0:T(8,128)(2,1)}) custom-call(s32[1]{0:T(128)} %bitcast.z_ref, f32[16,2048]{1,0:T(8,128)} %get-tuple-element.74.rows_ref, bf16[2048,1024]{1,0:T(8,128)(2,1)} %src_ref.15), custom_call_target="tpu_custom_call" | custom-call | flops 4294967296 | bytes 6291456 | tf_op jit(solution)/shard_map/pallas_call | solution.py:330
  176.1 63.0 %collective-permute-done.35.refs_18_.refs_12_ = bf16[4,256,512]{2,1,0:T(8,128)(2,1)} collective-permute-done((bf16[4,256,512]{2,1,0:T(8,128)(2,1)}, bf16[4,256,512]{2,1,0:T(8,128)(2,1)}, u32[]{:S(2)}, u32[]{:S(2)}) %collective-permute-start.35) | collective-permute-done | bytes 1048608 | tf_op jit(solution)/shard_map/ppermute | solution.py:322
  239.1 1.6 collective-permute-start.29
  241.2 14.3 %shard_map.131 = (f32[4,1024,256]{2,1,0:T(8,128)}, f32[4,1024,256]{2,1,0:T(8,128)}, bf16[4,1024,256]{2,1,0:T(8,128)(2,1)}, bf16[4,1024,512]{2,1,0:T(8,128)(2,1)}) custom-call(s32[1]{0:T(128)} %bitcast.z_ref, bf16[4,128,1024]{2,1,0:T(8,128)(2,1)} %bitcast.6.refs_0_, bf16[4,128,1024]{2,1,0:T(8,128)(2,1)} %bitcast.7.refs_1_, ...), custom_call_target="tpu_custom_call" | custom-call | flops 5368709120 | bytes 32000000 | tf_op jit(solution)/shard_map/pallas_call | solution.py:330
  255.5 14.3 %k_fwd_other.1 = (bf16[4,128,256]{2,1,0:T(8,128)(2,1)}, bf16[4,128,256]{2,1,0:T(8,128)(2,1)}, bf16[4,128,256]{2,1,0:T(8,128)(2,1)}, bf16[4,128,256]{2,1,0:T(8,12...) custom-call(bf16[4,128,1024]{2,1,0:T(8,128)(2,1)} %bitcast.6.refs_0_, ...), custom_call_target="tpu_custom_call" | custom-call | flops 5368709120 | bytes 32000000 | tf_op jit(solution)/shard_map/k_fwd_other/pallas_call | solution.py:391
  269.9 1.6 collective-permute-start.18
  272.3 1.3 copy.14
  273.6 1.2 collective-permute-start.21
  274.8 1.5 collective-permute-start.22
  276.3 3.1 collective-permute-done.18
  279.5 4.6 collective-permute-done.19
  285.1 1.5 collective-permute-start.11
  286.7 15.4 %shard_map.139 = (bf16[4,128,256]{2,1,0:T(8,128)(2,1)}, bf16[4,128,256]{2,1,0:T(8,128)(2,1)}, bf16[4,128,256]{2,1,0:T(8,128)(2,1)}, bf16[4,128,256]{2,1,0:T(8,12...) custom-call(s32[1]{0:T(128)} %bitcast.z_ref, ...), custom_call_target="tpu_custom_call" | custom-call | flops 6442450944 | bytes 18432000 | tf_op jit(solution)/shard_map/pallas_call | solution.py:330
  302.1 9.4 %shard_map.141 = (bf16[4,128,256]{2,1,0:T(8,128)(2,1)}, bf16[4,128,256]{2,1,0:T(8,128)(2,1)}, bf16[4,128,256]{2,1,0:T(8,128)(2,1)}, bf16[4,128,256]{2,1,0:T(8,12...) custom-call(s32[1]{0:T(128)} %bitcast.z_ref, bf16[4,128,1024]{2,1,0:T(8,128)(2,1)} %bitcast.41.refs_0_.refs_16_, ...), custom_call_target="tpu_custom_call" | custom-call | flops 2147483648 | bytes 6144000 | tf_op jit(solution)/shard_map/pallas_call | solution.py:330
  312.2 1.4 collective-permute-start.14
  313.6 1.5 collective-permute-start.15
  315.1 1.0 collective-permute-start.16
  316.1 13.9 %shard_map.133 = (bf16[2048,256]{1,0:T(8,128)(2,1)}, f32[8,2048]{1,0:T(8,128)}) custom-call(s32[1]{0:T(128)} %bitcast.z_ref, f32[2048,16]{1,0:T(8,128)} %bitcast.62, bf16[2048,1024]{1,0:T(8,128)(2,1)} %src_ref.15, bf16[512,256]{1,0:T(8,128)(2,1)} %bitcast.97, bf16[512,256]{1,0:T(8,128)(2,1)} %bitcast.78, bf16[512,256]{1,0:T(8,128)(2,1)} %bitcast.81, ...), custom_call_target="tpu_custom_call" | custom-call | flops 8589934592 | bytes 6000000 | tf_op jit(solution)/shard_map/pallas_call | solution.py:330
  330.1 1.7 collective-permute-start.47
  332.1 4.8 collective-permute-done.14
  337.8 1.4 collective-permute-start.46
  339.2 1.6 collective-permute-start.27
  340.8 13.9 %shard_map.132 = (bf16[2048,256]{1,0:T(8,128)(2,1)}, f32[8,2048]{1,0:T(8,128)}) custom-call(s32[1]{0:T(128)} %bitcast.z_ref, f32[2048,16]{1,0:T(8,128)} %bitcast.63, bf16[2048,1024]{1,0:T(8,128)(2,1)} %src_ref.15, bf16[512,256]{1,0:T(8,128)(2,1)} %bitcast.96, bf16[512,256]{1,0:T(8,128)(2,1)} %bitcast.80, bf16[512,256]{1,0:T(8,128)(2,1)} %bitcast.83, ...), custom_call_target="tpu_custom_call" | custom-call | flops 8589934592 | bytes 6000000 | tf_op jit(solution)/shard_map/pallas_call | solution.py:330
  355.8 1.7 collective-permute-start.50
  357.5 1.7 collective-permute-start.40
  360.1 2.9 shard_map.135
  363.0 12.3 %collective-permute-done.48 = bf16[4,128,256]{2,1,0:T(8,128)(2,1)} collective-permute-done((bf16[4,128,256]{2,1,0:T(8,128)(2,1)S(1)}, bf16[4,128,256]{2,1,0:T(8,128)(2,1)}, u32[]{:S(2)}, u32[]{:S(2)}) %collective-permute-start.48) | collective-permute-done | bytes 262176 | tf_op jit(solution)/shard_map/ppermute | solution.py:327
  377.0 1.8 collective-permute-start.43
  379.7 10.4 %shard_map.143.refs_1_ = bf16[2048,256]{1,0:T(8,128)(2,1)} custom-call(s32[1]{0:T(128)} %bitcast.z_ref, f32[2048,16]{1,0:T(8,128)} %bitcast.64, bf16[192,2048]{1,0:T(8,128)(2,1)} %get-tuple-element.104.dl_ref, f32[32,1024]{1,0:T(8,128)} %bitcast.71, bf16[512,256]{1,0:T(8,128)(2,1)} %bitcast.76, bf16[512,256]{1,0:T(8,128)(2,1)} %bitcast.82, ...), custom_call_target="tpu_custom_call" | custom-call | flops 4294967296 | bytes 6000000 | tf_op jit(solution)/shard_map/pallas_call | solution.py:330
  390.1 1.6 collective-permute-start.25
  392.1 4.4 collective-permute-done.41
  396.5 1.6 collective-permute-start.53
  398.1 10.0 %shard_map.142.refs_0_ = bf16[2048,256]{1,0:T(8,128)(2,1)} custom-call(s32[1]{0:T(128)} %bitcast.z_ref, f32[2048,16]{1,0:T(8,128)} %bitcast.65, bf16[192,2048]{1,0:T(8,128)(2,1)} %get-tuple-element.104.dl_ref, f32[32,1024]{1,0:T(8,128)} %bitcast.72, bf16[512,256]{1,0:T(8,128)(2,1)} %bitcast.75, bf16[512,256]{1,0:T(8,128)(2,1)} %bitcast.39.refs_1_, ...), custom_call_target="tpu_custom_call" | custom-call | flops 4294967296 | bytes 6000000 | tf_op jit(solution)/shard_map/pallas_call | solution.py:330
  408.6 1.3 collective-permute-done.54
  410.7 3.5 collective-permute-done.55
  414.2 4.2 collective-permute-done.56
  418.5 1.6 collective-permute-start.57
  420.1 14.1 %shard_map.145 = (f32[4,1024,256]{2,1,0:T(8,128)}, f32[4,1024,256]{2,1,0:T(8,128)}, f32[4,256,1024]{2,1,0:T(8,128)}) custom-call(s32[1]{0:T(128)} %bitcast.z_ref, bf16[4,128,1024]{2,1,0:T(8,128)(2,1)} %bitcast.6.refs_0_, bf16[4,128,1024]{2,1,0:T(8,128)(2,1)} %bitcast.7.refs_1_, bf16[4,128,1024]{2,1,0:T(8,128)(2,1)} %bitcast.8.refs_2_, ...), custom_call_target="tpu_custom_call" | custom-call | flops 6442450944 | bytes 40000000 | tf_op jit(solution)/shard_map/pallas_call | solution.py:330
  434.2 50.5 %collective-permute-done.57 = f32[32,512]{1,0:T(8,128)S(1)} collective-permute-done((f32[32,512]{1,0:T(8,128)S(1)}, f32[32,512]{1,0:T(8,128)S(1)}, u32[]{:S(2)}, u32[]{:S(2)}) %collective-permute-start.57) | collective-permute-done | bytes 65568 | tf_op jit(solution)/shard_map/ppermute | solution.py:322
  486.3 6.7 %shard_map.134 = bf16[2048,1024]{1,0:T(8,128)(2,1)} custom-call(s32[1]{0:T(128)} %bitcast.z_ref, bf16[2048,256]{1,0:T(8,128)(2,1)} %get-tuple-element.91.refs_0_, bf16[2048,256]{1,0:T(8,128)(2,1)} %get-tuple-element.100.refs_1_, bf16[2048,256]{1,0:T(8,128)(2,1)} %collective-permute-done.24.refs_2_, bf16[2048,256]{1,0:T(8,128)(2,1)} %copy-done.6), custom_call_target="tpu_custom_call" | custom-call | flops 1000000 | bytes 8000000 | tf_op jit(solution)/shard_map/pallas_call | solution.py:330
  493.0 6.7 %shard_map.144 = bf16[2048,1024]{1,0:T(8,128)(2,1)} custom-call(s32[1]{0:T(128)} %bitcast.z_ref, bf16[2048,256]{1,0:T(8,128)(2,1)} %shard_map.142.refs_0_, bf16[2048,256]{1,0:T(8,128)(2,1)} %shard_map.143.refs_1_, bf16[2048,256]{1,0:T(8,128)(2,1)} %collective-permute-done.52.refs_2_, bf16[2048,256]{1,0:T(8,128)(2,1)} %collective-permute-done.53.refs_3_), custom_call_target="tpu_custom_call" | custom-call | flops 1000000 | bytes 8000000 | tf_op jit(solution)/shard_map/pallas_call | solution.py:330
  (166 shorter events, 14.9 us)
Async XLA Ops:
  18.2 74.7 %collective-permute-start.5 = (bf16[512,1024]{1,0:T(8,128)(2,1)}, bf16[512,1024]{1,0:T(8,128)(2,1)}, u32[]{:S(2)}, u32[]{:S(2)}) collective-permute-start(bf16[512,1024]{1,0:T(8,128)(2,1)} %get-tuple-element.80), channel_id=1, source_target_pairs={{0,3},{1,2},{2,1},{3,0},{4,7},{5,6},{6,5},{7,4},{8,11},{9,10},{10,... | collective-permute-start | bytes 3145736 | tf_op jit(solution)/shard_map/ppermute | solution.py:327
  20.8 78.4 %collective-permute-start.6 = (bf16[512,1024]{1,0:T(8,128)(2,1)}, bf16[512,1024]{1,0:T(8,128)(2,1)}, u32[]{:S(2)}, u32[]{:S(2)}) collective-permute-start(bf16[512,1024]{1,0:T(8,128)(2,1)} %get-tuple-element.81), channel_id=1, source_target_pairs={{0,5},{1,4},{2,7},{3,6},{4,1},{5,0},{6,3},{7,2},{8,13},{9,12},{10,... | collective-permute-start | bytes 3145736 | tf_op jit(solution)/shard_map/ppermute | solution.py:327
  22.6 79.6 %collective-permute-start.1 = (bf16[512,1024]{1,0:T(8,128)(2,1)}, bf16[512,1024]{1,0:T(8,128)(2,1)}, u32[]{:S(2)}, u32[]{:S(2)}) collective-permute-start(bf16[512,1024]{1,0:T(8,128)(2,1)} %get-tuple-element.75), channel_id=1, source_target_pairs={{0,7},{1,6},{2,5},{3,4},{4,3},{5,2},{6,1},{7,0},{8,15},{9,14},{10,... | collective-permute-start | bytes 3145736 | tf_op jit(solution)/shard_map/ppermute | solution.py:327
  28.4 51.9 %collective-permute-start.28 = (bf16[512,512]{1,0:T(8,128)(2,1)}, bf16[512,512]{1,0:T(8,128)(2,1)S(1)}, u32[]{:S(2)}, u32[]{:S(2)}) collective-permute-start(bf16[512,512]{1,0:T(8,128)(2,1)} %get-tuple-element.105), channel_id=1, source_target_pairs={{0,6},{1,7},{2,4},{3,5},{4,2},{5,3},{6,0},{7,1},{8,14},{9,15},{10,... | collective-permute-start | bytes 1572872 | tf_op jit(solution)/shard_map/ppermute | solution.py:327
  30.7 60.6 %collective-permute-start.30 = (bf16[512,512]{1,0:T(8,128)(2,1)}, bf16[512,512]{1,0:T(8,128)(2,1)S(1)}, u32[]{:S(2)}, u32[]{:S(2)}) collective-permute-start(bf16[512,512]{1,0:T(8,128)(2,1)} %get-tuple-element.106), channel_id=1, source_target_pairs={{0,7},{1,6},{2,5},{3,4},{4,3},{5,2},{6,1},{7,0},{8,15},{9,14},{10,... | collective-permute-start | bytes 1572872 | tf_op jit(solution)/shard_map/ppermute | solution.py:327
  48.2 52.4 %copy-start = (bf16[4,256,1024]{2,1,0:T(8,128)(2,1)S(1)}, bf16[4,256,1024]{2,1,0:T(8,128)(2,1)}, u32[]{:S(2)}) copy-start(bf16[4,256,1024]{2,1,0:T(8,128)(2,1)} %refs_8_.3) | copy-start | bytes 6291460
  80.2 23.5 %collective-permute-start.4 = (bf16[512,1024]{1,0:T(8,128)(2,1)}, bf16[512,1024]{1,0:T(8,128)(2,1)}, u32[]{:S(2)}, u32[]{:S(2)}) collective-permute-start(bf16[512,1024]{1,0:T(8,128)(2,1)} %get-tuple-element.79), channel_id=1, source_target_pairs={{0,1},{1,0},{2,3},{3,2},{4,5},{5,4},{6,7},{7,6},{8,9},{9,8},{10,11... | collective-permute-start | bytes 3145736 | tf_op jit(solution)/shard_map/ppermute | solution.py:327
  91.4 26.3 %collective-permute-start.2 = (bf16[512,1024]{1,0:T(8,128)(2,1)}, bf16[512,1024]{1,0:T(8,128)(2,1)}, u32[]{:S(2)}, u32[]{:S(2)}) collective-permute-start(bf16[512,1024]{1,0:T(8,128)(2,1)} %get-tuple-element.76), channel_id=1, source_target_pairs={{0,2},{1,3},{2,0},{3,1},{4,6},{5,7},{6,4},{7,5},{8,10},{9,11},{10,... | collective-permute-start | bytes 3145736 | tf_op jit(solution)/shard_map/ppermute | solution.py:327
  92.9 47.7 %collective-permute-start.3 = (bf16[512,1024]{1,0:T(8,128)(2,1)}, bf16[512,1024]{1,0:T(8,128)(2,1)}, u32[]{:S(2)}, u32[]{:S(2)}) collective-permute-start(bf16[512,1024]{1,0:T(8,128)(2,1)} %get-tuple-element.77), channel_id=1, source_target_pairs={{0,4},{1,5},{2,6},{3,7},{4,0},{5,1},{6,2},{7,3},{8,12},{9,13},{10,... | collective-permute-start | bytes 3145736 | tf_op jit(solution)/shard_map/ppermute | solution.py:327
  99.1 41.4 %collective-permute-start = (bf16[512,1024]{1,0:T(8,128)(2,1)}, bf16[512,1024]{1,0:T(8,128)(2,1)}, u32[]{:S(2)}, u32[]{:S(2)}) collective-permute-start(bf16[512,1024]{1,0:T(8,128)(2,1)} %shard_map.127), channel_id=1, source_target_pairs={{0,6},{1,7},{2,4},{3,5},{4,2},{5,3},{6,0},{7,1},{8,14},{9,15},{10,... | collective-permute-start | bytes 3145736 | tf_op jit(solution)/shard_map/ppermute | solution.py:327
  102.1 38.5 %collective-permute-start.9 = (bf16[4,256,512]{2,1,0:T(8,128)(2,1)}, bf16[4,256,512]{2,1,0:T(8,128)(2,1)S(1)}, u32[]{:S(2)}, u32[]{:S(2)}) collective-permute-start(bf16[4,256,512]{2,1,0:T(8,128)(2,1)} %get-tuple-element.143), channel_id=1, source_target_pairs={{0,8},{8,0},{1,9},{9,1},{2,10},{10,2},{3,11},{11,3},{4,12},{12,4},... | collective-permute-start | bytes 3145736 | tf_op jit(solution)/shard_map/ppermute | solution.py:322
  103.7 135.4 %collective-permute-start.7 = (bf16[4,1024,256]{2,1,0:T(8,128)(2,1)}, bf16[4,1024,256]{2,1,0:T(8,128)(2,1)S(1)}, u32[]{:S(2)}, u32[]{:S(2)}) collective-permute-start(bf16[4,1024,256]{2,1,0:T(8,128)(2,1)} %refs_6_.1), channel_id=1, source_target_pairs={{0,8},{8,0},{1,9},{9,1},{2,10},{10,2},{3,11},{11,3},{4,12},{12,4},... | collective-permute-start | bytes 6291464 | tf_op jit(solution)/shard_map/ppermute | solution.py:322
  117.7 123.1 %collective-permute-start.8 = (bf16[4,1024,256]{2,1,0:T(8,128)(2,1)}, bf16[4,1024,256]{2,1,0:T(8,128)(2,1)}, u32[]{:S(2)}, u32[]{:S(2)}) collective-permute-start(bf16[4,1024,256]{2,1,0:T(8,128)(2,1)} %refs_7_.1), channel_id=1, source_target_pairs={{0,8},{8,0},{1,9},{9,1},{2,10},{10,2},{3,11},{11,3},{4,12},{12,4},... | collective-permute-start | bytes 6291464 | tf_op jit(solution)/shard_map/ppermute | solution.py:322
  140.6 24.9 %collective-permute-start.38 = (bf16[512,1024]{1,0:T(8,128)(2,1)}, bf16[512,1024]{1,0:T(8,128)(2,1)}, u32[]{:S(2)}, u32[]{:S(2)}) collective-permute-start(bf16[512,1024]{1,0:T(8,128)(2,1)} %get-tuple-element.118), channel_id=1, source_target_pairs={{0,3},{1,2},{2,1},{3,0},{4,7},{5,6},{6,5},{7,4},{8,11},{9,10},{10,... | collective-permute-start | bytes 3145736 | tf_op jit(solution)/shard_map/ppermute | solution.py:327
  140.6 25.7 %collective-permute-start.39 = (bf16[512,1024]{1,0:T(8,128)(2,1)}, bf16[512,1024]{1,0:T(8,128)(2,1)}, u32[]{:S(2)}, u32[]{:S(2)}) collective-permute-start(bf16[512,1024]{1,0:T(8,128)(2,1)} %get-tuple-element.119), channel_id=1, source_target_pairs={{0,5},{1,4},{2,7},{3,6},{4,1},{5,0},{6,3},{7,2},{8,13},{9,12},{10,... | collective-permute-start | bytes 3145736 | tf_op jit(solution)/shard_map/ppermute | solution.py:327
  140.6 98.5 %collective-permute-start.35 = (bf16[4,256,512]{2,1,0:T(8,128)(2,1)}, bf16[4,256,512]{2,1,0:T(8,128)(2,1)}, u32[]{:S(2)}, u32[]{:S(2)}) collective-permute-start(bf16[4,256,512]{2,1,0:T(8,128)(2,1)} %get-tuple-element.142), channel_id=1, source_target_pairs={{0,8},{8,0},{1,9},{9,1},{2,10},{10,2},{3,11},{11,3},{4,12},{12,4},... | collective-permute-start | bytes 3145736 | tf_op jit(solution)/shard_map/ppermute | solution.py:322
  165.5 106.0 %collective-permute-start.32 = (bf16[512,1024]{1,0:T(8,128)(2,1)}, bf16[512,1024]{1,0:T(8,128)(2,1)S(1)}, u32[]{:S(2)}, u32[]{:S(2)}) collective-permute-start(bf16[512,1024]{1,0:T(8,128)(2,1)} %get-tuple-element.107), channel_id=1, source_target_pairs={{0,2},{1,3},{2,0},{3,1},{4,6},{5,7},{6,4},{7,5},{8,10},{9,11},{10,... | collective-permute-start | bytes 3145736 | tf_op jit(solution)/shard_map/ppermute | solution.py:327
  166.2 105.6 %collective-permute-start.33 = (bf16[512,1024]{1,0:T(8,128)(2,1)}, bf16[512,1024]{1,0:T(8,128)(2,1)}, u32[]{:S(2)}, u32[]{:S(2)}) collective-permute-start(bf16[512,1024]{1,0:T(8,128)(2,1)} %get-tuple-element.108), channel_id=1, source_target_pairs={{0,4},{1,5},{2,6},{3,7},{4,0},{5,1},{6,2},{7,3},{8,12},{9,13},{10,... | collective-permute-start | bytes 3145736 | tf_op jit(solution)/shard_map/ppermute | solution.py:327
  239.1 34.4 %collective-permute-start.34 = (bf16[512,1024]{1,0:T(8,128)(2,1)}, bf16[512,1024]{1,0:T(8,128)(2,1)}, u32[]{:S(2)}, u32[]{:S(2)}) collective-permute-start(bf16[512,1024]{1,0:T(8,128)(2,1)} %get-tuple-element.110), channel_id=1, source_target_pairs={{0,1},{1,0},{2,3},{3,2},{4,5},{5,4},{6,7},{7,6},{8,9},{9,8},{10,11... | collective-permute-start | bytes 3145736 | tf_op jit(solution)/shard_map/ppermute | solution.py:327
  239.1 30.7 %collective-permute-start.29 = (bf16[512,512]{1,0:T(8,128)(2,1)}, bf16[512,512]{1,0:T(8,128)(2,1)}, u32[]{:S(2)}, u32[]{:S(2)}) collective-permute-start(bf16[512,512]{1,0:T(8,128)(2,1)} %copy-done.7), channel_id=1, source_target_pairs={{0,8},{8,0},{1,9},{9,1},{2,10},{10,2},{3,11},{11,3},{4,12},{12,4},... | collective-permute-start | bytes 1572872 | tf_op jit(solution)/shard_map/ppermute | solution.py:322
  240.8 29.2 %collective-permute-start.31 = (bf16[512,512]{1,0:T(8,128)(2,1)}, bf16[512,512]{1,0:T(8,128)(2,1)}, u32[]{:S(2)}, u32[]{:S(2)}) collective-permute-start(bf16[512,512]{1,0:T(8,128)(2,1)} %copy-done.8), channel_id=1, source_target_pairs={{0,8},{8,0},{1,9},{9,1},{2,10},{10,2},{3,11},{11,3},{4,12},{12,4},... | collective-permute-start | bytes 1572872 | tf_op jit(solution)/shard_map/ppermute | solution.py:322
  269.9 4.9 collective-permute-start.17
  269.9 9.4 %collective-permute-start.18 = (bf16[4,128,256]{2,1,0:T(8,128)(2,1)}, bf16[4,128,256]{2,1,0:T(8,128)(2,1)S(1)}, u32[]{:S(2)}, u32[]{:S(2)}) collective-permute-start(bf16[4,128,256]{2,1,0:T(8,128)(2,1)} %get-tuple-element.94), channel_id=1, source_target_pairs={{0,2},{1,3},{2,0},{3,1},{4,6},{5,7},{6,4},{7,5},{8,10},{9,11},{10,... | collective-permute-start | bytes 786440 | tf_op jit(solution)/shard_map/ppermute | solution.py:327
  271.5 12.6 %collective-permute-start.19 = (bf16[4,128,256]{2,1,0:T(8,128)(2,1)}, bf16[4,128,256]{2,1,0:T(8,128)(2,1)S(1)}, u32[]{:S(2)}, u32[]{:S(2)}) collective-permute-start(bf16[4,128,256]{2,1,0:T(8,128)(2,1)} %get-tuple-element.95), channel_id=1, source_target_pairs={{0,3},{1,2},{2,1},{3,0},{4,7},{5,6},{6,5},{7,4},{8,11},{9,10},{10,... | collective-permute-start | bytes 786440 | tf_op jit(solution)/shard_map/ppermute | solution.py:327
  271.8 13.3 %collective-permute-start.20 = (bf16[4,128,256]{2,1,0:T(8,128)(2,1)}, bf16[4,128,256]{2,1,0:T(8,128)(2,1)S(1)}, u32[]{:S(2)}, u32[]{:S(2)}) collective-permute-start(bf16[4,128,256]{2,1,0:T(8,128)(2,1)} %get-tuple-element.96), channel_id=1, source_target_pairs={{0,4},{1,5},{2,6},{3,7},{4,0},{5,1},{6,2},{7,3},{8,12},{9,13},{10,... | collective-permute-start | bytes 786440 | tf_op jit(solution)/shard_map/ppermute | solution.py:327
  273.6 37.9 %collective-permute-start.21 = (bf16[4,128,256]{2,1,0:T(8,128)(2,1)}, bf16[4,128,256]{2,1,0:T(8,128)(2,1)S(1)}, u32[]{:S(2)}, u32[]{:S(2)}) collective-permute-start(bf16[4,128,256]{2,1,0:T(8,128)(2,1)} %get-tuple-element.97), channel_id=1, source_target_pairs={{0,5},{1,4},{2,7},{3,6},{4,1},{5,0},{6,3},{7,2},{8,13},{9,12},{10,... | collective-permute-start | bytes 786440 | tf_op jit(solution)/shard_map/ppermute | solution.py:327
  274.8 27.2 %copy-start.28 = (bf16[4,128,256]{2,1,0:T(8,128)(2,1)}, bf16[4,128,256]{2,1,0:T(8,128)(2,1)S(1)}, u32[]{:S(2)}) copy-start(bf16[4,128,256]{2,1,0:T(8,128)(2,1)S(1)} %collective-permute-done.17) | copy-start | bytes 786436
  274.8 36.8 %collective-permute-start.22 = (bf16[4,128,256]{2,1,0:T(8,128)(2,1)}, bf16[4,128,256]{2,1,0:T(8,128)(2,1)S(1)}, u32[]{:S(2)}, u32[]{:S(2)}) collective-permute-start(bf16[4,128,256]{2,1,0:T(8,128)(2,1)} %get-tuple-element.98), channel_id=1, source_target_pairs={{0,6},{1,7},{2,4},{3,5},{4,2},{5,3},{6,0},{7,1},{8,14},{9,15},{10,... | collective-permute-start | bytes 786440 | tf_op jit(solution)/shard_map/ppermute | solution.py:327
  279.4 32.8 %collective-permute-start.23 = (bf16[4,128,256]{2,1,0:T(8,128)(2,1)}, bf16[4,128,256]{2,1,0:T(8,128)(2,1)}, u32[]{:S(2)}, u32[]{:S(2)}) collective-permute-start(bf16[4,128,256]{2,1,0:T(8,128)(2,1)} %get-tuple-element.99), channel_id=1, source_target_pairs={{0,7},{1,6},{2,5},{3,4},{4,3},{5,2},{6,1},{7,0},{8,15},{9,14},{10,... | collective-permute-start | bytes 786440 | tf_op jit(solution)/shard_map/ppermute | solution.py:327
  284.2 29.4 %collective-permute-start.10 = (bf16[4,128,256]{2,1,0:T(8,128)(2,1)}, bf16[4,128,256]{2,1,0:T(8,128)(2,1)S(1)}, u32[]{:S(2)}, u32[]{:S(2)}) collective-permute-start(bf16[4,128,256]{2,1,0:T(8,128)(2,1)} %get-tuple-element.84), channel_id=1, source_target_pairs={{0,1},{1,0},{2,3},{3,2},{4,5},{5,4},{6,7},{7,6},{8,9},{9,8},{10,11... | collective-permute-start | bytes 786440 | tf_op jit(solution)/shard_map/ppermute | solution.py:327
  285.1 30.0 %collective-permute-start.11 = (bf16[4,128,256]{2,1,0:T(8,128)(2,1)}, bf16[4,128,256]{2,1,0:T(8,128)(2,1)S(1)}, u32[]{:S(2)}, u32[]{:S(2)}) collective-permute-start(bf16[4,128,256]{2,1,0:T(8,128)(2,1)} %get-tuple-element.85), channel_id=1, source_target_pairs={{0,2},{1,3},{2,0},{3,1},{4,6},{5,7},{6,4},{7,5},{8,10},{9,11},{10,... | collective-permute-start | bytes 786440 | tf_op jit(solution)/shard_map/ppermute | solution.py:327
  311.5 18.5 %collective-permute-start.12 = (bf16[4,128,256]{2,1,0:T(8,128)(2,1)S(1)}, bf16[4,128,256]{2,1,0:T(8,128)(2,1)S(1)}, u32[]{:S(2)}, u32[]{:S(2)}) collective-permute-start(bf16[4,128,256]{2,1,0:T(8,128)(2,1)S(1)} %copy-done.24), channel_id=1, source_target_pairs={{0,3},{1,2},{2,1},{3,0},{4,7},{5,6},{6,5},{7,4},{8,11},{9,10},{10,... | collective-permute-start | bytes 786440 | tf_op jit(solution)/shard_map/ppermute | solution.py:327
  311.6 20.4 %collective-permute-start.13 = (bf16[4,128,256]{2,1,0:T(8,128)(2,1)S(1)}, bf16[4,128,256]{2,1,0:T(8,128)(2,1)S(1)}, u32[]{:S(2)}, u32[]{:S(2)}) collective-permute-start(bf16[4,128,256]{2,1,0:T(8,128)(2,1)S(1)} %copy-done.23), channel_id=1, source_target_pairs={{0,4},{1,5},{2,6},{3,7},{4,0},{5,1},{6,2},{7,3},{8,12},{9,13},{10,... | collective-permute-start | bytes 786440 | tf_op jit(solution)/shard_map/ppermute | solution.py:327
  312.2 24.7 %collective-permute-start.14 = (bf16[4,128,256]{2,1,0:T(8,128)(2,1)S(1)}, bf16[4,128,256]{2,1,0:T(8,128)(2,1)S(1)}, u32[]{:S(2)}, u32[]{:S(2)}) collective-permute-start(bf16[4,128,256]{2,1,0:T(8,128)(2,1)S(1)} %copy-done.22), channel_id=1, source_target_pairs={{0,5},{1,4},{2,7},{3,6},{4,1},{5,0},{6,3},{7,2},{8,13},{9,12},{10,... | collective-permute-start | bytes 786440 | tf_op jit(solution)/shard_map/ppermute | solution.py:327
  313.6 24.2 %collective-permute-start.15 = (bf16[4,128,256]{2,1,0:T(8,128)(2,1)S(1)}, bf16[4,128,256]{2,1,0:T(8,128)(2,1)}, u32[]{:S(2)}, u32[]{:S(2)}) collective-permute-start(bf16[4,128,256]{2,1,0:T(8,128)(2,1)S(1)} %copy-done.21), channel_id=1, source_target_pairs={{0,6},{1,7},{2,4},{3,5},{4,2},{5,3},{6,0},{7,1},{8,14},{9,15},{10,... | collective-permute-start | bytes 786440 | tf_op jit(solution)/shard_map/ppermute | solution.py:327
  315.1 24.1 %collective-permute-start.16 = (bf16[4,128,256]{2,1,0:T(8,128)(2,1)S(1)}, bf16[4,128,256]{2,1,0:T(8,128)(2,1)}, u32[]{:S(2)}, u32[]{:S(2)}) collective-permute-start(bf16[4,128,256]{2,1,0:T(8,128)(2,1)S(1)} %copy-done.19), channel_id=1, source_target_pairs={{0,7},{1,6},{2,5},{3,4},{4,3},{5,2},{6,1},{7,0},{8,15},{9,14},{10,... | collective-permute-start | bytes 786440 | tf_op jit(solution)/shard_map/ppermute | solution.py:327
  330.1 24.7 %collective-permute-start.47 = (bf16[4,128,256]{2,1,0:T(8,128)(2,1)}, bf16[4,128,256]{2,1,0:T(8,128)(2,1)S(1)}, u32[]{:S(2)}, u32[]{:S(2)}) collective-permute-start(bf16[4,128,256]{2,1,0:T(8,128)(2,1)} %get-tuple-element.128), channel_id=1, source_target_pairs={{0,3},{1,2},{2,1},{3,0},{4,7},{5,6},{6,5},{7,4},{8,11},{9,10},{10,... | collective-permute-start | bytes 786440 | tf_op jit(solution)/shard_map/ppermute | solution.py:327
  332.1 23.2 %collective-permute-start.49 = (bf16[4,128,256]{2,1,0:T(8,128)(2,1)}, bf16[4,128,256]{2,1,0:T(8,128)(2,1)S(1)}, u32[]{:S(2)}, u32[]{:S(2)}) collective-permute-start(bf16[4,128,256]{2,1,0:T(8,128)(2,1)} %get-tuple-element.130), channel_id=1, source_target_pairs={{0,5},{1,4},{2,7},{3,6},{4,1},{5,0},{6,3},{7,2},{8,13},{9,12},{10,... | collective-permute-start | bytes 786440 | tf_op jit(solution)/shard_map/ppermute | solution.py:327
  336.9 18.9 %collective-permute-start.45 = (bf16[4,128,256]{2,1,0:T(8,128)(2,1)S(1)}, bf16[4,128,256]{2,1,0:T(8,128)(2,1)S(1)}, u32[]{:S(2)}, u32[]{:S(2)}) collective-permute-start(bf16[4,128,256]{2,1,0:T(8,128)(2,1)S(1)} %copy-done.26), channel_id=1, source_target_pairs={{0,1},{1,0},{2,3},{3,2},{4,5},{5,4},{6,7},{7,6},{8,9},{9,8},{10,11... | collective-permute-start | bytes 786440 | tf_op jit(solution)/shard_map/ppermute | solution.py:327
  337.8 19.6 %collective-permute-start.46 = (bf16[4,128,256]{2,1,0:T(8,128)(2,1)S(1)}, bf16[4,128,256]{2,1,0:T(8,128)(2,1)}, u32[]{:S(2)}, u32[]{:S(2)}) collective-permute-start(bf16[4,128,256]{2,1,0:T(8,128)(2,1)S(1)} %copy-done.25), channel_id=1, source_target_pairs={{0,2},{1,3},{2,0},{3,1},{4,6},{5,7},{6,4},{7,5},{8,10},{9,11},{10,... | collective-permute-start | bytes 786440 | tf_op jit(solution)/shard_map/ppermute | solution.py:327
  339.2 18.3 %collective-permute-start.27 = (f32[8,2048]{1,0:T(8,128)}, f32[8,2048]{1,0:T(8,128)S(1)}, u32[]{:S(2)}, u32[]{:S(2)}) collective-permute-start(f32[8,2048]{1,0:T(8,128)} %get-tuple-element.103.refs_1_), channel_id=1, source_target_pairs={{0,8},{8,0},{1,9},{9,1},{2,10},{10,2},{3,11},{11,3},{4,12},{12,4},... | collective-permute-start | bytes 196616 | tf_op jit(solution)/shard_map/ppermute | solution.py:322
  354.7 24.1 %copy-start.13 = (bf16[4,128,256]{2,1,0:T(8,128)(2,1)S(1)}, bf16[4,128,256]{2,1,0:T(8,128)(2,1)}, u32[]{:S(2)}) copy-start(bf16[4,128,256]{2,1,0:T(8,128)(2,1)} %get-tuple-element.124) | copy-start | bytes 786436
  354.7 24.9 %copy-start.27 = (bf16[4,128,256]{2,1,0:T(8,128)(2,1)}, bf16[4,128,256]{2,1,0:T(8,128)(2,1)S(1)}, u32[]{:S(2)}) copy-start(bf16[4,128,256]{2,1,0:T(8,128)(2,1)S(1)} %collective-permute-done.47) | copy-start | bytes 786436
  354.8 4.5 collective-permute-start.26
  355.2 24.4 %copy-start.29 = (bf16[4,128,256]{2,1,0:T(8,128)(2,1)}, bf16[4,128,256]{2,1,0:T(8,128)(2,1)S(1)}, u32[]{:S(2)}) copy-start(bf16[4,128,256]{2,1,0:T(8,128)(2,1)S(1)} %collective-permute-done.49) | copy-start | bytes 786436
  355.2 20.1 %collective-permute-start.48 = (bf16[4,128,256]{2,1,0:T(8,128)(2,1)S(1)}, bf16[4,128,256]{2,1,0:T(8,128)(2,1)}, u32[]{:S(2)}, u32[]{:S(2)}) collective-permute-start(bf16[4,128,256]{2,1,0:T(8,128)(2,1)S(1)} %copy-done.20), channel_id=1, source_target_pairs={{0,4},{1,5},{2,6},{3,7},{4,0},{5,1},{6,2},{7,3},{8,12},{9,13},{10,... | collective-permute-start | bytes 786440 | tf_op jit(solution)/shard_map/ppermute | solution.py:327
  355.8 23.8 %copy-start.32 = (bf16[4,128,256]{2,1,0:T(8,128)(2,1)}, bf16[4,128,256]{2,1,0:T(8,128)(2,1)S(1)}, u32[]{:S(2)}) copy-start(bf16[4,128,256]{2,1,0:T(8,128)(2,1)S(1)} %collective-permute-done.45) | copy-start | bytes 786436
  355.8 19.5 %collective-permute-start.50 = (bf16[4,128,256]{2,1,0:T(8,128)(2,1)S(1)}, bf16[4,128,256]{2,1,0:T(8,128)(2,1)}, u32[]{:S(2)}, u32[]{:S(2)}) collective-permute-start(bf16[4,128,256]{2,1,0:T(8,128)(2,1)S(1)} %copy-done.18), channel_id=1, source_target_pairs={{0,6},{1,7},{2,4},{3,5},{4,2},{5,3},{6,0},{7,1},{8,14},{9,15},{10,... | collective-permute-start | bytes 786440 | tf_op jit(solution)/shard_map/ppermute | solution.py:327
  357.5 18.6 %collective-permute-start.51 = (bf16[4,128,256]{2,1,0:T(8,128)(2,1)S(1)}, bf16[4,128,256]{2,1,0:T(8,128)(2,1)}, u32[]{:S(2)}, u32[]{:S(2)}) collective-permute-start(bf16[4,128,256]{2,1,0:T(8,128)(2,1)S(1)} %copy-done.16), channel_id=1, source_target_pairs={{0,7},{1,6},{2,5},{3,4},{4,3},{5,2},{6,1},{7,0},{8,15},{9,14},{10,... | collective-permute-start | bytes 786440 | tf_op jit(solution)/shard_map/ppermute | solution.py:327
  357.5 19.5 %collective-permute-start.40 = (bf16[4,128,256]{2,1,0:T(8,128)(2,1)S(1)}, bf16[4,128,256]{2,1,0:T(8,128)(2,1)S(1)}, u32[]{:S(2)}, u32[]{:S(2)}) collective-permute-start(bf16[4,128,256]{2,1,0:T(8,128)(2,1)S(1)} %copy-done.17), channel_id=1, source_target_pairs={{0,3},{1,2},{2,1},{3,0},{4,7},{5,6},{6,5},{7,4},{8,11},{9,10},{10,... | collective-permute-start | bytes 786440 | tf_op jit(solution)/shard_map/ppermute | solution.py:327
  359.3 19.6 %collective-permute-start.42 = (bf16[4,128,256]{2,1,0:T(8,128)(2,1)S(1)}, bf16[4,128,256]{2,1,0:T(8,128)(2,1)S(1)}, u32[]{:S(2)}, u32[]{:S(2)}) collective-permute-start(bf16[4,128,256]{2,1,0:T(8,128)(2,1)S(1)} %copy-done.15), channel_id=1, source_target_pairs={{0,5},{1,4},{2,7},{3,6},{4,1},{5,0},{6,3},{7,2},{8,13},{9,12},{10,... | collective-permute-start | bytes 786440 | tf_op jit(solution)/shard_map/ppermute | solution.py:327
  375.3 14.7 %collective-permute-start.36 = (bf16[4,128,256]{2,1,0:T(8,128)(2,1)S(1)}, bf16[4,128,256]{2,1,0:T(8,128)(2,1)}, u32[]{:S(2)}, u32[]{:S(2)}) collective-permute-start(bf16[4,128,256]{2,1,0:T(8,128)(2,1)S(1)} %copy-done.14), channel_id=1, source_target_pairs={{0,1},{1,0},{2,3},{3,2},{4,5},{5,4},{6,7},{7,6},{8,9},{9,8},{10,11... | collective-permute-start | bytes 786440 | tf_op jit(solution)/shard_map/ppermute | solution.py:327
  375.3 16.3 %collective-permute-start.37 = (bf16[4,128,256]{2,1,0:T(8,128)(2,1)}, bf16[4,128,256]{2,1,0:T(8,128)(2,1)}, u32[]{:S(2)}, u32[]{:S(2)}) collective-permute-start(bf16[4,128,256]{2,1,0:T(8,128)(2,1)} %get-tuple-element.117), channel_id=1, source_target_pairs={{0,2},{1,3},{2,0},{3,1},{4,6},{5,7},{6,4},{7,5},{8,10},{9,11},{10,... | collective-permute-start | bytes 786440 | tf_op jit(solution)/shard_map/ppermute | solution.py:327
  376.0 20.5 %collective-permute-start.41 = (bf16[4,128,256]{2,1,0:T(8,128)(2,1)}, bf16[4,128,256]{2,1,0:T(8,128)(2,1)}, u32[]{:S(2)}, u32[]{:S(2)}) collective-permute-start(bf16[4,128,256]{2,1,0:T(8,128)(2,1)} %get-tuple-element.121), channel_id=1, source_target_pairs={{0,4},{1,5},{2,6},{3,7},{4,0},{5,1},{6,2},{7,3},{8,12},{9,13},{10,... | collective-permute-start | bytes 786440 | tf_op jit(solution)/shard_map/ppermute | solution.py:327
  377.0 21.1 %collective-permute-start.43 = (bf16[4,128,256]{2,1,0:T(8,128)(2,1)}, bf16[4,128,256]{2,1,0:T(8,128)(2,1)}, u32[]{:S(2)}, u32[]{:S(2)}) collective-permute-start(bf16[4,128,256]{2,1,0:T(8,128)(2,1)} %get-tuple-element.123), channel_id=1, source_target_pairs={{0,6},{1,7},{2,4},{3,5},{4,2},{5,3},{6,0},{7,1},{8,14},{9,15},{10,... | collective-permute-start | bytes 786440 | tf_op jit(solution)/shard_map/ppermute | solution.py:327
  378.9 19.2 %collective-permute-start.44 = (bf16[4,128,256]{2,1,0:T(8,128)(2,1)S(1)}, bf16[4,128,256]{2,1,0:T(8,128)(2,1)}, u32[]{:S(2)}, u32[]{:S(2)}) collective-permute-start(bf16[4,128,256]{2,1,0:T(8,128)(2,1)S(1)} %copy-done.13), channel_id=1, source_target_pairs={{0,7},{1,6},{2,5},{3,4},{4,3},{5,2},{6,1},{7,0},{8,15},{9,14},{10,... | collective-permute-start | bytes 786440 | tf_op jit(solution)/shard_map/ppermute | solution.py:327
  390.1 95.3 %collective-permute-start.25 = (bf16[2048,256]{1,0:T(8,128)(2,1)S(1)}, bf16[2048,256]{1,0:T(8,128)(2,1)S(1)}, u32[]{:S(2)}, u32[]{:S(2)}) collective-permute-start(bf16[2048,256]{1,0:T(8,128)(2,1)S(1)} %copy-done.4), channel_id=1, source_target_pairs={{0,8},{8,0},{1,9},{9,1},{2,10},{10,2},{3,11},{11,3},{4,12},{12,4},... | collective-permute-start | bytes 3145736 | tf_op jit(solution)/shard_map/ppermute | solution.py:322
  391.6 93.7 %collective-permute-start.24 = (bf16[2048,256]{1,0:T(8,128)(2,1)S(1)}, bf16[2048,256]{1,0:T(8,128)(2,1)}, u32[]{:S(2)}, u32[]{:S(2)}) collective-permute-start(bf16[2048,256]{1,0:T(8,128)(2,1)S(1)} %copy-done.5), channel_id=1, source_target_pairs={{0,8},{8,0},{1,9},{9,1},{2,10},{10,2},{3,11},{11,3},{4,12},{12,4},... | collective-permute-start | bytes 3145736 | tf_op jit(solution)/shard_map/ppermute | solution.py:322
  396.5 96.5 %collective-permute-start.53 = (bf16[2048,256]{1,0:T(8,128)(2,1)}, bf16[2048,256]{1,0:T(8,128)(2,1)}, u32[]{:S(2)}, u32[]{:S(2)}) collective-permute-start(bf16[2048,256]{1,0:T(8,128)(2,1)} %shard_map.143.refs_1_), channel_id=1, source_target_pairs={{0,8},{8,0},{1,9},{9,1},{2,10},{10,2},{3,11},{11,3},{4,12},{12,4},... | collective-permute-start | bytes 3145736 | tf_op jit(solution)/shard_map/ppermute | solution.py:322
  408.1 84.9 %collective-permute-start.52 = (bf16[2048,256]{1,0:T(8,128)(2,1)}, bf16[2048,256]{1,0:T(8,128)(2,1)}, u32[]{:S(2)}, u32[]{:S(2)}) collective-permute-start(bf16[2048,256]{1,0:T(8,128)(2,1)} %shard_map.142.refs_0_), channel_id=1, source_target_pairs={{0,8},{8,0},{1,9},{9,1},{2,10},{10,2},{3,11},{11,3},{4,12},{12,4},... | collective-permute-start | bytes 3145736 | tf_op jit(solution)/shard_map/ppermute | solution.py:322
  408.6 1.3 collective-permute-start.54
  409.8 4.3 collective-permute-start.55
  414.1 4.3 collective-permute-start.56
  418.5 66.2 %collective-permute-start.57 = (f32[32,512]{1,0:T(8,128)S(1)}, f32[32,512]{1,0:T(8,128)S(1)}, u32[]{:S(2)}, u32[]{:S(2)}) collective-permute-start(f32[32,512]{1,0:T(8,128)S(1)} %add.19), channel_id=1, source_target_pairs={{0,8},{8,0},{1,9},{9,1},{2,10},{10,2},{3,11},{11,3},{4,12},{12,4},... | collective-permute-start | bytes 196616 | tf_op jit(solution)/shard_map/ppermute | solution.py:322
  (37 other events, 451.9 us)
where the time goes:
time: 501 us; the launch traced here: 500 us
  waiting for transfers between devices  235 us (47%)
  Pallas kernels  205 us (41%)
  starting transfers between devices  52.4 us (10%)
    pallas_call x19, Pallas kernels, call(): pl.pallas_call(kernel, grid_spec=pltpu.PrefetchScalarGridSpec(num_scalar_...  186 us
    ppermute x45, waiting for transfers between devices, to_peer(): return lax.ppermute(val, 'ep', [(i, i ^ d) for i in range(n_src)])  122 us
    ppermute x13, waiting for transfers between devices, across(): return lax.ppermute(val, 'tp', swap)  114 us
    ppermute x45, starting transfers between devices, to_peer(): return lax.ppermute(val, 'ep', [(i, i ^ d) for i in range(n_src)])  37.3 us
    ppermute x13, starting transfers between devices, across(): return lax.ppermute(val, 'tp', swap)  15.1 us
    pallas_call x1, Pallas kernels, local_step(): pl.pallas_call(functools.partial(forward_other_kernel, n_src=n_src, n_chu...  14.3 us
  transfers between devices with their start and end apart: 58, of which 18 were waited for; matrix products, arithmetic and copies ran while one was open for 1% of the time, Pallas kernels for 36%

commit v1 on v0

v1 whole, which is shorter than its diff:
```python
import functools

import jax
import jax.numpy as jnp
from jax import lax
from jax.experimental import pallas as pl
from jax.experimental.pallas import tpu as pltpu
from jax.sharding import PartitionSpec as P


GELU_COEF = 0.7978845608028654
F32 = jnp.float32
BF16 = jnp.bfloat16
NT = (((1,), (1,)), ((), ()))
TN = (((0,), (0,)), ((), ()))
TILE = 256
GATHER_TILE = 256
GROUP = 2
TOKEN_TILE = 512


def gelu_parts(pre_act):
    inner_arg = GELU_COEF * (pre_act + 0.044715 * pre_act * pre_act * pre_act)
    tanh_val = jnp.tanh(inner_arg)
    gelu_val = 0.5 * pre_act * (1.0 + tanh_val)
    gelu_slope = 0.5 * (1.0 + tanh_val) + 0.5 * pre_act * (1.0 - tanh_val * tanh_val) * GELU_COEF * (1.0 + 0.134145 * pre_act * pre_act)
    return gelu_val, gelu_slope


def split3(val):
    high = val.astype(BF16)
    rest = val - high.astype(F32)
    mid = rest.astype(BF16)
    return high, mid, (rest - mid.astype(F32)).astype(BF16)


def route_kernel(me_ref, x_ref, wt_ref, one_ref, two_ref, rows_ref, prob_ref, first_ref, *, slot_cap, own_experts, peer):
    n_experts, n_tokens = prob_ref.shape
    pieces = jnp.concatenate(split3(wt_ref[...]), axis=0)
    raw = lax.dot_general(pieces, x_ref[...], NT, preferred_element_type=F32)
    logits = raw[:n_experts] + raw[n_experts:2 * n_experts] + raw[2 * n_experts:]
    expo = jnp.exp(logits - jnp.max(logits, axis=0, keepdims=True))
    prob = expo / jnp.sum(expo, axis=0, keepdims=True)
    prob_ref[...] = prob
    expert = lax.broadcasted_iota(jnp.int32, (n_experts, n_tokens), 0)
    id_one, id_two = one_ref[...], two_ref[...]
    hot_one = jnp.where(id_one == expert, 1.0, 0.0)
    hot_two = jnp.where(id_two == expert, 1.0, 0.0)
    hots = jnp.concatenate([hot_one, hot_two], axis=0)
    before = lax.broadcasted_iota(jnp.int32, (TILE, TILE), 0) < lax.broadcasted_iota(jnp.int32, (TILE, TILE), 1)
    tri = jnp.where(before, 1.0, 0.0).astype(BF16)
    run = jnp.zeros((2 * n_experts, 1), F32)
    counts = []
    for b in range(n_tokens // TILE):
        part = hots[:, b * TILE:(b + 1) * TILE]
        counts.append(jnp.dot(part.astype(BF16), tri, preferred_element_type=F32) + run)
        run = run + jnp.sum(part, axis=1, keepdims=True)
    count = jnp.concatenate(counts, axis=1)
    pos_one = jnp.sum(count[:n_experts] * hot_one, axis=0, keepdims=True)
    pos_two = jnp.sum((count[n_experts:] + run[:n_experts]) * hot_two, axis=0, keepdims=True)
    prob_one = jnp.sum(prob * hot_one, axis=0, keepdims=True)
    prob_two = jnp.sum(prob * hot_two, axis=0, keepdims=True)
    turn = me_ref[0] * (own_experts * slot_cap)

    def slot_of(ids, pos):
        place = pos.astype(jnp.int32)
        slot = jnp.where(place < slot_cap, ids * slot_cap + place, n_experts * slot_cap)
        return jnp.bitwise_xor(slot, turn).astype(F32)

    gate_sum = prob_one + prob_two
    slot_one, slot_two = slot_of(id_one, pos_one), slot_of(id_two, pos_two)
    block = first_ref.shape[0]
    slot = (peer * block + lax.broadcasted_iota(jnp.int32, (block, n_tokens), 0)).astype(F32)
    hit = jnp.logical_or(slot_one == slot, slot_two == slot)
    first_ref[...] = jnp.dot(jnp.where(hit, 1.0, 0.0).astype(BF16), x_ref[...], preferred_element_type=F32).astype(BF16)
    rows_ref[...] = jnp.concatenate(
        [slot_one, slot_two, prob_one / gate_sum, prob_two / gate_sum, prob_one, prob_two, jnp.zeros((10, n_tokens), F32)],
        axis=0)


def gather_kernel(z_ref, rows_ref, src_ref, *outs, peers, per, scaled):
    step = pl.program_id(0)
    n_tokens = src_ref.shape[0]
    peer = sum(jnp.where(step // per == i, d, 0) for i, d in enumerate(peers))
    slot = (peer * per + step % per) * GATHER_TILE + lax.broadcasted_iota(jnp.int32, (GATHER_TILE, n_tokens), 0)
    slot = slot.astype(F32)
    hit_one = rows_ref[0:1, :] == slot
    hit_two = rows_ref[1:2, :] == slot
    pick = jnp.where(jnp.logical_or(hit_one, hit_two), 1.0, 0.0).astype(BF16)
    val = jnp.dot(pick, src_ref[...], preferred_element_type=F32)
    if scaled:
        gate = jnp.where(hit_one, rows_ref[2:3, :], 0.0) + jnp.where(hit_two, rows_ref[3:4, :], 0.0)
        val = jnp.sum(gate, axis=1, keepdims=True) * val
    val = val.astype(BF16)
    for i, out in enumerate(outs):
        @pl.when(step // per == i)
        def _(out=out):
            out[...] = val


def forward_own_kernel(z_ref, *refs, n_src, cols):
    xs = refs[:n_src]
    wa, wb, wc, gv_ref, sv_ref, h_ref, part_ref = refs[n_src:]
    cap = xs[0].shape[1]
    col = pl.ds(pl.multiple_of(z_ref[0] * cols, cols), cols)
    group = GROUP
    for first in range(0, n_src, group):
        x = jnp.concatenate([r[0] for r in xs[first:first + group]], axis=0)
        rows = slice(first * cap, (first + group) * cap)
        pre_a = jnp.dot(x, wa[0], preferred_element_type=F32)
        pre_b = jnp.dot(x, wb[0], preferred_element_type=F32)
        gelu_val, gelu_slope = gelu_parts(pre_a)
        hidden = (gelu_val * pre_b).astype(BF16)
        gv_ref[0, rows, :] = gelu_val
        sv_ref[0, rows, :] = pre_b * gelu_slope
        h_ref[0, rows, :] = hidden
        part_ref[0, rows, :] = jnp.dot(hidden, wc[0, :, col], preferred_element_type=F32).astype(BF16)


def forward_other_kernel(*refs, n_src, n_chunk):
    xs = refs[:n_src]
    part_ref, part2_ref, wa, wb, wc = refs[n_src:n_src + 5]
    outs = refs[n_src + 5:n_src + 5 + n_chunk * n_src]
    gv_ref, sv_ref = refs[n_src + 5 + n_chunk * n_src:]
    parts = jnp.concatenate([part_ref[0], part2_ref[0]], axis=0)
    cap = xs[0].shape[1]
    wide = outs[0].shape[2]
    group = GROUP
    for first in range(0, n_src, GROUP):
        x = jnp.concatenate([r[0] for r in xs[first:first + GROUP]], axis=0)
        rows = slice(first * cap, (first + GROUP) * cap)
        pre_a = jnp.dot(x, wa[0], preferred_element_type=F32)
        pre_b = jnp.dot(x, wb[0], preferred_element_type=F32)
        gelu_val, gelu_slope = gelu_parts(pre_a)
        hidden = (gelu_val * pre_b).astype(BF16)
        gv_ref[0, rows, :] = gelu_val
        sv_ref[0, rows, :] = pre_b * gelu_slope
        part = jnp.dot(hidden, wc[0], preferred_element_type=F32).astype(BF16).astype(F32)
        total = (parts[rows].astype(F32) + part).astype(BF16)
        for c in range(n_chunk):
            for i in range(group):
                outs[c * n_src + first + i][0] = total[i * cap:(i + 1) * cap, c * wide:(c + 1) * wide]


def put_rows(z, rows, ref, dest):
    if len(ref) == 1:
        dest[rows, :] = ref[0][0]
        return
    cols = ref[0].shape[2]
    dest[rows, pl.ds(pl.multiple_of(z * cols, cols), cols)] = ref[0][0]
    dest[rows, pl.ds(pl.multiple_of((1 - z) * cols, cols), cols)] = ref[1][0]


def group_refs(refs, widths):
    groups, at = [], 0
    for w in widths:
        groups.append(refs[at:at + w])
        at += w
    return groups, refs[at:]


def backward_kernel(z_ref, *refs, widths, saved_widths, cols, n_chunk):
    dos, refs = group_refs(refs, widths)
    n_src = len(widths)
    saved, refs = group_refs(refs, saved_widths)
    wa, wb, wc, wa2, wb2, wcz, wcn = refs[:7]
    outs = refs[7:7 + n_chunk * n_src]
    da_ref, db_ref, do_ref = refs[7 + n_chunk * n_src:]
    gv, sv, gv2, sv2 = [jnp.concatenate([r[0] for r in group], axis=0) if len(group) > 1 else group[0][0] for group in saved]
    cap = dos[0][0].shape[1]
    z = z_ref[0]
    near = pl.ds(pl.multiple_of(z * cols, cols), cols)
    far = pl.ds(pl.multiple_of((1 - z) * cols, cols), cols)
    wide = cols // n_chunk
    group = GROUP
    for first in range(0, n_src, group):
        rows = slice(first * cap, (first + group) * cap)
        for i in range(first, first + group):
            put_rows(z, slice(i * cap, (i + 1) * cap), dos[i], do_ref)
        total = None
        for k, (a_ref, b_ref, slope, gelu) in enumerate(((wa, wb, sv, gv), (wa2, wb2, sv2, gv2))):
            if k == 0:
                dhid = lax.dot_general(do_ref[rows, :], wc[0], NT, preferred_element_type=F32)
            else:
                dhid = lax.dot_general(do_ref[rows, near], wcz[0], NT, preferred_element_type=F32)
                dhid = dhid + lax.dot_general(do_ref[rows, far], wcn[0], NT, preferred_element_type=F32)
            grad_a = (dhid * slope[rows]).astype(BF16)
            grad_b = (dhid * gelu[rows]).astype(BF16)
            if k == 0:
                da_ref[0, rows, :] = grad_a
                db_ref[0, rows, :] = grad_b
            part = lax.dot_general(grad_a, a_ref[0, near, :], NT, preferred_element_type=F32)
            part = part + lax.dot_general(grad_b, b_ref[0, near, :], NT, preferred_element_type=F32)
            part = part.astype(BF16).astype(F32)
            total = part if total is None else total + part
        total = total.astype(BF16)
        for c in range(n_chunk):
            for i in range(group):
                outs[c * n_src + first + i][0] = total[i * cap:(i + 1) * cap, c * wide:(c + 1) * wide]


def weight_grad_kernel(z_ref, *refs, n_src, widths):
    xs = refs[:n_src]
    dos, refs = group_refs(refs[n_src:], widths)
    h_ref, h2_ref, da_ref, da2_ref, db_ref, db2_ref, ga_ref, gb_ref, gc_ref, do_ref = refs
    cap = xs[0].shape[1]
    for i, ref in enumerate(dos):
        put_rows(z_ref[0], slice(i * cap, (i + 1) * cap), ref, do_ref)
    x = jnp.concatenate([r[0] for r in xs], axis=0)
    grad_a = jnp.concatenate([da_ref[0], da2_ref[0]], axis=0)
    grad_b = jnp.concatenate([db_ref[0], db2_ref[0]], axis=0)
    ga_ref[0] = lax.dot_general(x, grad_a, TN, preferred_element_type=F32)
    gb_ref[0] = lax.dot_general(x, grad_b, TN, preferred_element_type=F32)
    gc_ref[0] = lax.dot_general(jnp.concatenate([h_ref[0], h2_ref[0]], axis=0), do_ref[...], TN, preferred_element_type=F32)


def slot_picks(cols_ref):
    lane = lax.broadcasted_iota(jnp.int32, (TOKEN_TILE, 128), 1).astype(F32)
    picks = []
    for k in range(2):
        slot = cols_ref[:, k:k + 1]
        blk = jnp.floor(slot * (1.0 / 128.0))
        hot = jnp.where(slot - 128.0 * blk == lane, 1.0, 0.0).astype(BF16)
        picks.append((jnp.broadcast_to(blk, (TOKEN_TILE, 128)).astype(BF16), hot))
    return picks


def combine_out_kernel(z_ref, cols_ref, dy_ref, *refs, n_src):
    srcs = refs[:n_src]
    y_ref, dg_ref = refs[n_src:]
    blocks = srcs[0].shape[0] // 128
    picks = slot_picks(cols_ref)
    zero = jnp.zeros((TOKEN_TILE, 128), BF16)
    both = None
    for d in range(n_src):
        pick = jnp.concatenate(
            [jnp.concatenate([jnp.where(blk == jnp.asarray(d * blocks + b, BF16), hot, zero) for b in range(blocks)], axis=1) for blk, hot in picks], axis=0)
        part = jnp.dot(pick, srcs[d][...], preferred_element_type=F32)
        both = part if both is None else both + part
    dy = dy_ref[...].astype(F32)
    one, two = both[:TOKEN_TILE], both[TOKEN_TILE:]
    y_ref[...] = (cols_ref[:, 2:3] * one + cols_ref[:, 3:4] * two).astype(BF16)
    dg_one = jnp.sum(dy * one, axis=1, keepdims=True)
    dg_two = jnp.sum(dy * two, axis=1, keepdims=True)
    wide = jnp.concatenate([dg_one, dg_two, jnp.zeros((TOKEN_TILE, 126), F32)], axis=1)
    dg_ref[...] = wide.T[:8, :]


def logit_grad_kernel(z_ref, rows_ref, prob_ref, one_ref, two_ref, x_ref, *refs, n_chunk):
    dgs, (dl_ref, dw_ref) = refs[:2 * n_chunk], refs[2 * n_chunk:]
    n_experts, n_tokens = prob_ref.shape
    mine = sum(r[0:2, :] for r in dgs[:n_chunk])
    other = sum(r[0:2, :] for r in dgs[n_chunk:])
    dgate = mine + other
    dg_one, dg_two = dgate[0:1], dgate[1:2]
    gate_one, gate_two = rows_ref[2:3, :], rows_ref[3:4, :]
    prob_one, prob_two = rows_ref[4:5, :], rows_ref[5:6, :]
    shared = dg_one * gate_one + dg_two * gate_two
    gate_sum = prob_one + prob_two
    dp_one = (dg_one - shared) / gate_sum
    dp_two = (dg_two - shared) / gate_sum
    centre = dp_one * prob_one + dp_two * prob_two
    expert = lax.broadcasted_iota(jnp.int32, (n_experts, n_tokens), 0)
    inner = jnp.where(one_ref[...] == expert, dp_one, 0.0) + jnp.where(two_ref[...] == expert, dp_two, 0.0) - centre
    high, mid, low = split3(prob_ref[...] * inner)
    dl_ref[...] = jnp.concatenate([high, high, mid, high, low, mid], axis=0)
    raw = jnp.dot(jnp.concatenate([high, mid, low], axis=0), x_ref[...], preferred_element_type=F32)
    dw_ref[...] = raw[:n_experts] + raw[n_experts:2 * n_experts] + raw[2 * n_experts:]


def combine_in_kernel(z_ref, cols_ref, dl_ref, wt_ref, *refs, n_src):
    srcs, dx_ref = refs[:n_src], refs[n_src]
    blocks = srcs[0].shape[0] // 128
    (blk_one, hot_one), (blk_two, hot_two) = slot_picks(cols_ref)
    zero = jnp.zeros((TOKEN_TILE, 128), BF16)
    acc = None
    for d in range(n_src):
        parts = []
        for b in range(blocks):
            this = jnp.asarray(d * blocks + b, BF16)
            parts.append(jnp.where(blk_one == this, hot_one, jnp.where(blk_two == this, hot_two, zero)))
        part = jnp.dot(jnp.concatenate(parts, axis=1), srcs[d][...], preferred_element_type=F32)
        acc = part if acc is None else acc + part
    high, mid, low = split3(wt_ref[...])
    weights = jnp.concatenate([high, mid, high, low, high, mid], axis=0)
    back = lax.dot_general(dl_ref[...], weights, TN, preferred_element_type=F32)
    dx_ref[...] = (acc + back).astype(BF16)


def place_kernel(z_ref, *refs):
    pieces, out = refs[:-1], refs[-1]
    n_chunk = len(pieces) // 2
    wide = pieces[0].shape[1]
    for side in range(2):
        @pl.when(pl.program_id(1) == side)
        def _(side=side):
            for c in range(n_chunk):
                out[:, c * wide:(c + 1) * wide] = pieces[side * n_chunk + c][...]


def place_last_kernel(z_ref, kept_ref, piece_ref, out_ref):
    out_ref[...] = piece_ref[...]


def cost(flops, nbytes, trans=0):
    return pl.CostEstimate(flops=int(flops), bytes_accessed=int(nbytes), transcendentals=int(trans))


def solution(mesh):
    tp_size = mesh.shape["tp"]
    n_src = mesh.shape["ep"]
    n_chunk = 2
    diag = [n_src - 2, n_src - 1]
    early = diag + [0, 1]
    late = [2, 4, 3, 5]
    src_order = early + late
    first_peer = 6

    def local_step(x_rows, w_router, first_ids, second_ids, w_gelu, w_lin, w_out, dy_rows):
        n_tokens, model = x_rows.shape
        n_experts = w_router.shape[1]
        own, width = w_gelu.shape[0], w_gelu.shape[2]
        slot_cap = 2 * n_tokens // n_experts
        block = own * slot_cap
        cols = model // tp_size
        wide = cols // n_chunk
        rows_all = n_src * slot_cap
        rows_early = len(early) * slot_cap
        rows_late = len(late) * slot_cap
        sds = jax.ShapeDtypeStruct
        me = lax.axis_index("ep").astype(jnp.int32).reshape(1)
        z = lax.axis_index("tp").astype(jnp.int32).reshape(1)
        swap = [(i, tp_size - 1 - i) for i in range(tp_size)]

        def across(val):
            return lax.ppermute(val, "tp", swap)

        def to_peer(val, d):
            if d == 0:
                return val
            return lax.ppermute(val, "ep", [(i, i ^ d) for i in range(n_src)])

        def call(kernel, grid, in_specs, out_specs, out_shape, estimate, args, scratch=()):
            return pl.pallas_call(
                kernel,
                grid_spec=pltpu.PrefetchScalarGridSpec(num_scalar_prefetch=1, grid=grid, in_specs=in_specs, out_specs=out_specs, scratch_shapes=list(scratch)),
                out_shape=out_shape, cost_estimate=estimate)(z, *args)

        wa2, wb2 = across(w_gelu), across(w_lin)
        wt = w_router.T
        id_one, id_two = first_ids.reshape(1, n_tokens), second_ids.reshape(1, n_tokens)
        rows, prob, first_x = pl.pallas_call(
            functools.partial(route_kernel, slot_cap=slot_cap, own_experts=own, peer=first_peer),
            in_specs=[pl.BlockSpec(memory_space=pltpu.SMEM)] + [pl.BlockSpec(memory_space=pltpu.VMEM)] * 4,
            out_shape=(sds((16, n_tokens), F32), sds((n_experts, n_tokens), F32), sds((block, model), BF16)),
            cost_estimate=cost(2 * 96 * n_tokens * model, 2 * n_tokens * model, n_experts * n_tokens),
            name="route",
        )(me, x_rows, wt, id_one, id_two)
        token_cols = rows.T
        wcz = across(lax.dynamic_slice_in_dim(w_out, (1 - z[0]) * cols, cols, 2))
        wcn = across(lax.dynamic_slice_in_dim(w_out, z[0] * cols, cols, 2))

        per = block // GATHER_TILE

        def gather(src, peers, scaled, part=False):
            width_out = cols if part else model

            def out_map(g, z, i):
                return (jnp.clip(g - i * per, 0, per - 1), 0)

            def src_map(g, z):
                return (0, z[0] if part else 0)

            return call(
                functools.partial(gather_kernel, peers=peers, per=per, scaled=scaled), (len(peers) * per,),
                [pl.BlockSpec((16, n_tokens), lambda g, z: (0, 0)), pl.BlockSpec((n_tokens, width_out), src_map)],
                [pl.BlockSpec((GATHER_TILE, width_out), functools.partial(out_map, i=i)) for i in range(len(peers))],
                [sds((block, width_out), BF16)] * len(peers),
                cost(2 * len(peers) * block * n_tokens * width_out, 2 * (n_tokens + len(peers) * block) * width_out),
                (rows, src))

        xs, dos = [None] * n_src, [None] * n_src
        xs[first_peer] = to_peer(first_x, first_peer).reshape(own, slot_cap, model)
        for peers in ([4, 2], [7, 1, 0], [5, 3]):
            for d, val in zip(peers, gather(x_rows, peers, False)):
                xs[d] = to_peer(val, d).reshape(own, slot_cap, model)
        for peers in (diag, [4, 2]):
            for d, val in zip(peers, gather(dy_rows, peers, True, part=True)):
                mine = to_peer(val, d)
                dos[d] = tuple(v.reshape(own, slot_cap, cols) for v in (mine, across(mine)))
        for peers in ([1, 0], [5, 3]):
            for d, val in zip(peers, gather(dy_rows, peers, True)):
                dos[d] = (to_peer(val, d).reshape(own, slot_cap, model),)
        xs = [xs[d] for d in src_order]

        def whole(a, b, at=0):
            return pl.BlockSpec((1, a, b), lambda e, *_: (e, at, 0))

        def forward_own(lo, hi):
            n_rows = (hi - lo) * slot_cap
            return call(
                functools.partial(forward_own_kernel, n_src=hi - lo, cols=cols), (own,),
                [whole(slot_cap, model)] * (hi - lo) + [whole(model, width)] * 2 + [whole(width, model)],
                [whole(n_rows, width)] * 3 + [whole(n_rows, cols)],
                [sds((own, n_rows, width), F32)] * 2 + [sds((own, n_rows, width), BF16), sds((own, n_rows, cols), BF16)],
                cost(2 * own * n_rows * width * (2 * model + cols), 8e3 * own * n_rows, own * n_rows * width),
                (*xs[lo:hi], w_gelu, w_lin, w_out))

        cuts = (0, n_src - 2, n_src)
        own_parts = [forward_own(cuts[i], cuts[i + 1]) for i in range(2)]
        part_rows = [(cuts[i + 1] - cuts[i]) * slot_cap for i in range(2)]
        fwd = pl.pallas_call(
            functools.partial(forward_other_kernel, n_src=n_src, n_chunk=n_chunk), grid=(own,),
            in_specs=[whole(slot_cap, model)] * n_src + [whole(r, cols) for r in part_rows] + [whole(model, width)] * 2 + [whole(width, cols)],
            out_specs=[whole(slot_cap, wide)] * (n_src * n_chunk) + [whole(rows_all, width)] * 2,
            out_shape=[sds((own, slot_cap, wide), BF16)] * (n_src * n_chunk) + [sds((own, rows_all, width), F32)] * 2,
            cost_estimate=cost(2 * own * rows_all * width * (2 * model + cols), 32e6, own * rows_all * width),
            name="k_fwd_other")(*xs, own_parts[0][3], own_parts[1][3], wa2, wb2, wcz)
        gv2, sv2 = fwd[n_chunk * n_src:]
        back_out = []
        for c in range(n_chunk):
            got = [None] * n_src
            for i, d in enumerate(src_order):
                got[d] = to_peer(fwd[c * n_src + i], d).reshape(block, wide)
            back_out.append(got)

        def backward(peers, at):
            n_rows = len(peers) * slot_cap
            lo, hi = at * slot_cap, at * slot_cap + n_rows
            args = [v for d in peers for v in dos[d]]
            saved, specs, counts = [], [], []
            for source in ([p[0] for p in own_parts], [p[1] for p in own_parts], [gv2], [sv2]):
                base, n = 0, 0
                for arr in source:
                    rows_in = arr.shape[1]
                    a, b = max(lo, base), min(hi, base + rows_in)
                    if a < b:
                        step = b - a
                        saved.append(arr)
                        specs.append(whole(step, width, (a - base) // step))
                        n += 1
                    base += rows_in
                counts.append(n)
            return call(
                functools.partial(backward_kernel, widths=[len(dos[d]) for d in peers], saved_widths=counts, cols=cols, n_chunk=n_chunk), (own,),
                [whole(slot_cap, v.shape[2]) for v in args] + specs + [whole(model, width)] * 2 + [whole(width, model)] + [whole(model, width)] * 2 + [whole(width, cols)] * 2,
                [whole(slot_cap, wide)] * (len(peers) * n_chunk) + [whole(n_rows, width)] * 2,
                [sds((own, slot_cap, wide), BF16)] * (len(peers) * n_chunk) + [sds((own, n_rows, width), BF16)] * 2,
                cost(4 * own * n_rows * width * (model + 2 * cols), 6e3 * own * n_rows),
                (*args, *saved, w_gelu, w_lin, w_out, wa2, wb2, wcz, wcn),
                [pltpu.VMEM((n_rows, model), BF16)])

        bwd_a = backward(early, 0)
        bwd_b = backward(late, len(early))
        back_in = []
        for c in range(n_chunk):
            got = [None] * n_src
            for peers, vals in ((early, bwd_a), (late, bwd_b)):
                for i, d in enumerate(peers):
                    got[d] = to_peer(vals[c * len(peers) + i], d).reshape(block, wide)
            back_in.append(got)

        all_dos = [v for d in src_order for v in dos[d]]
        grad_wa, grad_wb, grad_wc = call(
            functools.partial(weight_grad_kernel, n_src=n_src, widths=[len(dos[d]) for d in src_order]), (own,),
            [whole(slot_cap, model)] * n_src + [whole(slot_cap, v.shape[2]) for v in all_dos] + [whole(r, width) for r in part_rows] + [whole(rows_early, width), whole(rows_late, width)] * 2,
            [whole(model, width), whole(model, width), whole(width, model)],
            [sds((own, model, width), F32)] * 2 + [sds((own, width, model), F32)],
            cost(6 * own * rows_all * width * model, 40e6),
            (*xs, *all_dos, own_parts[0][2], own_parts[1][2], bwd_a[-2], bwd_b[-2], bwd_a[-1], bwd_b[-1]),
            [pltpu.VMEM((rows_all, model), BF16)])

        def resident(a, b):
            return pl.BlockSpec((a, b), lambda i, *_: (0, 0))

        def tiles(b, col=None):
            return pl.BlockSpec((TOKEN_TILE, b), lambda i, z: (i, 0 if col is None else z[0] * n_chunk + col))

        n_tiles = (n_tokens // TOKEN_TILE,)
        y_mine, y_other, dg_mine, dg_other = [], [], [], []
        for c in range(n_chunk):
            y, dg = call(
                functools.partial(combine_out_kernel, n_src=n_src), n_tiles,
                [tiles(16), tiles(wide, c)] + [resident(block, wide)] * n_src,
                [tiles(wide), pl.BlockSpec((8, TOKEN_TILE), lambda i, z: (0, i))],
                [sds((n_tokens, wide), BF16), sds((8, n_tokens), F32)],
                cost(4 * n_tokens * n_src * block * wide, 6e6),
                (token_cols, dy_rows, *back_out[c]))
            y_mine.append(y)
            dg_mine.append(dg)
            dg_other.append(across(dg))
            y_other.append(across(y))

        dl, dw = call(
            functools.partial(logit_grad_kernel, n_chunk=n_chunk), (1,),
            [resident(16, n_tokens), resident(n_experts, n_tokens), resident(1, n_tokens), resident(1, n_tokens), pl.BlockSpec((n_tokens, cols), lambda i, z: (0, z[0]))] + [resident(8, n_tokens)] * (2 * n_chunk),
            [resident(6 * n_experts, n_tokens), resident(n_experts, cols)],
            [sds((6 * n_experts, n_tokens), BF16), sds((n_experts, cols), F32)],
            cost(2 * 96 * n_tokens * cols, 4e6),
            (rows, prob, id_one, id_two, x_rows, *dg_mine, *dg_other))

        dx_mine, dx_other = [], []
        for c in range(n_chunk):
            dx = call(
                functools.partial(combine_in_kernel, n_src=n_src), n_tiles,
                [tiles(16), pl.BlockSpec((6 * n_experts, TOKEN_TILE), lambda i, z: (0, i)), pl.BlockSpec((n_experts, wide), lambda i, z: (0, z[0] * n_chunk + c))] + [resident(block, wide)] * n_src,
                tiles(wide), sds((n_tokens, wide), BF16),
                cost(2 * n_tokens * n_src * block * wide, 6e6),
                (token_cols, dl, wt, *back_in[c]))
            dx_mine.append(dx)
            dx_other.append(across(dx))
        bit = 1
        while bit < n_src:
            dw = dw + to_peer(dw, bit)
            bit *= 2
        dw_other = across(dw)

        def place(pieces):
            return call(
                place_kernel, (2, 2), [pl.BlockSpec((n_tokens // 2, wide), lambda i, h, z: (i, 0))] * len(pieces),
                pl.BlockSpec((n_tokens // 2, cols), lambda i, h, z: (i, z[0] + h - 2 * h * z[0])),
                sds((n_tokens, model), BF16), cost(1e6, 8e6), pieces)

        act_out = place(y_mine + y_other)
        first_dx = place(dx_mine + dx_other[:-1] + dx_mine[-1:])
        grad_in = pl.pallas_call(
            place_last_kernel,
            grid_spec=pltpu.PrefetchScalarGridSpec(
                num_scalar_prefetch=1, grid=(2,),
                in_specs=[pl.BlockSpec(memory_space=pl.ANY), pl.BlockSpec((n_tokens // 2, wide), lambda i, z: (i, 0))],
                out_specs=pl.BlockSpec((n_tokens // 2, wide), lambda i, z: (i, (1 - z[0]) * n_chunk + n_chunk - 1))),
            out_shape=sds((n_tokens, model), BF16), input_output_aliases={1: 0},
            cost_estimate=cost(1e6, 2e6), name="k_place_dx1")(z, first_dx, dx_other[-1])
        grad_router = jnp.where(z[0] == 0, jnp.concatenate([dw, dw_other], axis=1), jnp.concatenate([dw_other, dw], axis=1)).T
        return act_out, grad_in, grad_wa, grad_wb, grad_wc, grad_router

    return jax.shard_map(local_step, mesh=mesh, in_specs=(P("ep", None), P(), P("ep"), P("ep"), P("ep", None, "tp"), P("ep", None, "tp"), P("ep", "tp", None), P("ep", None)), out_specs=(P("ep", None), P("ep", None), P("ep", None, "tp"), P("ep", None, "tp"), P("ep", "tp", None), P()), check_vma=False)
```

time: 501 us -> 497 us (level)
  Pallas kernels: 205 us -> 197 us
  starting transfers between devices: 52.4 us -> 58.9 us
    pallas_call x19, Pallas kernels: 186 us -> 173 us  [call(): pl.pallas_call(kernel, grid_spec=pltpu.PrefetchScalarGridSpec(num_scalar_...]
    ppermute x13 -> x15, starting transfers between devices: 15.1 us -> 17.9 us  [across(): return lax.ppermute(val, 'tp', swap)]
    ppermute x13 -> x15, waiting for transfers between devices: 114 us -> 113 us  [across(): return lax.ppermute(val, 'tp', swap)]
  transfers between devices with their start and end apart: 58 -> 60, of which waited for: 18 -> 19; matrix products, arithmetic and copies ran while one was open for 1% -> 1% of each run, Pallas kernels for 36% -> 37%
where the time goes in v1:
time: 497 us
  waiting for transfers between devices  234 us (47%)
  Pallas kernels  197 us (40%)
  starting transfers between devices  58.9 us (12%)
  local copies, waits for them, and re-layouts  5.71 us (1%)
    pallas_call x19, Pallas kernels, call(): pl.pallas_call(kernel, grid_spec=pltpu.PrefetchScalarGridSpec(num_scalar_...  173 us
    ppermute x45, waiting for transfers between devices, to_peer(): return lax.ppermute(val, 'ep', [(i, i ^ d) for i in range(n_src)])  121 us
    ppermute x15, waiting for transfers between devices, across(): return lax.ppermute(val, 'tp', swap)  113 us
    ppermute x45, starting transfers between devices, to_peer(): return lax.ppermute(val, 'ep', [(i, i ^ d) for i in range(n_src)])  40.9 us
    ppermute x15, starting transfers between devices, across(): return lax.ppermute(val, 'tp', swap)  17.9 us
    pallas_call x1, Pallas kernels, local_step(): pl.pallas_call(functools.partial(forward_other_kernel, n_src=n_src, n_chu...  14.3 us
  transfers between devices with their start and end apart: 60, of which 19 were waited for; matrix products, arithmetic and copies ran while one was open for 1% of the time, Pallas kernels for 37%

profile of v1, /device:TPU:0, one launch (start us, length us, event | category | flops | bytes accessed | tf_op | source)
XLA Modules:
  0.0 496.9 jit_solution(13237826720826557152)
XLA Ops:
  0.6 7.3 %route.1 = (f32[16,2048]{1,0:T(8,128)}, f32[32,2048]{1,0:T(8,128)}, bf16[512,1024]{1,0:T(8,128)(2,1)}) custom-call(s32[1]{0:T(128)} %bitcast.1.me_ref, bf16[2048,1024]{1,0:T(8,128)(2,1)} %x_ref.3, f32[32,1024]{1,0:T(8,128)} %bitcast.88, s32[1,2048]{1,0:T(1,128)} %bitcast.91, s32[1,2048]{1,0:T(1,128)} %bitcast.93), custom_call_target="tpu_custom_call" | custom-call | flops 402653184 | bytes 4194304 | tf_op jit(solution)/shard_map/route/pallas_call | solution.py:352
  7.9 5.8 %shard_map.139 = (bf16[512,512]{1,0:T(8,128)(2,1)}, bf16[512,512]{1,0:T(8,128)(2,1)}) custom-call(s32[1]{0:T(128)} %bitcast.z_ref, f32[16,2048]{1,0:T(8,128)} %get-tuple-element.79.rows_ref, bf16[2048,1024]{1,0:T(8,128)(2,1)} %src_ref.13), custom_call_target="tpu_custom_call" | custom-call | flops 2147483648 | bytes 3145728 | tf_op jit(solution)/shard_map/pallas_call | solution.py:344
  13.7 3.2 collective-permute-start.35
  16.9 11.6 %shard_map.127 = (bf16[512,1024]{1,0:T(8,128)(2,1)}, bf16[512,1024]{1,0:T(8,128)(2,1)}, bf16[512,1024]{1,0:T(8,128)(2,1)}) custom-call(s32[1]{0:T(128)} %bitcast.z_ref, f32[16,2048]{1,0:T(8,128)} %get-tuple-element.79.rows_ref, bf16[2048,1024]{1,0:T(8,128)(2,1)} %x_ref.3), custom_call_target="tpu_custom_call" | custom-call | flops 6442450944 | bytes 7340032 | tf_op jit(solution)/shard_map/pallas_call | solution.py:344
  30.2 5.8 %shard_map.136 = (bf16[512,512]{1,0:T(8,128)(2,1)}, bf16[512,512]{1,0:T(8,128)(2,1)}) custom-call(s32[1]{0:T(128)} %bitcast.z_ref, f32[16,2048]{1,0:T(8,128)} %get-tuple-element.79.rows_ref, bf16[2048,1024]{1,0:T(8,128)(2,1)} %src_ref.13), custom_call_target="tpu_custom_call" | custom-call | flops 2147483648 | bytes 3145728 | tf_op jit(solution)/shard_map/pallas_call | solution.py:344
  36.0 2.9 collective-permute-start.28
  39.7 8.8 %shard_map.128 = (bf16[512,1024]{1,0:T(8,128)(2,1)}, bf16[512,1024]{1,0:T(8,128)(2,1)}) custom-call(s32[1]{0:T(128)} %bitcast.z_ref, f32[16,2048]{1,0:T(8,128)} %get-tuple-element.79.rows_ref, bf16[2048,1024]{1,0:T(8,128)(2,1)} %x_ref.3), custom_call_target="tpu_custom_call" | custom-call | flops 4294967296 | bytes 6291456 | tf_op jit(solution)/shard_map/pallas_call | solution.py:344
  48.5 40.0 %collective-permute-done.37 = bf16[512,512]{1,0:T(8,128)(2,1)S(1)} collective-permute-done((bf16[512,512]{1,0:T(8,128)(2,1)}, bf16[512,512]{1,0:T(8,128)(2,1)S(1)}, u32[]{:S(2)}, u32[]{:S(2)}) %collective-permute-start.37) | collective-permute-done | bytes 524320 | tf_op jit(solution)/shard_map/ppermute | solution.py:341
  88.9 1.7 collective-permute-start.4
  90.6 1.4 collective-permute-start
  92.0 1.6 collective-permute-start.7
  94.1 1.5 constant_dynamic-slice_fusion
  95.6 8.6 %shard_map.129 = (bf16[512,1024]{1,0:T(8,128)(2,1)}, bf16[512,1024]{1,0:T(8,128)(2,1)}) custom-call(s32[1]{0:T(128)} %bitcast.z_ref, f32[16,2048]{1,0:T(8,128)} %get-tuple-element.79.rows_ref, bf16[2048,1024]{1,0:T(8,128)(2,1)} %x_ref.3), custom_call_target="tpu_custom_call" | custom-call | flops 4294967296 | bytes 6291456 | tf_op jit(solution)/shard_map/pallas_call | solution.py:344
  104.2 10.7 %collective-permute-done.3 = bf16[512,1024]{1,0:T(8,128)(2,1)} collective-permute-done((bf16[512,1024]{1,0:T(8,128)(2,1)}, bf16[512,1024]{1,0:T(8,128)(2,1)}, u32[]{:S(2)}, u32[]{:S(2)}) %collective-permute-start.3) | collective-permute-done | bytes 1048608 | tf_op jit(solution)/shard_map/ppermute | solution.py:341
  114.9 20.0 %collective-permute-done.4 = bf16[512,1024]{1,0:T(8,128)(2,1)} collective-permute-done((bf16[512,1024]{1,0:T(8,128)(2,1)}, bf16[512,1024]{1,0:T(8,128)(2,1)}, u32[]{:S(2)}, u32[]{:S(2)}) %collective-permute-start.4) | collective-permute-done | bytes 1048608 | tf_op jit(solution)/shard_map/ppermute | solution.py:341
  134.9 3.0 collective-permute-done
  137.8 1.7 collective-permute-start.9
  139.5 9.3 %shard_map.140 = (bf16[512,1024]{1,0:T(8,128)(2,1)}, bf16[512,1024]{1,0:T(8,128)(2,1)}) custom-call(s32[1]{0:T(128)} %bitcast.z_ref, f32[16,2048]{1,0:T(8,128)} %get-tuple-element.79.rows_ref, bf16[2048,1024]{1,0:T(8,128)(2,1)} %src_ref.13), custom_call_target="tpu_custom_call" | custom-call | flops 4294967296 | bytes 6291456 | tf_op jit(solution)/shard_map/pallas_call | solution.py:344
  148.8 9.1 %collective-permute-done.5 = bf16[512,1024]{1,0:T(8,128)(2,1)S(1)} collective-permute-done((bf16[512,1024]{1,0:T(8,128)(2,1)}, bf16[512,1024]{1,0:T(8,128)(2,1)S(1)}, u32[]{:S(2)}, u32[]{:S(2)}) %collective-permute-start.5) | collective-permute-done | bytes 1048608 | tf_op jit(solution)/shard_map/ppermute | solution.py:341
  159.6 46.7 %collective-permute-done.9.refs_12_.refs_15_.refs_17_ = bf16[4,256,512]{2,1,0:T(8,128)(2,1)S(1)} collective-permute-done((bf16[4,256,512]{2,1,0:T(8,128)(2,1)}, bf16[4,256,512]{2,1,0:T(8,128)(2,1)S(1)}, u32[]{:S(2)}, u32[]{:S(2)}) %collective-permute-start.9) | collective-permute-done | bytes 1048608 | tf_op jit(solution)/shard_map/ppermute | solution.py:336
  206.4 1.6 collective-permute-start.33
  208.0 1.3 copy.15
  209.2 11.7 %shard_map.130 = (f32[4,768,256]{2,1,0:T(8,128)}, f32[4,768,256]{2,1,0:T(8,128)}, bf16[4,768,256]{2,1,0:T(8,128)(2,1)}, bf16[4,768,512]{2,1,0:T(8,128)(2,1)}) custom-call(s32[1]{0:T(128)} %bitcast.z_ref, bf16[4,128,1024]{2,1,0:T(8,128)(2,1)} %bitcast.6.refs_0_, bf16[4,128,1024]{2,1,0:T(8,128)(2,1)} %bitcast.7.refs_1_, bf16[4,128,1024]{2,1,0:T(8,128)(2,1)} %bitcast.112, ...), custom_call_target="tpu_custom_call" | custom-call | flops 4026531840 | bytes 24576000 | tf_op jit(solution)/shard_map/pallas_call | solution.py:344
  221.4 1.6 collective-permute-start.38
  223.0 6.6 %shard_map.131 = (f32[4,256,256]{2,1,0:T(8,128)}, f32[4,256,256]{2,1,0:T(8,128)}, bf16[4,256,256]{2,1,0:T(8,128)(2,1)}, bf16[4,256,512]{2,1,0:T(8,128)(2,1)}) custom-call(s32[1]{0:T(128)} %bitcast.z_ref, bf16[4,128,1024]{2,1,0:T(8,128)(2,1)} %bitcast.60, bf16[4,128,1024]{2,1,0:T(8,128)(2,1)} %bitcast.63, bf16[4,1024,256]{2,1,0:T(8,128)(2,1)} %refs_12_.3, ...), custom_call_target="tpu_custom_call" | custom-call | flops 1342177280 | bytes 8192000 | tf_op jit(solution)/shard_map/pallas_call | solution.py:344
  229.6 14.3 %k_fwd_other.1 = (bf16[4,128,256]{2,1,0:T(8,128)(2,1)}, bf16[4,128,256]{2,1,0:T(8,128)(2,1)}, bf16[4,128,256]{2,1,0:T(8,128)(2,1)}, bf16[4,128,256]{2,1,0:T(8,12...) custom-call(bf16[4,128,1024]{2,1,0:T(8,128)(2,1)} %bitcast.6.refs_0_, ...), custom_call_target="tpu_custom_call" | custom-call | flops 5368709120 | bytes 32000000 | tf_op jit(solution)/shard_map/k_fwd_other/pallas_call | solution.py:412
  243.9 8.5 %collective-permute-done.38 = bf16[512,512]{1,0:T(8,128)(2,1)S(1)} collective-permute-done((bf16[512,512]{1,0:T(8,128)(2,1)}, bf16[512,512]{1,0:T(8,128)(2,1)S(1)}, u32[]{:S(2)}, u32[]{:S(2)}) %collective-permute-start.38) | collective-permute-done | bytes 524320 | tf_op jit(solution)/shard_map/ppermute | solution.py:336
  254.5 1.4 collective-permute-start.21
  256.0 9.3 %shard_map.137 = (bf16[512,1024]{1,0:T(8,128)(2,1)}, bf16[512,1024]{1,0:T(8,128)(2,1)}) custom-call(s32[1]{0:T(128)} %bitcast.z_ref, f32[16,2048]{1,0:T(8,128)} %get-tuple-element.79.rows_ref, bf16[2048,1024]{1,0:T(8,128)(2,1)} %src_ref.13), custom_call_target="tpu_custom_call" | custom-call | flops 4294967296 | bytes 6291456 | tf_op jit(solution)/shard_map/pallas_call | solution.py:344
  265.3 1.5 collective-permute-start.22
  269.9 12.5 %shard_map.141 = (bf16[4,128,256]{2,1,0:T(8,128)(2,1)}, bf16[4,128,256]{2,1,0:T(8,128)(2,1)}, bf16[4,128,256]{2,1,0:T(8,128)(2,1)}, bf16[4,128,256]{2,1,0:T(8,12...) custom-call(s32[1]{0:T(128)} %bitcast.z_ref, ...), custom_call_target="tpu_custom_call" | custom-call | flops 4294967296 | bytes 12288000 | tf_op jit(solution)/shard_map/pallas_call | solution.py:344
  285.7 2.1 collective-permute-start.15
  287.8 2.8 collective-permute-done.12
  290.6 2.7 collective-permute-start.16
  293.3 12.7 %shard_map.133 = (bf16[2048,256]{1,0:T(8,128)(2,1)}, f32[8,2048]{1,0:T(8,128)}) custom-call(s32[1]{0:T(128)} %bitcast.z_ref, f32[2048,16]{1,0:T(8,128)} %bitcast.70, bf16[2048,1024]{1,0:T(8,128)(2,1)} %src_ref.13, bf16[512,256]{1,0:T(8,128)(2,1)} %bitcast.116, bf16[512,256]{1,0:T(8,128)(2,1)} %bitcast.97, bf16[512,256]{1,0:T(8,128)(2,1)} %bitcast.98, ...), custom_call_target="tpu_custom_call" | custom-call | flops 8589934592 | bytes 6000000 | tf_op jit(solution)/shard_map/pallas_call | solution.py:344
  306.0 1.5 collective-permute-start.29
  307.5 1.5 collective-permute-start.31
  310.8 12.6 %shard_map.132 = (bf16[2048,256]{1,0:T(8,128)(2,1)}, f32[8,2048]{1,0:T(8,128)}) custom-call(s32[1]{0:T(128)} %bitcast.z_ref, f32[2048,16]{1,0:T(8,128)} %bitcast.71, bf16[2048,1024]{1,0:T(8,128)(2,1)} %src_ref.13, bf16[512,256]{1,0:T(8,128)(2,1)} %bitcast.115, bf16[512,256]{1,0:T(8,128)(2,1)} %bitcast.100, bf16[512,256]{1,0:T(8,128)(2,1)} %bitcast.102, ...), custom_call_target="tpu_custom_call" | custom-call | flops 8589934592 | bytes 6000000 | tf_op jit(solution)/shard_map/pallas_call | solution.py:344
  324.3 5.7 %collective-permute-done.31 = bf16[512,512]{1,0:T(8,128)(2,1)S(1)} collective-permute-done((bf16[512,512]{1,0:T(8,128)(2,1)}, bf16[512,512]{1,0:T(8,128)(2,1)S(1)}, u32[]{:S(2)}, u32[]{:S(2)}) %collective-permute-start.31) | collective-permute-done | bytes 524320 | tf_op jit(solution)/shard_map/ppermute | solution.py:336
  330.0 1.6 collective-permute-start.27
  332.3 12.4 %shard_map.138 = (bf16[4,128,256]{2,1,0:T(8,128)(2,1)}, bf16[4,128,256]{2,1,0:T(8,128)(2,1)}, bf16[4,128,256]{2,1,0:T(8,128)(2,1)}, bf16[4,128,256]{2,1,0:T(8,12...) custom-call(s32[1]{0:T(128)} %bitcast.z_ref, ...), custom_call_target="tpu_custom_call" | custom-call | flops 4294967296 | bytes 12288000 | tf_op jit(solution)/shard_map/pallas_call | solution.py:344
  344.8 1.2 collective-permute-start.43
  347.2 1.5 collective-permute-start.45
  348.7 1.3 collective-permute-start.46
  350.0 3.1 shard_map.135
  353.0 12.3 %collective-permute-done.43 = bf16[4,128,256]{2,1,0:T(8,128)(2,1)S(1)} collective-permute-done((bf16[4,128,256]{2,1,0:T(8,128)(2,1)}, bf16[4,128,256]{2,1,0:T(8,128)(2,1)S(1)}, u32[]{:S(2)}, u32[]{:S(2)}) %collective-permute-start.43) | collective-permute-done | bytes 262176 | tf_op jit(solution)/shard_map/ppermute | solution.py:341
  365.4 1.2 collective-permute-start.50
  366.6 4.5 collective-permute-done.44
  371.8 1.5 collective-permute-start.52
  373.2 1.2 collective-permute-start.53
  374.5 8.7 %shard_map.142.refs_0_ = bf16[2048,256]{1,0:T(8,128)(2,1)} custom-call(s32[1]{0:T(128)} %bitcast.z_ref, f32[2048,16]{1,0:T(8,128)} %bitcast.72, bf16[192,2048]{1,0:T(8,128)(2,1)} %get-tuple-element.111.dl_ref, f32[32,1024]{1,0:T(8,128)} %bitcast.89, bf16[512,256]{1,0:T(8,128)(2,1)} %bitcast.103, bf16[512,256]{1,0:T(8,128)(2,1)} %bitcast.109, ...), custom_call_target="tpu_custom_call" | custom-call | flops 4294967296 | bytes 6000000 | tf_op jit(solution)/shard_map/pallas_call | solution.py:344
  383.2 4.7 collective-permute-done.50
  388.6 1.4 collective-permute-start.25
  389.9 3.7 collective-permute-done.51
  395.7 8.8 %shard_map.143.refs_1_.refs_3_ = bf16[2048,256]{1,0:T(8,128)(2,1)} custom-call(s32[1]{0:T(128)} %bitcast.z_ref, f32[2048,16]{1,0:T(8,128)} %bitcast.73, bf16[192,2048]{1,0:T(8,128)(2,1)} %get-tuple-element.111.dl_ref, f32[32,1024]{1,0:T(8,128)} %bitcast.90, bf16[512,256]{1,0:T(8,128)(2,1)} %bitcast.96, bf16[512,256]{1,0:T(8,128)(2,1)} %bitcast.51.refs_1_, ...), custom_call_target="tpu_custom_call" | custom-call | flops 4294967296 | bytes 6000000 | tf_op jit(solution)/shard_map/pallas_call | solution.py:344
  405.4 1.3 collective-permute-done.56
  407.1 3.8 collective-permute-done.57
  411.5 3.8 collective-permute-done.58
  415.3 1.2 collective-permute-start.59
  416.5 14.2 %shard_map.145 = (f32[4,1024,256]{2,1,0:T(8,128)}, f32[4,1024,256]{2,1,0:T(8,128)}, f32[4,256,1024]{2,1,0:T(8,128)}) custom-call(s32[1]{0:T(128)} %bitcast.z_ref, bf16[4,128,1024]{2,1,0:T(8,128)(2,1)} %bitcast.6.refs_0_, bf16[4,128,1024]{2,1,0:T(8,128)(2,1)} %bitcast.7.refs_1_, bf16[4,128,1024]{2,1,0:T(8,128)(2,1)} %bitcast.114, ...), custom_call_target="tpu_custom_call" | custom-call | flops 6442450944 | bytes 40000000 | tf_op jit(solution)/shard_map/pallas_call | solution.py:344
  430.6 51.9 %collective-permute-done.59 = f32[32,512]{1,0:T(8,128)S(1)} collective-permute-done((f32[32,512]{1,0:T(8,128)S(1)}, f32[32,512]{1,0:T(8,128)S(1)}, u32[]{:S(2)}, u32[]{:S(2)}) %collective-permute-start.59) | collective-permute-done | bytes 65568 | tf_op jit(solution)/shard_map/ppermute | solution.py:336
  484.2 5.3 %shard_map.134 = bf16[2048,1024]{1,0:T(8,128)(2,1)} custom-call(s32[1]{0:T(128)} %bitcast.z_ref, bf16[2048,256]{1,0:T(8,128)(2,1)} %get-tuple-element.98.refs_0_, bf16[2048,256]{1,0:T(8,128)(2,1)} %get-tuple-element.107.refs_1_, bf16[2048,256]{1,0:T(8,128)(2,1)} %collective-permute-done.24.refs_2_, bf16[2048,256]{1,0:T(8,128)(2,1)} %copy-done.8), custom_call_target="tpu_custom_call" | custom-call | flops 1000000 | bytes 8000000 | tf_op jit(solution)/shard_map/pallas_call | solution.py:344
  489.5 5.3 %shard_map.144.kept_ref = bf16[2048,1024]{1,0:T(8,128)(2,1)} custom-call(s32[1]{0:T(128)} %bitcast.z_ref, bf16[2048,256]{1,0:T(8,128)(2,1)} %shard_map.142.refs_0_, bf16[2048,256]{1,0:T(8,128)(2,1)} %shard_map.143.refs_1_.refs_3_, bf16[2048,256]{1,0:T(8,128)(2,1)} %collective-permute-done.54.refs_2_, bf16[2048,256]{1,0:T(8,128)(2,1)} %shard_map.143.refs_1_.refs_3_), custom_call_target="tpu_custom_call" | custom-call | flops 1000000 | bytes 8000000 | tf_op jit(solution)/shard_map/pallas_call | solution.py:344
  494.8 2.0 k_place_dx1.1
  (176 shorter events, 25.7 us)
Async XLA Ops:
  13.7 25.2 %collective-permute-start.35 = (bf16[512,512]{1,0:T(8,128)(2,1)}, bf16[512,512]{1,0:T(8,128)(2,1)S(1)}, u32[]{:S(2)}, u32[]{:S(2)}) collective-permute-start(bf16[512,512]{1,0:T(8,128)(2,1)} %get-tuple-element.122), channel_id=1, source_target_pairs={{0,2},{1,3},{2,0},{3,1},{4,6},{5,7},{6,4},{7,5},{8,10},{9,11},{10,... | collective-permute-start | bytes 1572872 | tf_op jit(solution)/shard_map/ppermute | solution.py:341
  28.5 63.5 %collective-permute-start.1 = (bf16[512,1024]{1,0:T(8,128)(2,1)}, bf16[512,1024]{1,0:T(8,128)(2,1)}, u32[]{:S(2)}, u32[]{:S(2)}) collective-permute-start(bf16[512,1024]{1,0:T(8,128)(2,1)} %get-tuple-element.81), channel_id=1, source_target_pairs={{0,7},{1,6},{2,5},{3,4},{4,3},{5,2},{6,1},{7,0},{8,15},{9,14},{10,... | collective-permute-start | bytes 3145736 | tf_op jit(solution)/shard_map/ppermute | solution.py:341
  29.2 64.5 %collective-permute-start.2 = (bf16[512,1024]{1,0:T(8,128)(2,1)}, bf16[512,1024]{1,0:T(8,128)(2,1)}, u32[]{:S(2)}, u32[]{:S(2)}) collective-permute-start(bf16[512,1024]{1,0:T(8,128)(2,1)} %get-tuple-element.83), channel_id=1, source_target_pairs={{0,1},{1,0},{2,3},{3,2},{4,5},{5,4},{6,7},{7,6},{8,9},{9,8},{10,11... | collective-permute-start | bytes 3145736 | tf_op jit(solution)/shard_map/ppermute | solution.py:341
  30.1 58.4 %collective-permute-start.37 = (bf16[512,512]{1,0:T(8,128)(2,1)}, bf16[512,512]{1,0:T(8,128)(2,1)S(1)}, u32[]{:S(2)}, u32[]{:S(2)}) collective-permute-start(bf16[512,512]{1,0:T(8,128)(2,1)} %get-tuple-element.123), channel_id=1, source_target_pairs={{0,4},{1,5},{2,6},{3,7},{4,0},{5,1},{6,2},{7,3},{8,12},{9,13},{10,... | collective-permute-start | bytes 1572872 | tf_op jit(solution)/shard_map/ppermute | solution.py:341
  36.0 52.9 %collective-permute-start.28 = (bf16[512,512]{1,0:T(8,128)(2,1)}, bf16[512,512]{1,0:T(8,128)(2,1)S(1)}, u32[]{:S(2)}, u32[]{:S(2)}) collective-permute-start(bf16[512,512]{1,0:T(8,128)(2,1)} %get-tuple-element.112), channel_id=1, source_target_pairs={{0,6},{1,7},{2,4},{3,5},{4,2},{5,3},{6,0},{7,1},{8,14},{9,15},{10,... | collective-permute-start | bytes 1572872 | tf_op jit(solution)/shard_map/ppermute | solution.py:341
  39.7 54.4 %copy-start = (bf16[4,256,1024]{2,1,0:T(8,128)(2,1)S(1)}, bf16[4,256,1024]{2,1,0:T(8,128)(2,1)}, u32[]{:S(2)}) copy-start(bf16[4,256,1024]{2,1,0:T(8,128)(2,1)} %refs_14_.1) | copy-start | bytes 6291460
  39.7 50.9 %collective-permute-start.30 = (bf16[512,512]{1,0:T(8,128)(2,1)}, bf16[512,512]{1,0:T(8,128)(2,1)}, u32[]{:S(2)}, u32[]{:S(2)}) collective-permute-start(bf16[512,512]{1,0:T(8,128)(2,1)} %get-tuple-element.113), channel_id=1, source_target_pairs={{0,7},{1,6},{2,5},{3,4},{4,3},{5,2},{6,1},{7,0},{8,15},{9,14},{10,... | collective-permute-start | bytes 1572872 | tf_op jit(solution)/shard_map/ppermute | solution.py:341
  88.5 26.3 %collective-permute-start.3 = (bf16[512,1024]{1,0:T(8,128)(2,1)}, bf16[512,1024]{1,0:T(8,128)(2,1)}, u32[]{:S(2)}, u32[]{:S(2)}) collective-permute-start(bf16[512,1024]{1,0:T(8,128)(2,1)} %get-tuple-element.84), channel_id=1, source_target_pairs={{0,2},{1,3},{2,0},{3,1},{4,6},{5,7},{6,4},{7,5},{8,10},{9,11},{10,... | collective-permute-start | bytes 3145736 | tf_op jit(solution)/shard_map/ppermute | solution.py:341
  88.9 46.0 %collective-permute-start.4 = (bf16[512,1024]{1,0:T(8,128)(2,1)}, bf16[512,1024]{1,0:T(8,128)(2,1)}, u32[]{:S(2)}, u32[]{:S(2)}) collective-permute-start(bf16[512,1024]{1,0:T(8,128)(2,1)} %get-tuple-element.85), channel_id=1, source_target_pairs={{0,4},{1,5},{2,6},{3,7},{4,0},{5,1},{6,2},{7,3},{8,12},{9,13},{10,... | collective-permute-start | bytes 3145736 | tf_op jit(solution)/shard_map/ppermute | solution.py:341
  90.6 47.2 %collective-permute-start = (bf16[512,1024]{1,0:T(8,128)(2,1)}, bf16[512,1024]{1,0:T(8,128)(2,1)}, u32[]{:S(2)}, u32[]{:S(2)}) collective-permute-start(bf16[512,1024]{1,0:T(8,128)(2,1)} %get-tuple-element.80), channel_id=1, source_target_pairs={{0,6},{1,7},{2,4},{3,5},{4,2},{5,3},{6,0},{7,1},{8,14},{9,15},{10,... | collective-permute-start | bytes 3145736 | tf_op jit(solution)/shard_map/ppermute | solution.py:341
  92.0 128.9 %collective-permute-start.7 = (bf16[4,1024,256]{2,1,0:T(8,128)(2,1)}, bf16[4,1024,256]{2,1,0:T(8,128)(2,1)}, u32[]{:S(2)}, u32[]{:S(2)}) collective-permute-start(bf16[4,1024,256]{2,1,0:T(8,128)(2,1)} %refs_12_.3), channel_id=1, source_target_pairs={{0,8},{8,0},{1,9},{9,1},{2,10},{10,2},{3,11},{11,3},{4,12},{12,4},... | collective-permute-start | bytes 6291464 | tf_op jit(solution)/shard_map/ppermute | solution.py:336
  93.6 127.8 %collective-permute-start.8 = (bf16[4,1024,256]{2,1,0:T(8,128)(2,1)}, bf16[4,1024,256]{2,1,0:T(8,128)(2,1)}, u32[]{:S(2)}, u32[]{:S(2)}) collective-permute-start(bf16[4,1024,256]{2,1,0:T(8,128)(2,1)} %refs_13_.1), channel_id=1, source_target_pairs={{0,8},{8,0},{1,9},{9,1},{2,10},{10,2},{3,11},{11,3},{4,12},{12,4},... | collective-permute-start | bytes 6291464 | tf_op jit(solution)/shard_map/ppermute | solution.py:336
  114.9 43.0 %collective-permute-start.5 = (bf16[512,1024]{1,0:T(8,128)(2,1)}, bf16[512,1024]{1,0:T(8,128)(2,1)S(1)}, u32[]{:S(2)}, u32[]{:S(2)}) collective-permute-start(bf16[512,1024]{1,0:T(8,128)(2,1)} %get-tuple-element.86), channel_id=1, source_target_pairs={{0,3},{1,2},{2,1},{3,0},{4,7},{5,6},{6,5},{7,4},{8,11},{9,10},{10,... | collective-permute-start | bytes 3145736 | tf_op jit(solution)/shard_map/ppermute | solution.py:341
  134.9 24.5 %collective-permute-start.6 = (bf16[512,1024]{1,0:T(8,128)(2,1)}, bf16[512,1024]{1,0:T(8,128)(2,1)S(1)}, u32[]{:S(2)}, u32[]{:S(2)}) collective-permute-start(bf16[512,1024]{1,0:T(8,128)(2,1)} %get-tuple-element.87), channel_id=1, source_target_pairs={{0,5},{1,4},{2,7},{3,6},{4,1},{5,0},{6,3},{7,2},{8,13},{9,12},{10,... | collective-permute-start | bytes 3145736 | tf_op jit(solution)/shard_map/ppermute | solution.py:341
  137.8 70.1 %copy-start.17 = (f32[16,2048]{1,0:T(8,128)S(1)}, f32[16,2048]{1,0:T(8,128)}, u32[]{:S(2)}) copy-start(f32[16,2048]{1,0:T(8,128)} %get-tuple-element.79.rows_ref) | copy-start | bytes 393220
  137.8 68.5 %collective-permute-start.9 = (bf16[4,256,512]{2,1,0:T(8,128)(2,1)}, bf16[4,256,512]{2,1,0:T(8,128)(2,1)S(1)}, u32[]{:S(2)}, u32[]{:S(2)}) collective-permute-start(bf16[4,256,512]{2,1,0:T(8,128)(2,1)} %get-tuple-element.153), channel_id=1, source_target_pairs={{0,8},{8,0},{1,9},{9,1},{2,10},{10,2},{3,11},{11,3},{4,12},{12,4},... | collective-permute-start | bytes 3145736 | tf_op jit(solution)/shard_map/ppermute | solution.py:336
  157.9 63.0 %copy-start.3 = (bf16[512,1024]{1,0:T(8,128)(2,1)}, bf16[512,1024]{1,0:T(8,128)(2,1)S(1)}, u32[]{:S(2)}) copy-start(bf16[512,1024]{1,0:T(8,128)(2,1)S(1)} %collective-permute-done.5) | copy-start | bytes 3145732
  157.9 95.5 %collective-permute-start.39 = (bf16[512,1024]{1,0:T(8,128)(2,1)}, bf16[512,1024]{1,0:T(8,128)(2,1)}, u32[]{:S(2)}, u32[]{:S(2)}) collective-permute-start(bf16[512,1024]{1,0:T(8,128)(2,1)} %get-tuple-element.124), channel_id=1, source_target_pairs={{0,3},{1,2},{2,1},{3,0},{4,7},{5,6},{6,5},{7,4},{8,11},{9,10},{10,... | collective-permute-start | bytes 3145736 | tf_op jit(solution)/shard_map/ppermute | solution.py:341
  159.4 47.0 %copy-start.4 = (bf16[512,1024]{1,0:T(8,128)(2,1)}, bf16[512,1024]{1,0:T(8,128)(2,1)S(1)}, u32[]{:S(2)}) copy-start(bf16[512,1024]{1,0:T(8,128)(2,1)S(1)} %collective-permute-done.6) | copy-start | bytes 3145732
  159.4 94.0 %collective-permute-start.40 = (bf16[512,1024]{1,0:T(8,128)(2,1)}, bf16[512,1024]{1,0:T(8,128)(2,1)}, u32[]{:S(2)}, u32[]{:S(2)}) collective-permute-start(bf16[512,1024]{1,0:T(8,128)(2,1)} %get-tuple-element.125), channel_id=1, source_target_pairs={{0,5},{1,4},{2,7},{3,6},{4,1},{5,0},{6,3},{7,2},{8,13},{9,12},{10,... | collective-permute-start | bytes 3145736 | tf_op jit(solution)/shard_map/ppermute | solution.py:341
  206.4 48.2 %collective-permute-start.33 = (bf16[4,256,512]{2,1,0:T(8,128)(2,1)}, bf16[4,256,512]{2,1,0:T(8,128)(2,1)S(1)}, u32[]{:S(2)}, u32[]{:S(2)}) collective-permute-start(bf16[4,256,512]{2,1,0:T(8,128)(2,1)} %get-tuple-element.152), channel_id=1, source_target_pairs={{0,8},{8,0},{1,9},{9,1},{2,10},{10,2},{3,11},{11,3},{4,12},{12,4},... | collective-permute-start | bytes 3145736 | tf_op jit(solution)/shard_map/ppermute | solution.py:336
  220.9 22.9 %collective-permute-start.36 = (bf16[512,512]{1,0:T(8,128)(2,1)}, bf16[512,512]{1,0:T(8,128)(2,1)S(1)}, u32[]{:S(2)}, u32[]{:S(2)}) collective-permute-start(bf16[512,512]{1,0:T(8,128)(2,1)} %copy-done.9), channel_id=1, source_target_pairs={{0,8},{8,0},{1,9},{9,1},{2,10},{10,2},{3,11},{11,3},{4,12},{12,4},... | collective-permute-start | bytes 1572872 | tf_op jit(solution)/shard_map/ppermute | solution.py:336
  221.4 31.0 %collective-permute-start.38 = (bf16[512,512]{1,0:T(8,128)(2,1)}, bf16[512,512]{1,0:T(8,128)(2,1)S(1)}, u32[]{:S(2)}, u32[]{:S(2)}) collective-permute-start(bf16[512,512]{1,0:T(8,128)(2,1)} %copy-done.10), channel_id=1, source_target_pairs={{0,8},{8,0},{1,9},{9,1},{2,10},{10,2},{3,11},{11,3},{4,12},{12,4},... | collective-permute-start | bytes 1572872 | tf_op jit(solution)/shard_map/ppermute | solution.py:336
  243.9 21.4 %collective-permute-start.17 = (bf16[4,128,256]{2,1,0:T(8,128)(2,1)}, bf16[4,128,256]{2,1,0:T(8,128)(2,1)S(1)}, u32[]{:S(2)}, u32[]{:S(2)}) collective-permute-start(bf16[4,128,256]{2,1,0:T(8,128)(2,1)} %get-tuple-element.100), channel_id=1, source_target_pairs={{0,1},{1,0},{2,3},{3,2},{4,5},{5,4},{6,7},{7,6},{8,9},{9,8},{10,11... | collective-permute-start | bytes 786440 | tf_op jit(solution)/shard_map/ppermute | solution.py:341
  252.4 14.4 %collective-permute-start.18 = (bf16[4,128,256]{2,1,0:T(8,128)(2,1)}, bf16[4,128,256]{2,1,0:T(8,128)(2,1)S(1)}, u32[]{:S(2)}, u32[]{:S(2)}) collective-permute-start(bf16[4,128,256]{2,1,0:T(8,128)(2,1)} %get-tuple-element.101), channel_id=1, source_target_pairs={{0,2},{1,3},{2,0},{3,1},{4,6},{5,7},{6,4},{7,5},{8,10},{9,11},{10,... | collective-permute-start | bytes 786440 | tf_op jit(solution)/shard_map/ppermute | solution.py:341
  253.4 13.8 %collective-permute-start.19 = (bf16[4,128,256]{2,1,0:T(8,128)(2,1)}, bf16[4,128,256]{2,1,0:T(8,128)(2,1)S(1)}, u32[]{:S(2)}, u32[]{:S(2)}) collective-permute-start(bf16[4,128,256]{2,1,0:T(8,128)(2,1)} %get-tuple-element.102), channel_id=1, source_target_pairs={{0,3},{1,2},{2,1},{3,0},{4,7},{5,6},{6,5},{7,4},{8,11},{9,10},{10,... | collective-permute-start | bytes 786440 | tf_op jit(solution)/shard_map/ppermute | solution.py:341
  253.4 15.0 %collective-permute-start.20 = (bf16[4,128,256]{2,1,0:T(8,128)(2,1)}, bf16[4,128,256]{2,1,0:T(8,128)(2,1)S(1)}, u32[]{:S(2)}, u32[]{:S(2)}) collective-permute-start(bf16[4,128,256]{2,1,0:T(8,128)(2,1)} %get-tuple-element.103), channel_id=1, source_target_pairs={{0,4},{1,5},{2,6},{3,7},{4,0},{5,1},{6,2},{7,3},{8,12},{9,13},{10,... | collective-permute-start | bytes 786440 | tf_op jit(solution)/shard_map/ppermute | solution.py:341
  254.5 14.8 %collective-permute-start.21 = (bf16[4,128,256]{2,1,0:T(8,128)(2,1)}, bf16[4,128,256]{2,1,0:T(8,128)(2,1)}, u32[]{:S(2)}, u32[]{:S(2)}) collective-permute-start(bf16[4,128,256]{2,1,0:T(8,128)(2,1)} %get-tuple-element.104), channel_id=1, source_target_pairs={{0,5},{1,4},{2,7},{3,6},{4,1},{5,0},{6,3},{7,2},{8,13},{9,12},{10,... | collective-permute-start | bytes 786440 | tf_op jit(solution)/shard_map/ppermute | solution.py:341
  265.3 17.0 %collective-permute-start.22 = (bf16[4,128,256]{2,1,0:T(8,128)(2,1)}, bf16[4,128,256]{2,1,0:T(8,128)(2,1)S(1)}, u32[]{:S(2)}, u32[]{:S(2)}) collective-permute-start(bf16[4,128,256]{2,1,0:T(8,128)(2,1)} %get-tuple-element.105), channel_id=1, source_target_pairs={{0,6},{1,7},{2,4},{3,5},{4,2},{5,3},{6,0},{7,1},{8,14},{9,15},{10,... | collective-permute-start | bytes 786440 | tf_op jit(solution)/shard_map/ppermute | solution.py:341
  266.8 16.3 %collective-permute-start.23 = (bf16[4,128,256]{2,1,0:T(8,128)(2,1)}, bf16[4,128,256]{2,1,0:T(8,128)(2,1)}, u32[]{:S(2)}, u32[]{:S(2)}) collective-permute-start(bf16[4,128,256]{2,1,0:T(8,128)(2,1)} %get-tuple-element.106), channel_id=1, source_target_pairs={{0,7},{1,6},{2,5},{3,4},{4,3},{5,2},{6,1},{7,0},{8,15},{9,14},{10,... | collective-permute-start | bytes 786440 | tf_op jit(solution)/shard_map/ppermute | solution.py:341
  267.2 16.2 %collective-permute-start.10 = (bf16[4,128,256]{2,1,0:T(8,128)(2,1)}, bf16[4,128,256]{2,1,0:T(8,128)(2,1)S(1)}, u32[]{:S(2)}, u32[]{:S(2)}) collective-permute-start(bf16[4,128,256]{2,1,0:T(8,128)(2,1)} %get-tuple-element.91), channel_id=1, source_target_pairs={{0,1},{1,0},{2,3},{3,2},{4,5},{5,4},{6,7},{7,6},{8,9},{9,8},{10,11... | collective-permute-start | bytes 786440 | tf_op jit(solution)/shard_map/ppermute | solution.py:341
  268.4 17.3 %collective-permute-start.11 = (bf16[4,128,256]{2,1,0:T(8,128)(2,1)}, bf16[4,128,256]{2,1,0:T(8,128)(2,1)S(1)}, u32[]{:S(2)}, u32[]{:S(2)}) collective-permute-start(bf16[4,128,256]{2,1,0:T(8,128)(2,1)} %get-tuple-element.92), channel_id=1, source_target_pairs={{0,2},{1,3},{2,0},{3,1},{4,6},{5,7},{6,4},{7,5},{8,10},{9,11},{10,... | collective-permute-start | bytes 786440 | tf_op jit(solution)/shard_map/ppermute | solution.py:341
  269.3 21.2 %collective-permute-start.12 = (bf16[4,128,256]{2,1,0:T(8,128)(2,1)S(1)}, bf16[4,128,256]{2,1,0:T(8,128)(2,1)S(1)}, u32[]{:S(2)}, u32[]{:S(2)}) collective-permute-start(bf16[4,128,256]{2,1,0:T(8,128)(2,1)S(1)} %copy-done.30), channel_id=1, source_target_pairs={{0,3},{1,2},{2,1},{3,0},{4,7},{5,6},{6,5},{7,4},{8,11},{9,10},{10,... | collective-permute-start | bytes 786440 | tf_op jit(solution)/shard_map/ppermute | solution.py:341
  282.4 47.6 %collective-permute-start.32 = (bf16[512,1024]{1,0:T(8,128)(2,1)}, bf16[512,1024]{1,0:T(8,128)(2,1)S(1)}, u32[]{:S(2)}, u32[]{:S(2)}) collective-permute-start(bf16[512,1024]{1,0:T(8,128)(2,1)} %get-tuple-element.115), channel_id=1, source_target_pairs={{0,1},{1,0},{2,3},{3,2},{4,5},{5,4},{6,7},{7,6},{8,9},{9,8},{10,11... | collective-permute-start | bytes 3145736 | tf_op jit(solution)/shard_map/ppermute | solution.py:341
  283.1 22.8 %collective-permute-start.13 = (bf16[4,128,256]{2,1,0:T(8,128)(2,1)S(1)}, bf16[4,128,256]{2,1,0:T(8,128)(2,1)}, u32[]{:S(2)}, u32[]{:S(2)}) collective-permute-start(bf16[4,128,256]{2,1,0:T(8,128)(2,1)S(1)} %copy-done.29), channel_id=1, source_target_pairs={{0,4},{1,5},{2,6},{3,7},{4,0},{5,1},{6,2},{7,3},{8,12},{9,13},{10,... | collective-permute-start | bytes 786440 | tf_op jit(solution)/shard_map/ppermute | solution.py:341
  283.5 24.0 %collective-permute-start.14 = (bf16[4,128,256]{2,1,0:T(8,128)(2,1)S(1)}, bf16[4,128,256]{2,1,0:T(8,128)(2,1)}, u32[]{:S(2)}, u32[]{:S(2)}) collective-permute-start(bf16[4,128,256]{2,1,0:T(8,128)(2,1)S(1)} %copy-done.28), channel_id=1, source_target_pairs={{0,5},{1,4},{2,7},{3,6},{4,1},{5,0},{6,3},{7,2},{8,13},{9,12},{10,... | collective-permute-start | bytes 786440 | tf_op jit(solution)/shard_map/ppermute | solution.py:341
  285.7 23.3 %collective-permute-start.15 = (bf16[4,128,256]{2,1,0:T(8,128)(2,1)S(1)}, bf16[4,128,256]{2,1,0:T(8,128)(2,1)}, u32[]{:S(2)}, u32[]{:S(2)}) collective-permute-start(bf16[4,128,256]{2,1,0:T(8,128)(2,1)S(1)} %copy-done.27), channel_id=1, source_target_pairs={{0,6},{1,7},{2,4},{3,5},{4,2},{5,3},{6,0},{7,1},{8,14},{9,15},{10,... | collective-permute-start | bytes 786440 | tf_op jit(solution)/shard_map/ppermute | solution.py:341
  290.6 19.2 %collective-permute-start.16 = (bf16[4,128,256]{2,1,0:T(8,128)(2,1)S(1)}, bf16[4,128,256]{2,1,0:T(8,128)(2,1)}, u32[]{:S(2)}, u32[]{:S(2)}) collective-permute-start(bf16[4,128,256]{2,1,0:T(8,128)(2,1)S(1)} %copy-done.26), channel_id=1, source_target_pairs={{0,7},{1,6},{2,5},{3,4},{4,3},{5,2},{6,1},{7,0},{8,15},{9,14},{10,... | collective-permute-start | bytes 786440 | tf_op jit(solution)/shard_map/ppermute | solution.py:341
  306.0 17.5 %collective-permute-start.29 = (bf16[512,512]{1,0:T(8,128)(2,1)S(1)}, bf16[512,512]{1,0:T(8,128)(2,1)S(1)}, u32[]{:S(2)}, u32[]{:S(2)}) collective-permute-start(bf16[512,512]{1,0:T(8,128)(2,1)S(1)} %copy-done.12), channel_id=1, source_target_pairs={{0,8},{8,0},{1,9},{9,1},{2,10},{10,2},{3,11},{11,3},{4,12},{12,4},... | collective-permute-start | bytes 1572872 | tf_op jit(solution)/shard_map/ppermute | solution.py:336
  307.5 22.5 %collective-permute-start.31 = (bf16[512,512]{1,0:T(8,128)(2,1)}, bf16[512,512]{1,0:T(8,128)(2,1)S(1)}, u32[]{:S(2)}, u32[]{:S(2)}) collective-permute-start(bf16[512,512]{1,0:T(8,128)(2,1)} %collective-permute-done.30), channel_id=1, source_target_pairs={{0,8},{8,0},{1,9},{9,1},{2,10},{10,2},{3,11},{11,3},{4,12},{12,4},... | collective-permute-start | bytes 1572872 | tf_op jit(solution)/shard_map/ppermute | solution.py:336
  309.0 22.6 %collective-permute-start.48 = (bf16[4,128,256]{2,1,0:T(8,128)(2,1)S(1)}, bf16[4,128,256]{2,1,0:T(8,128)(2,1)S(1)}, u32[]{:S(2)}, u32[]{:S(2)}) collective-permute-start(bf16[4,128,256]{2,1,0:T(8,128)(2,1)S(1)} %copy-done.32), channel_id=1, source_target_pairs={{0,2},{1,3},{2,0},{3,1},{4,6},{5,7},{6,4},{7,5},{8,10},{9,11},{10,... | collective-permute-start | bytes 786440 | tf_op jit(solution)/shard_map/ppermute | solution.py:341
  309.8 34.9 %collective-permute-start.49 = (bf16[4,128,256]{2,1,0:T(8,128)(2,1)}, bf16[4,128,256]{2,1,0:T(8,128)(2,1)}, u32[]{:S(2)}, u32[]{:S(2)}) collective-permute-start(bf16[4,128,256]{2,1,0:T(8,128)(2,1)} %get-tuple-element.137), channel_id=1, source_target_pairs={{0,3},{1,2},{2,1},{3,0},{4,7},{5,6},{6,5},{7,4},{8,11},{9,10},{10,... | collective-permute-start | bytes 786440 | tf_op jit(solution)/shard_map/ppermute | solution.py:341
  323.4 22.5 %collective-permute-start.41 = (bf16[4,128,256]{2,1,0:T(8,128)(2,1)}, bf16[4,128,256]{2,1,0:T(8,128)(2,1)}, u32[]{:S(2)}, u32[]{:S(2)}) collective-permute-start(bf16[4,128,256]{2,1,0:T(8,128)(2,1)} %get-tuple-element.128), channel_id=1, source_target_pairs={{0,2},{1,3},{2,0},{3,1},{4,6},{5,7},{6,4},{7,5},{8,10},{9,11},{10,... | collective-permute-start | bytes 786440 | tf_op jit(solution)/shard_map/ppermute | solution.py:341
  330.0 17.2 %collective-permute-start.42 = (bf16[4,128,256]{2,1,0:T(8,128)(2,1)}, bf16[4,128,256]{2,1,0:T(8,128)(2,1)}, u32[]{:S(2)}, u32[]{:S(2)}) collective-permute-start(bf16[4,128,256]{2,1,0:T(8,128)(2,1)} %get-tuple-element.129), channel_id=1, source_target_pairs={{0,3},{1,2},{2,1},{3,0},{4,7},{5,6},{6,5},{7,4},{8,11},{9,10},{10,... | collective-permute-start | bytes 786440 | tf_op jit(solution)/shard_map/ppermute | solution.py:341
  330.0 17.2 %collective-permute-start.27 = (f32[8,2048]{1,0:T(8,128)S(1)}, f32[8,2048]{1,0:T(8,128)S(1)}, u32[]{:S(2)}, u32[]{:S(2)}) collective-permute-start(f32[8,2048]{1,0:T(8,128)S(1)} %copy-done.18), channel_id=1, source_target_pairs={{0,8},{8,0},{1,9},{9,1},{2,10},{10,2},{3,11},{11,3},{4,12},{12,4},... | collective-permute-start | bytes 196616 | tf_op jit(solution)/shard_map/ppermute | solution.py:336
  331.6 17.1 %collective-permute-start.26 = (f32[8,2048]{1,0:T(8,128)}, f32[8,2048]{1,0:T(8,128)S(1)}, u32[]{:S(2)}, u32[]{:S(2)}) collective-permute-start(f32[8,2048]{1,0:T(8,128)} %get-tuple-element.109.refs_0_), channel_id=1, source_target_pairs={{0,8},{8,0},{1,9},{9,1},{2,10},{10,2},{3,11},{11,3},{4,12},{12,4},... | collective-permute-start | bytes 196616 | tf_op jit(solution)/shard_map/ppermute | solution.py:336
  344.8 20.6 %collective-permute-start.43 = (bf16[4,128,256]{2,1,0:T(8,128)(2,1)}, bf16[4,128,256]{2,1,0:T(8,128)(2,1)S(1)}, u32[]{:S(2)}, u32[]{:S(2)}) collective-permute-start(bf16[4,128,256]{2,1,0:T(8,128)(2,1)} %get-tuple-element.130), channel_id=1, source_target_pairs={{0,4},{1,5},{2,6},{3,7},{4,0},{5,1},{6,2},{7,3},{8,12},{9,13},{10,... | collective-permute-start | bytes 786440 | tf_op jit(solution)/shard_map/ppermute | solution.py:341
  346.0 25.1 %collective-permute-start.44 = (bf16[4,128,256]{2,1,0:T(8,128)(2,1)S(1)}, bf16[4,128,256]{2,1,0:T(8,128)(2,1)S(1)}, u32[]{:S(2)}, u32[]{:S(2)}) collective-permute-start(bf16[4,128,256]{2,1,0:T(8,128)(2,1)S(1)} %copy-done.24), channel_id=1, source_target_pairs={{0,5},{1,4},{2,7},{3,6},{4,1},{5,0},{6,3},{7,2},{8,13},{9,12},{10,... | collective-permute-start | bytes 786440 | tf_op jit(solution)/shard_map/ppermute | solution.py:341
  347.2 24.5 %collective-permute-start.34 = (bf16[4,128,256]{2,1,0:T(8,128)(2,1)}, bf16[4,128,256]{2,1,0:T(8,128)(2,1)S(1)}, u32[]{:S(2)}, u32[]{:S(2)}) collective-permute-start(bf16[4,128,256]{2,1,0:T(8,128)(2,1)} %get-tuple-element.121), channel_id=1, source_target_pairs={{0,1},{1,0},{2,3},{3,2},{4,5},{5,4},{6,7},{7,6},{8,9},{9,8},{10,11... | collective-permute-start | bytes 786440 | tf_op jit(solution)/shard_map/ppermute | solution.py:341
  347.2 24.5 %collective-permute-start.45 = (bf16[4,128,256]{2,1,0:T(8,128)(2,1)}, bf16[4,128,256]{2,1,0:T(8,128)(2,1)S(1)}, u32[]{:S(2)}, u32[]{:S(2)}) collective-permute-start(bf16[4,128,256]{2,1,0:T(8,128)(2,1)} %get-tuple-element.132), channel_id=1, source_target_pairs={{0,6},{1,7},{2,4},{3,5},{4,2},{5,3},{6,0},{7,1},{8,14},{9,15},{10,... | collective-permute-start | bytes 786440 | tf_op jit(solution)/shard_map/ppermute | solution.py:341
  348.7 24.5 %collective-permute-start.46 = (bf16[4,128,256]{2,1,0:T(8,128)(2,1)}, bf16[4,128,256]{2,1,0:T(8,128)(2,1)S(1)}, u32[]{:S(2)}, u32[]{:S(2)}) collective-permute-start(bf16[4,128,256]{2,1,0:T(8,128)(2,1)} %get-tuple-element.133), channel_id=1, source_target_pairs={{0,7},{1,6},{2,5},{3,4},{4,3},{5,2},{6,1},{7,0},{8,15},{9,14},{10,... | collective-permute-start | bytes 786440 | tf_op jit(solution)/shard_map/ppermute | solution.py:341
  365.4 22.5 %collective-permute-start.50 = (bf16[4,128,256]{2,1,0:T(8,128)(2,1)S(1)}, bf16[4,128,256]{2,1,0:T(8,128)(2,1)S(1)}, u32[]{:S(2)}, u32[]{:S(2)}) collective-permute-start(bf16[4,128,256]{2,1,0:T(8,128)(2,1)S(1)} %copy-done.23), channel_id=1, source_target_pairs={{0,4},{1,5},{2,6},{3,7},{4,0},{5,1},{6,2},{7,3},{8,12},{9,13},{10,... | collective-permute-start | bytes 786440 | tf_op jit(solution)/shard_map/ppermute | solution.py:341
  371.1 22.5 %collective-permute-start.51 = (bf16[4,128,256]{2,1,0:T(8,128)(2,1)S(1)}, bf16[4,128,256]{2,1,0:T(8,128)(2,1)}, u32[]{:S(2)}, u32[]{:S(2)}) collective-permute-start(bf16[4,128,256]{2,1,0:T(8,128)(2,1)S(1)} %copy-done.22), channel_id=1, source_target_pairs={{0,5},{1,4},{2,7},{3,6},{4,1},{5,0},{6,3},{7,2},{8,13},{9,12},{10,... | collective-permute-start | bytes 786440 | tf_op jit(solution)/shard_map/ppermute | solution.py:341
  371.7 22.8 %collective-permute-start.47 = (bf16[4,128,256]{2,1,0:T(8,128)(2,1)}, bf16[4,128,256]{2,1,0:T(8,128)(2,1)}, u32[]{:S(2)}, u32[]{:S(2)}) collective-permute-start(bf16[4,128,256]{2,1,0:T(8,128)(2,1)} %get-tuple-element.135), channel_id=1, source_target_pairs={{0,1},{1,0},{2,3},{3,2},{4,5},{5,4},{6,7},{7,6},{8,9},{9,8},{10,11... | collective-permute-start | bytes 786440 | tf_op jit(solution)/shard_map/ppermute | solution.py:341
  371.8 23.9 %collective-permute-start.52 = (bf16[4,128,256]{2,1,0:T(8,128)(2,1)}, bf16[4,128,256]{2,1,0:T(8,128)(2,1)}, u32[]{:S(2)}, u32[]{:S(2)}) collective-permute-start(bf16[4,128,256]{2,1,0:T(8,128)(2,1)} %get-tuple-element.140), channel_id=1, source_target_pairs={{0,6},{1,7},{2,4},{3,5},{4,2},{5,3},{6,0},{7,1},{8,14},{9,15},{10,... | collective-permute-start | bytes 786440 | tf_op jit(solution)/shard_map/ppermute | solution.py:341
  373.2 22.4 %collective-permute-start.53 = (bf16[4,128,256]{2,1,0:T(8,128)(2,1)}, bf16[4,128,256]{2,1,0:T(8,128)(2,1)}, u32[]{:S(2)}, u32[]{:S(2)}) collective-permute-start(bf16[4,128,256]{2,1,0:T(8,128)(2,1)} %get-tuple-element.141), channel_id=1, source_target_pairs={{0,7},{1,6},{2,5},{3,4},{4,3},{5,2},{6,1},{7,0},{8,15},{9,14},{10,... | collective-permute-start | bytes 786440 | tf_op jit(solution)/shard_map/ppermute | solution.py:341
  388.6 94.7 %collective-permute-start.25 = (bf16[2048,256]{1,0:T(8,128)(2,1)S(1)}, bf16[2048,256]{1,0:T(8,128)(2,1)S(1)}, u32[]{:S(2)}, u32[]{:S(2)}) collective-permute-start(bf16[2048,256]{1,0:T(8,128)(2,1)S(1)} %copy-done.6), channel_id=1, source_target_pairs={{0,8},{8,0},{1,9},{9,1},{2,10},{10,2},{3,11},{11,3},{4,12},{12,4},... | collective-permute-start | bytes 3145736 | tf_op jit(solution)/shard_map/ppermute | solution.py:336
  393.6 89.6 %collective-permute-start.24 = (bf16[2048,256]{1,0:T(8,128)(2,1)S(1)}, bf16[2048,256]{1,0:T(8,128)(2,1)}, u32[]{:S(2)}, u32[]{:S(2)}) collective-permute-start(bf16[2048,256]{1,0:T(8,128)(2,1)S(1)} %copy-done.7), channel_id=1, source_target_pairs={{0,8},{8,0},{1,9},{9,1},{2,10},{10,2},{3,11},{11,3},{4,12},{12,4},... | collective-permute-start | bytes 3145736 | tf_op jit(solution)/shard_map/ppermute | solution.py:336
  394.5 95.0 %collective-permute-start.54 = (bf16[2048,256]{1,0:T(8,128)(2,1)}, bf16[2048,256]{1,0:T(8,128)(2,1)}, u32[]{:S(2)}, u32[]{:S(2)}) collective-permute-start(bf16[2048,256]{1,0:T(8,128)(2,1)} %shard_map.142.refs_0_), channel_id=1, source_target_pairs={{0,8},{8,0},{1,9},{9,1},{2,10},{10,2},{3,11},{11,3},{4,12},{12,4},... | collective-permute-start | bytes 3145736 | tf_op jit(solution)/shard_map/ppermute | solution.py:336
  404.5 90.3 %collective-permute-start.55 = (bf16[2048,256]{1,0:T(8,128)(2,1)}, bf16[2048,256]{1,0:T(8,128)(2,1)}, u32[]{:S(2)}, u32[]{:S(2)}) collective-permute-start(bf16[2048,256]{1,0:T(8,128)(2,1)} %shard_map.143.refs_1_.refs_3_), channel_id=1, source_target_pairs={{0,8},{8,0},{1,9},{9,1},{2,10},{10,2},{3,11},{11,3},{4,12},{12,4},... | collective-permute-start | bytes 3145736 | tf_op jit(solution)/shard_map/ppermute | solution.py:336
  405.4 1.3 collective-permute-start.56
  406.6 4.3 collective-permute-start.57
  411.0 4.3 collective-permute-start.58
  415.3 67.3 %collective-permute-start.59 = (f32[32,512]{1,0:T(8,128)S(1)}, f32[32,512]{1,0:T(8,128)S(1)}, u32[]{:S(2)}, u32[]{:S(2)}) collective-permute-start(f32[32,512]{1,0:T(8,128)S(1)} %add.19), channel_id=1, source_target_pairs={{0,8},{8,0},{1,9},{9,1},{2,10},{10,2},{3,11},{11,3},{4,12},{12,4},... | collective-permute-start | bytes 196616 | tf_op jit(solution)/shard_map/ppermute | solution.py:336
  (42 other events, 414.4 us)

commit v2 on v1

--- a/solution.py
+++ b/solution.py
@@ -172,12 +172,14 @@
     near = pl.ds(pl.multiple_of(z * cols, cols), cols)
     far = pl.ds(pl.multiple_of((1 - z) * cols, cols), cols)
     wide = cols // n_chunk
+    head = pl.ds(pl.multiple_of(z * cols, cols), wide)
+    shared = (slice(wide, cols), slice(cols + wide, 2 * cols))
     group = GROUP
     for first in range(0, n_src, group):
         rows = slice(first * cap, (first + group) * cap)
         for i in range(first, first + group):
             put_rows(z, slice(i * cap, (i + 1) * cap), dos[i], do_ref)
-        total = None
+        totals = [None, None]
         for k, (a_ref, b_ref, slope, gelu) in enumerate(((wa, wb, sv, gv), (wa2, wb2, sv2, gv2))):
             if k == 0:
                 dhid = lax.dot_general(do_ref[rows, :], wc[0], NT, preferred_element_type=F32)
@@ -189,14 +191,14 @@
             if k == 0:
                 da_ref[0, rows, :] = grad_a
                 db_ref[0, rows, :] = grad_b
-            part = lax.dot_general(grad_a, a_ref[0, near, :], NT, preferred_element_type=F32)
-            part = part + lax.dot_general(grad_b, b_ref[0, near, :], NT, preferred_element_type=F32)
-            part = part.astype(BF16).astype(F32)
-            total = part if total is None else total + part
-        total = total.astype(BF16)
-        for c in range(n_chunk):
+            for c, picks in enumerate(((head,), shared)):
+                parts = [lax.dot_general(grad_a, a_ref[0, p, :], NT, preferred_element_type=F32) + lax.dot_general(grad_b, b_ref[0, p, :], NT, preferred_element_type=F32) for p in picks]
+                part = jnp.concatenate(parts, axis=1).astype(BF16).astype(F32)
+                totals[c] = part if k == 0 else totals[c] + part
+        for c in range(2):
+            total = totals[c].astype(BF16)
             for i in range(group):
-                outs[c * n_src + first + i][0] = total[i * cap:(i + 1) * cap, c * wide:(c + 1) * wide]
+                outs[c * n_src + first + i][0] = total[i * cap:(i + 1) * cap]
 
 
 def weight_grad_kernel(z_ref, *refs, n_src, widths):
@@ -246,12 +248,9 @@
     dg_ref[...] = wide.T[:8, :]
 
 
-def logit_grad_kernel(z_ref, rows_ref, prob_ref, one_ref, two_ref, x_ref, *refs, n_chunk):
-    dgs, (dl_ref, dw_ref) = refs[:2 * n_chunk], refs[2 * n_chunk:]
+def logit_grad_kernel(z_ref, rows_ref, prob_ref, one_ref, two_ref, x_ref, dga_ref, dgb_ref, dl_ref, dw_ref):
     n_experts, n_tokens = prob_ref.shape
-    mine = sum(r[0:2, :] for r in dgs[:n_chunk])
-    other = sum(r[0:2, :] for r in dgs[n_chunk:])
-    dgate = mine + other
+    dgate = dga_ref[0:2, :] + dgb_ref[0:2, :]
     dg_one, dg_two = dgate[0:1], dgate[1:2]
     gate_one, gate_two = rows_ref[2:3, :], rows_ref[3:4, :]
     prob_one, prob_two = rows_ref[4:5, :], rows_ref[5:6, :]
@@ -268,8 +267,10 @@
     dw_ref[...] = raw[:n_experts] + raw[n_experts:2 * n_experts] + raw[2 * n_experts:]
 
 
-def combine_in_kernel(z_ref, cols_ref, dl_ref, wt_ref, *refs, n_src):
-    srcs, dx_ref = refs[:n_src], refs[n_src]
+def combine_in_kernel(z_ref, cols_ref, dl_ref, *refs, n_src, last):
+    n_w = 2 if last else 1
+    wts, refs = refs[:n_w], refs[n_w:]
+    srcs, refs = refs[:n_src], refs[n_src:]
     blocks = srcs[0].shape[0] // 128
     (blk_one, hot_one), (blk_two, hot_two) = slot_picks(cols_ref)
     zero = jnp.zeros((TOKEN_TILE, 128), BF16)
@@ -281,25 +282,27 @@
             parts.append(jnp.where(blk_one == this, hot_one, jnp.where(blk_two == this, hot_two, zero)))
         part = jnp.dot(jnp.concatenate(parts, axis=1), srcs[d][...], preferred_element_type=F32)
         acc = part if acc is None else acc + part
-    high, mid, low = split3(wt_ref[...])
+    high, mid, low = split3(jnp.concatenate([w[...] for w in wts], axis=1))
     weights = jnp.concatenate([high, mid, high, low, high, mid], axis=0)
     back = lax.dot_general(dl_ref[...], weights, TN, preferred_element_type=F32)
-    dx_ref[...] = (acc + back).astype(BF16)
-
-
-def place_kernel(z_ref, *refs):
-    pieces, out = refs[:-1], refs[-1]
-    n_chunk = len(pieces) // 2
-    wide = pieces[0].shape[1]
-    for side in range(2):
-        @pl.when(pl.program_id(1) == side)
-        def _(side=side):
-            for c in range(n_chunk):
-                out[:, c * wide:(c + 1) * wide] = pieces[side * n_chunk + c][...]
-
-
-def place_last_kernel(z_ref, kept_ref, piece_ref, out_ref):
-    out_ref[...] = piece_ref[...]
+    res = (acc + back).astype(BF16)
+    if not last:
+        refs[0][...] = res
+        return
+    mine, other, dx_ref = refs
+    wide = mine.shape[1]
+    low_side = z_ref[0] == 0
+    dx_ref[:, :wide] = jnp.where(low_side, mine[...], other[...])
+    dx_ref[:, wide:2 * wide] = res[:, :wide]
+    dx_ref[:, 2 * wide:3 * wide] = jnp.where(low_side, other[...], mine[...])
+    dx_ref[:, 3 * wide:] = res[:, wide:]
+
+
+def sum_kernel(z_ref, *refs):
+    parts, out = [r[...] for r in refs[:-1]], refs[-1]
+    while len(parts) > 1:
+        parts = [parts[i] + parts[i + 1] for i in range(0, len(parts), 2)]
+    out[...] = parts[0]
 
 
 def cost(flops, nbytes, trans=0):
@@ -310,6 +313,7 @@
     tp_size = mesh.shape["tp"]
     n_src = mesh.shape["ep"]
     n_chunk = 2
+    all_vmem = pltpu.CompilerParams(vmem_limit_bytes=67043328)
     diag = [n_src - 2, n_src - 1]
     early = diag + [0, 1]
     late = [2, 4, 3, 5]
@@ -344,7 +348,7 @@
             return pl.pallas_call(
                 kernel,
                 grid_spec=pltpu.PrefetchScalarGridSpec(num_scalar_prefetch=1, grid=grid, in_specs=in_specs, out_specs=out_specs, scratch_shapes=list(scratch)),
-                out_shape=out_shape, cost_estimate=estimate)(z, *args)
+                out_shape=out_shape, cost_estimate=estimate, compiler_params=all_vmem)(z, *args)
 
         wa2, wb2 = across(w_gelu), across(w_lin)
         wt = w_router.T
@@ -354,7 +358,7 @@
             in_specs=[pl.BlockSpec(memory_space=pltpu.SMEM)] + [pl.BlockSpec(memory_space=pltpu.VMEM)] * 4,
             out_shape=(sds((16, n_tokens), F32), sds((n_experts, n_tokens), F32), sds((block, model), BF16)),
             cost_estimate=cost(2 * 96 * n_tokens * model, 2 * n_tokens * model, n_experts * n_tokens),
-            name="route",
+            compiler_params=all_vmem, name="route",
         )(me, x_rows, wt, id_one, id_two)
         token_cols = rows.T
         wcz = across(lax.dynamic_slice_in_dim(w_out, (1 - z[0]) * cols, cols, 2))
@@ -410,19 +414,18 @@
         own_parts = [forward_own(cuts[i], cuts[i + 1]) for i in range(2)]
         part_rows = [(cuts[i + 1] - cuts[i]) * slot_cap for i in range(2)]
         fwd = pl.pallas_call(
-            functools.partial(forward_other_kernel, n_src=n_src, n_chunk=n_chunk), grid=(own,),
+            functools.partial(forward_other_kernel, n_src=n_src, n_chunk=1), grid=(own,),
             in_specs=[whole(slot_cap, model)] * n_src + [whole(r, cols) for r in part_rows] + [whole(model, width)] * 2 + [whole(width, cols)],
-            out_specs=[whole(slot_cap, wide)] * (n_src * n_chunk) + [whole(rows_all, width)] * 2,
-            out_shape=[sds((own, slot_cap, wide), BF16)] * (n_src * n_chunk) + [sds((own, rows_all, width), F32)] * 2,
+            out_specs=[whole(slot_cap, cols)] * n_src + [whole(rows_all, width)] * 2,
+            out_shape=[sds((own, slot_cap, cols), BF16)] * n_src + [sds((own, rows_all, width), F32)] * 2,
             cost_estimate=cost(2 * own * rows_all * width * (2 * model + cols), 32e6, own * rows_all * width),
-            name="k_fwd_other")(*xs, own_parts[0][3], own_parts[1][3], wa2, wb2, wcz)
-        gv2, sv2 = fwd[n_chunk * n_src:]
-        back_out = []
-        for c in range(n_chunk):
-            got = [None] * n_src
-            for i, d in enumerate(src_order):
-                got[d] = to_peer(fwd[c * n_src + i], d).reshape(block, wide)
-            back_out.append(got)
+            compiler_params=all_vmem, name="k_fwd_other")(*xs, own_parts[0][3], own_parts[1][3], wa2, wb2, wcz)
+        gv2, sv2 = fwd[n_src:]
+        back_out = [None] * n_src
+        for i, d in enumerate(src_order):
+            back_out[d] = to_peer(fwd[i], d).reshape(block, cols)
+
+        dx_widths = (wide, 2 * wide)
 
         def backward(peers, at):
             n_rows = len(peers) * slot_cap
@@ -444,8 +447,8 @@
             return call(
                 functools.partial(backward_kernel, widths=[len(dos[d]) for d in peers], saved_widths=counts, cols=cols, n_chunk=n_chunk), (own,),
                 [whole(slot_cap, v.shape[2]) for v in args] + specs + [whole(model, width)] * 2 + [whole(width, model)] + [whole(model, width)] * 2 + [whole(width, cols)] * 2,
-                [whole(slot_cap, wide)] * (len(peers) * n_chunk) + [whole(n_rows, width)] * 2,
-                [sds((own, slot_cap, wide), BF16)] * (len(peers) * n_chunk) + [sds((own, n_rows, width), BF16)] * 2,
+                [whole(slot_cap, w) for w in dx_widths for _ in peers] + [whole(n_rows, width)] * 2,
+                [sds((own, slot_cap, w), BF16) for w in dx_widths for _ in peers] + [sds((own, n_rows, width), BF16)] * 2,
                 cost(4 * own * n_rows * width * (model + 2 * cols), 6e3 * own * n_rows),
                 (*args, *saved, w_gelu, w_lin, w_out, wa2, wb2, wcz, wcn),
                 [pltpu.VMEM((n_rows, model), BF16)])
@@ -457,7 +460,7 @@
             got = [None] * n_src
             for peers, vals in ((early, bwd_a), (late, bwd_b)):
                 for i, d in enumerate(peers):
-                    got[d] = to_peer(vals[c * len(peers) + i], d).reshape(block, wide)
+                    got[d] = to_peer(vals[c * len(peers) + i], d).reshape(block, dx_widths[c])
             back_in.append(got)
 
         all_dos = [v for d in src_order for v in dos[d]]
@@ -477,61 +480,52 @@
             return pl.BlockSpec((TOKEN_TILE, b), lambda i, z: (i, 0 if col is None else z[0] * n_chunk + col))
 
         n_tiles = (n_tokens // TOKEN_TILE,)
-        y_mine, y_other, dg_mine, dg_other = [], [], [], []
-        for c in range(n_chunk):
-            y, dg = call(
-                functools.partial(combine_out_kernel, n_src=n_src), n_tiles,
-                [tiles(16), tiles(wide, c)] + [resident(block, wide)] * n_src,
-                [tiles(wide), pl.BlockSpec((8, TOKEN_TILE), lambda i, z: (0, i))],
-                [sds((n_tokens, wide), BF16), sds((8, n_tokens), F32)],
-                cost(4 * n_tokens * n_src * block * wide, 6e6),
-                (token_cols, dy_rows, *back_out[c]))
-            y_mine.append(y)
-            dg_mine.append(dg)
-            dg_other.append(across(dg))
-            y_other.append(across(y))
+        y_mine, dg_mine = call(
+            functools.partial(combine_out_kernel, n_src=n_src), n_tiles,
+            [tiles(16), pl.BlockSpec((TOKEN_TILE, cols), lambda i, z: (i, z[0]))] + [resident(block, cols)] * n_src,
+            [tiles(cols), pl.BlockSpec((8, TOKEN_TILE), lambda i, z: (0, i))],
+            [sds((n_tokens, cols), BF16), sds((8, n_tokens), F32)],
+            cost(4 * n_tokens * n_src * block * cols, 12e6),
+            (token_cols, dy_rows, *back_out))
+        dg_other = across(dg_mine)
+        y_other = across(y_mine)
 
         dl, dw = call(
-            functools.partial(logit_grad_kernel, n_chunk=n_chunk), (1,),
-            [resident(16, n_tokens), resident(n_experts, n_tokens), resident(1, n_tokens), resident(1, n_tokens), pl.BlockSpec((n_tokens, cols), lambda i, z: (0, z[0]))] + [resident(8, n_tokens)] * (2 * n_chunk),
+            logit_grad_kernel, (1,),
+            [resident(16, n_tokens), resident(n_experts, n_tokens), resident(1, n_tokens), resident(1, n_tokens), pl.BlockSpec((n_tokens, cols), lambda i, z: (0, z[0]))] + [resident(8, n_tokens)] * 2,
             [resident(6 * n_experts, n_tokens), resident(n_experts, cols)],
             [sds((6 * n_experts, n_tokens), BF16), sds((n_experts, cols), F32)],
             cost(2 * 96 * n_tokens * cols, 4e6),
-            (rows, prob, id_one, id_two, x_rows, *dg_mine, *dg_other))
-
-        dx_mine, dx_other = [], []
-        for c in range(n_chunk):
-            dx = call(
-                functools.partial(combine_in_kernel, n_src=n_src), n_tiles,
-                [tiles(16), pl.BlockSpec((6 * n_experts, TOKEN_TILE), lambda i, z: (0, i)), pl.BlockSpec((n_experts, wide), lambda i, z: (0, z[0] * n_chunk + c))] + [resident(block, wide)] * n_src,
-                tiles(wide), sds((n_tokens, wide), BF16),
-                cost(2 * n_tokens * n_src * block * wide, 6e6),
-                (token_cols, dl, wt, *back_in[c]))
-            dx_mine.append(dx)
-            dx_other.append(across(dx))
-        bit = 1
-        while bit < n_src:
-            dw = dw + to_peer(dw, bit)
-            bit *= 2
+            (rows, prob, id_one, id_two, x_rows, dg_mine, dg_other))
+
+        def combine_in(last, extra, srcs):
+            quarters = [(lambda i, z: (0, 1)), (lambda i, z: (0, 3))] if last else [lambda i, z: (0, z[0] * n_chunk)]
+            return call(
+                functools.partial(combine_in_kernel, n_src=n_src, last=last), n_tiles,
+                [tiles(16), pl.BlockSpec((6 * n_experts, TOKEN_TILE), lambda i, z: (0, i))] + [pl.BlockSpec((n_experts, wide), q) for q in quarters]
+                + [resident(block, v.shape[1]) for v in srcs] + [tiles(wide)] * len(extra),
+                tiles(model if last else wide), sds((n_tokens, model if last else wide), BF16),
+                cost(2 * n_tokens * n_src * block * srcs[0].shape[1], 8e6),
+                (token_cols, dl, *([wt] * len(quarters)), *srcs, *extra))
+
+        dx_mine = combine_in(False, (), back_in[0])
+        dx_other = across(dx_mine)
+        grad_in = combine_in(True, (dx_mine, dx_other), back_in[1])
+
+        def add_all(parts):
+            return call(sum_kernel, (1,), [resident(n_experts, cols)] * len(parts), resident(n_experts, cols), sds((n_experts, cols), F32), cost(1e6, 4e5), parts)
+
+        dw = add_all((dw, to_peer(dw, 2), to_peer(dw, 4), to_peer(dw, 6)))
+        dw = add_all((dw, to_peer(dw, 1)))
         dw_other = across(dw)
 
-        def place(pieces):
-            return call(
-                place_kernel, (2, 2), [pl.BlockSpec((n_tokens // 2, wide), lambda i, h, z: (i, 0))] * len(pieces),
-                pl.BlockSpec((n_tokens // 2, cols), lambda i, h, z: (i, z[0] + h - 2 * h * z[0])),
-                sds((n_tokens, model), BF16), cost(1e6, 8e6), pieces)
-
-        act_out = place(y_mine + y_other)
-        first_dx = place(dx_mine + dx_other[:-1] + dx_mine[-1:])
-        grad_in = pl.pallas_call(
-            place_last_kernel,
-            grid_spec=pltpu.PrefetchScalarGridSpec(
-                num_scalar_prefetch=1, grid=(2,),
-                in_specs=[pl.BlockSpec(memory_space=pl.ANY), pl.BlockSpec((n_tokens // 2, wide), lambda i, z: (i, 0))],
-                out_specs=pl.BlockSpec((n_tokens // 2, wide), lambda i, z: (i, (1 - z[0]) * n_chunk + n_chunk - 1))),
-            out_shape=sds((n_tokens, model), BF16), input_output_aliases={1: 0},
-            cost_estimate=cost(1e6, 2e6), name="k_place_dx1")(z, first_dx, dx_other[-1])
-        grad_router = jnp.where(z[0] == 0, jnp.concatenate([dw, dw_other], axis=1), jnp.concatenate([dw_other, dw], axis=1)).T
+        lower = z[0] == 0
+
+        def join(mine, other):
+            return jnp.where(lower, jnp.concatenate([mine, other], axis=1), jnp.concatenate([other, mine], axis=1))
+
+        act_out = join(y_mine, y_other)
+        grad_router = join(dw, dw_other).T
         return act_out, grad_in, grad_wa, grad_wb, grad_wc, grad_router
 
     return jax.shard_map(local_step, mesh=mesh, in_specs=(P("ep", None), P(), P("ep"), P("ep"), P("ep", None, "tp"), P("ep", None, "tp"), P("ep", "tp", None), P("ep", None)), out_specs=(P("ep", None), P("ep", None), P("ep", None, "tp"), P("ep", None, "tp"), P("ep", "tp", None), P()), check_vma=False)

time: 497 us -> 452 us (0.909)
  waiting for transfers between devices: 234 us -> 193 us
  starting transfers between devices: 58.9 us -> 49 us
  other arithmetic: 0.7 us -> 7.99 us
    ppermute x15 -> x12, waiting for transfers between devices: 113 us -> 87.1 us  [across(): return lax.ppermute(val, 'tp', swap)]
    ppermute x45 -> x39, waiting for transfers between devices: 121 us -> 106 us  [to_peer(): return lax.ppermute(val, 'ep', [(i, i ^ d) for i in range(n_src)])]
    select_n x0 -> x1, other arithmetic: none -> 6.38 us  [join(): jnp.where(lower, jnp.concatenate([mine, other], axis=1), jnp.concatenate(...]
    ppermute x15 -> x12, starting transfers between devices: 17.9 us -> 12.6 us  [across(): return lax.ppermute(val, 'tp', swap)]
    ppermute x45 -> x39, starting transfers between devices: 40.9 us -> 36.4 us  [to_peer(): return lax.ppermute(val, 'ep', [(i, i ^ d) for i in range(n_src)])]
    pallas_call x19 -> x18, Pallas kernels: 173 us -> 173 us  [call(): pl.pallas_call(kernel, grid_spec=pltpu.PrefetchScalarGridSpec(num_scalar_...]
  transfers between devices with their start and end apart: 60 -> 51, of which waited for: 19 -> 15; matrix products, arithmetic and copies ran while one was open for 1% -> 2% of each run, Pallas kernels for 37% -> 39%
where the time goes in v2:
time: 452 us; the launch traced here: 450 us
  Pallas kernels  194 us (43%)
  waiting for transfers between devices  193 us (43%)
  starting transfers between devices  49 us (11%)
  other arithmetic  7.99 us (2%)
  local copies, waits for them, and re-layouts  5.22 us (1%)
    pallas_call x18, Pallas kernels, call(): pl.pallas_call(kernel, grid_spec=pltpu.PrefetchScalarGridSpec(num_scalar_...  173 us
    ppermute x39, waiting for transfers between devices, to_peer(): return lax.ppermute(val, 'ep', [(i, i ^ d) for i in range(n_src)])  106 us
    ppermute x12, waiting for transfers between devices, across(): return lax.ppermute(val, 'tp', swap)  87.1 us
    ppermute x39, starting transfers between devices, to_peer(): return lax.ppermute(val, 'ep', [(i, i ^ d) for i in range(n_src)])  36.4 us
    pallas_call x1, Pallas kernels, local_step(): pl.pallas_call(functools.partial(forward_other_kernel, n_src=n_src, n_chu...  13.9 us
    ppermute x12, starting transfers between devices, across(): return lax.ppermute(val, 'tp', swap)  12.6 us
  transfers between devices with their start and end apart: 51, of which 15 were waited for; matrix products, arithmetic and copies ran while one was open for 2% of the time, Pallas kernels for 39%

profile of v2, /device:TPU:0, one launch (start us, length us, event | category | flops | bytes accessed | tf_op | source)
XLA Modules:
  0.0 450.2 jit_solution(16044109155766635925)
XLA Ops:
  0.6 7.3 %route.1 = (f32[16,2048]{1,0:T(8,128)}, f32[32,2048]{1,0:T(8,128)}, bf16[512,1024]{1,0:T(8,128)(2,1)}) custom-call(s32[1]{0:T(128)} %bitcast.1.me_ref, bf16[2048,1024]{1,0:T(8,128)(2,1)} %x_ref.3, f32[32,1024]{1,0:T(8,128)} %bitcast.57, s32[1,2048]{1,0:T(1,128)} %bitcast.61, s32[1,2048]{1,0:T(1,128)} %bitcast.63), custom_call_target="tpu_custom_call" | custom-call | flops 402653184 | bytes 4194304 | tf_op jit(solution)/shard_map/route/pallas_call | solution.py:356
  7.9 11.6 %shard_map.127 = (bf16[512,1024]{1,0:T(8,128)(2,1)}, bf16[512,1024]{1,0:T(8,128)(2,1)}, bf16[512,1024]{1,0:T(8,128)(2,1)}) custom-call(s32[1]{0:T(128)} %bitcast.z_ref, f32[16,2048]{1,0:T(8,128)} %get-tuple-element.69.rows_ref, bf16[2048,1024]{1,0:T(8,128)(2,1)} %x_ref.3), custom_call_target="tpu_custom_call" | custom-call | flops 6442450944 | bytes 7340032 | tf_op jit(solution)/shard_map/pallas_call | solution.py:348
  19.5 3.6 collective-permute-start.1
  23.1 0.7 collective-permute-start.2
  23.7 8.6 %shard_map.128 = (bf16[512,1024]{1,0:T(8,128)(2,1)}, bf16[512,1024]{1,0:T(8,128)(2,1)}) custom-call(s32[1]{0:T(128)} %bitcast.z_ref, f32[16,2048]{1,0:T(8,128)} %get-tuple-element.69.rows_ref, bf16[2048,1024]{1,0:T(8,128)(2,1)} %x_ref.3), custom_call_target="tpu_custom_call" | custom-call | flops 4294967296 | bytes 6291456 | tf_op jit(solution)/shard_map/pallas_call | solution.py:348
  32.9 3.0 collective-permute-start
  35.8 11.1 %collective-permute-done.1 = bf16[512,1024]{1,0:T(8,128)(2,1)} collective-permute-done((bf16[512,1024]{1,0:T(8,128)(2,1)}, bf16[512,1024]{1,0:T(8,128)(2,1)}, u32[]{:S(2)}, u32[]{:S(2)}) %collective-permute-start.1) | collective-permute-done | bytes 1048608 | tf_op jit(solution)/shard_map/ppermute | solution.py:345
  47.0 2.5 collective-permute-start.7
  49.5 8.6 %shard_map.129 = (bf16[512,1024]{1,0:T(8,128)(2,1)}, bf16[512,1024]{1,0:T(8,128)(2,1)}) custom-call(s32[1]{0:T(128)} %bitcast.z_ref, f32[16,2048]{1,0:T(8,128)} %get-tuple-element.69.rows_ref, bf16[2048,1024]{1,0:T(8,128)(2,1)} %x_ref.3), custom_call_target="tpu_custom_call" | custom-call | flops 4294967296 | bytes 6291456 | tf_op jit(solution)/shard_map/pallas_call | solution.py:348
  58.1 12.4 %collective-permute-done.3 = bf16[512,1024]{1,0:T(8,128)(2,1)} collective-permute-done((bf16[512,1024]{1,0:T(8,128)(2,1)}, bf16[512,1024]{1,0:T(8,128)(2,1)}, u32[]{:S(2)}, u32[]{:S(2)}) %collective-permute-start.3) | collective-permute-done | bytes 1048608 | tf_op jit(solution)/shard_map/ppermute | solution.py:345
  70.4 1.2 collective-permute-start.5
  72.2 3.0 constant_dynamic-slice_fusion
  75.2 17.8 %collective-permute-done = bf16[512,1024]{1,0:T(8,128)(2,1)} collective-permute-done((bf16[512,1024]{1,0:T(8,128)(2,1)}, bf16[512,1024]{1,0:T(8,128)(2,1)}, u32[]{:S(2)}, u32[]{:S(2)}) %collective-permute-start) | collective-permute-done | bytes 1048608 | tf_op jit(solution)/shard_map/ppermute | solution.py:345
  93.0 1.6 collective-permute-start.9
  94.6 5.8 %shard_map.137 = (bf16[512,512]{1,0:T(8,128)(2,1)}, bf16[512,512]{1,0:T(8,128)(2,1)}) custom-call(s32[1]{0:T(128)} %bitcast.z_ref, f32[16,2048]{1,0:T(8,128)} %get-tuple-element.69.rows_ref, bf16[2048,1024]{1,0:T(8,128)(2,1)} %src_ref.13), custom_call_target="tpu_custom_call" | custom-call | flops 2147483648 | bytes 3145728 | tf_op jit(solution)/shard_map/pallas_call | solution.py:348
  100.3 15.0 %collective-permute-done.5 = bf16[512,1024]{1,0:T(8,128)(2,1)} collective-permute-done((bf16[512,1024]{1,0:T(8,128)(2,1)}, bf16[512,1024]{1,0:T(8,128)(2,1)}, u32[]{:S(2)}, u32[]{:S(2)}) %collective-permute-start.5) | collective-permute-done | bytes 1048608 | tf_op jit(solution)/shard_map/ppermute | solution.py:345
  115.4 1.5 collective-permute-start.26
  116.9 5.8 %shard_map.134 = (bf16[512,512]{1,0:T(8,128)(2,1)}, bf16[512,512]{1,0:T(8,128)(2,1)}) custom-call(s32[1]{0:T(128)} %bitcast.z_ref, f32[16,2048]{1,0:T(8,128)} %get-tuple-element.69.rows_ref, bf16[2048,1024]{1,0:T(8,128)(2,1)} %src_ref.13), custom_call_target="tpu_custom_call" | custom-call | flops 2147483648 | bytes 3145728 | tf_op jit(solution)/shard_map/pallas_call | solution.py:348
  122.7 11.6 %shard_map.130 = (f32[4,768,256]{2,1,0:T(8,128)}, f32[4,768,256]{2,1,0:T(8,128)}, bf16[4,768,256]{2,1,0:T(8,128)(2,1)}, bf16[4,768,512]{2,1,0:T(8,128)(2,1)}) custom-call(s32[1]{0:T(128)} %bitcast.z_ref, bf16[4,128,1024]{2,1,0:T(8,128)(2,1)} %bitcast.6.refs_0_, bf16[4,128,1024]{2,1,0:T(8,128)(2,1)} %bitcast.7.refs_1_, bf16[4,128,1024]{2,1,0:T(8,128)(2,1)} %bitcast.67, ...), custom_call_target="tpu_custom_call" | custom-call | flops 4026531840 | bytes 24576000 | tf_op jit(solution)/shard_map/pallas_call | solution.py:348
  134.9 6.5 %shard_map.131 = (f32[4,256,256]{2,1,0:T(8,128)}, f32[4,256,256]{2,1,0:T(8,128)}, bf16[4,256,256]{2,1,0:T(8,128)(2,1)}, bf16[4,256,512]{2,1,0:T(8,128)(2,1)}) custom-call(s32[1]{0:T(128)} %bitcast.z_ref, bf16[4,128,1024]{2,1,0:T(8,128)(2,1)} %bitcast.12.refs_0_.refs_6_, bf16[4,128,1024]{2,1,0:T(8,128)(2,1)} %bitcast.13.refs_1_.refs_7_, ...), custom_call_target="tpu_custom_call" | custom-call | flops 1342177280 | bytes 8192000 | tf_op jit(solution)/shard_map/pallas_call | solution.py:348
  141.4 1.6 collective-permute-start.19
  143.0 20.1 %collective-permute-done.9.refs_12_.refs_15_.refs_17_ = bf16[4,256,512]{2,1,0:T(8,128)(2,1)} collective-permute-done((bf16[4,256,512]{2,1,0:T(8,128)(2,1)}, bf16[4,256,512]{2,1,0:T(8,128)(2,1)}, u32[]{:S(2)}, u32[]{:S(2)}) %collective-permute-start.9) | collective-permute-done | bytes 1048608 | tf_op jit(solution)/shard_map/ppermute | solution.py:340
  163.1 1.4 collective-permute-start.21
  164.5 1.6 collective-permute-start.27
  166.1 13.9 %k_fwd_other.1 = (bf16[4,128,512]{2,1,0:T(8,128)(2,1)}, bf16[4,128,512]{2,1,0:T(8,128)(2,1)}, bf16[4,128,512]{2,1,0:T(8,128)(2,1)}, bf16[4,128,512]{2,1,0:T(8,12...) custom-call(bf16[4,128,1024]{2,1,0:T(8,128)(2,1)} %bitcast.6.refs_0_, ...), custom_call_target="tpu_custom_call" | custom-call | flops 5368709120 | bytes 32000000 | tf_op jit(solution)/shard_map/k_fwd_other/pallas_call | solution.py:416
  180.0 1.1 collective-permute-start.10
  181.6 0.9 collective-permute-start.12
  183.0 1.6 collective-permute-start.14
  185.0 11.2 %collective-permute-done.11 = bf16[4,128,512]{2,1,0:T(8,128)(2,1)} collective-permute-done((bf16[4,128,512]{2,1,0:T(8,128)(2,1)}, bf16[4,128,512]{2,1,0:T(8,128)(2,1)}, u32[]{:S(2)}, u32[]{:S(2)}) %collective-permute-start.11) | collective-permute-done | bytes 524320 | tf_op jit(solution)/shard_map/ppermute | solution.py:345
  196.2 9.3 %shard_map.138 = (bf16[512,1024]{1,0:T(8,128)(2,1)}, bf16[512,1024]{1,0:T(8,128)(2,1)}) custom-call(s32[1]{0:T(128)} %bitcast.z_ref, f32[16,2048]{1,0:T(8,128)} %get-tuple-element.69.rows_ref, bf16[2048,1024]{1,0:T(8,128)(2,1)} %src_ref.13), custom_call_target="tpu_custom_call" | custom-call | flops 4294967296 | bytes 6291456 | tf_op jit(solution)/shard_map/pallas_call | solution.py:348
  205.5 2.2 copy.14
  207.7 9.3 %shard_map.135 = (bf16[512,1024]{1,0:T(8,128)(2,1)}, bf16[512,1024]{1,0:T(8,128)(2,1)}) custom-call(s32[1]{0:T(128)} %bitcast.z_ref, f32[16,2048]{1,0:T(8,128)} %get-tuple-element.69.rows_ref, bf16[2048,1024]{1,0:T(8,128)(2,1)} %src_ref.13), custom_call_target="tpu_custom_call" | custom-call | flops 4294967296 | bytes 6291456 | tf_op jit(solution)/shard_map/pallas_call | solution.py:348
  217.0 1.7 collective-permute-start.30
  218.8 12.0 %collective-permute-done.14 = bf16[4,128,512]{2,1,0:T(8,128)(2,1)} collective-permute-done((bf16[4,128,512]{2,1,0:T(8,128)(2,1)}, bf16[4,128,512]{2,1,0:T(8,128)(2,1)}, u32[]{:S(2)}, u32[]{:S(2)}) %collective-permute-start.14) | collective-permute-done | bytes 524320 | tf_op jit(solution)/shard_map/ppermute | solution.py:345
  231.6 1.6 collective-permute-start.29
  233.2 22.3 %shard_map.132 = (bf16[2048,512]{1,0:T(8,128)(2,1)}, f32[8,2048]{1,0:T(8,128)}) custom-call(s32[1]{0:T(128)} %bitcast.z_ref, f32[2048,16]{1,0:T(8,128)} %bitcast.54, bf16[2048,1024]{1,0:T(8,128)(2,1)} %src_ref.13, bf16[512,512]{1,0:T(8,128)(2,1)} %bitcast.70, bf16[512,512]{1,0:T(8,128)(2,1)} %bitcast.15.refs_1_, bf16[512,512]{1,0:T(8,128)(2,1)} %bitcast.16.refs_2_, ...), custom_call_target="tpu_custom_call" | custom-call | flops 17179869184 | bytes 12000000 | tf_op jit(solution)/shard_map/pallas_call | solution.py:348
  255.5 12.6 %collective-permute-done.29 = bf16[512,512]{1,0:T(8,128)(2,1)} collective-permute-done((bf16[512,512]{1,0:T(8,128)(2,1)}, bf16[512,512]{1,0:T(8,128)(2,1)}, u32[]{:S(2)}, u32[]{:S(2)}) %collective-permute-start.29) | collective-permute-done | bytes 524320 | tf_op jit(solution)/shard_map/ppermute | solution.py:340
  268.5 1.6 collective-permute-start.22
  270.5 14.9 %shard_map.139 = (bf16[4,128,256]{2,1,0:T(8,128)(2,1)}, bf16[4,128,256]{2,1,0:T(8,128)(2,1)}, bf16[4,128,256]{2,1,0:T(8,128)(2,1)}, bf16[4,128,256]{2,1,0:T(8,12...) custom-call(s32[1]{0:T(128)} %bitcast.z_ref, ...), custom_call_target="tpu_custom_call" | custom-call | flops 4294967296 | bytes 12288000 | tf_op jit(solution)/shard_map/pallas_call | solution.py:348
  285.4 0.7 collective-permute-start.39
  286.1 8.4 %collective-permute-done.18.dgb_ref = f32[8,2048]{1,0:T(8,128)} collective-permute-done((f32[8,2048]{1,0:T(8,128)}, f32[8,2048]{1,0:T(8,128)}, u32[]{:S(2)}, u32[]{:S(2)}) %collective-permute-start.18) | collective-permute-done | bytes 65568 | tf_op jit(solution)/shard_map/ppermute | solution.py:340
  294.6 3.1 shard_map.133
  298.2 0.7 collective-permute-start.32
  298.9 1.3 collective-permute-start.46
  300.2 1.5 collective-permute-start.47
  301.7 1.8 collective-permute-done.40
  303.5 0.8 collective-permute-start.48
  304.2 14.9 %shard_map.136 = (bf16[4,128,256]{2,1,0:T(8,128)(2,1)}, bf16[4,128,256]{2,1,0:T(8,128)(2,1)}, bf16[4,128,256]{2,1,0:T(8,128)(2,1)}, bf16[4,128,256]{2,1,0:T(8,12...) custom-call(s32[1]{0:T(128)} %bitcast.z_ref, ...), custom_call_target="tpu_custom_call" | custom-call | flops 4294967296 | bytes 12288000 | tf_op jit(solution)/shard_map/pallas_call | solution.py:348
  319.6 1.3 collective-permute-start.38
  321.5 1.7 collective-permute-start.44
  323.2 1.6 shard_map.143.refs_0_
  324.8 14.4 %collective-permute-done.42 = bf16[4,128,256]{2,1,0:T(8,128)(2,1)} collective-permute-done((bf16[4,128,256]{2,1,0:T(8,128)(2,1)}, bf16[4,128,256]{2,1,0:T(8,128)(2,1)}, u32[]{:S(2)}, u32[]{:S(2)}) %collective-permute-start.42) | collective-permute-done | bytes 262176 | tf_op jit(solution)/shard_map/ppermute | solution.py:345
  339.4 1.0 collective-permute-start.34
  341.7 8.5 %shard_map.140.refs_10_ = bf16[2048,256]{1,0:T(8,128)(2,1)} custom-call(s32[1]{0:T(128)} %bitcast.z_ref, f32[2048,16]{1,0:T(8,128)} %bitcast.55, bf16[192,2048]{1,0:T(8,128)(2,1)} %get-tuple-element.91.dl_ref, f32[32,1024]{1,0:T(8,128)} %bitcast.58, bf16[512,256]{1,0:T(8,128)(2,1)} %bitcast.66, bf16[512,256]{1,0:T(8,128)(2,1)} %bitcast.43.refs_2_, ...), custom_call_target="tpu_custom_call" | custom-call | flops 4294967296 | bytes 8000000 | tf_op jit(solution)/shard_map/pallas_call | solution.py:348
  350.2 1.6 collective-permute-start.45
  351.8 1.5 shard_map.144
  353.9 0.6 collective-permute-done.34
  354.5 9.5 %collective-permute-done.35 = bf16[4,128,512]{2,1,0:T(8,128)(2,1)} collective-permute-done((bf16[4,128,512]{2,1,0:T(8,128)(2,1)}, bf16[4,128,512]{2,1,0:T(8,128)(2,1)}, u32[]{:S(2)}, u32[]{:S(2)}) %collective-permute-start.35) | collective-permute-done | bytes 524320 | tf_op jit(solution)/shard_map/ppermute | solution.py:345
  364.0 3.2 collective-permute-start.36
  367.2 46.0 %collective-permute-done.50 = f32[32,512]{1,0:T(8,128)} collective-permute-done((f32[32,512]{1,0:T(8,128)}, f32[32,512]{1,0:T(8,128)}, u32[]{:S(2)}, u32[]{:S(2)}) %collective-permute-start.50) | collective-permute-done | bytes 65568 | tf_op jit(solution)/shard_map/ppermute | solution.py:340
  413.3 14.4 %shard_map.142 = (f32[4,1024,256]{2,1,0:T(8,128)}, f32[4,1024,256]{2,1,0:T(8,128)}, f32[4,256,1024]{2,1,0:T(8,128)}) custom-call(s32[1]{0:T(128)} %bitcast.z_ref, bf16[4,128,1024]{2,1,0:T(8,128)(2,1)} %bitcast.6.refs_0_, bf16[4,128,1024]{2,1,0:T(8,128)(2,1)} %bitcast.7.refs_1_, bf16[4,128,1024]{2,1,0:T(8,128)(2,1)} %bitcast.69, ...), custom_call_target="tpu_custom_call" | custom-call | flops 6442450944 | bytes 40000000 | tf_op jit(solution)/shard_map/pallas_call | solution.py:348
  427.7 1.6 fusion
  429.3 14.5 %shard_map.141 = bf16[2048,1024]{1,0:T(8,128)(2,1)} custom-call(s32[1]{0:T(128)} %bitcast.z_ref, f32[2048,16]{1,0:T(8,128)} %bitcast.56, bf16[192,2048]{1,0:T(8,128)(2,1)} %get-tuple-element.91.dl_ref, f32[32,1024]{1,0:T(8,128)} %bitcast.59, f32[32,1024]{1,0:T(8,128)} %bitcast.60, bf16[512,512]{1,0:T(8,128)(2,1)} %bitcast.65, ...), custom_call_target="tpu_custom_call" | custom-call | flops 8589934592 | bytes 8000000 | tf_op jit(solution)/shard_map/pallas_call | solution.py:348
  443.8 6.4 %maximum_select_fusion = bf16[2048,1024]{1,0:T(8,128)(2,1)} fusion(bf16[2048,512]{1,0:T(8,128)(2,1)} %collective-permute-done.17, bf16[2048,512]{1,0:T(8,128)(2,1)} %get-tuple-element.88, pred[]{:T(512)S(6)} %eq.3), kind=kLoop, calls=%fused_computation | loop fusion | flops 18874368 | bytes 8388609 | tf_op jit(solution)/shard_map/jit(_where)/select_n | solution.py:525
  (62 shorter events, 8.5 us)
Async XLA Ops:
  19.5 27.5 %collective-permute-start.1 = (bf16[512,1024]{1,0:T(8,128)(2,1)}, bf16[512,1024]{1,0:T(8,128)(2,1)}, u32[]{:S(2)}, u32[]{:S(2)}) collective-permute-start(bf16[512,1024]{1,0:T(8,128)(2,1)} %get-tuple-element.71), channel_id=1, source_target_pairs={{0,7},{1,6},{2,5},{3,4},{4,3},{5,2},{6,1},{7,0},{8,15},{9,14},{10,... | collective-permute-start | bytes 3145736 | tf_op jit(solution)/shard_map/ppermute | solution.py:345
  23.1 26.4 %collective-permute-start.2 = (bf16[512,1024]{1,0:T(8,128)(2,1)}, bf16[512,1024]{1,0:T(8,128)(2,1)}, u32[]{:S(2)}, u32[]{:S(2)}) collective-permute-start(bf16[512,1024]{1,0:T(8,128)(2,1)} %get-tuple-element.73), channel_id=1, source_target_pairs={{0,1},{1,0},{2,3},{3,2},{4,5},{5,4},{6,7},{7,6},{8,9},{9,8},{10,11... | collective-permute-start | bytes 3145736 | tf_op jit(solution)/shard_map/ppermute | solution.py:345
  32.3 38.1 %collective-permute-start.3 = (bf16[512,1024]{1,0:T(8,128)(2,1)}, bf16[512,1024]{1,0:T(8,128)(2,1)}, u32[]{:S(2)}, u32[]{:S(2)}) collective-permute-start(bf16[512,1024]{1,0:T(8,128)(2,1)} %get-tuple-element.74), channel_id=1, source_target_pairs={{0,2},{1,3},{2,0},{3,1},{4,6},{5,7},{6,4},{7,5},{8,10},{9,11},{10,... | collective-permute-start | bytes 3145736 | tf_op jit(solution)/shard_map/ppermute | solution.py:345
  32.9 38.7 %collective-permute-start.4 = (bf16[512,1024]{1,0:T(8,128)(2,1)}, bf16[512,1024]{1,0:T(8,128)(2,1)}, u32[]{:S(2)}, u32[]{:S(2)}) collective-permute-start(bf16[512,1024]{1,0:T(8,128)(2,1)} %get-tuple-element.75), channel_id=1, source_target_pairs={{0,4},{1,5},{2,6},{3,7},{4,0},{5,1},{6,2},{7,3},{8,12},{9,13},{10,... | collective-permute-start | bytes 3145736 | tf_op jit(solution)/shard_map/ppermute | solution.py:345
  32.9 60.1 %collective-permute-start = (bf16[512,1024]{1,0:T(8,128)(2,1)}, bf16[512,1024]{1,0:T(8,128)(2,1)}, u32[]{:S(2)}, u32[]{:S(2)}) collective-permute-start(bf16[512,1024]{1,0:T(8,128)(2,1)} %get-tuple-element.70), channel_id=1, source_target_pairs={{0,6},{1,7},{2,4},{3,5},{4,2},{5,3},{6,0},{7,1},{8,14},{9,15},{10,... | collective-permute-start | bytes 3145736 | tf_op jit(solution)/shard_map/ppermute | solution.py:345
  47.0 117.5 %collective-permute-start.7 = (bf16[4,1024,256]{2,1,0:T(8,128)(2,1)}, bf16[4,1024,256]{2,1,0:T(8,128)(2,1)}, u32[]{:S(2)}, u32[]{:S(2)}) collective-permute-start(bf16[4,1024,256]{2,1,0:T(8,128)(2,1)} %refs_12_.3), channel_id=1, source_target_pairs={{0,8},{8,0},{1,9},{9,1},{2,10},{10,2},{3,11},{11,3},{4,12},{12,4},... | collective-permute-start | bytes 6291464 | tf_op jit(solution)/shard_map/ppermute | solution.py:340
  49.4 116.7 %collective-permute-start.8 = (bf16[4,1024,256]{2,1,0:T(8,128)(2,1)}, bf16[4,1024,256]{2,1,0:T(8,128)(2,1)}, u32[]{:S(2)}, u32[]{:S(2)}) collective-permute-start(bf16[4,1024,256]{2,1,0:T(8,128)(2,1)} %refs_13_.1), channel_id=1, source_target_pairs={{0,8},{8,0},{1,9},{9,1},{2,10},{10,2},{3,11},{11,3},{4,12},{12,4},... | collective-permute-start | bytes 6291464 | tf_op jit(solution)/shard_map/ppermute | solution.py:340
  70.4 45.0 %collective-permute-start.5 = (bf16[512,1024]{1,0:T(8,128)(2,1)}, bf16[512,1024]{1,0:T(8,128)(2,1)}, u32[]{:S(2)}, u32[]{:S(2)}) collective-permute-start(bf16[512,1024]{1,0:T(8,128)(2,1)} %get-tuple-element.76), channel_id=1, source_target_pairs={{0,3},{1,2},{2,1},{3,0},{4,7},{5,6},{6,5},{7,4},{8,11},{9,10},{10,... | collective-permute-start | bytes 3145736 | tf_op jit(solution)/shard_map/ppermute | solution.py:345
  71.6 62.7 %collective-permute-start.6 = (bf16[512,1024]{1,0:T(8,128)(2,1)}, bf16[512,1024]{1,0:T(8,128)(2,1)}, u32[]{:S(2)}, u32[]{:S(2)}) collective-permute-start(bf16[512,1024]{1,0:T(8,128)(2,1)} %get-tuple-element.77), channel_id=1, source_target_pairs={{0,5},{1,4},{2,7},{3,6},{4,1},{5,0},{6,3},{7,2},{8,13},{9,12},{10,... | collective-permute-start | bytes 3145736 | tf_op jit(solution)/shard_map/ppermute | solution.py:345
  93.0 70.1 %collective-permute-start.9 = (bf16[4,256,512]{2,1,0:T(8,128)(2,1)}, bf16[4,256,512]{2,1,0:T(8,128)(2,1)}, u32[]{:S(2)}, u32[]{:S(2)}) collective-permute-start(bf16[4,256,512]{2,1,0:T(8,128)(2,1)} %get-tuple-element.133), channel_id=1, source_target_pairs={{0,8},{8,0},{1,9},{9,1},{2,10},{10,2},{3,11},{11,3},{4,12},{12,4},... | collective-permute-start | bytes 3145736 | tf_op jit(solution)/shard_map/ppermute | solution.py:340
  115.4 26.0 %collective-permute-start.26 = (bf16[512,512]{1,0:T(8,128)(2,1)}, bf16[512,512]{1,0:T(8,128)(2,1)}, u32[]{:S(2)}, u32[]{:S(2)}) collective-permute-start(bf16[512,512]{1,0:T(8,128)(2,1)} %get-tuple-element.102), channel_id=1, source_target_pairs={{0,2},{1,3},{2,0},{3,1},{4,6},{5,7},{6,4},{7,5},{8,10},{9,11},{10,... | collective-permute-start | bytes 1572872 | tf_op jit(solution)/shard_map/ppermute | solution.py:345
  134.3 46.7 %collective-permute-start.28 = (bf16[512,512]{1,0:T(8,128)(2,1)}, bf16[512,512]{1,0:T(8,128)(2,1)}, u32[]{:S(2)}, u32[]{:S(2)}) collective-permute-start(bf16[512,512]{1,0:T(8,128)(2,1)} %get-tuple-element.103), channel_id=1, source_target_pairs={{0,4},{1,5},{2,6},{3,7},{4,0},{5,1},{6,2},{7,3},{8,12},{9,13},{10,... | collective-permute-start | bytes 1572872 | tf_op jit(solution)/shard_map/ppermute | solution.py:345
  141.4 40.2 %collective-permute-start.19 = (bf16[512,512]{1,0:T(8,128)(2,1)}, bf16[512,512]{1,0:T(8,128)(2,1)}, u32[]{:S(2)}, u32[]{:S(2)}) collective-permute-start(bf16[512,512]{1,0:T(8,128)(2,1)} %get-tuple-element.92), channel_id=1, source_target_pairs={{0,6},{1,7},{2,4},{3,5},{4,2},{5,3},{6,0},{7,1},{8,14},{9,15},{10,... | collective-permute-start | bytes 1572872 | tf_op jit(solution)/shard_map/ppermute | solution.py:345
  163.1 19.4 %collective-permute-start.21 = (bf16[512,512]{1,0:T(8,128)(2,1)}, bf16[512,512]{1,0:T(8,128)(2,1)}, u32[]{:S(2)}, u32[]{:S(2)}) collective-permute-start(bf16[512,512]{1,0:T(8,128)(2,1)} %get-tuple-element.93), channel_id=1, source_target_pairs={{0,7},{1,6},{2,5},{3,4},{4,3},{5,2},{6,1},{7,0},{8,15},{9,14},{10,... | collective-permute-start | bytes 1572872 | tf_op jit(solution)/shard_map/ppermute | solution.py:345
  164.5 18.5 %collective-permute-start.27 = (bf16[512,512]{1,0:T(8,128)(2,1)}, bf16[512,512]{1,0:T(8,128)(2,1)}, u32[]{:S(2)}, u32[]{:S(2)}) collective-permute-start(bf16[512,512]{1,0:T(8,128)(2,1)} %collective-permute-done.26), channel_id=1, source_target_pairs={{0,8},{8,0},{1,9},{9,1},{2,10},{10,2},{3,11},{11,3},{4,12},{12,4},... | collective-permute-start | bytes 1572872 | tf_op jit(solution)/shard_map/ppermute | solution.py:340
  180.0 4.6 %collective-permute-start.10 = (bf16[4,128,512]{2,1,0:T(8,128)(2,1)}, bf16[4,128,512]{2,1,0:T(8,128)(2,1)}, u32[]{:S(2)}, u32[]{:S(2)}) collective-permute-start(bf16[4,128,512]{2,1,0:T(8,128)(2,1)} %get-tuple-element.81), channel_id=1, source_target_pairs={{0,1},{1,0},{2,3},{3,2},{4,5},{5,4},{6,7},{7,6},{8,9},{9,8},{10,11... | collective-permute-start | bytes 1572872 | tf_op jit(solution)/shard_map/ppermute | solution.py:345
  181.1 15.1 %collective-permute-start.11 = (bf16[4,128,512]{2,1,0:T(8,128)(2,1)}, bf16[4,128,512]{2,1,0:T(8,128)(2,1)}, u32[]{:S(2)}, u32[]{:S(2)}) collective-permute-start(bf16[4,128,512]{2,1,0:T(8,128)(2,1)} %get-tuple-element.82), channel_id=1, source_target_pairs={{0,2},{1,3},{2,0},{3,1},{4,6},{5,7},{6,4},{7,5},{8,10},{9,11},{10,... | collective-permute-start | bytes 1572872 | tf_op jit(solution)/shard_map/ppermute | solution.py:345
  181.6 35.4 %collective-permute-start.12 = (bf16[4,128,512]{2,1,0:T(8,128)(2,1)}, bf16[4,128,512]{2,1,0:T(8,128)(2,1)}, u32[]{:S(2)}, u32[]{:S(2)}) collective-permute-start(bf16[4,128,512]{2,1,0:T(8,128)(2,1)} %get-tuple-element.83), channel_id=1, source_target_pairs={{0,3},{1,2},{2,1},{3,0},{4,7},{5,6},{6,5},{7,4},{8,11},{9,10},{10,... | collective-permute-start | bytes 1572872 | tf_op jit(solution)/shard_map/ppermute | solution.py:345
  182.5 36.2 %collective-permute-start.13 = (bf16[4,128,512]{2,1,0:T(8,128)(2,1)}, bf16[4,128,512]{2,1,0:T(8,128)(2,1)}, u32[]{:S(2)}, u32[]{:S(2)}) collective-permute-start(bf16[4,128,512]{2,1,0:T(8,128)(2,1)} %get-tuple-element.84), channel_id=1, source_target_pairs={{0,4},{1,5},{2,6},{3,7},{4,0},{5,1},{6,2},{7,3},{8,12},{9,13},{10,... | collective-permute-start | bytes 1572872 | tf_op jit(solution)/shard_map/ppermute | solution.py:345
  183.0 47.8 %collective-permute-start.14 = (bf16[4,128,512]{2,1,0:T(8,128)(2,1)}, bf16[4,128,512]{2,1,0:T(8,128)(2,1)}, u32[]{:S(2)}, u32[]{:S(2)}) collective-permute-start(bf16[4,128,512]{2,1,0:T(8,128)(2,1)} %get-tuple-element.85), channel_id=1, source_target_pairs={{0,5},{1,4},{2,7},{3,6},{4,1},{5,0},{6,3},{7,2},{8,13},{9,12},{10,... | collective-permute-start | bytes 1572872 | tf_op jit(solution)/shard_map/ppermute | solution.py:345
  184.6 46.7 %collective-permute-start.15 = (bf16[4,128,512]{2,1,0:T(8,128)(2,1)}, bf16[4,128,512]{2,1,0:T(8,128)(2,1)}, u32[]{:S(2)}, u32[]{:S(2)}) collective-permute-start(bf16[4,128,512]{2,1,0:T(8,128)(2,1)} %get-tuple-element.86), channel_id=1, source_target_pairs={{0,6},{1,7},{2,4},{3,5},{4,2},{5,3},{6,0},{7,1},{8,14},{9,15},{10,... | collective-permute-start | bytes 1572872 | tf_op jit(solution)/shard_map/ppermute | solution.py:345
  196.2 35.4 %collective-permute-start.16 = (bf16[4,128,512]{2,1,0:T(8,128)(2,1)}, bf16[4,128,512]{2,1,0:T(8,128)(2,1)}, u32[]{:S(2)}, u32[]{:S(2)}) collective-permute-start(bf16[4,128,512]{2,1,0:T(8,128)(2,1)} %get-tuple-element.87), channel_id=1, source_target_pairs={{0,7},{1,6},{2,5},{3,4},{4,3},{5,2},{6,1},{7,0},{8,15},{9,14},{10,... | collective-permute-start | bytes 1572872 | tf_op jit(solution)/shard_map/ppermute | solution.py:345
  217.0 51.4 %collective-permute-start.30 = (bf16[512,1024]{1,0:T(8,128)(2,1)}, bf16[512,1024]{1,0:T(8,128)(2,1)}, u32[]{:S(2)}, u32[]{:S(2)}) collective-permute-start(bf16[512,1024]{1,0:T(8,128)(2,1)} %get-tuple-element.104), channel_id=1, source_target_pairs={{0,3},{1,2},{2,1},{3,0},{4,7},{5,6},{6,5},{7,4},{8,11},{9,10},{10,... | collective-permute-start | bytes 3145736 | tf_op jit(solution)/shard_map/ppermute | solution.py:345
  218.7 51.3 %collective-permute-start.31 = (bf16[512,1024]{1,0:T(8,128)(2,1)}, bf16[512,1024]{1,0:T(8,128)(2,1)}, u32[]{:S(2)}, u32[]{:S(2)}) collective-permute-start(bf16[512,1024]{1,0:T(8,128)(2,1)} %get-tuple-element.105), channel_id=1, source_target_pairs={{0,5},{1,4},{2,7},{3,6},{4,1},{5,0},{6,3},{7,2},{8,13},{9,12},{10,... | collective-permute-start | bytes 3145736 | tf_op jit(solution)/shard_map/ppermute | solution.py:345
  230.8 39.7 %collective-permute-start.24 = (bf16[4,256,512]{2,1,0:T(8,128)(2,1)}, bf16[4,256,512]{2,1,0:T(8,128)(2,1)}, u32[]{:S(2)}, u32[]{:S(2)}) collective-permute-start(bf16[4,256,512]{2,1,0:T(8,128)(2,1)} %get-tuple-element.132), channel_id=1, source_target_pairs={{0,8},{8,0},{1,9},{9,1},{2,10},{10,2},{3,11},{11,3},{4,12},{12,4},... | collective-permute-start | bytes 3145736 | tf_op jit(solution)/shard_map/ppermute | solution.py:340
  231.3 67.7 %collective-permute-start.23 = (bf16[512,1024]{1,0:T(8,128)(2,1)}, bf16[512,1024]{1,0:T(8,128)(2,1)}, u32[]{:S(2)}, u32[]{:S(2)}) collective-permute-start(bf16[512,1024]{1,0:T(8,128)(2,1)} %get-tuple-element.95), channel_id=1, source_target_pairs={{0,1},{1,0},{2,3},{3,2},{4,5},{5,4},{6,7},{7,6},{8,9},{9,8},{10,11... | collective-permute-start | bytes 3145736 | tf_op jit(solution)/shard_map/ppermute | solution.py:345
  231.6 36.5 %collective-permute-start.29 = (bf16[512,512]{1,0:T(8,128)(2,1)}, bf16[512,512]{1,0:T(8,128)(2,1)}, u32[]{:S(2)}, u32[]{:S(2)}) collective-permute-start(bf16[512,512]{1,0:T(8,128)(2,1)} %collective-permute-done.28), channel_id=1, source_target_pairs={{0,8},{8,0},{1,9},{9,1},{2,10},{10,2},{3,11},{11,3},{4,12},{12,4},... | collective-permute-start | bytes 1572872 | tf_op jit(solution)/shard_map/ppermute | solution.py:340
  268.0 29.6 %collective-permute-start.20 = (bf16[512,512]{1,0:T(8,128)(2,1)}, bf16[512,512]{1,0:T(8,128)(2,1)}, u32[]{:S(2)}, u32[]{:S(2)}) collective-permute-start(bf16[512,512]{1,0:T(8,128)(2,1)} %collective-permute-done.19), channel_id=1, source_target_pairs={{0,8},{8,0},{1,9},{9,1},{2,10},{10,2},{3,11},{11,3},{4,12},{12,4},... | collective-permute-start | bytes 1572872 | tf_op jit(solution)/shard_map/ppermute | solution.py:340
  268.5 29.7 %collective-permute-start.22 = (bf16[512,512]{1,0:T(8,128)(2,1)}, bf16[512,512]{1,0:T(8,128)(2,1)}, u32[]{:S(2)}, u32[]{:S(2)}) collective-permute-start(bf16[512,512]{1,0:T(8,128)(2,1)} %collective-permute-done.21), channel_id=1, source_target_pairs={{0,8},{8,0},{1,9},{9,1},{2,10},{10,2},{3,11},{11,3},{4,12},{12,4},... | collective-permute-start | bytes 1572872 | tf_op jit(solution)/shard_map/ppermute | solution.py:340
  270.1 24.5 %collective-permute-start.18 = (f32[8,2048]{1,0:T(8,128)}, f32[8,2048]{1,0:T(8,128)}, u32[]{:S(2)}, u32[]{:S(2)}) collective-permute-start(f32[8,2048]{1,0:T(8,128)} %get-tuple-element.90.dga_ref), channel_id=1, source_target_pairs={{0,8},{8,0},{1,9},{9,1},{2,10},{10,2},{3,11},{11,3},{4,12},{12,4},... | collective-permute-start | bytes 196616 | tf_op jit(solution)/shard_map/ppermute | solution.py:340
  285.4 14.8 %collective-permute-start.39 = (bf16[4,128,256]{2,1,0:T(8,128)(2,1)}, bf16[4,128,256]{2,1,0:T(8,128)(2,1)}, u32[]{:S(2)}, u32[]{:S(2)}) collective-permute-start(bf16[4,128,256]{2,1,0:T(8,128)(2,1)} %get-tuple-element.116), channel_id=1, source_target_pairs={{0,2},{1,3},{2,0},{3,1},{4,6},{5,7},{6,4},{7,5},{8,10},{9,11},{10,... | collective-permute-start | bytes 786440 | tf_op jit(solution)/shard_map/ppermute | solution.py:345
  294.5 8.9 %collective-permute-start.40 = (bf16[4,128,256]{2,1,0:T(8,128)(2,1)}, bf16[4,128,256]{2,1,0:T(8,128)(2,1)}, u32[]{:S(2)}, u32[]{:S(2)}) collective-permute-start(bf16[4,128,256]{2,1,0:T(8,128)(2,1)} %get-tuple-element.117), channel_id=1, source_target_pairs={{0,3},{1,2},{2,1},{3,0},{4,7},{5,6},{6,5},{7,4},{8,11},{9,10},{10,... | collective-permute-start | bytes 786440 | tf_op jit(solution)/shard_map/ppermute | solution.py:345
  297.6 21.5 %collective-permute-start.41 = (bf16[4,128,256]{2,1,0:T(8,128)(2,1)}, bf16[4,128,256]{2,1,0:T(8,128)(2,1)}, u32[]{:S(2)}, u32[]{:S(2)}) collective-permute-start(bf16[4,128,256]{2,1,0:T(8,128)(2,1)} %get-tuple-element.118), channel_id=1, source_target_pairs={{0,4},{1,5},{2,6},{3,7},{4,0},{5,1},{6,2},{7,3},{8,12},{9,13},{10,... | collective-permute-start | bytes 786440 | tf_op jit(solution)/shard_map/ppermute | solution.py:345
  298.2 43.0 %collective-permute-start.32 = (bf16[4,128,512]{2,1,0:T(8,128)(2,1)}, bf16[4,128,512]{2,1,0:T(8,128)(2,1)}, u32[]{:S(2)}, u32[]{:S(2)}) collective-permute-start(bf16[4,128,512]{2,1,0:T(8,128)(2,1)} %get-tuple-element.108), channel_id=1, source_target_pairs={{0,2},{1,3},{2,0},{3,1},{4,6},{5,7},{6,4},{7,5},{8,10},{9,11},{10,... | collective-permute-start | bytes 1572872 | tf_op jit(solution)/shard_map/ppermute | solution.py:345
  298.9 20.7 %collective-permute-start.46 = (f32[32,512]{1,0:T(8,128)}, f32[32,512]{1,0:T(8,128)}, u32[]{:S(2)}, u32[]{:S(2)}) collective-permute-start(f32[32,512]{1,0:T(8,128)} %get-tuple-element.131.refs_0_), channel_id=1, source_target_pairs={{0,2},{1,3},{2,0},{3,1},{4,6},{5,7},{6,4},{7,5},{8,10},{9,11},{10,... | collective-permute-start | bytes 196616 | tf_op jit(solution)/shard_map/ppermute | solution.py:345
  300.2 20.7 %collective-permute-start.47 = (f32[32,512]{1,0:T(8,128)}, f32[32,512]{1,0:T(8,128)}, u32[]{:S(2)}, u32[]{:S(2)}) collective-permute-start(f32[32,512]{1,0:T(8,128)} %get-tuple-element.131.refs_0_), channel_id=1, source_target_pairs={{0,4},{1,5},{2,6},{3,7},{4,0},{5,1},{6,2},{7,3},{8,12},{9,13},{10,... | collective-permute-start | bytes 196616 | tf_op jit(solution)/shard_map/ppermute | solution.py:345
  303.5 18.0 %collective-permute-start.48 = (f32[32,512]{1,0:T(8,128)}, f32[32,512]{1,0:T(8,128)}, u32[]{:S(2)}, u32[]{:S(2)}) collective-permute-start(f32[32,512]{1,0:T(8,128)} %get-tuple-element.131.refs_0_), channel_id=1, source_target_pairs={{0,6},{1,7},{2,4},{3,5},{4,2},{5,3},{6,0},{7,1},{8,14},{9,15},{10,... | collective-permute-start | bytes 196616 | tf_op jit(solution)/shard_map/ppermute | solution.py:345
  319.2 20.0 %collective-permute-start.42 = (bf16[4,128,256]{2,1,0:T(8,128)(2,1)}, bf16[4,128,256]{2,1,0:T(8,128)(2,1)}, u32[]{:S(2)}, u32[]{:S(2)}) collective-permute-start(bf16[4,128,256]{2,1,0:T(8,128)(2,1)} %get-tuple-element.119), channel_id=1, source_target_pairs={{0,5},{1,4},{2,7},{3,6},{4,1},{5,0},{6,3},{7,2},{8,13},{9,12},{10,... | collective-permute-start | bytes 786440 | tf_op jit(solution)/shard_map/ppermute | solution.py:345
  319.6 19.8 %collective-permute-start.38 = (bf16[4,128,256]{2,1,0:T(8,128)(2,1)}, bf16[4,128,256]{2,1,0:T(8,128)(2,1)}, u32[]{:S(2)}, u32[]{:S(2)}) collective-permute-start(bf16[4,128,256]{2,1,0:T(8,128)(2,1)} %get-tuple-element.115), channel_id=1, source_target_pairs={{0,1},{1,0},{2,3},{3,2},{4,5},{5,4},{6,7},{7,6},{8,9},{9,8},{10,11... | collective-permute-start | bytes 786440 | tf_op jit(solution)/shard_map/ppermute | solution.py:345
  320.9 19.4 %collective-permute-start.43 = (bf16[4,128,256]{2,1,0:T(8,128)(2,1)}, bf16[4,128,256]{2,1,0:T(8,128)(2,1)}, u32[]{:S(2)}, u32[]{:S(2)}) collective-permute-start(bf16[4,128,256]{2,1,0:T(8,128)(2,1)} %get-tuple-element.120), channel_id=1, source_target_pairs={{0,6},{1,7},{2,4},{3,5},{4,2},{5,3},{6,0},{7,1},{8,14},{9,15},{10,... | collective-permute-start | bytes 786440 | tf_op jit(solution)/shard_map/ppermute | solution.py:345
  321.5 19.3 %collective-permute-start.44 = (bf16[4,128,256]{2,1,0:T(8,128)(2,1)}, bf16[4,128,256]{2,1,0:T(8,128)(2,1)}, u32[]{:S(2)}, u32[]{:S(2)}) collective-permute-start(bf16[4,128,256]{2,1,0:T(8,128)(2,1)} %get-tuple-element.121), channel_id=1, source_target_pairs={{0,7},{1,6},{2,5},{3,4},{4,3},{5,2},{6,1},{7,0},{8,15},{9,14},{10,... | collective-permute-start | bytes 786440 | tf_op jit(solution)/shard_map/ppermute | solution.py:345
  339.2 14.2 %collective-permute-start.33 = (bf16[4,128,512]{2,1,0:T(8,128)(2,1)}, bf16[4,128,512]{2,1,0:T(8,128)(2,1)}, u32[]{:S(2)}, u32[]{:S(2)}) collective-permute-start(bf16[4,128,512]{2,1,0:T(8,128)(2,1)} %get-tuple-element.109), channel_id=1, source_target_pairs={{0,3},{1,2},{2,1},{3,0},{4,7},{5,6},{6,5},{7,4},{8,11},{9,10},{10,... | collective-permute-start | bytes 1572872 | tf_op jit(solution)/shard_map/ppermute | solution.py:345
  339.4 15.1 %collective-permute-start.34 = (bf16[4,128,512]{2,1,0:T(8,128)(2,1)}, bf16[4,128,512]{2,1,0:T(8,128)(2,1)}, u32[]{:S(2)}, u32[]{:S(2)}) collective-permute-start(bf16[4,128,512]{2,1,0:T(8,128)(2,1)} %get-tuple-element.110), channel_id=1, source_target_pairs={{0,4},{1,5},{2,6},{3,7},{4,0},{5,1},{6,2},{7,3},{8,12},{9,13},{10,... | collective-permute-start | bytes 1572872 | tf_op jit(solution)/shard_map/ppermute | solution.py:345
  340.3 23.7 %collective-permute-start.35 = (bf16[4,128,512]{2,1,0:T(8,128)(2,1)}, bf16[4,128,512]{2,1,0:T(8,128)(2,1)}, u32[]{:S(2)}, u32[]{:S(2)}) collective-permute-start(bf16[4,128,512]{2,1,0:T(8,128)(2,1)} %get-tuple-element.111), channel_id=1, source_target_pairs={{0,5},{1,4},{2,7},{3,6},{4,1},{5,0},{6,3},{7,2},{8,13},{9,12},{10,... | collective-permute-start | bytes 1572872 | tf_op jit(solution)/shard_map/ppermute | solution.py:345
  340.8 103.1 %collective-permute-start.17 = (bf16[2048,512]{1,0:T(8,128)(2,1)}, bf16[2048,512]{1,0:T(8,128)(2,1)}, u32[]{:S(2)}, u32[]{:S(2)}) collective-permute-start(bf16[2048,512]{1,0:T(8,128)(2,1)} %get-tuple-element.88), channel_id=1, source_target_pairs={{0,8},{8,0},{1,9},{9,1},{2,10},{10,2},{3,11},{11,3},{4,12},{12,4},... | collective-permute-start | bytes 6291464 | tf_op jit(solution)/shard_map/ppermute | solution.py:340
  341.2 9.0 %collective-permute-start.49 = (f32[32,512]{1,0:T(8,128)}, f32[32,512]{1,0:T(8,128)}, u32[]{:S(2)}, u32[]{:S(2)}) collective-permute-start(f32[32,512]{1,0:T(8,128)} %shard_map.143.refs_0_), channel_id=1, source_target_pairs={{0,1},{1,0},{2,3},{3,2},{4,5},{5,4},{6,7},{7,6},{8,9},{9,8},{10,11... | collective-permute-start | bytes 196616 | tf_op jit(solution)/shard_map/ppermute | solution.py:345
  350.2 79.1 %collective-permute-start.45 = (bf16[2048,256]{1,0:T(8,128)(2,1)}, bf16[2048,256]{1,0:T(8,128)(2,1)}, u32[]{:S(2)}, u32[]{:S(2)}) collective-permute-start(bf16[2048,256]{1,0:T(8,128)(2,1)} %shard_map.140.refs_10_), channel_id=1, source_target_pairs={{0,8},{8,0},{1,9},{9,1},{2,10},{10,2},{3,11},{11,3},{4,12},{12,4},... | collective-permute-start | bytes 3145736 | tf_op jit(solution)/shard_map/ppermute | solution.py:340
  353.4 59.8 %collective-permute-start.50 = (f32[32,512]{1,0:T(8,128)}, f32[32,512]{1,0:T(8,128)}, u32[]{:S(2)}, u32[]{:S(2)}) collective-permute-start(f32[32,512]{1,0:T(8,128)} %shard_map.144), channel_id=1, source_target_pairs={{0,8},{8,0},{1,9},{9,1},{2,10},{10,2},{3,11},{11,3},{4,12},{12,4},... | collective-permute-start | bytes 196616 | tf_op jit(solution)/shard_map/ppermute | solution.py:340
  354.5 74.8 %collective-permute-start.25 = (bf16[4,128,512]{2,1,0:T(8,128)(2,1)}, bf16[4,128,512]{2,1,0:T(8,128)(2,1)}, u32[]{:S(2)}, u32[]{:S(2)}) collective-permute-start(bf16[4,128,512]{2,1,0:T(8,128)(2,1)} %get-tuple-element.101), channel_id=1, source_target_pairs={{0,1},{1,0},{2,3},{3,2},{4,5},{5,4},{6,7},{7,6},{8,9},{9,8},{10,11... | collective-permute-start | bytes 1572872 | tf_op jit(solution)/shard_map/ppermute | solution.py:345
  364.0 65.3 %collective-permute-start.36 = (bf16[4,128,512]{2,1,0:T(8,128)(2,1)}, bf16[4,128,512]{2,1,0:T(8,128)(2,1)}, u32[]{:S(2)}, u32[]{:S(2)}) collective-permute-start(bf16[4,128,512]{2,1,0:T(8,128)(2,1)} %get-tuple-element.112), channel_id=1, source_target_pairs={{0,6},{1,7},{2,4},{3,5},{4,2},{5,3},{6,0},{7,1},{8,14},{9,15},{10,... | collective-permute-start | bytes 1572872 | tf_op jit(solution)/shard_map/ppermute | solution.py:345
  413.2 16.1 %collective-permute-start.37 = (bf16[4,128,512]{2,1,0:T(8,128)(2,1)}, bf16[4,128,512]{2,1,0:T(8,128)(2,1)}, u32[]{:S(2)}, u32[]{:S(2)}) collective-permute-start(bf16[4,128,512]{2,1,0:T(8,128)(2,1)} %get-tuple-element.113), channel_id=1, source_target_pairs={{0,7},{1,6},{2,5},{3,4},{4,3},{5,2},{6,1},{7,0},{8,15},{9,14},{10,... | collective-permute-start | bytes 1572872 | tf_op jit(solution)/shard_map/ppermute | solution.py:345

commit v3 on v2

--- a/solution.py
+++ b/solution.py
@@ -34,14 +34,8 @@
     return high, mid, (rest - mid.astype(F32)).astype(BF16)
 
 
-def route_kernel(me_ref, x_ref, wt_ref, one_ref, two_ref, rows_ref, prob_ref, first_ref, *, slot_cap, own_experts, peer):
-    n_experts, n_tokens = prob_ref.shape
-    pieces = jnp.concatenate(split3(wt_ref[...]), axis=0)
-    raw = lax.dot_general(pieces, x_ref[...], NT, preferred_element_type=F32)
-    logits = raw[:n_experts] + raw[n_experts:2 * n_experts] + raw[2 * n_experts:]
-    expo = jnp.exp(logits - jnp.max(logits, axis=0, keepdims=True))
-    prob = expo / jnp.sum(expo, axis=0, keepdims=True)
-    prob_ref[...] = prob
+def slots_kernel(me_ref, x_ref, one_ref, two_ref, slots_ref, first_ref, *, slot_cap, own_experts, n_experts, peer):
+    n_tokens = x_ref.shape[0]
     expert = lax.broadcasted_iota(jnp.int32, (n_experts, n_tokens), 0)
     id_one, id_two = one_ref[...], two_ref[...]
     hot_one = jnp.where(id_one == expert, 1.0, 0.0)
@@ -58,8 +52,6 @@
     count = jnp.concatenate(counts, axis=1)
     pos_one = jnp.sum(count[:n_experts] * hot_one, axis=0, keepdims=True)
     pos_two = jnp.sum((count[n_experts:] + run[:n_experts]) * hot_two, axis=0, keepdims=True)
-    prob_one = jnp.sum(prob * hot_one, axis=0, keepdims=True)
-    prob_two = jnp.sum(prob * hot_two, axis=0, keepdims=True)
     turn = me_ref[0] * (own_experts * slot_cap)
 
     def slot_of(ids, pos):
@@ -67,15 +59,28 @@
         slot = jnp.where(place < slot_cap, ids * slot_cap + place, n_experts * slot_cap)
         return jnp.bitwise_xor(slot, turn).astype(F32)
 
-    gate_sum = prob_one + prob_two
     slot_one, slot_two = slot_of(id_one, pos_one), slot_of(id_two, pos_two)
+    slots_ref[...] = jnp.concatenate([slot_one, slot_two, jnp.zeros((6, n_tokens), F32)], axis=0)
     block = first_ref.shape[0]
     slot = (peer * block + lax.broadcasted_iota(jnp.int32, (block, n_tokens), 0)).astype(F32)
     hit = jnp.logical_or(slot_one == slot, slot_two == slot)
     first_ref[...] = jnp.dot(jnp.where(hit, 1.0, 0.0).astype(BF16), x_ref[...], preferred_element_type=F32).astype(BF16)
+
+
+def route_kernel(x_ref, wt_ref, one_ref, two_ref, slots_ref, rows_ref, prob_ref):
+    n_experts, n_tokens = prob_ref.shape
+    pieces = jnp.concatenate(split3(wt_ref[...]), axis=0)
+    raw = lax.dot_general(pieces, x_ref[...], NT, preferred_element_type=F32)
+    logits = raw[:n_experts] + raw[n_experts:2 * n_experts] + raw[2 * n_experts:]
+    expo = jnp.exp(logits - jnp.max(logits, axis=0, keepdims=True))
+    prob = expo / jnp.sum(expo, axis=0, keepdims=True)
+    prob_ref[...] = prob
+    expert = lax.broadcasted_iota(jnp.int32, (n_experts, n_tokens), 0)
+    prob_one = jnp.sum(jnp.where(one_ref[...] == expert, prob, 0.0), axis=0, keepdims=True)
+    prob_two = jnp.sum(jnp.where(two_ref[...] == expert, prob, 0.0), axis=0, keepdims=True)
+    gate_sum = prob_one + prob_two
     rows_ref[...] = jnp.concatenate(
-        [slot_one, slot_two, prob_one / gate_sum, prob_two / gate_sum, prob_one, prob_two, jnp.zeros((10, n_tokens), F32)],
-        axis=0)
+        [slots_ref[0:2, :], prob_one / gate_sum, prob_two / gate_sum, prob_one, prob_two, jnp.zeros((10, n_tokens), F32)], axis=0)
 
 
 def gather_kernel(z_ref, rows_ref, src_ref, *outs, peers, per, scaled):
@@ -204,7 +209,8 @@
 def weight_grad_kernel(z_ref, *refs, n_src, widths):
     xs = refs[:n_src]
     dos, refs = group_refs(refs[n_src:], widths)
-    h_ref, h2_ref, da_ref, da2_ref, db_ref, db2_ref, ga_ref, gb_ref, gc_ref, do_ref = refs
+    h_ref, h2_ref, da_ref, da2_ref, db_ref, db2_ref, d0, d2, d4, d6, ga_ref, gb_ref, gc_ref, dw_ref, do_ref = refs
+    dw_ref[...] = (d0[...] + d2[...]) + (d4[...] + d6[...])
     cap = xs[0].shape[1]
     for i, ref in enumerate(dos):
         put_rows(z_ref[0], slice(i * cap, (i + 1) * cap), ref, do_ref)
@@ -227,29 +233,41 @@
     return picks
 
 
-def combine_out_kernel(z_ref, cols_ref, dy_ref, *refs, n_src):
-    srcs = refs[:n_src]
-    y_ref, dg_ref = refs[n_src:]
+def add_rows(total, picks, srcs, peers):
+    zero = jnp.zeros((TOKEN_TILE, 128), BF16)
     blocks = srcs[0].shape[0] // 128
-    picks = slot_picks(cols_ref)
-    zero = jnp.zeros((TOKEN_TILE, 128), BF16)
-    both = None
-    for d in range(n_src):
+    for d, src in zip(peers, srcs):
         pick = jnp.concatenate(
             [jnp.concatenate([jnp.where(blk == jnp.asarray(d * blocks + b, BF16), hot, zero) for b in range(blocks)], axis=1) for blk, hot in picks], axis=0)
-        part = jnp.dot(pick, srcs[d][...], preferred_element_type=F32)
-        both = part if both is None else both + part
+        part = jnp.dot(pick, src[...], preferred_element_type=F32)
+        total = part if total is None else total + part
+    return total
+
+
+def combine_first_kernel(z_ref, cols_ref, *refs, peers):
+    both = add_rows(None, slot_picks(cols_ref), refs[:-2], peers)
+    refs[-2][...] = both[:TOKEN_TILE]
+    refs[-1][...] = both[TOKEN_TILE:]
+
+
+def combine_out_kernel(z_ref, cols_ref, dy_ref, one_ref, two_ref, *refs, peers):
+    y_ref, dg_ref, out_ref = refs[-3:]
+    both = jnp.concatenate([one_ref[...], two_ref[...]], axis=0)
+    both = add_rows(both, slot_picks(cols_ref), refs[:-3], peers)
     dy = dy_ref[...].astype(F32)
     one, two = both[:TOKEN_TILE], both[TOKEN_TILE:]
-    y_ref[...] = (cols_ref[:, 2:3] * one + cols_ref[:, 3:4] * two).astype(BF16)
+    out = (cols_ref[:, 2:3] * one + cols_ref[:, 3:4] * two).astype(BF16)
+    y_ref[...] = out
+    out_ref[...] = out
     dg_one = jnp.sum(dy * one, axis=1, keepdims=True)
     dg_two = jnp.sum(dy * two, axis=1, keepdims=True)
     wide = jnp.concatenate([dg_one, dg_two, jnp.zeros((TOKEN_TILE, 126), F32)], axis=1)
     dg_ref[...] = wide.T[:8, :]
 
 
-def logit_grad_kernel(z_ref, rows_ref, prob_ref, one_ref, two_ref, x_ref, dga_ref, dgb_ref, dl_ref, dw_ref):
+def logit_grad_kernel(z_ref, rows_ref, prob_ref, one_ref, two_ref, x_ref, *refs):
     n_experts, n_tokens = prob_ref.shape
+    dga_ref, dgb_ref, dl_ref, dw_ref = refs
     dgate = dga_ref[0:2, :] + dgb_ref[0:2, :]
     dg_one, dg_two = dgate[0:1], dgate[1:2]
     gate_one, gate_two = rows_ref[2:3, :], rows_ref[3:4, :]
@@ -289,20 +307,24 @@
     if not last:
         refs[0][...] = res
         return
-    mine, other, dx_ref = refs
+    mine, other, near_ref, far_ref, dx_ref, dw_ref = refs
     wide = mine.shape[1]
     low_side = z_ref[0] == 0
+
+    @pl.when(pl.program_id(0) == 0)
+    def _():
+        near, far = near_ref[...], far_ref[...]
+        dw_ref[...] = jnp.concatenate([jnp.where(low_side, near, far), jnp.where(low_side, far, near)], axis=1)
+
     dx_ref[:, :wide] = jnp.where(low_side, mine[...], other[...])
     dx_ref[:, wide:2 * wide] = res[:, :wide]
     dx_ref[:, 2 * wide:3 * wide] = jnp.where(low_side, other[...], mine[...])
     dx_ref[:, 3 * wide:] = res[:, wide:]
 
 
-def sum_kernel(z_ref, *refs):
-    parts, out = [r[...] for r in refs[:-1]], refs[-1]
-    while len(parts) > 1:
-        parts = [parts[i] + parts[i + 1] for i in range(0, len(parts), 2)]
-    out[...] = parts[0]
+def place_kernel(z_ref, kept_ref, piece_ref, own_core, pair_core, dw_ref, out_ref):
+    out_ref[...] = piece_ref[...]
+    dw_ref[...] = own_core[...] + pair_core[...]
 
 
 def cost(flops, nbytes, trans=0):
@@ -319,6 +341,7 @@
     late = [2, 4, 3, 5]
     src_order = early + late
     first_peer = 6
+    out_early, out_late = [0, 1, 6], [4, 2, 7, 5, 3]
 
     def local_step(x_rows, w_router, first_ids, second_ids, w_gelu, w_lin, w_out, dy_rows):
         n_tokens, model = x_rows.shape
@@ -353,13 +376,21 @@
         wa2, wb2 = across(w_gelu), across(w_lin)
         wt = w_router.T
         id_one, id_two = first_ids.reshape(1, n_tokens), second_ids.reshape(1, n_tokens)
-        rows, prob, first_x = pl.pallas_call(
-            functools.partial(route_kernel, slot_cap=slot_cap, own_experts=own, peer=first_peer),
-            in_specs=[pl.BlockSpec(memory_space=pltpu.SMEM)] + [pl.BlockSpec(memory_space=pltpu.VMEM)] * 4,
-            out_shape=(sds((16, n_tokens), F32), sds((n_experts, n_tokens), F32), sds((block, model), BF16)),
+        in_vmem = pl.BlockSpec(memory_space=pltpu.VMEM)
+        slots, first_x = pl.pallas_call(
+            functools.partial(slots_kernel, slot_cap=slot_cap, own_experts=own, n_experts=n_experts, peer=first_peer),
+            in_specs=[pl.BlockSpec(memory_space=pltpu.SMEM)] + [in_vmem] * 3,
+            out_shape=(sds((8, n_tokens), F32), sds((block, model), BF16)),
+            cost_estimate=cost(2 * block * n_tokens * model, 2 * n_tokens * model),
+            compiler_params=all_vmem, name="k_slots",
+        )(me, x_rows, id_one, id_two)
+        rows, prob = pl.pallas_call(
+            route_kernel,
+            in_specs=[in_vmem] * 5,
+            out_shape=(sds((16, n_tokens), F32), sds((n_experts, n_tokens), F32)),
             cost_estimate=cost(2 * 96 * n_tokens * model, 2 * n_tokens * model, n_experts * n_tokens),
-            compiler_params=all_vmem, name="route",
-        )(me, x_rows, wt, id_one, id_two)
+            compiler_params=all_vmem, name="k_route",
+        )(x_rows, wt, id_one, id_two, slots)
         token_cols = rows.T
         wcz = across(lax.dynamic_slice_in_dim(w_out, (1 - z[0]) * cols, cols, 2))
         wcn = across(lax.dynamic_slice_in_dim(w_out, z[0] * cols, cols, 2))
@@ -377,11 +408,11 @@
 
             return call(
                 functools.partial(gather_kernel, peers=peers, per=per, scaled=scaled), (len(peers) * per,),
-                [pl.BlockSpec((16, n_tokens), lambda g, z: (0, 0)), pl.BlockSpec((n_tokens, width_out), src_map)],
+                [pl.BlockSpec((16 if scaled else 8, n_tokens), lambda g, z: (0, 0)), pl.BlockSpec((n_tokens, width_out), src_map)],
                 [pl.BlockSpec((GATHER_TILE, width_out), functools.partial(out_map, i=i)) for i in range(len(peers))],
                 [sds((block, width_out), BF16)] * len(peers),
                 cost(2 * len(peers) * block * n_tokens * width_out, 2 * (n_tokens + len(peers) * block) * width_out),
-                (rows, src))
+                (rows if scaled else slots, src))
 
         xs, dos = [None] * n_src, [None] * n_src
         xs[first_peer] = to_peer(first_x, first_peer).reshape(own, slot_cap, model)
@@ -463,16 +494,6 @@
                     got[d] = to_peer(vals[c * len(peers) + i], d).reshape(block, dx_widths[c])
             back_in.append(got)
 
-        all_dos = [v for d in src_order for v in dos[d]]
-        grad_wa, grad_wb, grad_wc = call(
-            functools.partial(weight_grad_kernel, n_src=n_src, widths=[len(dos[d]) for d in src_order]), (own,),
-            [whole(slot_cap, model)] * n_src + [whole(slot_cap, v.shape[2]) for v in all_dos] + [whole(r, width) for r in part_rows] + [whole(rows_early, width), whole(rows_late, width)] * 2,
-            [whole(model, width), whole(model, width), whole(width, model)],
-            [sds((own, model, width), F32)] * 2 + [sds((own, width, model), F32)],
-            cost(6 * own * rows_all * width * model, 40e6),
-            (*xs, *all_dos, own_parts[0][2], own_parts[1][2], bwd_a[-2], bwd_b[-2], bwd_a[-1], bwd_b[-1]),
-            [pltpu.VMEM((rows_all, model), BF16)])
-
         def resident(a, b):
             return pl.BlockSpec((a, b), lambda i, *_: (0, 0))
 
@@ -480,13 +501,20 @@
             return pl.BlockSpec((TOKEN_TILE, b), lambda i, z: (i, 0 if col is None else z[0] * n_chunk + col))
 
         n_tiles = (n_tokens // TOKEN_TILE,)
-        y_mine, dg_mine = call(
-            functools.partial(combine_out_kernel, n_src=n_src), n_tiles,
-            [tiles(16), pl.BlockSpec((TOKEN_TILE, cols), lambda i, z: (i, z[0]))] + [resident(block, cols)] * n_src,
-            [tiles(cols), pl.BlockSpec((8, TOKEN_TILE), lambda i, z: (0, i))],
-            [sds((n_tokens, cols), BF16), sds((8, n_tokens), F32)],
-            cost(4 * n_tokens * n_src * block * cols, 12e6),
-            (token_cols, dy_rows, *back_out))
+        any_spec = pl.BlockSpec(memory_space=pl.ANY)
+
+        one, two = call(
+            functools.partial(combine_first_kernel, peers=out_early), n_tiles,
+            [tiles(16)] + [resident(block, cols)] * len(out_early), [tiles(cols)] * 2, [sds((n_tokens, cols), F32)] * 2,
+            cost(4 * n_tokens * len(out_early) * block * cols, 12e6),
+            (token_cols, *[back_out[d] for d in out_early]))
+        y_mine, dg_mine, act_out = call(
+            functools.partial(combine_out_kernel, peers=out_late), n_tiles,
+            [tiles(16), pl.BlockSpec((TOKEN_TILE, cols), lambda i, z: (i, z[0]))] + [tiles(cols)] * 2 + [resident(block, cols)] * len(out_late),
+            [tiles(cols), pl.BlockSpec((8, TOKEN_TILE), lambda i, z: (0, i)), pl.BlockSpec((TOKEN_TILE, cols), lambda i, z: (i, z[0]))],
+            [sds((n_tokens, cols), BF16), sds((8, n_tokens), F32), sds((n_tokens, model), BF16)],
+            cost(4 * n_tokens * len(out_late) * block * cols, 16e6),
+            (token_cols, dy_rows, one, two, *[back_out[d] for d in out_late]))
         dg_other = across(dg_mine)
         y_other = across(y_mine)
 
@@ -498,34 +526,39 @@
             cost(2 * 96 * n_tokens * cols, 4e6),
             (rows, prob, id_one, id_two, x_rows, dg_mine, dg_other))
 
+        all_dos = [v for d in src_order for v in dos[d]]
+        grad_wa, grad_wb, grad_wc, dw_core = call(
+            functools.partial(weight_grad_kernel, n_src=n_src, widths=[len(dos[d]) for d in src_order]), (own,),
+            [whole(slot_cap, model)] * n_src + [whole(slot_cap, v.shape[2]) for v in all_dos] + [whole(r, width) for r in part_rows] + [whole(rows_early, width), whole(rows_late, width)] * 2 + [resident(n_experts, cols)] * 4,
+            [whole(model, width), whole(model, width), whole(width, model), resident(n_experts, cols)],
+            [sds((own, model, width), F32)] * 2 + [sds((own, width, model), F32), sds((n_experts, cols), F32)],
+            cost(6 * own * rows_all * width * model, 40e6),
+            (*xs, *all_dos, own_parts[0][2], own_parts[1][2], bwd_a[-2], bwd_b[-2], bwd_a[-1], bwd_b[-1], dw, to_peer(dw, 2), to_peer(dw, 4), to_peer(dw, 6)),
+            [pltpu.VMEM((rows_all, model), BF16)])
+
+        dw_near, act_out = pl.pallas_call(
+            place_kernel,
+            grid_spec=pltpu.PrefetchScalarGridSpec(
+                num_scalar_prefetch=1, grid=n_tiles, in_specs=[pl.BlockSpec(memory_space=pl.ANY), tiles(cols)] + [resident(n_experts, cols)] * 2,
+                out_specs=[resident(n_experts, cols), pl.BlockSpec((TOKEN_TILE, cols), lambda i, z: (i, 1 - z[0]))]),
+            out_shape=[sds((n_experts, cols), F32), sds((n_tokens, model), BF16)], input_output_aliases={1: 1}, cost_estimate=cost(1e6, 4e6),
+            compiler_params=all_vmem, name="k_place_y")(z, act_out, y_other, dw_core, to_peer(dw_core, 1))
+        routers = (dw_near, across(dw_near))
+
         def combine_in(last, extra, srcs):
             quarters = [(lambda i, z: (0, 1)), (lambda i, z: (0, 3))] if last else [lambda i, z: (0, z[0] * n_chunk)]
             return call(
                 functools.partial(combine_in_kernel, n_src=n_src, last=last), n_tiles,
                 [tiles(16), pl.BlockSpec((6 * n_experts, TOKEN_TILE), lambda i, z: (0, i))] + [pl.BlockSpec((n_experts, wide), q) for q in quarters]
-                + [resident(block, v.shape[1]) for v in srcs] + [tiles(wide)] * len(extra),
-                tiles(model if last else wide), sds((n_tokens, model if last else wide), BF16),
+                + [resident(block, v.shape[1]) for v in srcs] + [tiles(wide)] * len(extra) + ([resident(n_experts, cols)] * len(routers) if last else []),
+                [tiles(model), resident(n_experts, model)] if last else tiles(wide),
+                [sds((n_tokens, model), BF16), sds((n_experts, model), F32)] if last else sds((n_tokens, wide), BF16),
                 cost(2 * n_tokens * n_src * block * srcs[0].shape[1], 8e6),
-                (token_cols, dl, *([wt] * len(quarters)), *srcs, *extra))
+                (token_cols, dl, *([wt] * len(quarters)), *srcs, *extra, *(routers if last else ())))
 
         dx_mine = combine_in(False, (), back_in[0])
         dx_other = across(dx_mine)
-        grad_in = combine_in(True, (dx_mine, dx_other), back_in[1])
-
-        def add_all(parts):
-            return call(sum_kernel, (1,), [resident(n_experts, cols)] * len(parts), resident(n_experts, cols), sds((n_experts, cols), F32), cost(1e6, 4e5), parts)
-
-        dw = add_all((dw, to_peer(dw, 2), to_peer(dw, 4), to_peer(dw, 6)))
-        dw = add_all((dw, to_peer(dw, 1)))
-        dw_other = across(dw)
-
-        lower = z[0] == 0
-
-        def join(mine, other):
-            return jnp.where(lower, jnp.concatenate([mine, other], axis=1), jnp.concatenate([other, mine], axis=1))
-
-        act_out = join(y_mine, y_other)
-        grad_router = join(dw, dw_other).T
-        return act_out, grad_in, grad_wa, grad_wb, grad_wc, grad_router
+        grad_in, grad_router = combine_in(True, (dx_mine, dx_other), back_in[1])
+        return act_out, grad_in, grad_wa, grad_wb, grad_wc, grad_router.T
 
     return jax.shard_map(local_step, mesh=mesh, in_specs=(P("ep", None), P(), P("ep"), P("ep"), P("ep", None, "tp"), P("ep", None, "tp"), P("ep", "tp", None), P("ep", None)), out_specs=(P("ep", None), P("ep", None), P("ep", None, "tp"), P("ep", None, "tp"), P("ep", "tp", None), P()), check_vma=False)

time: 452 us -> 452 us (level)
  Pallas kernels: 194 us -> 202 us
  other arithmetic: 7.99 us -> 0 us
    pallas_call x1 -> x3, Pallas kernels: 7.26 us -> 14.1 us  [the longest x1 5.78 us: local_step(): pl.pallas_call(functools.partial(slots_kernel, slot_cap=slot_cap, own_exp...]
    ppermute x39, waiting for transfers between devices: 106 us -> 99.6 us  [to_peer(): return lax.ppermute(val, 'ep', [(i, i ^ d) for i in range(n_src)])]
    select_n x1 -> x0, other arithmetic: 6.38 us -> none  [join(): jnp.where(lower, jnp.concatenate([mine, other], axis=1), jnp.concatenate(...]
    ppermute x12, waiting for transfers between devices: 87.1 us -> 92.2 us  [across(): return lax.ppermute(val, 'tp', swap)]
    pallas_call x18 -> x17, Pallas kernels: 173 us -> 174 us  [call(): pl.pallas_call(kernel, grid_spec=pltpu.PrefetchScalarGridSpec(num_scalar_...]
  transfers between devices with their start and end apart: 51 -> 51, of which waited for: 15 -> 11; matrix products, arithmetic and copies ran while one was open for 2% -> 1% of each run, Pallas kernels for 39% -> 40%
where the time goes in v3:
time: 452 us
  Pallas kernels  202 us (45%)
  waiting for transfers between devices  192 us (42%)
  starting transfers between devices  52.3 us (12%)
  local copies, waits for them, and re-layouts  5.26 us (1%)
    pallas_call x17, Pallas kernels, call(): pl.pallas_call(kernel, grid_spec=pltpu.PrefetchScalarGridSpec(num_scalar_...  174 us
    ppermute x39, waiting for transfers between devices, to_peer(): return lax.ppermute(val, 'ep', [(i, i ^ d) for i in range(n_src)])  99.6 us
    ppermute x12, waiting for transfers between devices, across(): return lax.ppermute(val, 'tp', swap)  92.2 us
    ppermute x39, starting transfers between devices, to_peer(): return lax.ppermute(val, 'ep', [(i, i ^ d) for i in range(n_src)])  39.2 us
    pallas_call x1, Pallas kernels, local_step(): pl.pallas_call(functools.partial(forward_other_kernel, n_src=n_src, n_chu...  13.9 us
    ppermute x12, starting transfers between devices, across(): return lax.ppermute(val, 'tp', swap)  13.1 us
  transfers between devices with their start and end apart: 51, of which 11 were waited for; matrix products, arithmetic and copies ran while one was open for 1% of the time, Pallas kernels for 40%

profile of v3, /device:TPU:0, one launch (start us, length us, event | category | flops | bytes accessed | tf_op | source)
XLA Modules:
  0.0 451.7 jit_solution(16572089680672747771)
XLA Ops:
  0.6 5.8 %k_slots.1 = (f32[8,2048]{1,0:T(8,128)}, bf16[512,1024]{1,0:T(8,128)(2,1)}) custom-call(s32[1]{0:T(128)} %bitcast.4.me_ref, bf16[2048,1024]{1,0:T(8,128)(2,1)} %x_ref.5, s32[1,2048]{1,0:T(1,128)} %bitcast.61, s32[1,2048]{1,0:T(1,128)} %bitcast.64), custom_call_target="tpu_custom_call" | custom-call | flops 2147483648 | bytes 4194304 | tf_op jit(solution)/shard_map/k_slots/pallas_call | solution.py:380
  6.4 4.2 collective-permute-start
  10.6 8.5 %shard_map.128 = (bf16[512,1024]{1,0:T(8,128)(2,1)}, bf16[512,1024]{1,0:T(8,128)(2,1)}) custom-call(s32[1]{0:T(128)} %bitcast.z_ref, f32[8,2048]{1,0:T(8,128)} %get-tuple-element.78.slots_ref.rows_ref, bf16[2048,1024]{1,0:T(8,128)(2,1)} %x_ref.5), custom_call_target="tpu_custom_call" | custom-call | flops 4294967296 | bytes 6291456 | tf_op jit(solution)/shard_map/pallas_call | solution.py:371
  19.7 4.5 k_route.1
  24.2 5.8 %shard_map.136 = (bf16[512,512]{1,0:T(8,128)(2,1)}, bf16[512,512]{1,0:T(8,128)(2,1)}) custom-call(s32[1]{0:T(128)} %bitcast.z_ref, f32[16,2048]{1,0:T(8,128)} %get-tuple-element.79.rows_ref, bf16[2048,1024]{1,0:T(8,128)(2,1)} %src_ref.13), custom_call_target="tpu_custom_call" | custom-call | flops 2147483648 | bytes 3145728 | tf_op jit(solution)/shard_map/pallas_call | solution.py:371
  30.0 1.5 collective-permute-start.23
  32.0 1.5 collective-permute-start.4
  33.5 11.5 %shard_map.127 = (bf16[512,1024]{1,0:T(8,128)(2,1)}, bf16[512,1024]{1,0:T(8,128)(2,1)}, bf16[512,1024]{1,0:T(8,128)(2,1)}) custom-call(s32[1]{0:T(128)} %bitcast.z_ref, f32[8,2048]{1,0:T(8,128)} %get-tuple-element.78.slots_ref.rows_ref, bf16[2048,1024]{1,0:T(8,128)(2,1)} %x_ref.5), custom_call_target="tpu_custom_call" | custom-call | flops 6442450944 | bytes 7340032 | tf_op jit(solution)/shard_map/pallas_call | solution.py:371
  45.0 23.0 %collective-permute-done.23 = bf16[512,512]{1,0:T(8,128)(2,1)} collective-permute-done((bf16[512,512]{1,0:T(8,128)(2,1)}, bf16[512,512]{1,0:T(8,128)(2,1)}, u32[]{:S(2)}, u32[]{:S(2)}) %collective-permute-start.23) | collective-permute-done | bytes 524320 | tf_op jit(solution)/shard_map/ppermute | solution.py:368
  68.0 1.5 collective-permute-start.2
  69.6 1.6 collective-permute-start.7
  71.6 3.0 constant_dynamic-slice_fusion
  74.6 8.5 %shard_map.129 = (bf16[512,1024]{1,0:T(8,128)(2,1)}, bf16[512,1024]{1,0:T(8,128)(2,1)}) custom-call(s32[1]{0:T(128)} %bitcast.z_ref, f32[8,2048]{1,0:T(8,128)} %get-tuple-element.78.slots_ref.rows_ref, bf16[2048,1024]{1,0:T(8,128)(2,1)} %x_ref.5), custom_call_target="tpu_custom_call" | custom-call | flops 4294967296 | bytes 6291456 | tf_op jit(solution)/shard_map/pallas_call | solution.py:371
  83.2 1.6 collective-permute-start.9
  84.8 9.1 %collective-permute-done.1 = bf16[512,1024]{1,0:T(8,128)(2,1)} collective-permute-done((bf16[512,1024]{1,0:T(8,128)(2,1)}, bf16[512,1024]{1,0:T(8,128)(2,1)}, u32[]{:S(2)}, u32[]{:S(2)}) %collective-permute-start.1) | collective-permute-done | bytes 1048608 | tf_op jit(solution)/shard_map/ppermute | solution.py:368
  94.2 1.3 collective-permute-start.6
  95.5 5.8 %shard_map.134 = (bf16[512,512]{1,0:T(8,128)(2,1)}, bf16[512,512]{1,0:T(8,128)(2,1)}) custom-call(s32[1]{0:T(128)} %bitcast.z_ref, f32[16,2048]{1,0:T(8,128)} %get-tuple-element.79.rows_ref, bf16[2048,1024]{1,0:T(8,128)(2,1)} %src_ref.13), custom_call_target="tpu_custom_call" | custom-call | flops 2147483648 | bytes 3145728 | tf_op jit(solution)/shard_map/pallas_call | solution.py:371
  101.4 11.7 %shard_map.130 = (f32[4,768,256]{2,1,0:T(8,128)}, f32[4,768,256]{2,1,0:T(8,128)}, bf16[4,768,256]{2,1,0:T(8,128)(2,1)}, bf16[4,768,512]{2,1,0:T(8,128)(2,1)}) custom-call(s32[1]{0:T(128)} %bitcast.z_ref, bf16[4,128,1024]{2,1,0:T(8,128)(2,1)} %bitcast.6.refs_0_, bf16[4,128,1024]{2,1,0:T(8,128)(2,1)} %bitcast.7.refs_1_, bf16[4,128,1024]{2,1,0:T(8,128)(2,1)} %bitcast.69, ...), custom_call_target="tpu_custom_call" | custom-call | flops 4026531840 | bytes 24576000 | tf_op jit(solution)/shard_map/pallas_call | solution.py:371
  113.0 71.8 %collective-permute-done.9.refs_12_.refs_15_.refs_17_ = bf16[4,256,512]{2,1,0:T(8,128)(2,1)} collective-permute-done((bf16[4,256,512]{2,1,0:T(8,128)(2,1)}, bf16[4,256,512]{2,1,0:T(8,128)(2,1)}, u32[]{:S(2)}, u32[]{:S(2)}) %collective-permute-start.9) | collective-permute-done | bytes 1048608 | tf_op jit(solution)/shard_map/ppermute | solution.py:363
  184.9 1.5 collective-permute-start.18
  186.4 1.6 collective-permute-start.24
  188.4 6.5 %shard_map.131 = (f32[4,256,256]{2,1,0:T(8,128)}, f32[4,256,256]{2,1,0:T(8,128)}, bf16[4,256,256]{2,1,0:T(8,128)(2,1)}, bf16[4,256,512]{2,1,0:T(8,128)(2,1)}) custom-call(s32[1]{0:T(128)} %bitcast.z_ref, bf16[4,128,1024]{2,1,0:T(8,128)(2,1)} %bitcast.12.refs_0_.refs_6_, bf16[4,128,1024]{2,1,0:T(8,128)(2,1)} %bitcast.13.refs_1_.refs_7_, ...), custom_call_target="tpu_custom_call" | custom-call | flops 1342177280 | bytes 8192000 | tf_op jit(solution)/shard_map/pallas_call | solution.py:371
  195.0 1.6 collective-permute-start.29
  196.6 13.9 %k_fwd_other.1 = (bf16[4,128,512]{2,1,0:T(8,128)(2,1)}, bf16[4,128,512]{2,1,0:T(8,128)(2,1)}, bf16[4,128,512]{2,1,0:T(8,128)(2,1)}, bf16[4,128,512]{2,1,0:T(8,12...) custom-call(bf16[4,128,1024]{2,1,0:T(8,128)(2,1)} %bitcast.6.refs_0_, ...), custom_call_target="tpu_custom_call" | custom-call | flops 5368709120 | bytes 32000000 | tf_op jit(solution)/shard_map/k_fwd_other/pallas_call | solution.py:447
  211.2 1.5 collective-permute-start.11
  212.7 0.9 collective-permute-start.12
  213.5 1.1 collective-permute-start.13
  214.7 9.3 %shard_map.137 = (bf16[512,1024]{1,0:T(8,128)(2,1)}, bf16[512,1024]{1,0:T(8,128)(2,1)}) custom-call(s32[1]{0:T(128)} %bitcast.z_ref, f32[16,2048]{1,0:T(8,128)} %get-tuple-element.79.rows_ref, bf16[2048,1024]{1,0:T(8,128)(2,1)} %src_ref.13), custom_call_target="tpu_custom_call" | custom-call | flops 4294967296 | bytes 6291456 | tf_op jit(solution)/shard_map/pallas_call | solution.py:371
  223.9 2.2 copy.15
  226.2 9.4 %shard_map.135 = (bf16[512,1024]{1,0:T(8,128)(2,1)}, bf16[512,1024]{1,0:T(8,128)(2,1)}) custom-call(s32[1]{0:T(128)} %bitcast.z_ref, f32[16,2048]{1,0:T(8,128)} %get-tuple-element.79.rows_ref, bf16[2048,1024]{1,0:T(8,128)(2,1)} %src_ref.13), custom_call_target="tpu_custom_call" | custom-call | flops 4294967296 | bytes 6291456 | tf_op jit(solution)/shard_map/pallas_call | solution.py:371
  235.7 1.7 collective-permute-start.28
  237.4 1.0 collective-permute-start.14
  238.3 1.7 collective-permute-start.15
  240.1 10.1 %shard_map.132 = (f32[2048,512]{1,0:T(8,128)}, f32[2048,512]{1,0:T(8,128)}) custom-call(s32[1]{0:T(128)} %bitcast.z_ref, f32[2048,16]{1,0:T(8,128)} %bitcast.53, bf16[512,512]{1,0:T(8,128)(2,1)} %bitcast.72, bf16[512,512]{1,0:T(8,128)(2,1)} %bitcast.15.refs_1_, bf16[512,512]{1,0:T(8,128)(2,1)} %bitcast.16.refs_2_), custom_call_target="tpu_custom_call" | custom-call | flops 6442450944 | bytes 12000000 | tf_op jit(solution)/shard_map/pallas_call | solution.py:371
  250.2 23.4 %collective-permute-done.14 = bf16[4,128,512]{2,1,0:T(8,128)(2,1)} collective-permute-done((bf16[4,128,512]{2,1,0:T(8,128)(2,1)}, bf16[4,128,512]{2,1,0:T(8,128)(2,1)}, u32[]{:S(2)}, u32[]{:S(2)}) %collective-permute-start.14) | collective-permute-done | bytes 524320 | tf_op jit(solution)/shard_map/ppermute | solution.py:368
  273.6 9.4 %collective-permute-done.15 = bf16[4,128,512]{2,1,0:T(8,128)(2,1)} collective-permute-done((bf16[4,128,512]{2,1,0:T(8,128)(2,1)}, bf16[4,128,512]{2,1,0:T(8,128)(2,1)}, u32[]{:S(2)}, u32[]{:S(2)}) %collective-permute-start.15) | collective-permute-done | bytes 524320 | tf_op jit(solution)/shard_map/ppermute | solution.py:368
  283.0 1.5 collective-permute-start.19
  285.0 16.5 %shard_map.133 = (bf16[2048,512]{1,0:T(8,128)(2,1)}, f32[8,2048]{1,0:T(8,128)}, bf16[2048,1024]{1,0:T(8,128)(2,1)}) custom-call(s32[1]{0:T(128)} %bitcast.z_ref, f32[2048,16]{1,0:T(8,128)} %bitcast.54, bf16[2048,1024]{1,0:T(8,128)(2,1)} %src_ref.13, f32[2048,512]{1,0:T(8,128)} %get-tuple-element.93.one_ref, f32[2048,512]{1,0:T(8,128)} %get-tuple-element.94.two_ref, ...), custom_call_target="tpu_custom_call" | custom-call | flops 10737418240 | bytes 16000000 | tf_op jit(solution)/shard_map/pallas_call | solution.py:371
  301.5 1.6 collective-permute-start.17
  303.1 14.9 %shard_map.139 = (bf16[4,128,256]{2,1,0:T(8,128)(2,1)}, bf16[4,128,256]{2,1,0:T(8,128)(2,1)}, bf16[4,128,256]{2,1,0:T(8,128)(2,1)}, bf16[4,128,256]{2,1,0:T(8,12...) custom-call(s32[1]{0:T(128)} %bitcast.z_ref, ...), custom_call_target="tpu_custom_call" | custom-call | flops 4294967296 | bytes 12288000 | tf_op jit(solution)/shard_map/pallas_call | solution.py:371
  318.1 1.8 collective-permute-start.43
  319.9 1.9 collective-permute-start.45
  321.9 14.9 %shard_map.138 = (bf16[4,128,256]{2,1,0:T(8,128)(2,1)}, bf16[4,128,256]{2,1,0:T(8,128)(2,1)}, bf16[4,128,256]{2,1,0:T(8,128)(2,1)}, bf16[4,128,256]{2,1,0:T(8,12...) custom-call(s32[1]{0:T(128)} %bitcast.z_ref, ...), custom_call_target="tpu_custom_call" | custom-call | flops 4294967296 | bytes 12288000 | tf_op jit(solution)/shard_map/pallas_call | solution.py:371
  337.3 2.4 collective-permute-start.47
  339.7 15.9 %collective-permute-done.30.refs_1_ = f32[8,2048]{1,0:T(8,128)} collective-permute-done((f32[8,2048]{1,0:T(8,128)}, f32[8,2048]{1,0:T(8,128)}, u32[]{:S(2)}, u32[]{:S(2)}) %collective-permute-start.30) | collective-permute-done | bytes 65568 | tf_op jit(solution)/shard_map/ppermute | solution.py:363
  355.7 1.1 collective-permute-start.48
  356.8 3.0 shard_map.140
  359.8 1.2 collective-permute-start.36
  361.0 1.2 collective-permute-start.33
  362.2 1.1 collective-permute-start.32
  363.3 1.9 collective-permute-done.48
  365.2 1.5 collective-permute-start.31
  366.7 8.5 %shard_map.142.refs_10_ = bf16[2048,256]{1,0:T(8,128)(2,1)} custom-call(s32[1]{0:T(128)} %bitcast.z_ref, f32[2048,16]{1,0:T(8,128)} %bitcast.55, bf16[192,2048]{1,0:T(8,128)(2,1)} %get-tuple-element.127.dl_ref, f32[32,1024]{1,0:T(8,128)} %bitcast.58, bf16[512,256]{1,0:T(8,128)(2,1)} %bitcast.68, bf16[512,256]{1,0:T(8,128)(2,1)} %bitcast.43.refs_2_, ...), custom_call_target="tpu_custom_call" | custom-call | flops 4294967296 | bytes 8000000 | tf_op jit(solution)/shard_map/pallas_call | solution.py:371
  375.2 3.2 collective-permute-done.33.refs_29_
  378.9 1.2 collective-permute-start.38
  380.1 1.7 collective-permute-start.49
  381.8 13.7 %shard_map.141 = (f32[4,1024,256]{2,1,0:T(8,128)}, f32[4,1024,256]{2,1,0:T(8,128)}, f32[4,256,1024]{2,1,0:T(8,128)}, f32[32,512]{1,0:T(8,128)}) custom-call(s32[1]{0:T(128)} %bitcast.z_ref, bf16[4,128,1024]{2,1,0:T(8,128)(2,1)} %bitcast.6.refs_0_, bf16[4,128,1024]{2,1,0:T(8,128)(2,1)} %bitcast.7.refs_1_, bf16[4,128,1024]{2,1,0:T(8,128)(2,1)} %bitcast.71, ...), custom_call_target="tpu_custom_call" | custom-call | flops 6442450944 | bytes 40000000 | tf_op jit(solution)/shard_map/pallas_call | solution.py:371
  396.2 1.0 collective-permute-done.34.pair_core
  397.2 0.8 collective-permute-start.40
  397.9 1.6 collective-permute-start.41
  399.6 3.8 k_place_y.1
  403.4 28.6 %collective-permute-done.39 = bf16[4,128,512]{2,1,0:T(8,128)(2,1)} collective-permute-done((bf16[4,128,512]{2,1,0:T(8,128)(2,1)}, bf16[4,128,512]{2,1,0:T(8,128)(2,1)}, u32[]{:S(2)}, u32[]{:S(2)}) %collective-permute-start.39) | collective-permute-done | bytes 524320 | tf_op jit(solution)/shard_map/ppermute | solution.py:368
  432.3 4.4 collective-permute-done.50.refs_13_
  436.8 14.9 %shard_map.143 = (bf16[2048,1024]{1,0:T(8,128)(2,1)}, f32[32,1024]{1,0:T(8,128)}) custom-call(s32[1]{0:T(128)} %bitcast.z_ref, f32[2048,16]{1,0:T(8,128)} %bitcast.56, bf16[192,2048]{1,0:T(8,128)(2,1)} %get-tuple-element.127.dl_ref, f32[32,1024]{1,0:T(8,128)} %bitcast.59, f32[32,1024]{1,0:T(8,128)} %bitcast.60, bf16[512,512]{1,0:T(8,128)(2,1)} %bitcast.67, ...), custom_call_target="tpu_custom_call" | custom-call | flops 8589934592 | bytes 8000000 | tf_op jit(solution)/shard_map/pallas_call | solution.py:371
  (61 shorter events, 5.8 us)
Async XLA Ops:
  6.4 63.1 %collective-permute-start = (bf16[512,1024]{1,0:T(8,128)(2,1)}, bf16[512,1024]{1,0:T(8,128)(2,1)}, u32[]{:S(2)}, u32[]{:S(2)}) collective-permute-start(bf16[512,1024]{1,0:T(8,128)(2,1)} %get-tuple-element.80), channel_id=1, source_target_pairs={{0,6},{1,7},{2,4},{3,5},{4,2},{5,3},{6,0},{7,1},{8,14},{9,15},{10,... | collective-permute-start | bytes 3145736 | tf_op jit(solution)/shard_map/ppermute | solution.py:368
  19.1 52.0 %collective-permute-start.3 = (bf16[512,1024]{1,0:T(8,128)(2,1)}, bf16[512,1024]{1,0:T(8,128)(2,1)}, u32[]{:S(2)}, u32[]{:S(2)}) collective-permute-start(bf16[512,1024]{1,0:T(8,128)(2,1)} %get-tuple-element.84), channel_id=1, source_target_pairs={{0,2},{1,3},{2,0},{3,1},{4,6},{5,7},{6,4},{7,5},{8,10},{9,11},{10,... | collective-permute-start | bytes 3145736 | tf_op jit(solution)/shard_map/ppermute | solution.py:368
  30.0 38.0 %collective-permute-start.23 = (bf16[512,512]{1,0:T(8,128)(2,1)}, bf16[512,512]{1,0:T(8,128)(2,1)}, u32[]{:S(2)}, u32[]{:S(2)}) collective-permute-start(bf16[512,512]{1,0:T(8,128)(2,1)} %get-tuple-element.106), channel_id=1, source_target_pairs={{0,2},{1,3},{2,0},{3,1},{4,6},{5,7},{6,4},{7,5},{8,10},{9,11},{10,... | collective-permute-start | bytes 1572872 | tf_op jit(solution)/shard_map/ppermute | solution.py:368
  31.5 36.5 %collective-permute-start.25 = (bf16[512,512]{1,0:T(8,128)(2,1)}, bf16[512,512]{1,0:T(8,128)(2,1)}, u32[]{:S(2)}, u32[]{:S(2)}) collective-permute-start(bf16[512,512]{1,0:T(8,128)(2,1)} %get-tuple-element.107), channel_id=1, source_target_pairs={{0,4},{1,5},{2,6},{3,7},{4,0},{5,1},{6,2},{7,3},{8,12},{9,13},{10,... | collective-permute-start | bytes 1572872 | tf_op jit(solution)/shard_map/ppermute | solution.py:368
  32.0 51.2 %collective-permute-start.4 = (bf16[512,1024]{1,0:T(8,128)(2,1)}, bf16[512,1024]{1,0:T(8,128)(2,1)}, u32[]{:S(2)}, u32[]{:S(2)}) collective-permute-start(bf16[512,1024]{1,0:T(8,128)(2,1)} %get-tuple-element.85), channel_id=1, source_target_pairs={{0,4},{1,5},{2,6},{3,7},{4,0},{5,1},{6,2},{7,3},{8,12},{9,13},{10,... | collective-permute-start | bytes 3145736 | tf_op jit(solution)/shard_map/ppermute | solution.py:368
  68.0 25.8 %collective-permute-start.1 = (bf16[512,1024]{1,0:T(8,128)(2,1)}, bf16[512,1024]{1,0:T(8,128)(2,1)}, u32[]{:S(2)}, u32[]{:S(2)}) collective-permute-start(bf16[512,1024]{1,0:T(8,128)(2,1)} %get-tuple-element.81), channel_id=1, source_target_pairs={{0,7},{1,6},{2,5},{3,4},{4,3},{5,2},{6,1},{7,0},{8,15},{9,14},{10,... | collective-permute-start | bytes 3145736 | tf_op jit(solution)/shard_map/ppermute | solution.py:368
  68.0 26.2 %collective-permute-start.2 = (bf16[512,1024]{1,0:T(8,128)(2,1)}, bf16[512,1024]{1,0:T(8,128)(2,1)}, u32[]{:S(2)}, u32[]{:S(2)}) collective-permute-start(bf16[512,1024]{1,0:T(8,128)(2,1)} %get-tuple-element.83), channel_id=1, source_target_pairs={{0,1},{1,0},{2,3},{3,2},{4,5},{5,4},{6,7},{7,6},{8,9},{9,8},{10,11... | collective-permute-start | bytes 3145736 | tf_op jit(solution)/shard_map/ppermute | solution.py:368
  69.6 118.4 %collective-permute-start.7 = (bf16[4,1024,256]{2,1,0:T(8,128)(2,1)}, bf16[4,1024,256]{2,1,0:T(8,128)(2,1)}, u32[]{:S(2)}, u32[]{:S(2)}) collective-permute-start(bf16[4,1024,256]{2,1,0:T(8,128)(2,1)} %refs_12_.3), channel_id=1, source_target_pairs={{0,8},{8,0},{1,9},{9,1},{2,10},{10,2},{3,11},{11,3},{4,12},{12,4},... | collective-permute-start | bytes 6291464 | tf_op jit(solution)/shard_map/ppermute | solution.py:363
  71.1 123.8 %collective-permute-start.8 = (bf16[4,1024,256]{2,1,0:T(8,128)(2,1)}, bf16[4,1024,256]{2,1,0:T(8,128)(2,1)}, u32[]{:S(2)}, u32[]{:S(2)}) collective-permute-start(bf16[4,1024,256]{2,1,0:T(8,128)(2,1)} %refs_13_.1), channel_id=1, source_target_pairs={{0,8},{8,0},{1,9},{9,1},{2,10},{10,2},{3,11},{11,3},{4,12},{12,4},... | collective-permute-start | bytes 6291464 | tf_op jit(solution)/shard_map/ppermute | solution.py:363
  83.2 101.7 %collective-permute-start.9 = (bf16[4,256,512]{2,1,0:T(8,128)(2,1)}, bf16[4,256,512]{2,1,0:T(8,128)(2,1)}, u32[]{:S(2)}, u32[]{:S(2)}) collective-permute-start(bf16[4,256,512]{2,1,0:T(8,128)(2,1)} %get-tuple-element.151), channel_id=1, source_target_pairs={{0,8},{8,0},{1,9},{9,1},{2,10},{10,2},{3,11},{11,3},{4,12},{12,4},... | collective-permute-start | bytes 3145736 | tf_op jit(solution)/shard_map/ppermute | solution.py:363
  93.8 92.5 %collective-permute-start.5 = (bf16[512,1024]{1,0:T(8,128)(2,1)}, bf16[512,1024]{1,0:T(8,128)(2,1)}, u32[]{:S(2)}, u32[]{:S(2)}) collective-permute-start(bf16[512,1024]{1,0:T(8,128)(2,1)} %get-tuple-element.86), channel_id=1, source_target_pairs={{0,3},{1,2},{2,1},{3,0},{4,7},{5,6},{6,5},{7,4},{8,11},{9,10},{10,... | collective-permute-start | bytes 3145736 | tf_op jit(solution)/shard_map/ppermute | solution.py:368
  94.2 92.1 %collective-permute-start.6 = (bf16[512,1024]{1,0:T(8,128)(2,1)}, bf16[512,1024]{1,0:T(8,128)(2,1)}, u32[]{:S(2)}, u32[]{:S(2)}) collective-permute-start(bf16[512,1024]{1,0:T(8,128)(2,1)} %get-tuple-element.87), channel_id=1, source_target_pairs={{0,5},{1,4},{2,7},{3,6},{4,1},{5,0},{6,3},{7,2},{8,13},{9,12},{10,... | collective-permute-start | bytes 3145736 | tf_op jit(solution)/shard_map/ppermute | solution.py:368
  184.9 25.6 %collective-permute-start.18 = (bf16[512,512]{1,0:T(8,128)(2,1)}, bf16[512,512]{1,0:T(8,128)(2,1)}, u32[]{:S(2)}, u32[]{:S(2)}) collective-permute-start(bf16[512,512]{1,0:T(8,128)(2,1)} %get-tuple-element.102), channel_id=1, source_target_pairs={{0,6},{1,7},{2,4},{3,5},{4,2},{5,3},{6,0},{7,1},{8,14},{9,15},{10,... | collective-permute-start | bytes 1572872 | tf_op jit(solution)/shard_map/ppermute | solution.py:368
  186.4 24.8 %collective-permute-start.20 = (bf16[512,512]{1,0:T(8,128)(2,1)}, bf16[512,512]{1,0:T(8,128)(2,1)}, u32[]{:S(2)}, u32[]{:S(2)}) collective-permute-start(bf16[512,512]{1,0:T(8,128)(2,1)} %get-tuple-element.103), channel_id=1, source_target_pairs={{0,7},{1,6},{2,5},{3,4},{4,3},{5,2},{6,1},{7,0},{8,15},{9,14},{10,... | collective-permute-start | bytes 1572872 | tf_op jit(solution)/shard_map/ppermute | solution.py:368
  186.4 26.3 %collective-permute-start.24 = (bf16[512,512]{1,0:T(8,128)(2,1)}, bf16[512,512]{1,0:T(8,128)(2,1)}, u32[]{:S(2)}, u32[]{:S(2)}) collective-permute-start(bf16[512,512]{1,0:T(8,128)(2,1)} %collective-permute-done.23), channel_id=1, source_target_pairs={{0,8},{8,0},{1,9},{9,1},{2,10},{10,2},{3,11},{11,3},{4,12},{12,4},... | collective-permute-start | bytes 1572872 | tf_op jit(solution)/shard_map/ppermute | solution.py:363
  188.0 25.6 %collective-permute-start.26 = (bf16[512,512]{1,0:T(8,128)(2,1)}, bf16[512,512]{1,0:T(8,128)(2,1)}, u32[]{:S(2)}, u32[]{:S(2)}) collective-permute-start(bf16[512,512]{1,0:T(8,128)(2,1)} %collective-permute-done.25), channel_id=1, source_target_pairs={{0,8},{8,0},{1,9},{9,1},{2,10},{10,2},{3,11},{11,3},{4,12},{12,4},... | collective-permute-start | bytes 1572872 | tf_op jit(solution)/shard_map/ppermute | solution.py:363
  195.0 40.6 %collective-permute-start.29 = (bf16[4,256,512]{2,1,0:T(8,128)(2,1)}, bf16[4,256,512]{2,1,0:T(8,128)(2,1)}, u32[]{:S(2)}, u32[]{:S(2)}) collective-permute-start(bf16[4,256,512]{2,1,0:T(8,128)(2,1)} %get-tuple-element.150), channel_id=1, source_target_pairs={{0,8},{8,0},{1,9},{9,1},{2,10},{10,2},{3,11},{11,3},{4,12},{12,4},... | collective-permute-start | bytes 3145736 | tf_op jit(solution)/shard_map/ppermute | solution.py:363
  210.5 25.2 %collective-permute-start.10 = (bf16[4,128,512]{2,1,0:T(8,128)(2,1)}, bf16[4,128,512]{2,1,0:T(8,128)(2,1)}, u32[]{:S(2)}, u32[]{:S(2)}) collective-permute-start(bf16[4,128,512]{2,1,0:T(8,128)(2,1)} %get-tuple-element.91), channel_id=1, source_target_pairs={{0,1},{1,0},{2,3},{3,2},{4,5},{5,4},{6,7},{7,6},{8,9},{9,8},{10,11... | collective-permute-start | bytes 1572872 | tf_op jit(solution)/shard_map/ppermute | solution.py:368
  211.2 26.2 %collective-permute-start.11 = (bf16[4,128,512]{2,1,0:T(8,128)(2,1)}, bf16[4,128,512]{2,1,0:T(8,128)(2,1)}, u32[]{:S(2)}, u32[]{:S(2)}) collective-permute-start(bf16[4,128,512]{2,1,0:T(8,128)(2,1)} %get-tuple-element.92), channel_id=1, source_target_pairs={{0,6},{1,7},{2,4},{3,5},{4,2},{5,3},{6,0},{7,1},{8,14},{9,15},{10,... | collective-permute-start | bytes 1572872 | tf_op jit(solution)/shard_map/ppermute | solution.py:368
  212.7 25.6 %collective-permute-start.12 = (bf16[4,128,512]{2,1,0:T(8,128)(2,1)}, bf16[4,128,512]{2,1,0:T(8,128)(2,1)}, u32[]{:S(2)}, u32[]{:S(2)}) collective-permute-start(bf16[4,128,512]{2,1,0:T(8,128)(2,1)} %get-tuple-element.95), channel_id=1, source_target_pairs={{0,4},{1,5},{2,6},{3,7},{4,0},{5,1},{6,2},{7,3},{8,12},{9,13},{10,... | collective-permute-start | bytes 1572872 | tf_op jit(solution)/shard_map/ppermute | solution.py:368
  213.5 26.5 %collective-permute-start.13 = (bf16[4,128,512]{2,1,0:T(8,128)(2,1)}, bf16[4,128,512]{2,1,0:T(8,128)(2,1)}, u32[]{:S(2)}, u32[]{:S(2)}) collective-permute-start(bf16[4,128,512]{2,1,0:T(8,128)(2,1)} %get-tuple-element.96), channel_id=1, source_target_pairs={{0,2},{1,3},{2,0},{3,1},{4,6},{5,7},{6,4},{7,5},{8,10},{9,11},{10,... | collective-permute-start | bytes 1572872 | tf_op jit(solution)/shard_map/ppermute | solution.py:368
  235.5 65.9 %collective-permute-start.27 = (bf16[512,1024]{1,0:T(8,128)(2,1)}, bf16[512,1024]{1,0:T(8,128)(2,1)}, u32[]{:S(2)}, u32[]{:S(2)}) collective-permute-start(bf16[512,1024]{1,0:T(8,128)(2,1)} %get-tuple-element.108), channel_id=1, source_target_pairs={{0,3},{1,2},{2,1},{3,0},{4,7},{5,6},{6,5},{7,4},{8,11},{9,10},{10,... | collective-permute-start | bytes 3145736 | tf_op jit(solution)/shard_map/ppermute | solution.py:368
  235.7 67.5 %collective-permute-start.28 = (bf16[512,1024]{1,0:T(8,128)(2,1)}, bf16[512,1024]{1,0:T(8,128)(2,1)}, u32[]{:S(2)}, u32[]{:S(2)}) collective-permute-start(bf16[512,1024]{1,0:T(8,128)(2,1)} %get-tuple-element.109), channel_id=1, source_target_pairs={{0,5},{1,4},{2,7},{3,6},{4,1},{5,0},{6,3},{7,2},{8,13},{9,12},{10,... | collective-permute-start | bytes 3145736 | tf_op jit(solution)/shard_map/ppermute | solution.py:368
  237.4 36.2 %collective-permute-start.14 = (bf16[4,128,512]{2,1,0:T(8,128)(2,1)}, bf16[4,128,512]{2,1,0:T(8,128)(2,1)}, u32[]{:S(2)}, u32[]{:S(2)}) collective-permute-start(bf16[4,128,512]{2,1,0:T(8,128)(2,1)} %get-tuple-element.97), channel_id=1, source_target_pairs={{0,7},{1,6},{2,5},{3,4},{4,3},{5,2},{6,1},{7,0},{8,15},{9,14},{10,... | collective-permute-start | bytes 1572872 | tf_op jit(solution)/shard_map/ppermute | solution.py:368
  238.3 44.6 %collective-permute-start.15 = (bf16[4,128,512]{2,1,0:T(8,128)(2,1)}, bf16[4,128,512]{2,1,0:T(8,128)(2,1)}, u32[]{:S(2)}, u32[]{:S(2)}) collective-permute-start(bf16[4,128,512]{2,1,0:T(8,128)(2,1)} %get-tuple-element.98), channel_id=1, source_target_pairs={{0,5},{1,4},{2,7},{3,6},{4,1},{5,0},{6,3},{7,2},{8,13},{9,12},{10,... | collective-permute-start | bytes 1572872 | tf_op jit(solution)/shard_map/ppermute | solution.py:368
  240.0 44.5 %collective-permute-start.16 = (bf16[4,128,512]{2,1,0:T(8,128)(2,1)}, bf16[4,128,512]{2,1,0:T(8,128)(2,1)}, u32[]{:S(2)}, u32[]{:S(2)}) collective-permute-start(bf16[4,128,512]{2,1,0:T(8,128)(2,1)} %get-tuple-element.99), channel_id=1, source_target_pairs={{0,3},{1,2},{2,1},{3,0},{4,7},{5,6},{6,5},{7,4},{8,11},{9,10},{10,... | collective-permute-start | bytes 1572872 | tf_op jit(solution)/shard_map/ppermute | solution.py:368
  273.6 48.2 %collective-permute-start.22 = (bf16[512,1024]{1,0:T(8,128)(2,1)}, bf16[512,1024]{1,0:T(8,128)(2,1)}, u32[]{:S(2)}, u32[]{:S(2)}) collective-permute-start(bf16[512,1024]{1,0:T(8,128)(2,1)} %get-tuple-element.105), channel_id=1, source_target_pairs={{0,1},{1,0},{2,3},{3,2},{4,5},{5,4},{6,7},{7,6},{8,9},{9,8},{10,11... | collective-permute-start | bytes 3145736 | tf_op jit(solution)/shard_map/ppermute | solution.py:368
  283.0 36.9 %collective-permute-start.19 = (bf16[512,512]{1,0:T(8,128)(2,1)}, bf16[512,512]{1,0:T(8,128)(2,1)}, u32[]{:S(2)}, u32[]{:S(2)}) collective-permute-start(bf16[512,512]{1,0:T(8,128)(2,1)} %collective-permute-done.18), channel_id=1, source_target_pairs={{0,8},{8,0},{1,9},{9,1},{2,10},{10,2},{3,11},{11,3},{4,12},{12,4},... | collective-permute-start | bytes 1572872 | tf_op jit(solution)/shard_map/ppermute | solution.py:363
  284.5 35.4 %collective-permute-start.21 = (bf16[512,512]{1,0:T(8,128)(2,1)}, bf16[512,512]{1,0:T(8,128)(2,1)}, u32[]{:S(2)}, u32[]{:S(2)}) collective-permute-start(bf16[512,512]{1,0:T(8,128)(2,1)} %collective-permute-done.20), channel_id=1, source_target_pairs={{0,8},{8,0},{1,9},{9,1},{2,10},{10,2},{3,11},{11,3},{4,12},{12,4},... | collective-permute-start | bytes 1572872 | tf_op jit(solution)/shard_map/ppermute | solution.py:363
  301.5 96.4 %collective-permute-start.17 = (bf16[2048,512]{1,0:T(8,128)(2,1)}, bf16[2048,512]{1,0:T(8,128)(2,1)}, u32[]{:S(2)}, u32[]{:S(2)}) collective-permute-start(bf16[2048,512]{1,0:T(8,128)(2,1)} %get-tuple-element.101), channel_id=1, source_target_pairs={{0,8},{8,0},{1,9},{9,1},{2,10},{10,2},{3,11},{11,3},{4,12},{12,4},... | collective-permute-start | bytes 6291464 | tf_op jit(solution)/shard_map/ppermute | solution.py:363
  318.1 18.8 %collective-permute-start.43 = (bf16[4,128,256]{2,1,0:T(8,128)(2,1)}, bf16[4,128,256]{2,1,0:T(8,128)(2,1)}, u32[]{:S(2)}, u32[]{:S(2)}) collective-permute-start(bf16[4,128,256]{2,1,0:T(8,128)(2,1)} %get-tuple-element.138), channel_id=1, source_target_pairs={{0,2},{1,3},{2,0},{3,1},{4,6},{5,7},{6,4},{7,5},{8,10},{9,11},{10,... | collective-permute-start | bytes 786440 | tf_op jit(solution)/shard_map/ppermute | solution.py:368
  319.9 17.3 %collective-permute-start.44 = (bf16[4,128,256]{2,1,0:T(8,128)(2,1)}, bf16[4,128,256]{2,1,0:T(8,128)(2,1)}, u32[]{:S(2)}, u32[]{:S(2)}) collective-permute-start(bf16[4,128,256]{2,1,0:T(8,128)(2,1)} %get-tuple-element.139), channel_id=1, source_target_pairs={{0,3},{1,2},{2,1},{3,0},{4,7},{5,6},{6,5},{7,4},{8,11},{9,10},{10,... | collective-permute-start | bytes 786440 | tf_op jit(solution)/shard_map/ppermute | solution.py:368
  319.9 17.4 %collective-permute-start.45 = (bf16[4,128,256]{2,1,0:T(8,128)(2,1)}, bf16[4,128,256]{2,1,0:T(8,128)(2,1)}, u32[]{:S(2)}, u32[]{:S(2)}) collective-permute-start(bf16[4,128,256]{2,1,0:T(8,128)(2,1)} %get-tuple-element.140), channel_id=1, source_target_pairs={{0,4},{1,5},{2,6},{3,7},{4,0},{5,1},{6,2},{7,3},{8,12},{9,13},{10,... | collective-permute-start | bytes 786440 | tf_op jit(solution)/shard_map/ppermute | solution.py:368
  321.8 33.9 %collective-permute-start.30 = (f32[8,2048]{1,0:T(8,128)}, f32[8,2048]{1,0:T(8,128)}, u32[]{:S(2)}, u32[]{:S(2)}) collective-permute-start(f32[8,2048]{1,0:T(8,128)} %get-tuple-element.123.refs_0_), channel_id=1, source_target_pairs={{0,8},{8,0},{1,9},{9,1},{2,10},{10,2},{3,11},{11,3},{4,12},{12,4},... | collective-permute-start | bytes 196616 | tf_op jit(solution)/shard_map/ppermute | solution.py:363
  336.8 23.0 %collective-permute-start.46 = (bf16[4,128,256]{2,1,0:T(8,128)(2,1)}, bf16[4,128,256]{2,1,0:T(8,128)(2,1)}, u32[]{:S(2)}, u32[]{:S(2)}) collective-permute-start(bf16[4,128,256]{2,1,0:T(8,128)(2,1)} %get-tuple-element.141), channel_id=1, source_target_pairs={{0,5},{1,4},{2,7},{3,6},{4,1},{5,0},{6,3},{7,2},{8,13},{9,12},{10,... | collective-permute-start | bytes 786440 | tf_op jit(solution)/shard_map/ppermute | solution.py:368
  337.2 23.8 %collective-permute-start.42 = (bf16[4,128,256]{2,1,0:T(8,128)(2,1)}, bf16[4,128,256]{2,1,0:T(8,128)(2,1)}, u32[]{:S(2)}, u32[]{:S(2)}) collective-permute-start(bf16[4,128,256]{2,1,0:T(8,128)(2,1)} %get-tuple-element.137), channel_id=1, source_target_pairs={{0,1},{1,0},{2,3},{3,2},{4,5},{5,4},{6,7},{7,6},{8,9},{9,8},{10,11... | collective-permute-start | bytes 786440 | tf_op jit(solution)/shard_map/ppermute | solution.py:368
  337.3 24.9 %collective-permute-start.47 = (bf16[4,128,256]{2,1,0:T(8,128)(2,1)}, bf16[4,128,256]{2,1,0:T(8,128)(2,1)}, u32[]{:S(2)}, u32[]{:S(2)}) collective-permute-start(bf16[4,128,256]{2,1,0:T(8,128)(2,1)} %get-tuple-element.142), channel_id=1, source_target_pairs={{0,6},{1,7},{2,4},{3,5},{4,2},{5,3},{6,0},{7,1},{8,14},{9,15},{10,... | collective-permute-start | bytes 786440 | tf_op jit(solution)/shard_map/ppermute | solution.py:368
  355.7 9.5 %collective-permute-start.48 = (bf16[4,128,256]{2,1,0:T(8,128)(2,1)}, bf16[4,128,256]{2,1,0:T(8,128)(2,1)}, u32[]{:S(2)}, u32[]{:S(2)}) collective-permute-start(bf16[4,128,256]{2,1,0:T(8,128)(2,1)} %get-tuple-element.143), channel_id=1, source_target_pairs={{0,7},{1,6},{2,5},{3,4},{4,3},{5,2},{6,1},{7,0},{8,15},{9,14},{10,... | collective-permute-start | bytes 786440 | tf_op jit(solution)/shard_map/ppermute | solution.py:368
  359.8 35.7 %collective-permute-start.36 = (bf16[4,128,512]{2,1,0:T(8,128)(2,1)}, bf16[4,128,512]{2,1,0:T(8,128)(2,1)}, u32[]{:S(2)}, u32[]{:S(2)}) collective-permute-start(bf16[4,128,512]{2,1,0:T(8,128)(2,1)} %get-tuple-element.130), channel_id=1, source_target_pairs={{0,2},{1,3},{2,0},{3,1},{4,6},{5,7},{6,4},{7,5},{8,10},{9,11},{10,... | collective-permute-start | bytes 1572872 | tf_op jit(solution)/shard_map/ppermute | solution.py:368
  361.0 17.4 %collective-permute-start.33 = (f32[32,512]{1,0:T(8,128)}, f32[32,512]{1,0:T(8,128)}, u32[]{:S(2)}, u32[]{:S(2)}) collective-permute-start(f32[32,512]{1,0:T(8,128)} %get-tuple-element.124.refs_26_), channel_id=1, source_target_pairs={{0,6},{1,7},{2,4},{3,5},{4,2},{5,3},{6,0},{7,1},{8,14},{9,15},{10,... | collective-permute-start | bytes 196616 | tf_op jit(solution)/shard_map/ppermute | solution.py:368
  362.2 16.7 %collective-permute-start.32 = (f32[32,512]{1,0:T(8,128)}, f32[32,512]{1,0:T(8,128)}, u32[]{:S(2)}, u32[]{:S(2)}) collective-permute-start(f32[32,512]{1,0:T(8,128)} %get-tuple-element.124.refs_26_), channel_id=1, source_target_pairs={{0,4},{1,5},{2,6},{3,7},{4,0},{5,1},{6,2},{7,3},{8,12},{9,13},{10,... | collective-permute-start | bytes 196616 | tf_op jit(solution)/shard_map/ppermute | solution.py:368
  365.2 14.9 %collective-permute-start.31 = (f32[32,512]{1,0:T(8,128)}, f32[32,512]{1,0:T(8,128)}, u32[]{:S(2)}, u32[]{:S(2)}) collective-permute-start(f32[32,512]{1,0:T(8,128)} %get-tuple-element.124.refs_26_), channel_id=1, source_target_pairs={{0,2},{1,3},{2,0},{3,1},{4,6},{5,7},{6,4},{7,5},{8,10},{9,11},{10,... | collective-permute-start | bytes 196616 | tf_op jit(solution)/shard_map/ppermute | solution.py:368
  378.4 17.2 %collective-permute-start.37 = (bf16[4,128,512]{2,1,0:T(8,128)(2,1)}, bf16[4,128,512]{2,1,0:T(8,128)(2,1)}, u32[]{:S(2)}, u32[]{:S(2)}) collective-permute-start(bf16[4,128,512]{2,1,0:T(8,128)(2,1)} %get-tuple-element.131), channel_id=1, source_target_pairs={{0,3},{1,2},{2,1},{3,0},{4,7},{5,6},{6,5},{7,4},{8,11},{9,10},{10,... | collective-permute-start | bytes 1572872 | tf_op jit(solution)/shard_map/ppermute | solution.py:368
  378.9 17.2 %collective-permute-start.38 = (bf16[4,128,512]{2,1,0:T(8,128)(2,1)}, bf16[4,128,512]{2,1,0:T(8,128)(2,1)}, u32[]{:S(2)}, u32[]{:S(2)}) collective-permute-start(bf16[4,128,512]{2,1,0:T(8,128)(2,1)} %get-tuple-element.132), channel_id=1, source_target_pairs={{0,4},{1,5},{2,6},{3,7},{4,0},{5,1},{6,2},{7,3},{8,12},{9,13},{10,... | collective-permute-start | bytes 1572872 | tf_op jit(solution)/shard_map/ppermute | solution.py:368
  380.1 52.2 %collective-permute-start.49 = (bf16[2048,256]{1,0:T(8,128)(2,1)}, bf16[2048,256]{1,0:T(8,128)(2,1)}, u32[]{:S(2)}, u32[]{:S(2)}) collective-permute-start(bf16[2048,256]{1,0:T(8,128)(2,1)} %shard_map.142.refs_10_), channel_id=1, source_target_pairs={{0,8},{8,0},{1,9},{9,1},{2,10},{10,2},{3,11},{11,3},{4,12},{12,4},... | collective-permute-start | bytes 3145736 | tf_op jit(solution)/shard_map/ppermute | solution.py:363
  395.5 1.6 collective-permute-start.34
  395.6 36.4 %collective-permute-start.39 = (bf16[4,128,512]{2,1,0:T(8,128)(2,1)}, bf16[4,128,512]{2,1,0:T(8,128)(2,1)}, u32[]{:S(2)}, u32[]{:S(2)}) collective-permute-start(bf16[4,128,512]{2,1,0:T(8,128)(2,1)} %get-tuple-element.133), channel_id=1, source_target_pairs={{0,5},{1,4},{2,7},{3,6},{4,1},{5,0},{6,3},{7,2},{8,13},{9,12},{10,... | collective-permute-start | bytes 1572872 | tf_op jit(solution)/shard_map/ppermute | solution.py:368
  396.1 36.2 %collective-permute-start.35 = (bf16[4,128,512]{2,1,0:T(8,128)(2,1)}, bf16[4,128,512]{2,1,0:T(8,128)(2,1)}, u32[]{:S(2)}, u32[]{:S(2)}) collective-permute-start(bf16[4,128,512]{2,1,0:T(8,128)(2,1)} %get-tuple-element.129), channel_id=1, source_target_pairs={{0,1},{1,0},{2,3},{3,2},{4,5},{5,4},{6,7},{7,6},{8,9},{9,8},{10,11... | collective-permute-start | bytes 1572872 | tf_op jit(solution)/shard_map/ppermute | solution.py:368
  397.2 35.2 %collective-permute-start.40 = (bf16[4,128,512]{2,1,0:T(8,128)(2,1)}, bf16[4,128,512]{2,1,0:T(8,128)(2,1)}, u32[]{:S(2)}, u32[]{:S(2)}) collective-permute-start(bf16[4,128,512]{2,1,0:T(8,128)(2,1)} %get-tuple-element.134), channel_id=1, source_target_pairs={{0,6},{1,7},{2,4},{3,5},{4,2},{5,3},{6,0},{7,1},{8,14},{9,15},{10,... | collective-permute-start | bytes 1572872 | tf_op jit(solution)/shard_map/ppermute | solution.py:368
  397.9 34.4 %collective-permute-start.41 = (bf16[4,128,512]{2,1,0:T(8,128)(2,1)}, bf16[4,128,512]{2,1,0:T(8,128)(2,1)}, u32[]{:S(2)}, u32[]{:S(2)}) collective-permute-start(bf16[4,128,512]{2,1,0:T(8,128)(2,1)} %get-tuple-element.135), channel_id=1, source_target_pairs={{0,7},{1,6},{2,5},{3,4},{4,3},{5,2},{6,1},{7,0},{8,15},{9,14},{10,... | collective-permute-start | bytes 1572872 | tf_op jit(solution)/shard_map/ppermute | solution.py:368
  432.0 4.8 %collective-permute-start.50 = (f32[32,512]{1,0:T(8,128)}, f32[32,512]{1,0:T(8,128)}, u32[]{:S(2)}, u32[]{:S(2)}) collective-permute-start(f32[32,512]{1,0:T(8,128)} %get-tuple-element.144.refs_12_), channel_id=1, source_target_pairs={{0,8},{8,0},{1,9},{9,1},{2,10},{10,2},{3,11},{11,3},{4,12},{12,4},... | collective-permute-start | bytes 196616 | tf_op jit(solution)/shard_map/ppermute | solution.py:363

commit v4 on v3

--- a/solution.py
+++ b/solution.py
@@ -17,6 +17,7 @@
 GATHER_TILE = 256
 GROUP = 2
 TOKEN_TILE = 512
+LANES = 128
 
 
 def gelu_parts(pre_act):
@@ -206,10 +207,11 @@
                 outs[c * n_src + first + i][0] = total[i * cap:(i + 1) * cap]
 
 
-def weight_grad_kernel(z_ref, *refs, n_src, widths):
+def weight_grad_kernel(z_ref, kept_ref, piece_ref, *refs, n_src, widths):
     xs = refs[:n_src]
     dos, refs = group_refs(refs[n_src:], widths)
-    h_ref, h2_ref, da_ref, da2_ref, db_ref, db2_ref, d0, d2, d4, d6, ga_ref, gb_ref, gc_ref, dw_ref, do_ref = refs
+    h_ref, h2_ref, da_ref, da2_ref, db_ref, db2_ref, d0, d2, d4, d6, ga_ref, gb_ref, gc_ref, dw_ref, out_ref, do_ref = refs
+    out_ref[...] = piece_ref[...]
     dw_ref[...] = (d0[...] + d2[...]) + (d4[...] + d6[...])
     cap = xs[0].shape[1]
     for i, ref in enumerate(dos):
@@ -285,50 +287,49 @@
     dw_ref[...] = raw[:n_experts] + raw[n_experts:2 * n_experts] + raw[2 * n_experts:]
 
 
-def combine_in_kernel(z_ref, cols_ref, dl_ref, *refs, n_src, last):
-    n_w = 2 if last else 1
-    wts, refs = refs[:n_w], refs[n_w:]
-    srcs, refs = refs[:n_src], refs[n_src:]
-    blocks = srcs[0].shape[0] // 128
+def add_token_rows(total, cols_ref, srcs, peers):
     (blk_one, hot_one), (blk_two, hot_two) = slot_picks(cols_ref)
-    zero = jnp.zeros((TOKEN_TILE, 128), BF16)
-    acc = None
-    for d in range(n_src):
+    zero = jnp.zeros((TOKEN_TILE, LANES), BF16)
+    blocks = srcs[0].shape[0] // LANES
+    for d, src in zip(peers, srcs):
         parts = []
         for b in range(blocks):
             this = jnp.asarray(d * blocks + b, BF16)
             parts.append(jnp.where(blk_one == this, hot_one, jnp.where(blk_two == this, hot_two, zero)))
-        part = jnp.dot(jnp.concatenate(parts, axis=1), srcs[d][...], preferred_element_type=F32)
-        acc = part if acc is None else acc + part
+        total = total + jnp.dot(jnp.concatenate(parts, axis=1), src[...], preferred_element_type=F32)
+    return total
+
+
+def combine_in_kernel(z_ref, cols_ref, dl_ref, *refs, peers):
+    srcs, wts, out_ref = refs[:len(peers)], refs[len(peers):-1], refs[-1]
     high, mid, low = split3(jnp.concatenate([w[...] for w in wts], axis=1))
     weights = jnp.concatenate([high, mid, high, low, high, mid], axis=0)
     back = lax.dot_general(dl_ref[...], weights, TN, preferred_element_type=F32)
-    res = (acc + back).astype(BF16)
-    if not last:
-        refs[0][...] = res
-        return
-    mine, other, near_ref, far_ref, dx_ref, dw_ref = refs
-    wide = mine.shape[1]
+    out_ref[...] = add_token_rows(back, cols_ref, srcs, peers).astype(out_ref.dtype)
+
+
+def combine_last_kernel(z_ref, cols_ref, acc_ref, *refs, peers):
+    srcs = refs[:len(peers)]
+    mine, other, own_core, pair_core, own_far, pair_far, dx_ref, dw_ref = refs[len(peers):]
+    res = add_token_rows(acc_ref[...], cols_ref, srcs, peers).astype(BF16)
     low_side = z_ref[0] == 0
 
     @pl.when(pl.program_id(0) == 0)
     def _():
-        near, far = near_ref[...], far_ref[...]
+        near, far = own_core[...] + pair_core[...], own_far[...] + pair_far[...]
         dw_ref[...] = jnp.concatenate([jnp.where(low_side, near, far), jnp.where(low_side, far, near)], axis=1)
 
-    dx_ref[:, :wide] = jnp.where(low_side, mine[...], other[...])
-    dx_ref[:, wide:2 * wide] = res[:, :wide]
-    dx_ref[:, 2 * wide:3 * wide] = jnp.where(low_side, other[...], mine[...])
-    dx_ref[:, 3 * wide:] = res[:, wide:]
-
-
-def place_kernel(z_ref, kept_ref, piece_ref, own_core, pair_core, dw_ref, out_ref):
-    out_ref[...] = piece_ref[...]
-    dw_ref[...] = own_core[...] + pair_core[...]
+    wide = mine.shape[1]
+    first, third = jnp.where(low_side, mine[...], other[...]), jnp.where(low_side, other[...], mine[...])
+    dx_ref[...] = jnp.concatenate([first, res[:, :wide], third, res[:, wide:]], axis=1)
 
 
 def cost(flops, nbytes, trans=0):
     return pl.CostEstimate(flops=int(flops), bytes_accessed=int(nbytes), transcendentals=int(trans))
+
+
+def peers_of(digits):
+    return [int(c) for c in digits]
 
 
 def solution(mesh):
@@ -336,12 +337,11 @@
     n_src = mesh.shape["ep"]
     n_chunk = 2
     all_vmem = pltpu.CompilerParams(vmem_limit_bytes=67043328)
-    diag = [n_src - 2, n_src - 1]
-    early = diag + [0, 1]
-    late = [2, 4, 3, 5]
+    early, late = peers_of("6701"), peers_of("2435")
     src_order = early + late
     first_peer = 6
-    out_early, out_late = [0, 1, 6], [4, 2, 7, 5, 3]
+    out_early, out_late = peers_of("016"), peers_of("42753")
+    in_early, in_late = peers_of("01624"), peers_of("357")
 
     def local_step(x_rows, w_router, first_ids, second_ids, w_gelu, w_lin, w_out, dy_rows):
         n_tokens, model = x_rows.shape
@@ -367,11 +367,11 @@
                 return val
             return lax.ppermute(val, "ep", [(i, i ^ d) for i in range(n_src)])
 
-        def call(kernel, grid, in_specs, out_specs, out_shape, estimate, args, scratch=()):
+        def call(kernel, grid, in_specs, out_specs, out_shape, estimate, args, scratch=(), aliases={}):
             return pl.pallas_call(
                 kernel,
                 grid_spec=pltpu.PrefetchScalarGridSpec(num_scalar_prefetch=1, grid=grid, in_specs=in_specs, out_specs=out_specs, scratch_shapes=list(scratch)),
-                out_shape=out_shape, cost_estimate=estimate, compiler_params=all_vmem)(z, *args)
+                out_shape=out_shape, cost_estimate=estimate, compiler_params=all_vmem, input_output_aliases=aliases)(z, *args)
 
         wa2, wb2 = across(w_gelu), across(w_lin)
         wt = w_router.T
@@ -416,14 +416,14 @@
 
         xs, dos = [None] * n_src, [None] * n_src
         xs[first_peer] = to_peer(first_x, first_peer).reshape(own, slot_cap, model)
-        for peers in ([4, 2], [7, 1, 0], [5, 3]):
+        for peers in map(peers_of, ("42", "710", "53")):
             for d, val in zip(peers, gather(x_rows, peers, False)):
                 xs[d] = to_peer(val, d).reshape(own, slot_cap, model)
-        for peers in (diag, [4, 2]):
+        for peers in map(peers_of, ("67", "42")):
             for d, val in zip(peers, gather(dy_rows, peers, True, part=True)):
                 mine = to_peer(val, d)
                 dos[d] = tuple(v.reshape(own, slot_cap, cols) for v in (mine, across(mine)))
-        for peers in ([1, 0], [5, 3]):
+        for peers in map(peers_of, ("10", "53")):
             for d, val in zip(peers, gather(dy_rows, peers, True)):
                 dos[d] = (to_peer(val, d).reshape(own, slot_cap, model),)
         xs = [xs[d] for d in src_order]
@@ -501,8 +501,6 @@
             return pl.BlockSpec((TOKEN_TILE, b), lambda i, z: (i, 0 if col is None else z[0] * n_chunk + col))
 
         n_tiles = (n_tokens // TOKEN_TILE,)
-        any_spec = pl.BlockSpec(memory_space=pl.ANY)
-
         one, two = call(
             functools.partial(combine_first_kernel, peers=out_early), n_tiles,
             [tiles(16)] + [resident(block, cols)] * len(out_early), [tiles(cols)] * 2, [sds((n_tokens, cols), F32)] * 2,
@@ -527,38 +525,36 @@
             (rows, prob, id_one, id_two, x_rows, dg_mine, dg_other))
 
         all_dos = [v for d in src_order for v in dos[d]]
-        grad_wa, grad_wb, grad_wc, dw_core = call(
+        assert n_tokens // TOKEN_TILE == own
+        grad_wa, grad_wb, grad_wc, dw_core, act_out = call(
             functools.partial(weight_grad_kernel, n_src=n_src, widths=[len(dos[d]) for d in src_order]), (own,),
-            [whole(slot_cap, model)] * n_src + [whole(slot_cap, v.shape[2]) for v in all_dos] + [whole(r, width) for r in part_rows] + [whole(rows_early, width), whole(rows_late, width)] * 2 + [resident(n_experts, cols)] * 4,
-            [whole(model, width), whole(model, width), whole(width, model), resident(n_experts, cols)],
-            [sds((own, model, width), F32)] * 2 + [sds((own, width, model), F32), sds((n_experts, cols), F32)],
+            [pl.BlockSpec(memory_space=pl.ANY), tiles(cols)] + [whole(slot_cap, model)] * n_src + [whole(slot_cap, v.shape[2]) for v in all_dos] + [whole(r, width) for r in part_rows] + [whole(rows_early, width), whole(rows_late, width)] * 2 + [resident(n_experts, cols)] * 4,
+            [whole(model, width), whole(model, width), whole(width, model), resident(n_experts, cols), pl.BlockSpec((TOKEN_TILE, cols), lambda e, z: (e, 1 - z[0]))],
+            [sds((own, model, width), F32)] * 2 + [sds((own, width, model), F32), sds((n_experts, cols), F32), sds((n_tokens, model), BF16)],
             cost(6 * own * rows_all * width * model, 40e6),
-            (*xs, *all_dos, own_parts[0][2], own_parts[1][2], bwd_a[-2], bwd_b[-2], bwd_a[-1], bwd_b[-1], dw, to_peer(dw, 2), to_peer(dw, 4), to_peer(dw, 6)),
-            [pltpu.VMEM((rows_all, model), BF16)])
-
-        dw_near, act_out = pl.pallas_call(
-            place_kernel,
-            grid_spec=pltpu.PrefetchScalarGridSpec(
-                num_scalar_prefetch=1, grid=n_tiles, in_specs=[pl.BlockSpec(memory_space=pl.ANY), tiles(cols)] + [resident(n_experts, cols)] * 2,
-                out_specs=[resident(n_experts, cols), pl.BlockSpec((TOKEN_TILE, cols), lambda i, z: (i, 1 - z[0]))]),
-            out_shape=[sds((n_experts, cols), F32), sds((n_tokens, model), BF16)], input_output_aliases={1: 1}, cost_estimate=cost(1e6, 4e6),
-            compiler_params=all_vmem, name="k_place_y")(z, act_out, y_other, dw_core, to_peer(dw_core, 1))
-        routers = (dw_near, across(dw_near))
-
-        def combine_in(last, extra, srcs):
-            quarters = [(lambda i, z: (0, 1)), (lambda i, z: (0, 3))] if last else [lambda i, z: (0, z[0] * n_chunk)]
+            (act_out, y_other, *xs, *all_dos, own_parts[0][2], own_parts[1][2], bwd_a[-2], bwd_b[-2], bwd_a[-1], bwd_b[-1], dw, to_peer(dw, 2), to_peer(dw, 4), to_peer(dw, 6)),
+            [pltpu.VMEM((rows_all, model), BF16)], {1: 4})
+        far_pair = lax.ppermute(dw_core, ("tp", "ep"), [(i, i ^ (n_src + 1)) for i in range(tp_size * n_src)])
+        routers = (dw_core, to_peer(dw_core, 1), across(dw_core), far_pair)
+
+        def combine_in(peers, srcs, quarters, dtype):
+            width_out = srcs[0].shape[1]
             return call(
-                functools.partial(combine_in_kernel, n_src=n_src, last=last), n_tiles,
-                [tiles(16), pl.BlockSpec((6 * n_experts, TOKEN_TILE), lambda i, z: (0, i))] + [pl.BlockSpec((n_experts, wide), q) for q in quarters]
-                + [resident(block, v.shape[1]) for v in srcs] + [tiles(wide)] * len(extra) + ([resident(n_experts, cols)] * len(routers) if last else []),
-                [tiles(model), resident(n_experts, model)] if last else tiles(wide),
-                [sds((n_tokens, model), BF16), sds((n_experts, model), F32)] if last else sds((n_tokens, wide), BF16),
-                cost(2 * n_tokens * n_src * block * srcs[0].shape[1], 8e6),
-                (token_cols, dl, *([wt] * len(quarters)), *srcs, *extra, *(routers if last else ())))
-
-        dx_mine = combine_in(False, (), back_in[0])
+                functools.partial(combine_in_kernel, peers=peers), n_tiles,
+                [tiles(16), pl.BlockSpec((6 * n_experts, TOKEN_TILE), lambda i, z: (0, i))] + [resident(block, width_out)] * len(peers) + [pl.BlockSpec((n_experts, wide), q) for q in quarters],
+                tiles(width_out), sds((n_tokens, width_out), dtype),
+                cost(2 * n_tokens * len(peers) * block * width_out, 8e6),
+                (token_cols, dl, *[srcs[d] for d in peers], *([wt] * len(quarters))))
+
+        dx_mine = combine_in(tuple(range(n_src)), back_in[0], [lambda i, z: (0, z[0] * n_chunk)], BF16)
         dx_other = across(dx_mine)
-        grad_in, grad_router = combine_in(True, (dx_mine, dx_other), back_in[1])
+        shared_part = combine_in(in_early, back_in[1], [lambda i, z: (0, 1), lambda i, z: (0, 3)], F32)
+        grad_in, grad_router = call(
+            functools.partial(combine_last_kernel, peers=in_late), n_tiles,
+            [tiles(16), tiles(2 * wide)] + [resident(block, 2 * wide)] * len(in_late) + [tiles(wide)] * 2 + [resident(n_experts, cols)] * len(routers),
+            [tiles(model), resident(n_experts, model)], [sds((n_tokens, model), BF16), sds((n_experts, model), F32)],
+            cost(2 * n_tokens * len(in_late) * block * 2 * wide, 12e6),
+            (token_cols, shared_part, *[back_in[1][d] for d in in_late], dx_mine, dx_other, *routers))
         return act_out, grad_in, grad_wa, grad_wb, grad_wc, grad_router.T
 
     return jax.shard_map(local_step, mesh=mesh, in_specs=(P("ep", None), P(), P("ep"), P("ep"), P("ep", None, "tp"), P("ep", None, "tp"), P("ep", "tp", None), P("ep", None)), out_specs=(P("ep", None), P("ep", None), P("ep", None, "tp"), P("ep", None, "tp"), P("ep", "tp", None), P()), check_vma=False)

time: 452 us -> 440 us (0.973)
  waiting for transfers between devices: 192 us -> 179 us
    ppermute x12, waiting for transfers between devices: 92.2 us -> 72.1 us  [across(): return lax.ppermute(val, 'tp', swap)]
    ppermute x39, waiting for transfers between devices: 99.6 us -> 107 us  [to_peer(): return lax.ppermute(val, 'ep', [(i, i ^ d) for i in range(n_src)])]
    pallas_call x17 -> x18, Pallas kernels: 174 us -> 179 us  [call(): pl.pallas_call(kernel, grid_spec=pltpu.PrefetchScalarGridSpec(num_scalar_...]
  transfers between devices with their start and end apart: 51 -> 52, of which waited for: 11 -> 13; matrix products, arithmetic and copies ran while one was open for 1% -> 1% of each run, Pallas kernels for 40% -> 43%
where the time goes in v4:
time: 440 us; the launch traced here: 439 us
  Pallas kernels  203 us (46%)
  waiting for transfers between devices  179 us (41%)
  starting transfers between devices  51.1 us (12%)
  local copies, waits for them, and re-layouts  5.21 us (1%)
    pallas_call x18, Pallas kernels, call(): pl.pallas_call(kernel, grid_spec=pltpu.PrefetchScalarGridSpec(num_scalar_...  179 us
    ppermute x39, waiting for transfers between devices, to_peer(): return lax.ppermute(val, 'ep', [(i, i ^ d) for i in range(n_src)])  107 us
    ppermute x12, waiting for transfers between devices, across(): return lax.ppermute(val, 'tp', swap)  72.1 us
    ppermute x39, starting transfers between devices, to_peer(): return lax.ppermute(val, 'ep', [(i, i ^ d) for i in range(n_src)])  36.7 us
    pallas_call x1, Pallas kernels, local_step(): pl.pallas_call(functools.partial(forward_other_kernel, n_src=n_src, n_chu...  13.9 us
    ppermute x12, starting transfers between devices, across(): return lax.ppermute(val, 'tp', swap)  13.5 us
  transfers between devices with their start and end apart: 52, of which 13 were waited for; matrix products, arithmetic and copies ran while one was open for 1% of the time, Pallas kernels for 43%

profile of v4, /device:TPU:0, one launch (start us, length us, event | category | flops | bytes accessed | tf_op | source)
XLA Modules:
  0.0 439.3 jit_solution(2098334802301335446)
XLA Ops:
  0.6 5.8 %k_slots.1 = (f32[8,2048]{1,0:T(8,128)}, bf16[512,1024]{1,0:T(8,128)(2,1)}) custom-call(s32[1]{0:T(128)} %bitcast.4.me_ref, bf16[2048,1024]{1,0:T(8,128)(2,1)} %x_ref.5, s32[1,2048]{1,0:T(1,128)} %bitcast.65, s32[1,2048]{1,0:T(1,128)} %bitcast.68), custom_call_target="tpu_custom_call" | custom-call | flops 2147483648 | bytes 4194304 | tf_op jit(solution)/shard_map/k_slots/pallas_call | solution.py:380
  6.4 4.2 collective-permute-start
  10.6 8.6 %shard_map.129 = (bf16[512,1024]{1,0:T(8,128)(2,1)}, bf16[512,1024]{1,0:T(8,128)(2,1)}) custom-call(s32[1]{0:T(128)} %bitcast.z_ref, f32[8,2048]{1,0:T(8,128)} %get-tuple-element.77.slots_ref.rows_ref, bf16[2048,1024]{1,0:T(8,128)(2,1)} %x_ref.5), custom_call_target="tpu_custom_call" | custom-call | flops 4294967296 | bytes 6291456 | tf_op jit(solution)/shard_map/pallas_call | solution.py:371
  19.2 8.6 %shard_map.128 = (bf16[512,1024]{1,0:T(8,128)(2,1)}, bf16[512,1024]{1,0:T(8,128)(2,1)}) custom-call(s32[1]{0:T(128)} %bitcast.z_ref, f32[8,2048]{1,0:T(8,128)} %get-tuple-element.77.slots_ref.rows_ref, bf16[2048,1024]{1,0:T(8,128)(2,1)} %x_ref.5), custom_call_target="tpu_custom_call" | custom-call | flops 4294967296 | bytes 6291456 | tf_op jit(solution)/shard_map/pallas_call | solution.py:371
  27.8 1.2 collective-permute-start.3
  29.4 11.5 %shard_map.127 = (bf16[512,1024]{1,0:T(8,128)(2,1)}, bf16[512,1024]{1,0:T(8,128)(2,1)}, bf16[512,1024]{1,0:T(8,128)(2,1)}) custom-call(s32[1]{0:T(128)} %bitcast.z_ref, f32[8,2048]{1,0:T(8,128)} %get-tuple-element.77.slots_ref.rows_ref, bf16[2048,1024]{1,0:T(8,128)(2,1)} %x_ref.5), custom_call_target="tpu_custom_call" | custom-call | flops 6442450944 | bytes 7340032 | tf_op jit(solution)/shard_map/pallas_call | solution.py:371
  40.9 1.5 collective-permute-start.1
  42.4 1.6 collective-permute-start.7
  44.0 13.0 %collective-permute-done.5 = bf16[512,1024]{1,0:T(8,128)(2,1)} collective-permute-done((bf16[512,1024]{1,0:T(8,128)(2,1)}, bf16[512,1024]{1,0:T(8,128)(2,1)}, u32[]{:S(2)}, u32[]{:S(2)}) %collective-permute-start.5) | collective-permute-done | bytes 1048608 | tf_op jit(solution)/shard_map/ppermute | solution.py:368
  57.0 1.6 collective-permute-start.8
  58.5 21.8 %collective-permute-done.3 = bf16[512,1024]{1,0:T(8,128)(2,1)} collective-permute-done((bf16[512,1024]{1,0:T(8,128)(2,1)}, bf16[512,1024]{1,0:T(8,128)(2,1)}, u32[]{:S(2)}, u32[]{:S(2)}) %collective-permute-start.3) | collective-permute-done | bytes 1048608 | tf_op jit(solution)/shard_map/ppermute | solution.py:368
  80.5 3.0 constant_dynamic-slice_fusion
  83.5 17.3 %collective-permute-done.1 = bf16[512,1024]{1,0:T(8,128)(2,1)} collective-permute-done((bf16[512,1024]{1,0:T(8,128)(2,1)}, bf16[512,1024]{1,0:T(8,128)(2,1)}, u32[]{:S(2)}, u32[]{:S(2)}) %collective-permute-start.1) | collective-permute-done | bytes 1048608 | tf_op jit(solution)/shard_map/ppermute | solution.py:368
  100.8 1.6 collective-permute-start.9
  102.4 4.5 %k_route.1 = (f32[16,2048]{1,0:T(8,128)}, f32[32,2048]{1,0:T(8,128)}) custom-call(bf16[2048,1024]{1,0:T(8,128)(2,1)} %x_ref.5, f32[32,1024]{1,0:T(8,128)} %bitcast.61, s32[1,2048]{1,0:T(1,128)} %bitcast.66, s32[1,2048]{1,0:T(1,128)} %bitcast.69, f32[8,2048]{1,0:T(8,128)} %get-tuple-element.77.slots_ref.rows_ref), custom_call_target="tpu_custom_call" | custom-call | flops 402653184 | bytes 4194304 | tf_op jit(solution)/shard_map/k_route/pallas_call | solution.py:387
  106.9 5.8 %shard_map.136 = (bf16[512,512]{1,0:T(8,128)(2,1)}, bf16[512,512]{1,0:T(8,128)(2,1)}) custom-call(s32[1]{0:T(128)} %bitcast.z_ref, f32[16,2048]{1,0:T(8,128)} %get-tuple-element.78.rows_ref, bf16[2048,1024]{1,0:T(8,128)(2,1)} %src_ref.13), custom_call_target="tpu_custom_call" | custom-call | flops 2147483648 | bytes 3145728 | tf_op jit(solution)/shard_map/pallas_call | solution.py:371
  112.7 1.3 collective-permute-start.23
  114.0 5.8 %shard_map.134 = (bf16[512,512]{1,0:T(8,128)(2,1)}, bf16[512,512]{1,0:T(8,128)(2,1)}) custom-call(s32[1]{0:T(128)} %bitcast.z_ref, f32[16,2048]{1,0:T(8,128)} %get-tuple-element.78.rows_ref, bf16[2048,1024]{1,0:T(8,128)(2,1)} %src_ref.13), custom_call_target="tpu_custom_call" | custom-call | flops 2147483648 | bytes 3145728 | tf_op jit(solution)/shard_map/pallas_call | solution.py:371
  119.8 11.7 %shard_map.130 = (f32[4,768,256]{2,1,0:T(8,128)}, f32[4,768,256]{2,1,0:T(8,128)}, bf16[4,768,256]{2,1,0:T(8,128)(2,1)}, bf16[4,768,512]{2,1,0:T(8,128)(2,1)}) custom-call(s32[1]{0:T(128)} %bitcast.z_ref, bf16[4,128,1024]{2,1,0:T(8,128)(2,1)} %bitcast.6.refs_0_, bf16[4,128,1024]{2,1,0:T(8,128)(2,1)} %bitcast.7.refs_1_, bf16[4,128,1024]{2,1,0:T(8,128)(2,1)} %bitcast.53, ...), custom_call_target="tpu_custom_call" | custom-call | flops 4026531840 | bytes 24576000 | tf_op jit(solution)/shard_map/pallas_call | solution.py:371
  131.5 1.6 collective-permute-start.25
  133.0 6.5 %shard_map.131 = (f32[4,256,256]{2,1,0:T(8,128)}, f32[4,256,256]{2,1,0:T(8,128)}, bf16[4,256,256]{2,1,0:T(8,128)(2,1)}, bf16[4,256,512]{2,1,0:T(8,128)(2,1)}) custom-call(s32[1]{0:T(128)} %bitcast.z_ref, bf16[4,128,1024]{2,1,0:T(8,128)(2,1)} %bitcast.12.refs_0_.refs_6_, bf16[4,128,1024]{2,1,0:T(8,128)(2,1)} %bitcast.13.refs_1_.refs_7_, ...), custom_call_target="tpu_custom_call" | custom-call | flops 1342177280 | bytes 8192000 | tf_op jit(solution)/shard_map/pallas_call | solution.py:371
  140.2 17.9 %collective-permute-done.9.refs_12_.refs_15_.refs_17_ = bf16[4,256,512]{2,1,0:T(8,128)(2,1)} collective-permute-done((bf16[4,256,512]{2,1,0:T(8,128)(2,1)}, bf16[4,256,512]{2,1,0:T(8,128)(2,1)}, u32[]{:S(2)}, u32[]{:S(2)}) %collective-permute-start.9) | collective-permute-done | bytes 1048608 | tf_op jit(solution)/shard_map/ppermute | solution.py:363
  158.1 1.6 collective-permute-start.24
  159.7 13.9 %k_fwd_other.1 = (bf16[4,128,512]{2,1,0:T(8,128)(2,1)}, bf16[4,128,512]{2,1,0:T(8,128)(2,1)}, bf16[4,128,512]{2,1,0:T(8,128)(2,1)}, bf16[4,128,512]{2,1,0:T(8,12...) custom-call(bf16[4,128,1024]{2,1,0:T(8,128)(2,1)} %bitcast.6.refs_0_, ...), custom_call_target="tpu_custom_call" | custom-call | flops 5368709120 | bytes 32000000 | tf_op jit(solution)/shard_map/k_fwd_other/pallas_call | solution.py:447
  173.6 0.9 collective-permute-start.10
  174.5 1.9 collective-permute-start.11
  176.4 9.3 %shard_map.137 = (bf16[512,1024]{1,0:T(8,128)(2,1)}, bf16[512,1024]{1,0:T(8,128)(2,1)}) custom-call(s32[1]{0:T(128)} %bitcast.z_ref, f32[16,2048]{1,0:T(8,128)} %get-tuple-element.78.rows_ref, bf16[2048,1024]{1,0:T(8,128)(2,1)} %src_ref.13), custom_call_target="tpu_custom_call" | custom-call | flops 4294967296 | bytes 6291456 | tf_op jit(solution)/shard_map/pallas_call | solution.py:371
  185.7 2.2 copy.15
  187.9 9.4 %shard_map.135 = (bf16[512,1024]{1,0:T(8,128)(2,1)}, bf16[512,1024]{1,0:T(8,128)(2,1)}) custom-call(s32[1]{0:T(128)} %bitcast.z_ref, f32[16,2048]{1,0:T(8,128)} %get-tuple-element.78.rows_ref, bf16[2048,1024]{1,0:T(8,128)(2,1)} %src_ref.13), custom_call_target="tpu_custom_call" | custom-call | flops 4294967296 | bytes 6291456 | tf_op jit(solution)/shard_map/pallas_call | solution.py:371
  197.8 1.1 collective-permute-start.13
  199.6 1.4 collective-permute-start.15
  201.7 10.1 %shard_map.132 = (f32[2048,512]{1,0:T(8,128)}, f32[2048,512]{1,0:T(8,128)}) custom-call(s32[1]{0:T(128)} %bitcast.z_ref, f32[2048,16]{1,0:T(8,128)} %bitcast.56, bf16[512,512]{1,0:T(8,128)(2,1)} %bitcast.73, bf16[512,512]{1,0:T(8,128)(2,1)} %bitcast.15.refs_1_, bf16[512,512]{1,0:T(8,128)(2,1)} %bitcast.16.refs_2_), custom_call_target="tpu_custom_call" | custom-call | flops 6442450944 | bytes 12000000 | tf_op jit(solution)/shard_map/pallas_call | solution.py:371
  211.8 2.1 collective-permute-done.12
  214.4 8.5 %collective-permute-done.14 = bf16[4,128,512]{2,1,0:T(8,128)(2,1)} collective-permute-done((bf16[4,128,512]{2,1,0:T(8,128)(2,1)}, bf16[4,128,512]{2,1,0:T(8,128)(2,1)}, u32[]{:S(2)}, u32[]{:S(2)}) %collective-permute-start.14) | collective-permute-done | bytes 524320 | tf_op jit(solution)/shard_map/ppermute | solution.py:368
  222.9 2.3 collective-permute-start.28
  225.1 7.8 %collective-permute-done.15 = bf16[4,128,512]{2,1,0:T(8,128)(2,1)} collective-permute-done((bf16[4,128,512]{2,1,0:T(8,128)(2,1)}, bf16[4,128,512]{2,1,0:T(8,128)(2,1)}, u32[]{:S(2)}, u32[]{:S(2)}) %collective-permute-start.15) | collective-permute-done | bytes 524320 | tf_op jit(solution)/shard_map/ppermute | solution.py:368
  232.9 2.1 collective-permute-start.22
  235.5 16.5 %shard_map.133 = (bf16[2048,512]{1,0:T(8,128)(2,1)}, f32[8,2048]{1,0:T(8,128)}, bf16[2048,1024]{1,0:T(8,128)(2,1)}) custom-call(s32[1]{0:T(128)} %bitcast.z_ref, f32[2048,16]{1,0:T(8,128)} %bitcast.57, bf16[2048,1024]{1,0:T(8,128)(2,1)} %src_ref.13, f32[2048,512]{1,0:T(8,128)} %get-tuple-element.92.one_ref, f32[2048,512]{1,0:T(8,128)} %get-tuple-element.93.two_ref, ...), custom_call_target="tpu_custom_call" | custom-call | flops 10737418240 | bytes 16000000 | tf_op jit(solution)/shard_map/pallas_call | solution.py:371
  252.0 1.6 collective-permute-start.17
  254.1 1.0 collective-permute-done.27
  255.6 14.9 %shard_map.139 = (bf16[4,128,256]{2,1,0:T(8,128)(2,1)}, bf16[4,128,256]{2,1,0:T(8,128)(2,1)}, bf16[4,128,256]{2,1,0:T(8,128)(2,1)}, bf16[4,128,256]{2,1,0:T(8,12...) custom-call(s32[1]{0:T(128)} %bitcast.z_ref, ...), custom_call_target="tpu_custom_call" | custom-call | flops 4294967296 | bytes 12288000 | tf_op jit(solution)/shard_map/pallas_call | solution.py:371
  270.5 1.2 collective-permute-start.42
  271.7 40.4 %collective-permute-done.19 = bf16[512,512]{1,0:T(8,128)(2,1)} collective-permute-done((bf16[512,512]{1,0:T(8,128)(2,1)}, bf16[512,512]{1,0:T(8,128)(2,1)}, u32[]{:S(2)}, u32[]{:S(2)}) %collective-permute-start.19) | collective-permute-done | bytes 524320 | tf_op jit(solution)/shard_map/ppermute | solution.py:363
  312.1 10.5 %collective-permute-done.21 = bf16[512,512]{1,0:T(8,128)(2,1)} collective-permute-done((bf16[512,512]{1,0:T(8,128)(2,1)}, bf16[512,512]{1,0:T(8,128)(2,1)}, u32[]{:S(2)}, u32[]{:S(2)}) %collective-permute-start.21) | collective-permute-done | bytes 524320 | tf_op jit(solution)/shard_map/ppermute | solution.py:363
  322.6 1.2 collective-permute-start.44
  323.9 14.9 %shard_map.138 = (bf16[4,128,256]{2,1,0:T(8,128)(2,1)}, bf16[4,128,256]{2,1,0:T(8,128)(2,1)}, bf16[4,128,256]{2,1,0:T(8,128)(2,1)}, bf16[4,128,256]{2,1,0:T(8,12...) custom-call(s32[1]{0:T(128)} %bitcast.z_ref, ...), custom_call_target="tpu_custom_call" | custom-call | flops 4294967296 | bytes 12288000 | tf_op jit(solution)/shard_map/pallas_call | solution.py:371
  338.8 0.9 collective-permute-start.41
  339.8 1.1 collective-permute-start.36
  341.7 1.6 collective-permute-start.46
  343.4 17.8 %collective-permute-done.46 = bf16[4,128,256]{2,1,0:T(8,128)(2,1)} collective-permute-done((bf16[4,128,256]{2,1,0:T(8,128)(2,1)}, bf16[4,128,256]{2,1,0:T(8,128)(2,1)}, u32[]{:S(2)}, u32[]{:S(2)}) %collective-permute-start.46) | collective-permute-done | bytes 262176 | tf_op jit(solution)/shard_map/ppermute | solution.py:368
  361.3 1.4 collective-permute-start.30
  362.6 3.2 collective-permute-done.30.refs_1_
  365.9 3.0 shard_map.140
  368.9 1.3 collective-permute-start.33
  371.0 1.3 collective-permute-start.31
  372.4 8.7 %shard_map.143.refs_3_ = bf16[2048,256]{1,0:T(8,128)(2,1)} custom-call(s32[1]{0:T(128)} %bitcast.z_ref, f32[2048,16]{1,0:T(8,128)} %bitcast.58, bf16[192,2048]{1,0:T(8,128)(2,1)} %get-tuple-element.125.dl_ref, bf16[512,256]{1,0:T(8,128)(2,1)} %bitcast.72, bf16[512,256]{1,0:T(8,128)(2,1)} %bitcast.43.refs_1_, bf16[512,256]{1,0:T(8,128)(2,1)} %bitcast.44.refs_2_, ...), custom_call_target="tpu_custom_call" | custom-call | flops 4294967296 | bytes 8000000 | tf_op jit(solution)/shard_map/pallas_call | solution.py:371
  382.1 1.5 collective-permute-start.35
  383.6 1.1 collective-permute-start.40
  384.7 1.5 collective-permute-start.48
  386.3 14.6 %shard_map.141 = (f32[4,1024,256]{2,1,0:T(8,128)}, f32[4,1024,256]{2,1,0:T(8,128)}, f32[4,256,1024]{2,1,0:T(8,128)}, f32[32,512]{1,0:T(8,128)}, bf16[2048,1024]{1,0:T(8,128)(2,1)}) custom-call(s32[1]{0:T(128)} %bitcast.z_ref, bf16[2048,1024]{1,0:T(8,128)(2,1)} %get-tuple-element.99.kept_ref, ...), custom_call_target="tpu_custom_call", output_to_operand_aliasing={{4}: (1, {})} | custom-call | flops 6442450944 | bytes 40000000 | tf_op jit(solution)/shard_map/pallas_call | solution.py:371
  400.8 17.2 %collective-permute-done.39 = bf16[4,128,512]{2,1,0:T(8,128)(2,1)} collective-permute-done((bf16[4,128,512]{2,1,0:T(8,128)(2,1)}, bf16[4,128,512]{2,1,0:T(8,128)(2,1)}, u32[]{:S(2)}, u32[]{:S(2)}) %collective-permute-start.39) | collective-permute-done | bytes 524320 | tf_op jit(solution)/shard_map/ppermute | solution.py:368
  418.0 0.9 collective-permute-start.51
  419.9 10.3 %shard_map.142.acc_ref = f32[2048,512]{1,0:T(8,128)} custom-call(s32[1]{0:T(128)} %bitcast.z_ref, f32[2048,16]{1,0:T(8,128)} %bitcast.59, bf16[192,2048]{1,0:T(8,128)(2,1)} %get-tuple-element.125.dl_ref, bf16[512,512]{1,0:T(8,128)(2,1)} %bitcast.71, bf16[512,512]{1,0:T(8,128)(2,1)} %bitcast.35.refs_1_, bf16[512,512]{1,0:T(8,128)(2,1)} %bitcast.36.refs_2_, ...), custom_call_target="tpu_custom_call" | custom-call | flops 5368709120 | bytes 8000000 | tf_op jit(solution)/shard_map/pallas_call | solution.py:371
  430.3 9.1 %shard_map.144 = (bf16[2048,1024]{1,0:T(8,128)(2,1)}, f32[32,1024]{1,0:T(8,128)}) custom-call(s32[1]{0:T(128)} %bitcast.z_ref, f32[2048,16]{1,0:T(8,128)} %bitcast.60, f32[2048,512]{1,0:T(8,128)} %shard_map.142.acc_ref, bf16[512,512]{1,0:T(8,128)(2,1)} %bitcast.39.refs_0_, bf16[512,512]{1,0:T(8,128)(2,1)} %bitcast.40.refs_1_, ...), custom_call_target="tpu_custom_call" | custom-call | flops 3221225472 | bytes 12000000 | tf_op jit(solution)/shard_map/pallas_call | solution.py:371
  (63 shorter events, 8.8 us)
Async XLA Ops:
  6.4 36.0 %collective-permute-start = (bf16[512,1024]{1,0:T(8,128)(2,1)}, bf16[512,1024]{1,0:T(8,128)(2,1)}, u32[]{:S(2)}, u32[]{:S(2)}) collective-permute-start(bf16[512,1024]{1,0:T(8,128)(2,1)} %get-tuple-element.79), channel_id=1, source_target_pairs={{0,6},{1,7},{2,4},{3,5},{4,2},{5,3},{6,0},{7,1},{8,14},{9,15},{10,... | collective-permute-start | bytes 3145736 | tf_op jit(solution)/shard_map/ppermute | solution.py:368
  19.2 37.8 %collective-permute-start.5 = (bf16[512,1024]{1,0:T(8,128)(2,1)}, bf16[512,1024]{1,0:T(8,128)(2,1)}, u32[]{:S(2)}, u32[]{:S(2)}) collective-permute-start(bf16[512,1024]{1,0:T(8,128)(2,1)} %get-tuple-element.85), channel_id=1, source_target_pairs={{0,3},{1,2},{2,1},{3,0},{4,7},{5,6},{6,5},{7,4},{8,11},{9,10},{10,... | collective-permute-start | bytes 3145736 | tf_op jit(solution)/shard_map/ppermute | solution.py:368
  27.8 52.6 %collective-permute-start.3 = (bf16[512,1024]{1,0:T(8,128)(2,1)}, bf16[512,1024]{1,0:T(8,128)(2,1)}, u32[]{:S(2)}, u32[]{:S(2)}) collective-permute-start(bf16[512,1024]{1,0:T(8,128)(2,1)} %get-tuple-element.83), channel_id=1, source_target_pairs={{0,2},{1,3},{2,0},{3,1},{4,6},{5,7},{6,4},{7,5},{8,10},{9,11},{10,... | collective-permute-start | bytes 3145736 | tf_op jit(solution)/shard_map/ppermute | solution.py:368
  28.9 51.4 %collective-permute-start.4 = (bf16[512,1024]{1,0:T(8,128)(2,1)}, bf16[512,1024]{1,0:T(8,128)(2,1)}, u32[]{:S(2)}, u32[]{:S(2)}) collective-permute-start(bf16[512,1024]{1,0:T(8,128)(2,1)} %get-tuple-element.84), channel_id=1, source_target_pairs={{0,4},{1,5},{2,6},{3,7},{4,0},{5,1},{6,2},{7,3},{8,12},{9,13},{10,... | collective-permute-start | bytes 3145736 | tf_op jit(solution)/shard_map/ppermute | solution.py:368
  40.9 59.9 %collective-permute-start.1 = (bf16[512,1024]{1,0:T(8,128)(2,1)}, bf16[512,1024]{1,0:T(8,128)(2,1)}, u32[]{:S(2)}, u32[]{:S(2)}) collective-permute-start(bf16[512,1024]{1,0:T(8,128)(2,1)} %get-tuple-element.80), channel_id=1, source_target_pairs={{0,7},{1,6},{2,5},{3,4},{4,3},{5,2},{6,1},{7,0},{8,15},{9,14},{10,... | collective-permute-start | bytes 3145736 | tf_op jit(solution)/shard_map/ppermute | solution.py:368
  42.4 115.8 %collective-permute-start.7 = (bf16[4,1024,256]{2,1,0:T(8,128)(2,1)}, bf16[4,1024,256]{2,1,0:T(8,128)(2,1)}, u32[]{:S(2)}, u32[]{:S(2)}) collective-permute-start(bf16[4,1024,256]{2,1,0:T(8,128)(2,1)} %refs_12_.3), channel_id=1, source_target_pairs={{0,8},{8,0},{1,9},{9,1},{2,10},{10,2},{3,11},{11,3},{4,12},{12,4},... | collective-permute-start | bytes 6291464 | tf_op jit(solution)/shard_map/ppermute | solution.py:363
  57.0 102.8 %collective-permute-start.8 = (bf16[4,1024,256]{2,1,0:T(8,128)(2,1)}, bf16[4,1024,256]{2,1,0:T(8,128)(2,1)}, u32[]{:S(2)}, u32[]{:S(2)}) collective-permute-start(bf16[4,1024,256]{2,1,0:T(8,128)(2,1)} %refs_13_.1), channel_id=1, source_target_pairs={{0,8},{8,0},{1,9},{9,1},{2,10},{10,2},{3,11},{11,3},{4,12},{12,4},... | collective-permute-start | bytes 6291464 | tf_op jit(solution)/shard_map/ppermute | solution.py:363
  80.4 32.3 %collective-permute-start.2 = (bf16[512,1024]{1,0:T(8,128)(2,1)}, bf16[512,1024]{1,0:T(8,128)(2,1)}, u32[]{:S(2)}, u32[]{:S(2)}) collective-permute-start(bf16[512,1024]{1,0:T(8,128)(2,1)} %get-tuple-element.82), channel_id=1, source_target_pairs={{0,1},{1,0},{2,3},{3,2},{4,5},{5,4},{6,7},{7,6},{8,9},{9,8},{10,11... | collective-permute-start | bytes 3145736 | tf_op jit(solution)/shard_map/ppermute | solution.py:368
  80.4 51.1 %collective-permute-start.6 = (bf16[512,1024]{1,0:T(8,128)(2,1)}, bf16[512,1024]{1,0:T(8,128)(2,1)}, u32[]{:S(2)}, u32[]{:S(2)}) collective-permute-start(bf16[512,1024]{1,0:T(8,128)(2,1)} %get-tuple-element.86), channel_id=1, source_target_pairs={{0,5},{1,4},{2,7},{3,6},{4,1},{5,0},{6,3},{7,2},{8,13},{9,12},{10,... | collective-permute-start | bytes 3145736 | tf_op jit(solution)/shard_map/ppermute | solution.py:368
  100.8 57.3 %collective-permute-start.9 = (bf16[4,256,512]{2,1,0:T(8,128)(2,1)}, bf16[4,256,512]{2,1,0:T(8,128)(2,1)}, u32[]{:S(2)}, u32[]{:S(2)}) collective-permute-start(bf16[4,256,512]{2,1,0:T(8,128)(2,1)} %get-tuple-element.149), channel_id=1, source_target_pairs={{0,8},{8,0},{1,9},{9,1},{2,10},{10,2},{3,11},{11,3},{4,12},{12,4},... | collective-permute-start | bytes 3145736 | tf_op jit(solution)/shard_map/ppermute | solution.py:363
  112.7 26.9 %collective-permute-start.23 = (bf16[512,512]{1,0:T(8,128)(2,1)}, bf16[512,512]{1,0:T(8,128)(2,1)}, u32[]{:S(2)}, u32[]{:S(2)}) collective-permute-start(bf16[512,512]{1,0:T(8,128)(2,1)} %get-tuple-element.105), channel_id=1, source_target_pairs={{0,2},{1,3},{2,0},{3,1},{4,6},{5,7},{6,4},{7,5},{8,10},{9,11},{10,... | collective-permute-start | bytes 1572872 | tf_op jit(solution)/shard_map/ppermute | solution.py:368
  131.5 43.1 %collective-permute-start.25 = (bf16[512,512]{1,0:T(8,128)(2,1)}, bf16[512,512]{1,0:T(8,128)(2,1)}, u32[]{:S(2)}, u32[]{:S(2)}) collective-permute-start(bf16[512,512]{1,0:T(8,128)(2,1)} %get-tuple-element.106), channel_id=1, source_target_pairs={{0,4},{1,5},{2,6},{3,7},{4,0},{5,1},{6,2},{7,3},{8,12},{9,13},{10,... | collective-permute-start | bytes 1572872 | tf_op jit(solution)/shard_map/ppermute | solution.py:368
  139.5 57.8 %collective-permute-start.18 = (bf16[512,512]{1,0:T(8,128)(2,1)}, bf16[512,512]{1,0:T(8,128)(2,1)}, u32[]{:S(2)}, u32[]{:S(2)}) collective-permute-start(bf16[512,512]{1,0:T(8,128)(2,1)} %get-tuple-element.101), channel_id=1, source_target_pairs={{0,6},{1,7},{2,4},{3,5},{4,2},{5,3},{6,0},{7,1},{8,14},{9,15},{10,... | collective-permute-start | bytes 1572872 | tf_op jit(solution)/shard_map/ppermute | solution.py:368
  158.1 39.7 %collective-permute-start.20 = (bf16[512,512]{1,0:T(8,128)(2,1)}, bf16[512,512]{1,0:T(8,128)(2,1)}, u32[]{:S(2)}, u32[]{:S(2)}) collective-permute-start(bf16[512,512]{1,0:T(8,128)(2,1)} %get-tuple-element.102), channel_id=1, source_target_pairs={{0,7},{1,6},{2,5},{3,4},{4,3},{5,2},{6,1},{7,0},{8,15},{9,14},{10,... | collective-permute-start | bytes 1572872 | tf_op jit(solution)/shard_map/ppermute | solution.py:368
  158.1 40.8 %collective-permute-start.24 = (bf16[512,512]{1,0:T(8,128)(2,1)}, bf16[512,512]{1,0:T(8,128)(2,1)}, u32[]{:S(2)}, u32[]{:S(2)}) collective-permute-start(bf16[512,512]{1,0:T(8,128)(2,1)} %collective-permute-done.23), channel_id=1, source_target_pairs={{0,8},{8,0},{1,9},{9,1},{2,10},{10,2},{3,11},{11,3},{4,12},{12,4},... | collective-permute-start | bytes 1572872 | tf_op jit(solution)/shard_map/ppermute | solution.py:363
  173.6 26.0 %collective-permute-start.10 = (bf16[4,128,512]{2,1,0:T(8,128)(2,1)}, bf16[4,128,512]{2,1,0:T(8,128)(2,1)}, u32[]{:S(2)}, u32[]{:S(2)}) collective-permute-start(bf16[4,128,512]{2,1,0:T(8,128)(2,1)} %get-tuple-element.90), channel_id=1, source_target_pairs={{0,1},{1,0},{2,3},{3,2},{4,5},{5,4},{6,7},{7,6},{8,9},{9,8},{10,11... | collective-permute-start | bytes 1572872 | tf_op jit(solution)/shard_map/ppermute | solution.py:368
  174.5 26.5 %collective-permute-start.11 = (bf16[4,128,512]{2,1,0:T(8,128)(2,1)}, bf16[4,128,512]{2,1,0:T(8,128)(2,1)}, u32[]{:S(2)}, u32[]{:S(2)}) collective-permute-start(bf16[4,128,512]{2,1,0:T(8,128)(2,1)} %get-tuple-element.91), channel_id=1, source_target_pairs={{0,6},{1,7},{2,4},{3,5},{4,2},{5,3},{6,0},{7,1},{8,14},{9,15},{10,... | collective-permute-start | bytes 1572872 | tf_op jit(solution)/shard_map/ppermute | solution.py:368
  197.3 16.6 %collective-permute-start.12 = (bf16[4,128,512]{2,1,0:T(8,128)(2,1)}, bf16[4,128,512]{2,1,0:T(8,128)(2,1)}, u32[]{:S(2)}, u32[]{:S(2)}) collective-permute-start(bf16[4,128,512]{2,1,0:T(8,128)(2,1)} %get-tuple-element.94), channel_id=1, source_target_pairs={{0,4},{1,5},{2,6},{3,7},{4,0},{5,1},{6,2},{7,3},{8,12},{9,13},{10,... | collective-permute-start | bytes 1572872 | tf_op jit(solution)/shard_map/ppermute | solution.py:368
  197.8 16.5 %collective-permute-start.13 = (bf16[4,128,512]{2,1,0:T(8,128)(2,1)}, bf16[4,128,512]{2,1,0:T(8,128)(2,1)}, u32[]{:S(2)}, u32[]{:S(2)}) collective-permute-start(bf16[4,128,512]{2,1,0:T(8,128)(2,1)} %get-tuple-element.95), channel_id=1, source_target_pairs={{0,2},{1,3},{2,0},{3,1},{4,6},{5,7},{6,4},{7,5},{8,10},{9,11},{10,... | collective-permute-start | bytes 1572872 | tf_op jit(solution)/shard_map/ppermute | solution.py:368
  198.9 23.9 %collective-permute-start.14 = (bf16[4,128,512]{2,1,0:T(8,128)(2,1)}, bf16[4,128,512]{2,1,0:T(8,128)(2,1)}, u32[]{:S(2)}, u32[]{:S(2)}) collective-permute-start(bf16[4,128,512]{2,1,0:T(8,128)(2,1)} %get-tuple-element.96), channel_id=1, source_target_pairs={{0,7},{1,6},{2,5},{3,4},{4,3},{5,2},{6,1},{7,0},{8,15},{9,14},{10,... | collective-permute-start | bytes 1572872 | tf_op jit(solution)/shard_map/ppermute | solution.py:368
  199.6 33.3 %collective-permute-start.15 = (bf16[4,128,512]{2,1,0:T(8,128)(2,1)}, bf16[4,128,512]{2,1,0:T(8,128)(2,1)}, u32[]{:S(2)}, u32[]{:S(2)}) collective-permute-start(bf16[4,128,512]{2,1,0:T(8,128)(2,1)} %get-tuple-element.97), channel_id=1, source_target_pairs={{0,5},{1,4},{2,7},{3,6},{4,1},{5,0},{6,3},{7,2},{8,13},{9,12},{10,... | collective-permute-start | bytes 1572872 | tf_op jit(solution)/shard_map/ppermute | solution.py:368
  201.0 34.0 %collective-permute-start.16 = (bf16[4,128,512]{2,1,0:T(8,128)(2,1)}, bf16[4,128,512]{2,1,0:T(8,128)(2,1)}, u32[]{:S(2)}, u32[]{:S(2)}) collective-permute-start(bf16[4,128,512]{2,1,0:T(8,128)(2,1)} %get-tuple-element.98), channel_id=1, source_target_pairs={{0,3},{1,2},{2,1},{3,0},{4,7},{5,6},{6,5},{7,4},{8,11},{9,10},{10,... | collective-permute-start | bytes 1572872 | tf_op jit(solution)/shard_map/ppermute | solution.py:368
  213.9 39.7 %collective-permute-start.29 = (bf16[4,256,512]{2,1,0:T(8,128)(2,1)}, bf16[4,256,512]{2,1,0:T(8,128)(2,1)}, u32[]{:S(2)}, u32[]{:S(2)}) collective-permute-start(bf16[4,256,512]{2,1,0:T(8,128)(2,1)} %get-tuple-element.148), channel_id=1, source_target_pairs={{0,8},{8,0},{1,9},{9,1},{2,10},{10,2},{3,11},{11,3},{4,12},{12,4},... | collective-permute-start | bytes 3145736 | tf_op jit(solution)/shard_map/ppermute | solution.py:363
  214.4 40.7 %collective-permute-start.27 = (bf16[512,1024]{1,0:T(8,128)(2,1)}, bf16[512,1024]{1,0:T(8,128)(2,1)}, u32[]{:S(2)}, u32[]{:S(2)}) collective-permute-start(bf16[512,1024]{1,0:T(8,128)(2,1)} %get-tuple-element.107), channel_id=1, source_target_pairs={{0,3},{1,2},{2,1},{3,0},{4,7},{5,6},{6,5},{7,4},{8,11},{9,10},{10,... | collective-permute-start | bytes 3145736 | tf_op jit(solution)/shard_map/ppermute | solution.py:368
  222.9 32.7 %collective-permute-start.28 = (bf16[512,1024]{1,0:T(8,128)(2,1)}, bf16[512,1024]{1,0:T(8,128)(2,1)}, u32[]{:S(2)}, u32[]{:S(2)}) collective-permute-start(bf16[512,1024]{1,0:T(8,128)(2,1)} %get-tuple-element.108), channel_id=1, source_target_pairs={{0,5},{1,4},{2,7},{3,6},{4,1},{5,0},{6,3},{7,2},{8,13},{9,12},{10,... | collective-permute-start | bytes 3145736 | tf_op jit(solution)/shard_map/ppermute | solution.py:368
  232.9 91.0 %collective-permute-start.22 = (bf16[512,1024]{1,0:T(8,128)(2,1)}, bf16[512,1024]{1,0:T(8,128)(2,1)}, u32[]{:S(2)}, u32[]{:S(2)}) collective-permute-start(bf16[512,1024]{1,0:T(8,128)(2,1)} %get-tuple-element.104), channel_id=1, source_target_pairs={{0,1},{1,0},{2,3},{3,2},{4,5},{5,4},{6,7},{7,6},{8,9},{9,8},{10,11... | collective-permute-start | bytes 3145736 | tf_op jit(solution)/shard_map/ppermute | solution.py:368
  235.0 17.0 %collective-permute-start.26 = (bf16[512,512]{1,0:T(8,128)(2,1)}, bf16[512,512]{1,0:T(8,128)(2,1)}, u32[]{:S(2)}, u32[]{:S(2)}) collective-permute-start(bf16[512,512]{1,0:T(8,128)(2,1)} %collective-permute-done.25), channel_id=1, source_target_pairs={{0,8},{8,0},{1,9},{9,1},{2,10},{10,2},{3,11},{11,3},{4,12},{12,4},... | collective-permute-start | bytes 1572872 | tf_op jit(solution)/shard_map/ppermute | solution.py:363
  252.0 132.7 %collective-permute-start.17 = (bf16[2048,512]{1,0:T(8,128)(2,1)}, bf16[2048,512]{1,0:T(8,128)(2,1)}, u32[]{:S(2)}, u32[]{:S(2)}) collective-permute-start(bf16[2048,512]{1,0:T(8,128)(2,1)} %get-tuple-element.100), channel_id=1, source_target_pairs={{0,8},{8,0},{1,9},{9,1},{2,10},{10,2},{3,11},{11,3},{4,12},{12,4},... | collective-permute-start | bytes 6291464 | tf_op jit(solution)/shard_map/ppermute | solution.py:363
  253.6 58.5 %collective-permute-start.19 = (bf16[512,512]{1,0:T(8,128)(2,1)}, bf16[512,512]{1,0:T(8,128)(2,1)}, u32[]{:S(2)}, u32[]{:S(2)}) collective-permute-start(bf16[512,512]{1,0:T(8,128)(2,1)} %collective-permute-done.18), channel_id=1, source_target_pairs={{0,8},{8,0},{1,9},{9,1},{2,10},{10,2},{3,11},{11,3},{4,12},{12,4},... | collective-permute-start | bytes 1572872 | tf_op jit(solution)/shard_map/ppermute | solution.py:363
  255.1 67.5 %collective-permute-start.21 = (bf16[512,512]{1,0:T(8,128)(2,1)}, bf16[512,512]{1,0:T(8,128)(2,1)}, u32[]{:S(2)}, u32[]{:S(2)}) collective-permute-start(bf16[512,512]{1,0:T(8,128)(2,1)} %collective-permute-done.20), channel_id=1, source_target_pairs={{0,8},{8,0},{1,9},{9,1},{2,10},{10,2},{3,11},{11,3},{4,12},{12,4},... | collective-permute-start | bytes 1572872 | tf_op jit(solution)/shard_map/ppermute | solution.py:363
  270.5 68.3 %collective-permute-start.42 = (bf16[4,128,256]{2,1,0:T(8,128)(2,1)}, bf16[4,128,256]{2,1,0:T(8,128)(2,1)}, u32[]{:S(2)}, u32[]{:S(2)}) collective-permute-start(bf16[4,128,256]{2,1,0:T(8,128)(2,1)} %get-tuple-element.136), channel_id=1, source_target_pairs={{0,2},{1,3},{2,0},{3,1},{4,6},{5,7},{6,4},{7,5},{8,10},{9,11},{10,... | collective-permute-start | bytes 786440 | tf_op jit(solution)/shard_map/ppermute | solution.py:368
  312.1 27.7 %collective-permute-start.43 = (bf16[4,128,256]{2,1,0:T(8,128)(2,1)}, bf16[4,128,256]{2,1,0:T(8,128)(2,1)}, u32[]{:S(2)}, u32[]{:S(2)}) collective-permute-start(bf16[4,128,256]{2,1,0:T(8,128)(2,1)} %get-tuple-element.137), channel_id=1, source_target_pairs={{0,3},{1,2},{2,1},{3,0},{4,7},{5,6},{6,5},{7,4},{8,11},{9,10},{10,... | collective-permute-start | bytes 786440 | tf_op jit(solution)/shard_map/ppermute | solution.py:368
  322.6 18.3 %collective-permute-start.44 = (bf16[4,128,256]{2,1,0:T(8,128)(2,1)}, bf16[4,128,256]{2,1,0:T(8,128)(2,1)}, u32[]{:S(2)}, u32[]{:S(2)}) collective-permute-start(bf16[4,128,256]{2,1,0:T(8,128)(2,1)} %get-tuple-element.138), channel_id=1, source_target_pairs={{0,4},{1,5},{2,6},{3,7},{4,0},{5,1},{6,2},{7,3},{8,12},{9,13},{10,... | collective-permute-start | bytes 786440 | tf_op jit(solution)/shard_map/ppermute | solution.py:368
  323.9 17.8 %collective-permute-start.45 = (bf16[4,128,256]{2,1,0:T(8,128)(2,1)}, bf16[4,128,256]{2,1,0:T(8,128)(2,1)}, u32[]{:S(2)}, u32[]{:S(2)}) collective-permute-start(bf16[4,128,256]{2,1,0:T(8,128)(2,1)} %get-tuple-element.139), channel_id=1, source_target_pairs={{0,5},{1,4},{2,7},{3,6},{4,1},{5,0},{6,3},{7,2},{8,13},{9,12},{10,... | collective-permute-start | bytes 786440 | tf_op jit(solution)/shard_map/ppermute | solution.py:368
  338.8 4.4 %collective-permute-start.41 = (bf16[4,128,256]{2,1,0:T(8,128)(2,1)}, bf16[4,128,256]{2,1,0:T(8,128)(2,1)}, u32[]{:S(2)}, u32[]{:S(2)}) collective-permute-start(bf16[4,128,256]{2,1,0:T(8,128)(2,1)} %get-tuple-element.135), channel_id=1, source_target_pairs={{0,1},{1,0},{2,3},{3,2},{4,5},{5,4},{6,7},{7,6},{8,9},{9,8},{10,11... | collective-permute-start | bytes 786440 | tf_op jit(solution)/shard_map/ppermute | solution.py:368
  339.8 30.5 %collective-permute-start.36 = (bf16[4,128,512]{2,1,0:T(8,128)(2,1)}, bf16[4,128,512]{2,1,0:T(8,128)(2,1)}, u32[]{:S(2)}, u32[]{:S(2)}) collective-permute-start(bf16[4,128,512]{2,1,0:T(8,128)(2,1)} %get-tuple-element.129), channel_id=1, source_target_pairs={{0,2},{1,3},{2,0},{3,1},{4,6},{5,7},{6,4},{7,5},{8,10},{9,11},{10,... | collective-permute-start | bytes 1572872 | tf_op jit(solution)/shard_map/ppermute | solution.py:368
  340.9 30.1 %collective-permute-start.37 = (bf16[4,128,512]{2,1,0:T(8,128)(2,1)}, bf16[4,128,512]{2,1,0:T(8,128)(2,1)}, u32[]{:S(2)}, u32[]{:S(2)}) collective-permute-start(bf16[4,128,512]{2,1,0:T(8,128)(2,1)} %get-tuple-element.130), channel_id=1, source_target_pairs={{0,4},{1,5},{2,6},{3,7},{4,0},{5,1},{6,2},{7,3},{8,12},{9,13},{10,... | collective-permute-start | bytes 1572872 | tf_op jit(solution)/shard_map/ppermute | solution.py:368
  341.7 19.6 %collective-permute-start.46 = (bf16[4,128,256]{2,1,0:T(8,128)(2,1)}, bf16[4,128,256]{2,1,0:T(8,128)(2,1)}, u32[]{:S(2)}, u32[]{:S(2)}) collective-permute-start(bf16[4,128,256]{2,1,0:T(8,128)(2,1)} %get-tuple-element.140), channel_id=1, source_target_pairs={{0,6},{1,7},{2,4},{3,5},{4,2},{5,3},{6,0},{7,1},{8,14},{9,15},{10,... | collective-permute-start | bytes 786440 | tf_op jit(solution)/shard_map/ppermute | solution.py:368
  343.3 25.6 %collective-permute-start.47 = (bf16[4,128,256]{2,1,0:T(8,128)(2,1)}, bf16[4,128,256]{2,1,0:T(8,128)(2,1)}, u32[]{:S(2)}, u32[]{:S(2)}) collective-permute-start(bf16[4,128,256]{2,1,0:T(8,128)(2,1)} %get-tuple-element.141), channel_id=1, source_target_pairs={{0,7},{1,6},{2,5},{3,4},{4,3},{5,2},{6,1},{7,0},{8,15},{9,14},{10,... | collective-permute-start | bytes 786440 | tf_op jit(solution)/shard_map/ppermute | solution.py:368
  361.3 4.6 %collective-permute-start.30 = (f32[8,2048]{1,0:T(8,128)}, f32[8,2048]{1,0:T(8,128)}, u32[]{:S(2)}, u32[]{:S(2)}) collective-permute-start(f32[8,2048]{1,0:T(8,128)} %get-tuple-element.122.refs_0_), channel_id=1, source_target_pairs={{0,8},{8,0},{1,9},{9,1},{2,10},{10,2},{3,11},{11,3},{4,12},{12,4},... | collective-permute-start | bytes 196616 | tf_op jit(solution)/shard_map/ppermute | solution.py:363
  365.9 15.3 %collective-permute-start.38 = (bf16[4,128,512]{2,1,0:T(8,128)(2,1)}, bf16[4,128,512]{2,1,0:T(8,128)(2,1)}, u32[]{:S(2)}, u32[]{:S(2)}) collective-permute-start(bf16[4,128,512]{2,1,0:T(8,128)(2,1)} %get-tuple-element.131), channel_id=1, source_target_pairs={{0,3},{1,2},{2,1},{3,0},{4,7},{5,6},{6,5},{7,4},{8,11},{9,10},{10,... | collective-permute-start | bytes 1572872 | tf_op jit(solution)/shard_map/ppermute | solution.py:368
  368.9 13.1 %collective-permute-start.33 = (f32[32,512]{1,0:T(8,128)}, f32[32,512]{1,0:T(8,128)}, u32[]{:S(2)}, u32[]{:S(2)}) collective-permute-start(f32[32,512]{1,0:T(8,128)} %get-tuple-element.123.refs_26_), channel_id=1, source_target_pairs={{0,6},{1,7},{2,4},{3,5},{4,2},{5,3},{6,0},{7,1},{8,14},{9,15},{10,... | collective-permute-start | bytes 196616 | tf_op jit(solution)/shard_map/ppermute | solution.py:368
  370.2 11.8 %collective-permute-start.32 = (f32[32,512]{1,0:T(8,128)}, f32[32,512]{1,0:T(8,128)}, u32[]{:S(2)}, u32[]{:S(2)}) collective-permute-start(f32[32,512]{1,0:T(8,128)} %get-tuple-element.123.refs_26_), channel_id=1, source_target_pairs={{0,4},{1,5},{2,6},{3,7},{4,0},{5,1},{6,2},{7,3},{8,12},{9,13},{10,... | collective-permute-start | bytes 196616 | tf_op jit(solution)/shard_map/ppermute | solution.py:368
  371.0 12.5 %collective-permute-start.31 = (f32[32,512]{1,0:T(8,128)}, f32[32,512]{1,0:T(8,128)}, u32[]{:S(2)}, u32[]{:S(2)}) collective-permute-start(f32[32,512]{1,0:T(8,128)} %get-tuple-element.123.refs_26_), channel_id=1, source_target_pairs={{0,2},{1,3},{2,0},{3,1},{4,6},{5,7},{6,4},{7,5},{8,10},{9,11},{10,... | collective-permute-start | bytes 196616 | tf_op jit(solution)/shard_map/ppermute | solution.py:368
  381.1 36.9 %collective-permute-start.39 = (bf16[4,128,512]{2,1,0:T(8,128)(2,1)}, bf16[4,128,512]{2,1,0:T(8,128)(2,1)}, u32[]{:S(2)}, u32[]{:S(2)}) collective-permute-start(bf16[4,128,512]{2,1,0:T(8,128)(2,1)} %get-tuple-element.132), channel_id=1, source_target_pairs={{0,5},{1,4},{2,7},{3,6},{4,1},{5,0},{6,3},{7,2},{8,13},{9,12},{10,... | collective-permute-start | bytes 1572872 | tf_op jit(solution)/shard_map/ppermute | solution.py:368
  381.9 37.0 %collective-permute-start.34 = (bf16[4,128,512]{2,1,0:T(8,128)(2,1)}, bf16[4,128,512]{2,1,0:T(8,128)(2,1)}, u32[]{:S(2)}, u32[]{:S(2)}) collective-permute-start(bf16[4,128,512]{2,1,0:T(8,128)(2,1)} %get-tuple-element.127), channel_id=1, source_target_pairs={{0,1},{1,0},{2,3},{3,2},{4,5},{5,4},{6,7},{7,6},{8,9},{9,8},{10,11... | collective-permute-start | bytes 1572872 | tf_op jit(solution)/shard_map/ppermute | solution.py:368
  382.1 37.7 %collective-permute-start.35 = (bf16[4,128,512]{2,1,0:T(8,128)(2,1)}, bf16[4,128,512]{2,1,0:T(8,128)(2,1)}, u32[]{:S(2)}, u32[]{:S(2)}) collective-permute-start(bf16[4,128,512]{2,1,0:T(8,128)(2,1)} %get-tuple-element.128), channel_id=1, source_target_pairs={{0,6},{1,7},{2,4},{3,5},{4,2},{5,3},{6,0},{7,1},{8,14},{9,15},{10,... | collective-permute-start | bytes 1572872 | tf_op jit(solution)/shard_map/ppermute | solution.py:368
  383.6 46.6 %collective-permute-start.40 = (bf16[4,128,512]{2,1,0:T(8,128)(2,1)}, bf16[4,128,512]{2,1,0:T(8,128)(2,1)}, u32[]{:S(2)}, u32[]{:S(2)}) collective-permute-start(bf16[4,128,512]{2,1,0:T(8,128)(2,1)} %get-tuple-element.133), channel_id=1, source_target_pairs={{0,7},{1,6},{2,5},{3,4},{4,3},{5,2},{6,1},{7,0},{8,15},{9,14},{10,... | collective-permute-start | bytes 1572872 | tf_op jit(solution)/shard_map/ppermute | solution.py:368
  384.7 45.5 %collective-permute-start.48 = (bf16[2048,256]{1,0:T(8,128)(2,1)}, bf16[2048,256]{1,0:T(8,128)(2,1)}, u32[]{:S(2)}, u32[]{:S(2)}) collective-permute-start(bf16[2048,256]{1,0:T(8,128)(2,1)} %shard_map.143.refs_3_), channel_id=1, source_target_pairs={{0,8},{8,0},{1,9},{9,1},{2,10},{10,2},{3,11},{11,3},{4,12},{12,4},... | collective-permute-start | bytes 3145736 | tf_op jit(solution)/shard_map/ppermute | solution.py:363
  418.0 12.2 %collective-permute-start.51 = (f32[32,512]{1,0:T(8,128)}, f32[32,512]{1,0:T(8,128)}, u32[]{:S(2)}, u32[]{:S(2)}) collective-permute-start(f32[32,512]{1,0:T(8,128)} %get-tuple-element.142.refs_5_), channel_id=1, source_target_pairs={{0,9},{1,8},{2,11},{3,10},{4,13},{5,12},{6,15},{7,14},{8,1},{9,0},... | collective-permute-start | bytes 196616 | tf_op jit(solution)/shard_map/ppermute | solution.py:537
  419.0 11.3 %collective-permute-start.50 = (f32[32,512]{1,0:T(8,128)}, f32[32,512]{1,0:T(8,128)}, u32[]{:S(2)}, u32[]{:S(2)}) collective-permute-start(f32[32,512]{1,0:T(8,128)} %get-tuple-element.142.refs_5_), channel_id=1, source_target_pairs={{0,8},{8,0},{1,9},{9,1},{2,10},{10,2},{3,11},{11,3},{4,12},{12,4},... | collective-permute-start | bytes 196616 | tf_op jit(solution)/shard_map/ppermute | solution.py:363
  419.8 10.5 %collective-permute-start.49 = (f32[32,512]{1,0:T(8,128)}, f32[32,512]{1,0:T(8,128)}, u32[]{:S(2)}, u32[]{:S(2)}) collective-permute-start(f32[32,512]{1,0:T(8,128)} %get-tuple-element.142.refs_5_), channel_id=1, source_target_pairs={{0,1},{1,0},{2,3},{3,2},{4,5},{5,4},{6,7},{7,6},{8,9},{9,8},{10,11... | collective-permute-start | bytes 196616 | tf_op jit(solution)/shard_map/ppermute | solution.py:368

commit v5 on v4

--- a/solution.py
+++ b/solution.py
@@ -15,8 +15,9 @@
 TN = (((0,), (0,)), ((), ()))
 TILE = 256
 GATHER_TILE = 256
-GROUP = 2
+GROUP = 4
 TOKEN_TILE = 512
+IN_TILE = 1024
 LANES = 128
 
 
@@ -207,11 +208,10 @@
                 outs[c * n_src + first + i][0] = total[i * cap:(i + 1) * cap]
 
 
-def weight_grad_kernel(z_ref, kept_ref, piece_ref, *refs, n_src, widths):
+def weight_grad_kernel(z_ref, *refs, n_src, widths):
     xs = refs[:n_src]
     dos, refs = group_refs(refs[n_src:], widths)
-    h_ref, h2_ref, da_ref, da2_ref, db_ref, db2_ref, d0, d2, d4, d6, ga_ref, gb_ref, gc_ref, dw_ref, out_ref, do_ref = refs
-    out_ref[...] = piece_ref[...]
+    h_ref, h2_ref, da_ref, da2_ref, db_ref, db2_ref, d0, d2, d4, d6, ga_ref, gb_ref, gc_ref, dw_ref, do_ref = refs
     dw_ref[...] = (d0[...] + d2[...]) + (d4[...] + d6[...])
     cap = xs[0].shape[1]
     for i, ref in enumerate(dos):
@@ -225,13 +225,13 @@
 
 
 def slot_picks(cols_ref):
-    lane = lax.broadcasted_iota(jnp.int32, (TOKEN_TILE, 128), 1).astype(F32)
+    lane = lax.broadcasted_iota(jnp.int32, (cols_ref.shape[0], 128), 1).astype(F32)
     picks = []
     for k in range(2):
         slot = cols_ref[:, k:k + 1]
         blk = jnp.floor(slot * (1.0 / 128.0))
         hot = jnp.where(slot - 128.0 * blk == lane, 1.0, 0.0).astype(BF16)
-        picks.append((jnp.broadcast_to(blk, (TOKEN_TILE, 128)).astype(BF16), hot))
+        picks.append((jnp.broadcast_to(blk, (cols_ref.shape[0], 128)).astype(BF16), hot))
     return picks
 
 
@@ -289,7 +289,7 @@
 
 def add_token_rows(total, cols_ref, srcs, peers):
     (blk_one, hot_one), (blk_two, hot_two) = slot_picks(cols_ref)
-    zero = jnp.zeros((TOKEN_TILE, LANES), BF16)
+    zero = jnp.zeros_like(hot_one)
     blocks = srcs[0].shape[0] // LANES
     for d, src in zip(peers, srcs):
         parts = []
@@ -306,6 +306,11 @@
     weights = jnp.concatenate([high, mid, high, low, high, mid], axis=0)
     back = lax.dot_general(dl_ref[...], weights, TN, preferred_element_type=F32)
     out_ref[...] = add_token_rows(back, cols_ref, srcs, peers).astype(out_ref.dtype)
+
+
+def combine_place_kernel(z_ref, kept_ref, piece_ref, *refs, peers):
+    refs[-1][...] = piece_ref[...]
+    combine_in_kernel(z_ref, *refs[:-1], peers=peers)
 
 
 def combine_last_kernel(z_ref, cols_ref, acc_ref, *refs, peers):
@@ -525,34 +530,42 @@
             (rows, prob, id_one, id_two, x_rows, dg_mine, dg_other))
 
         all_dos = [v for d in src_order for v in dos[d]]
-        assert n_tokens // TOKEN_TILE == own
-        grad_wa, grad_wb, grad_wc, dw_core, act_out = call(
+        grad_wa, grad_wb, grad_wc, dw_core = call(
             functools.partial(weight_grad_kernel, n_src=n_src, widths=[len(dos[d]) for d in src_order]), (own,),
-            [pl.BlockSpec(memory_space=pl.ANY), tiles(cols)] + [whole(slot_cap, model)] * n_src + [whole(slot_cap, v.shape[2]) for v in all_dos] + [whole(r, width) for r in part_rows] + [whole(rows_early, width), whole(rows_late, width)] * 2 + [resident(n_experts, cols)] * 4,
-            [whole(model, width), whole(model, width), whole(width, model), resident(n_experts, cols), pl.BlockSpec((TOKEN_TILE, cols), lambda e, z: (e, 1 - z[0]))],
-            [sds((own, model, width), F32)] * 2 + [sds((own, width, model), F32), sds((n_experts, cols), F32), sds((n_tokens, model), BF16)],
+            [whole(slot_cap, model)] * n_src + [whole(slot_cap, v.shape[2]) for v in all_dos] + [whole(r, width) for r in part_rows] + [whole(rows_early, width), whole(rows_late, width)] * 2 + [resident(n_experts, cols)] * 4,
+            [whole(model, width), whole(model, width), whole(width, model), resident(n_experts, cols)],
+            [sds((own, model, width), F32)] * 2 + [sds((own, width, model), F32), sds((n_experts, cols), F32)],
             cost(6 * own * rows_all * width * model, 40e6),
-            (act_out, y_other, *xs, *all_dos, own_parts[0][2], own_parts[1][2], bwd_a[-2], bwd_b[-2], bwd_a[-1], bwd_b[-1], dw, to_peer(dw, 2), to_peer(dw, 4), to_peer(dw, 6)),
-            [pltpu.VMEM((rows_all, model), BF16)], {1: 4})
+            (*xs, *all_dos, own_parts[0][2], own_parts[1][2], bwd_a[-2], bwd_b[-2], bwd_a[-1], bwd_b[-1], dw, to_peer(dw, 2), to_peer(dw, 4), to_peer(dw, 6)),
+            [pltpu.VMEM((rows_all, model), BF16)])
         far_pair = lax.ppermute(dw_core, ("tp", "ep"), [(i, i ^ (n_src + 1)) for i in range(tp_size * n_src)])
         routers = (dw_core, to_peer(dw_core, 1), across(dw_core), far_pair)
 
-        def combine_in(peers, srcs, quarters, dtype):
+        def in_tiles(b):
+            return pl.BlockSpec((IN_TILE, b), lambda i, z: (i, 0))
+
+        def combine_in(peers, srcs, quarters, dtype, place=None):
             width_out = srcs[0].shape[1]
+            in_specs = [in_tiles(16), pl.BlockSpec((6 * n_experts, IN_TILE), lambda i, z: (0, i))] + [resident(block, width_out)] * len(peers) + [pl.BlockSpec((n_experts, wide), q) for q in quarters]
+            out_spec, out_shape = in_tiles(width_out), sds((n_tokens, width_out), dtype)
+            estimate = cost(2 * n_tokens * len(peers) * block * width_out, 8e6)
+            args = (token_cols, dl, *[srcs[d] for d in peers], *([wt] * len(quarters)))
+            grid = (n_tokens // IN_TILE,)
+            if place is None:
+                return call(functools.partial(combine_in_kernel, peers=peers), grid, in_specs, out_spec, out_shape, estimate, args)
+            kept, piece = place
+            far_half = pl.BlockSpec((IN_TILE, cols), lambda i, z: (i, 1 - z[0]))
             return call(
-                functools.partial(combine_in_kernel, peers=peers), n_tiles,
-                [tiles(16), pl.BlockSpec((6 * n_experts, TOKEN_TILE), lambda i, z: (0, i))] + [resident(block, width_out)] * len(peers) + [pl.BlockSpec((n_experts, wide), q) for q in quarters],
-                tiles(width_out), sds((n_tokens, width_out), dtype),
-                cost(2 * n_tokens * len(peers) * block * width_out, 8e6),
-                (token_cols, dl, *[srcs[d] for d in peers], *([wt] * len(quarters))))
+                functools.partial(combine_place_kernel, peers=peers), grid, [pl.BlockSpec(memory_space=pl.ANY), in_tiles(cols)] + in_specs,
+                [out_spec, far_half], [out_shape, sds(kept.shape, BF16)], estimate, (kept, piece, *args), aliases={1: 1})
 
         dx_mine = combine_in(tuple(range(n_src)), back_in[0], [lambda i, z: (0, z[0] * n_chunk)], BF16)
         dx_other = across(dx_mine)
-        shared_part = combine_in(in_early, back_in[1], [lambda i, z: (0, 1), lambda i, z: (0, 3)], F32)
+        shared_part, act_out = combine_in(in_early, back_in[1], [lambda i, z: (0, 1), lambda i, z: (0, 3)], F32, (act_out, y_other))
         grad_in, grad_router = call(
-            functools.partial(combine_last_kernel, peers=in_late), n_tiles,
-            [tiles(16), tiles(2 * wide)] + [resident(block, 2 * wide)] * len(in_late) + [tiles(wide)] * 2 + [resident(n_experts, cols)] * len(routers),
-            [tiles(model), resident(n_experts, model)], [sds((n_tokens, model), BF16), sds((n_experts, model), F32)],
+            functools.partial(combine_last_kernel, peers=in_late), (n_tokens // IN_TILE,),
+            [in_tiles(16), in_tiles(2 * wide)] + [resident(block, 2 * wide)] * len(in_late) + [in_tiles(wide)] * 2 + [resident(n_experts, cols)] * len(routers),
+            [in_tiles(model), resident(n_experts, model)], [sds((n_tokens, model), BF16), sds((n_experts, model), F32)],
             cost(2 * n_tokens * len(in_late) * block * 2 * wide, 12e6),
             (token_cols, shared_part, *[back_in[1][d] for d in in_late], dx_mine, dx_other, *routers))
         return act_out, grad_in, grad_wa, grad_wb, grad_wc, grad_router.T

time: 440 us -> 422 us (0.959)
  waiting for transfers between devices: 179 us -> 156 us
  starting transfers between devices: 51.1 us -> 58.1 us
    ppermute x12, waiting for transfers between devices: 72.1 us -> 55 us  [across(): return lax.ppermute(val, 'tp', swap)]
    ppermute x1, starting transfers between devices: 0.94 us -> 8.82 us  [local_step(): lax.ppermute(dw_core, ('tp', 'ep'), [(i, i ^ n_src + 1) for i in range(tp...]
    ppermute x39, waiting for transfers between devices: 107 us -> 101 us  [to_peer(): return lax.ppermute(val, 'ep', [(i, i ^ d) for i in range(n_src)])]
  transfers between devices with their start and end apart: 52 -> 52, of which waited for: 13 -> 15; matrix products, arithmetic and copies ran while one was open for 1% -> 1% of each run, Pallas kernels for 43% -> 42%
where the time goes in v5:
time: 422 us
  Pallas kernels  202 us (48%)
  waiting for transfers between devices  156 us (37%)
  starting transfers between devices  58.1 us (14%)
  local copies, waits for them, and re-layouts  5.23 us (1%)
    pallas_call x18, Pallas kernels, call(): pl.pallas_call(kernel, grid_spec=pltpu.PrefetchScalarGridSpec(num_scalar_...  177 us
    ppermute x39, waiting for transfers between devices, to_peer(): return lax.ppermute(val, 'ep', [(i, i ^ d) for i in range(n_src)])  101 us
    ppermute x12, waiting for transfers between devices, across(): return lax.ppermute(val, 'tp', swap)  55 us
    ppermute x39, starting transfers between devices, to_peer(): return lax.ppermute(val, 'ep', [(i, i ^ d) for i in range(n_src)])  35.7 us
    pallas_call x1, Pallas kernels, local_step(): pl.pallas_call(functools.partial(forward_other_kernel, n_src=n_src, n_chu...  14.3 us
    ppermute x12, starting transfers between devices, across(): return lax.ppermute(val, 'tp', swap)  13.6 us
    ppermute x1, starting transfers between devices, local_step(): lax.ppermute(dw_core, ('tp', 'ep'), [(i, i ^ n_src + 1) for i in range(tp...  8.82 us
  transfers between devices with their start and end apart: 52, of which 15 were waited for; matrix products, arithmetic and copies ran while one was open for 1% of the time, Pallas kernels for 42%

profile of v5, /device:TPU:0, one launch (start us, length us, event | category | flops | bytes accessed | tf_op | source)
XLA Modules:
  0.0 421.6 jit_solution(11411307945194179127)
XLA Ops:
  0.6 5.8 %k_slots.1 = (f32[8,2048]{1,0:T(8,128)}, bf16[512,1024]{1,0:T(8,128)(2,1)}) custom-call(s32[1]{0:T(128)} %bitcast.4.me_ref, bf16[2048,1024]{1,0:T(8,128)(2,1)} %x_ref.5, s32[1,2048]{1,0:T(1,128)} %bitcast.62, s32[1,2048]{1,0:T(1,128)} %bitcast.65), custom_call_target="tpu_custom_call" | custom-call | flops 2147483648 | bytes 4194304 | tf_op jit(solution)/shard_map/k_slots/pallas_call | solution.py:385
  6.4 11.5 %shard_map.127 = (bf16[512,1024]{1,0:T(8,128)(2,1)}, bf16[512,1024]{1,0:T(8,128)(2,1)}, bf16[512,1024]{1,0:T(8,128)(2,1)}) custom-call(s32[1]{0:T(128)} %bitcast.z_ref, f32[8,2048]{1,0:T(8,128)} %get-tuple-element.78.slots_ref.rows_ref, bf16[2048,1024]{1,0:T(8,128)(2,1)} %x_ref.5), custom_call_target="tpu_custom_call" | custom-call | flops 6442450944 | bytes 7340032 | tf_op jit(solution)/shard_map/pallas_call | solution.py:376
  18.0 3.6 collective-permute-start.1
  21.5 0.7 collective-permute-start.2
  22.2 4.5 %k_route.1 = (f32[16,2048]{1,0:T(8,128)}, f32[32,2048]{1,0:T(8,128)}) custom-call(bf16[2048,1024]{1,0:T(8,128)(2,1)} %x_ref.5, f32[32,1024]{1,0:T(8,128)} %bitcast.58, s32[1,2048]{1,0:T(1,128)} %bitcast.63, s32[1,2048]{1,0:T(1,128)} %bitcast.66, f32[8,2048]{1,0:T(8,128)} %get-tuple-element.78.slots_ref.rows_ref), custom_call_target="tpu_custom_call" | custom-call | flops 402653184 | bytes 4194304 | tf_op jit(solution)/shard_map/k_route/pallas_call | solution.py:392
  26.7 5.8 %shard_map.138 = (bf16[512,512]{1,0:T(8,128)(2,1)}, bf16[512,512]{1,0:T(8,128)(2,1)}) custom-call(s32[1]{0:T(128)} %bitcast.z_ref, f32[16,2048]{1,0:T(8,128)} %get-tuple-element.79.rows_ref, bf16[2048,1024]{1,0:T(8,128)(2,1)} %src_ref.13), custom_call_target="tpu_custom_call" | custom-call | flops 2147483648 | bytes 3145728 | tf_op jit(solution)/shard_map/pallas_call | solution.py:376
  33.1 8.6 %shard_map.128 = (bf16[512,1024]{1,0:T(8,128)(2,1)}, bf16[512,1024]{1,0:T(8,128)(2,1)}) custom-call(s32[1]{0:T(128)} %bitcast.z_ref, f32[8,2048]{1,0:T(8,128)} %get-tuple-element.78.slots_ref.rows_ref, bf16[2048,1024]{1,0:T(8,128)(2,1)} %x_ref.5), custom_call_target="tpu_custom_call" | custom-call | flops 4294967296 | bytes 6291456 | tf_op jit(solution)/shard_map/pallas_call | solution.py:376
  41.6 2.0 collective-permute-start.3
  43.6 14.0 %collective-permute-done.27 = bf16[512,512]{1,0:T(8,128)(2,1)} collective-permute-done((bf16[512,512]{1,0:T(8,128)(2,1)}, bf16[512,512]{1,0:T(8,128)(2,1)}, u32[]{:S(2)}, u32[]{:S(2)}) %collective-permute-start.27) | collective-permute-done | bytes 524320 | tf_op jit(solution)/shard_map/ppermute | solution.py:373
  57.7 0.6 collective-permute-start.4
  58.3 2.4 collective-permute-start
  60.6 1.6 collective-permute-start.7
  62.7 3.0 constant_dynamic-slice_fusion
  65.7 8.5 %shard_map.129 = (bf16[512,1024]{1,0:T(8,128)(2,1)}, bf16[512,1024]{1,0:T(8,128)(2,1)}) custom-call(s32[1]{0:T(128)} %bitcast.z_ref, f32[8,2048]{1,0:T(8,128)} %get-tuple-element.78.slots_ref.rows_ref, bf16[2048,1024]{1,0:T(8,128)(2,1)} %x_ref.5), custom_call_target="tpu_custom_call" | custom-call | flops 4294967296 | bytes 6291456 | tf_op jit(solution)/shard_map/pallas_call | solution.py:376
  74.2 5.9 %collective-permute-done.3 = bf16[512,1024]{1,0:T(8,128)(2,1)} collective-permute-done((bf16[512,1024]{1,0:T(8,128)(2,1)}, bf16[512,1024]{1,0:T(8,128)(2,1)}, u32[]{:S(2)}, u32[]{:S(2)}) %collective-permute-start.3) | collective-permute-done | bytes 1048608 | tf_op jit(solution)/shard_map/ppermute | solution.py:373
  80.1 1.2 collective-permute-start.5
  81.3 24.3 %collective-permute-done.4 = bf16[512,1024]{1,0:T(8,128)(2,1)} collective-permute-done((bf16[512,1024]{1,0:T(8,128)(2,1)}, bf16[512,1024]{1,0:T(8,128)(2,1)}, u32[]{:S(2)}, u32[]{:S(2)}) %collective-permute-start.4) | collective-permute-done | bytes 1048608 | tf_op jit(solution)/shard_map/ppermute | solution.py:373
  105.6 1.5 collective-permute-start.9
  107.2 9.4 %shard_map.139 = (bf16[512,1024]{1,0:T(8,128)(2,1)}, bf16[512,1024]{1,0:T(8,128)(2,1)}) custom-call(s32[1]{0:T(128)} %bitcast.z_ref, f32[16,2048]{1,0:T(8,128)} %get-tuple-element.79.rows_ref, bf16[2048,1024]{1,0:T(8,128)(2,1)} %src_ref.13), custom_call_target="tpu_custom_call" | custom-call | flops 4294967296 | bytes 6291456 | tf_op jit(solution)/shard_map/pallas_call | solution.py:376
  116.5 8.6 %collective-permute-done.5 = bf16[512,1024]{1,0:T(8,128)(2,1)} collective-permute-done((bf16[512,1024]{1,0:T(8,128)(2,1)}, bf16[512,1024]{1,0:T(8,128)(2,1)}, u32[]{:S(2)}, u32[]{:S(2)}) %collective-permute-start.5) | collective-permute-done | bytes 1048608 | tf_op jit(solution)/shard_map/ppermute | solution.py:373
  125.1 1.2 collective-permute-start.31
  126.3 4.5 %collective-permute-done.6 = bf16[512,1024]{1,0:T(8,128)(2,1)} collective-permute-done((bf16[512,1024]{1,0:T(8,128)(2,1)}, bf16[512,1024]{1,0:T(8,128)(2,1)}, u32[]{:S(2)}, u32[]{:S(2)}) %collective-permute-start.6) | collective-permute-done | bytes 1048608 | tf_op jit(solution)/shard_map/ppermute | solution.py:373
  131.4 44.0 %collective-permute-done.9.refs_12_.refs_15_.refs_17_ = bf16[4,256,512]{2,1,0:T(8,128)(2,1)} collective-permute-done((bf16[4,256,512]{2,1,0:T(8,128)(2,1)}, bf16[4,256,512]{2,1,0:T(8,128)(2,1)}, u32[]{:S(2)}, u32[]{:S(2)}) %collective-permute-start.9) | collective-permute-done | bytes 1048608 | tf_op jit(solution)/shard_map/ppermute | solution.py:368
  175.4 1.6 collective-permute-start.24
  177.0 5.8 %shard_map.135 = (bf16[512,512]{1,0:T(8,128)(2,1)}, bf16[512,512]{1,0:T(8,128)(2,1)}) custom-call(s32[1]{0:T(128)} %bitcast.z_ref, f32[16,2048]{1,0:T(8,128)} %get-tuple-element.79.rows_ref, bf16[2048,1024]{1,0:T(8,128)(2,1)} %src_ref.13), custom_call_target="tpu_custom_call" | custom-call | flops 2147483648 | bytes 3145728 | tf_op jit(solution)/shard_map/pallas_call | solution.py:376
  182.8 11.6 %shard_map.130 = (f32[4,768,256]{2,1,0:T(8,128)}, f32[4,768,256]{2,1,0:T(8,128)}, bf16[4,768,256]{2,1,0:T(8,128)(2,1)}, bf16[4,768,512]{2,1,0:T(8,128)(2,1)}) custom-call(s32[1]{0:T(128)} %bitcast.z_ref, bf16[4,128,1024]{2,1,0:T(8,128)(2,1)} %bitcast.6.refs_0_, bf16[4,128,1024]{2,1,0:T(8,128)(2,1)} %bitcast.7.refs_1_, bf16[4,128,1024]{2,1,0:T(8,128)(2,1)} %bitcast.70, ...), custom_call_target="tpu_custom_call" | custom-call | flops 4026531840 | bytes 24576000 | tf_op jit(solution)/shard_map/pallas_call | solution.py:376
  194.9 1.6 collective-permute-start.30
  196.5 6.5 %shard_map.131 = (f32[4,256,256]{2,1,0:T(8,128)}, f32[4,256,256]{2,1,0:T(8,128)}, bf16[4,256,256]{2,1,0:T(8,128)(2,1)}, bf16[4,256,512]{2,1,0:T(8,128)(2,1)}) custom-call(s32[1]{0:T(128)} %bitcast.z_ref, bf16[4,128,1024]{2,1,0:T(8,128)(2,1)} %bitcast.12.refs_0_.refs_6_, bf16[4,128,1024]{2,1,0:T(8,128)(2,1)} %bitcast.13.refs_1_.refs_7_, ...), custom_call_target="tpu_custom_call" | custom-call | flops 1342177280 | bytes 8192000 | tf_op jit(solution)/shard_map/pallas_call | solution.py:376
  203.0 14.3 %k_fwd_other.1 = (bf16[4,128,512]{2,1,0:T(8,128)(2,1)}, bf16[4,128,512]{2,1,0:T(8,128)(2,1)}, bf16[4,128,512]{2,1,0:T(8,128)(2,1)}, bf16[4,128,512]{2,1,0:T(8,12...) custom-call(bf16[4,128,1024]{2,1,0:T(8,128)(2,1)} %bitcast.6.refs_0_, ...), custom_call_target="tpu_custom_call" | custom-call | flops 5368709120 | bytes 32000000 | tf_op jit(solution)/shard_map/k_fwd_other/pallas_call | solution.py:452
  217.8 4.1 collective-permute-done.30
  222.1 2.8 collective-permute-start.11
  224.9 0.6 collective-permute-start.12
  225.6 9.3 %shard_map.136 = (bf16[512,1024]{1,0:T(8,128)(2,1)}, bf16[512,1024]{1,0:T(8,128)(2,1)}) custom-call(s32[1]{0:T(128)} %bitcast.z_ref, f32[16,2048]{1,0:T(8,128)} %get-tuple-element.79.rows_ref, bf16[2048,1024]{1,0:T(8,128)(2,1)} %src_ref.13), custom_call_target="tpu_custom_call" | custom-call | flops 4294967296 | bytes 6291456 | tf_op jit(solution)/shard_map/pallas_call | solution.py:376
  234.9 2.2 copy.15
  237.1 14.1 %shard_map.140 = (bf16[4,128,256]{2,1,0:T(8,128)(2,1)}, bf16[4,128,256]{2,1,0:T(8,128)(2,1)}, bf16[4,128,256]{2,1,0:T(8,128)(2,1)}, bf16[4,128,256]{2,1,0:T(8,12...) custom-call(s32[1]{0:T(128)} %bitcast.z_ref, ...), custom_call_target="tpu_custom_call" | custom-call | flops 4294967296 | bytes 12288000 | tf_op jit(solution)/shard_map/pallas_call | solution.py:376
  251.4 2.6 collective-permute-start.14
  254.0 0.6 collective-permute-start.15
  254.6 9.5 %collective-permute-done.12 = bf16[4,128,512]{2,1,0:T(8,128)(2,1)} collective-permute-done((bf16[4,128,512]{2,1,0:T(8,128)(2,1)}, bf16[4,128,512]{2,1,0:T(8,128)(2,1)}, u32[]{:S(2)}, u32[]{:S(2)}) %collective-permute-start.12) | collective-permute-done | bytes 524320 | tf_op jit(solution)/shard_map/ppermute | solution.py:373
  264.1 10.1 %shard_map.132 = (f32[2048,512]{1,0:T(8,128)}, f32[2048,512]{1,0:T(8,128)}) custom-call(s32[1]{0:T(128)} %bitcast.z_ref, f32[2048,16]{1,0:T(8,128)} %bitcast.53, bf16[512,512]{1,0:T(8,128)(2,1)} %bitcast.73, bf16[512,512]{1,0:T(8,128)(2,1)} %bitcast.15.refs_1_, bf16[512,512]{1,0:T(8,128)(2,1)} %bitcast.16.refs_2_), custom_call_target="tpu_custom_call" | custom-call | flops 6442450944 | bytes 12000000 | tf_op jit(solution)/shard_map/pallas_call | solution.py:376
  274.7 2.9 collective-permute-done.14
  277.6 1.7 collective-permute-start.22
  279.3 7.1 %collective-permute-done.15 = bf16[4,128,512]{2,1,0:T(8,128)(2,1)} collective-permute-done((bf16[4,128,512]{2,1,0:T(8,128)(2,1)}, bf16[4,128,512]{2,1,0:T(8,128)(2,1)}, u32[]{:S(2)}, u32[]{:S(2)}) %collective-permute-start.15) | collective-permute-done | bytes 524320 | tf_op jit(solution)/shard_map/ppermute | solution.py:373
  286.8 1.2 collective-permute-done.16
  288.5 16.5 %shard_map.133 = (bf16[2048,512]{1,0:T(8,128)(2,1)}, f32[8,2048]{1,0:T(8,128)}, bf16[2048,1024]{1,0:T(8,128)(2,1)}) custom-call(s32[1]{0:T(128)} %bitcast.z_ref, f32[2048,16]{1,0:T(8,128)} %bitcast.54, bf16[2048,1024]{1,0:T(8,128)(2,1)} %src_ref.13, f32[2048,512]{1,0:T(8,128)} %get-tuple-element.93.one_ref, f32[2048,512]{1,0:T(8,128)} %get-tuple-element.94.two_ref, ...), custom_call_target="tpu_custom_call" | custom-call | flops 10737418240 | bytes 16000000 | tf_op jit(solution)/shard_map/pallas_call | solution.py:376
  305.0 2.0 collective-permute-start.41
  307.0 1.8 collective-permute-start.17
  308.8 14.1 %shard_map.137 = (bf16[4,128,256]{2,1,0:T(8,128)(2,1)}, bf16[4,128,256]{2,1,0:T(8,128)(2,1)}, bf16[4,128,256]{2,1,0:T(8,128)(2,1)}, bf16[4,128,256]{2,1,0:T(8,12...) custom-call(s32[1]{0:T(128)} %bitcast.z_ref, ...), custom_call_target="tpu_custom_call" | custom-call | flops 4294967296 | bytes 12288000 | tf_op jit(solution)/shard_map/pallas_call | solution.py:376
  323.0 2.9 collective-permute-start.43
  326.5 6.9 %collective-permute-done.43 = bf16[4,128,256]{2,1,0:T(8,128)(2,1)} collective-permute-done((bf16[4,128,256]{2,1,0:T(8,128)(2,1)}, bf16[4,128,256]{2,1,0:T(8,128)(2,1)}, u32[]{:S(2)}, u32[]{:S(2)}) %collective-permute-start.43) | collective-permute-done | bytes 262176 | tf_op jit(solution)/shard_map/ppermute | solution.py:373
  333.5 0.7 collective-permute-start.44
  334.2 15.1 %collective-permute-done.44 = bf16[4,128,256]{2,1,0:T(8,128)(2,1)} collective-permute-done((bf16[4,128,256]{2,1,0:T(8,128)(2,1)}, bf16[4,128,256]{2,1,0:T(8,128)(2,1)}, u32[]{:S(2)}, u32[]{:S(2)}) %collective-permute-start.44) | collective-permute-done | bytes 262176 | tf_op jit(solution)/shard_map/ppermute | solution.py:373
  349.6 6.9 %collective-permute-done.18.refs_1_ = f32[8,2048]{1,0:T(8,128)} collective-permute-done((f32[8,2048]{1,0:T(8,128)}, f32[8,2048]{1,0:T(8,128)}, u32[]{:S(2)}, u32[]{:S(2)}) %collective-permute-start.18) | collective-permute-done | bytes 65568 | tf_op jit(solution)/shard_map/ppermute | solution.py:368
  356.5 2.3 collective-permute-start.26
  358.7 3.0 shard_map.134
  361.7 0.9 collective-permute-start.46
  363.0 2.3 collective-permute-start.48
  365.2 8.4 %shard_map.142.refs_3_ = bf16[2048,256]{1,0:T(8,128)(2,1)} custom-call(s32[1]{0:T(128)} %bitcast.z_ref, f32[2048,16]{1,0:T(8,128)} %bitcast.55, bf16[192,2048]{1,0:T(8,128)(2,1)} %get-tuple-element.104.refs_1_.dl_ref, bf16[512,256]{1,0:T(8,128)(2,1)} %bitcast.69, bf16[512,256]{1,0:T(8,128)(2,1)} %bitcast.43.refs_1_, bf16[512,256]{1,0:T(8,128)(2,1)} %bitcast.44.refs_2_, ...), custom_call_target="tpu_custom_call" | custom-call | flops 4294967296 | bytes 8000000 | tf_op jit(solution)/shard_map/pallas_call | solution.py:376
  374.1 1.0 collective-permute-start.36
  375.1 1.3 collective-permute-start.37
  376.4 1.6 collective-permute-start.45
  378.0 13.7 %shard_map.143 = (f32[4,1024,256]{2,1,0:T(8,128)}, f32[4,1024,256]{2,1,0:T(8,128)}, f32[4,256,1024]{2,1,0:T(8,128)}, f32[32,512]{1,0:T(8,128)}) custom-call(s32[1]{0:T(128)} %bitcast.z_ref, bf16[4,128,1024]{2,1,0:T(8,128)(2,1)} %bitcast.6.refs_0_, bf16[4,128,1024]{2,1,0:T(8,128)(2,1)} %bitcast.7.refs_1_, bf16[4,128,1024]{2,1,0:T(8,128)(2,1)} %bitcast.72, ...), custom_call_target="tpu_custom_call" | custom-call | flops 6442450944 | bytes 40000000 | tf_op jit(solution)/shard_map/pallas_call | solution.py:376
  392.5 8.8 %collective-permute-start.51 = (f32[32,512]{1,0:T(8,128)}, f32[32,512]{1,0:T(8,128)}, u32[]{:S(2)}, u32[]{:S(2)}) collective-permute-start(f32[32,512]{1,0:T(8,128)} %get-tuple-element.144.refs_5_), channel_id=1, source_target_pairs={{0,9},{1,8},{2,11},{3,10},{4,13},{5,12},{6,15},{7,14},{8,1},{9,0},... | collective-permute-start | bytes 196616 | tf_op jit(solution)/shard_map/ppermute | solution.py:541
  401.3 11.2 %shard_map.141 = (f32[2048,512]{1,0:T(8,128)}, bf16[2048,1024]{1,0:T(8,128)(2,1)}) custom-call(s32[1]{0:T(128)} %bitcast.z_ref, bf16[2048,1024]{1,0:T(8,128)(2,1)} %get-tuple-element.100.kept_ref, bf16[2048,512]{1,0:T(8,128)(2,1)} %collective-permute-done.17.piece_ref, f32[2048,16]{1,0:T(8,128)} %bitcast.56, ...), custom_call_target="tpu_custom_call", output_to_operand_aliasing={{1}: (1, {})} | custom-call | flops 5368709120 | bytes 8000000 | tf_op jit(solution)/shard_map/pallas_call | solution.py:376
  412.5 9.1 %shard_map.144 = (bf16[2048,1024]{1,0:T(8,128)(2,1)}, f32[32,1024]{1,0:T(8,128)}) custom-call(s32[1]{0:T(128)} %bitcast.z_ref, f32[2048,16]{1,0:T(8,128)} %bitcast.57, f32[2048,512]{1,0:T(8,128)} %get-tuple-element.125.acc_ref, bf16[512,512]{1,0:T(8,128)(2,1)} %bitcast.39.refs_0_, bf16[512,512]{1,0:T(8,128)(2,1)} %bitcast.40.refs_1_, ...), custom_call_target="tpu_custom_call" | custom-call | flops 3221225472 | bytes 12000000 | tf_op jit(solution)/shard_map/pallas_call | solution.py:376
  (63 shorter events, 6.9 us)
Async XLA Ops:
  18.0 42.7 %collective-permute-start.1 = (bf16[512,1024]{1,0:T(8,128)(2,1)}, bf16[512,1024]{1,0:T(8,128)(2,1)}, u32[]{:S(2)}, u32[]{:S(2)}) collective-permute-start(bf16[512,1024]{1,0:T(8,128)(2,1)} %get-tuple-element.81), channel_id=1, source_target_pairs={{0,7},{1,6},{2,5},{3,4},{4,3},{5,2},{6,1},{7,0},{8,15},{9,14},{10,... | collective-permute-start | bytes 3145736 | tf_op jit(solution)/shard_map/ppermute | solution.py:373
  21.5 40.7 %collective-permute-start.2 = (bf16[512,1024]{1,0:T(8,128)(2,1)}, bf16[512,1024]{1,0:T(8,128)(2,1)}, u32[]{:S(2)}, u32[]{:S(2)}) collective-permute-start(bf16[512,1024]{1,0:T(8,128)(2,1)} %get-tuple-element.83), channel_id=1, source_target_pairs={{0,1},{1,0},{2,3},{3,2},{4,5},{5,4},{6,7},{7,6},{8,9},{9,8},{10,11... | collective-permute-start | bytes 3145736 | tf_op jit(solution)/shard_map/ppermute | solution.py:373
  32.5 25.2 %collective-permute-start.27 = (bf16[512,512]{1,0:T(8,128)(2,1)}, bf16[512,512]{1,0:T(8,128)(2,1)}, u32[]{:S(2)}, u32[]{:S(2)}) collective-permute-start(bf16[512,512]{1,0:T(8,128)(2,1)} %get-tuple-element.116), channel_id=1, source_target_pairs={{0,2},{1,3},{2,0},{3,1},{4,6},{5,7},{6,4},{7,5},{8,10},{9,11},{10,... | collective-permute-start | bytes 1572872 | tf_op jit(solution)/shard_map/ppermute | solution.py:373
  33.1 25.2 %collective-permute-start.29 = (bf16[512,512]{1,0:T(8,128)(2,1)}, bf16[512,512]{1,0:T(8,128)(2,1)}, u32[]{:S(2)}, u32[]{:S(2)}) collective-permute-start(bf16[512,512]{1,0:T(8,128)(2,1)} %get-tuple-element.117), channel_id=1, source_target_pairs={{0,4},{1,5},{2,6},{3,7},{4,0},{5,1},{6,2},{7,3},{8,12},{9,13},{10,... | collective-permute-start | bytes 1572872 | tf_op jit(solution)/shard_map/ppermute | solution.py:373
  41.6 38.5 %collective-permute-start.3 = (bf16[512,1024]{1,0:T(8,128)(2,1)}, bf16[512,1024]{1,0:T(8,128)(2,1)}, u32[]{:S(2)}, u32[]{:S(2)}) collective-permute-start(bf16[512,1024]{1,0:T(8,128)(2,1)} %get-tuple-element.84), channel_id=1, source_target_pairs={{0,2},{1,3},{2,0},{3,1},{4,6},{5,7},{6,4},{7,5},{8,10},{9,11},{10,... | collective-permute-start | bytes 3145736 | tf_op jit(solution)/shard_map/ppermute | solution.py:373
  57.7 48.0 %collective-permute-start.4 = (bf16[512,1024]{1,0:T(8,128)(2,1)}, bf16[512,1024]{1,0:T(8,128)(2,1)}, u32[]{:S(2)}, u32[]{:S(2)}) collective-permute-start(bf16[512,1024]{1,0:T(8,128)(2,1)} %get-tuple-element.85), channel_id=1, source_target_pairs={{0,4},{1,5},{2,6},{3,7},{4,0},{5,1},{6,2},{7,3},{8,12},{9,13},{10,... | collective-permute-start | bytes 3145736 | tf_op jit(solution)/shard_map/ppermute | solution.py:373
  58.3 47.4 %collective-permute-start = (bf16[512,1024]{1,0:T(8,128)(2,1)}, bf16[512,1024]{1,0:T(8,128)(2,1)}, u32[]{:S(2)}, u32[]{:S(2)}) collective-permute-start(bf16[512,1024]{1,0:T(8,128)(2,1)} %get-tuple-element.80), channel_id=1, source_target_pairs={{0,6},{1,7},{2,4},{3,5},{4,2},{5,3},{6,0},{7,1},{8,14},{9,15},{10,... | collective-permute-start | bytes 3145736 | tf_op jit(solution)/shard_map/ppermute | solution.py:373
  60.6 133.8 %collective-permute-start.7 = (bf16[4,1024,256]{2,1,0:T(8,128)(2,1)}, bf16[4,1024,256]{2,1,0:T(8,128)(2,1)}, u32[]{:S(2)}, u32[]{:S(2)}) collective-permute-start(bf16[4,1024,256]{2,1,0:T(8,128)(2,1)} %refs_12_.3), channel_id=1, source_target_pairs={{0,8},{8,0},{1,9},{9,1},{2,10},{10,2},{3,11},{11,3},{4,12},{12,4},... | collective-permute-start | bytes 6291464 | tf_op jit(solution)/shard_map/ppermute | solution.py:368
  62.2 132.7 %collective-permute-start.8 = (bf16[4,1024,256]{2,1,0:T(8,128)(2,1)}, bf16[4,1024,256]{2,1,0:T(8,128)(2,1)}, u32[]{:S(2)}, u32[]{:S(2)}) collective-permute-start(bf16[4,1024,256]{2,1,0:T(8,128)(2,1)} %refs_13_.1), channel_id=1, source_target_pairs={{0,8},{8,0},{1,9},{9,1},{2,10},{10,2},{3,11},{11,3},{4,12},{12,4},... | collective-permute-start | bytes 6291464 | tf_op jit(solution)/shard_map/ppermute | solution.py:368
  80.1 45.0 %collective-permute-start.5 = (bf16[512,1024]{1,0:T(8,128)(2,1)}, bf16[512,1024]{1,0:T(8,128)(2,1)}, u32[]{:S(2)}, u32[]{:S(2)}) collective-permute-start(bf16[512,1024]{1,0:T(8,128)(2,1)} %get-tuple-element.86), channel_id=1, source_target_pairs={{0,3},{1,2},{2,1},{3,0},{4,7},{5,6},{6,5},{7,4},{8,11},{9,10},{10,... | collective-permute-start | bytes 3145736 | tf_op jit(solution)/shard_map/ppermute | solution.py:373
  105.6 25.2 %collective-permute-start.6 = (bf16[512,1024]{1,0:T(8,128)(2,1)}, bf16[512,1024]{1,0:T(8,128)(2,1)}, u32[]{:S(2)}, u32[]{:S(2)}) collective-permute-start(bf16[512,1024]{1,0:T(8,128)(2,1)} %get-tuple-element.87), channel_id=1, source_target_pairs={{0,5},{1,4},{2,7},{3,6},{4,1},{5,0},{6,3},{7,2},{8,13},{9,12},{10,... | collective-permute-start | bytes 3145736 | tf_op jit(solution)/shard_map/ppermute | solution.py:373
  105.6 69.8 %collective-permute-start.9 = (bf16[4,256,512]{2,1,0:T(8,128)(2,1)}, bf16[4,256,512]{2,1,0:T(8,128)(2,1)}, u32[]{:S(2)}, u32[]{:S(2)}) collective-permute-start(bf16[4,256,512]{2,1,0:T(8,128)(2,1)} %get-tuple-element.151), channel_id=1, source_target_pairs={{0,8},{8,0},{1,9},{9,1},{2,10},{10,2},{3,11},{11,3},{4,12},{12,4},... | collective-permute-start | bytes 3145736 | tf_op jit(solution)/shard_map/ppermute | solution.py:368
  125.1 96.7 %collective-permute-start.31 = (bf16[512,1024]{1,0:T(8,128)(2,1)}, bf16[512,1024]{1,0:T(8,128)(2,1)}, u32[]{:S(2)}, u32[]{:S(2)}) collective-permute-start(bf16[512,1024]{1,0:T(8,128)(2,1)} %get-tuple-element.118), channel_id=1, source_target_pairs={{0,3},{1,2},{2,1},{3,0},{4,7},{5,6},{6,5},{7,4},{8,11},{9,10},{10,... | collective-permute-start | bytes 3145736 | tf_op jit(solution)/shard_map/ppermute | solution.py:373
  130.8 91.3 %collective-permute-start.32 = (bf16[512,1024]{1,0:T(8,128)(2,1)}, bf16[512,1024]{1,0:T(8,128)(2,1)}, u32[]{:S(2)}, u32[]{:S(2)}) collective-permute-start(bf16[512,1024]{1,0:T(8,128)(2,1)} %get-tuple-element.119), channel_id=1, source_target_pairs={{0,5},{1,4},{2,7},{3,6},{4,1},{5,0},{6,3},{7,2},{8,13},{9,12},{10,... | collective-permute-start | bytes 3145736 | tf_op jit(solution)/shard_map/ppermute | solution.py:373
  175.4 49.5 %collective-permute-start.24 = (bf16[4,256,512]{2,1,0:T(8,128)(2,1)}, bf16[4,256,512]{2,1,0:T(8,128)(2,1)}, u32[]{:S(2)}, u32[]{:S(2)}) collective-permute-start(bf16[4,256,512]{2,1,0:T(8,128)(2,1)} %get-tuple-element.150), channel_id=1, source_target_pairs={{0,8},{8,0},{1,9},{9,1},{2,10},{10,2},{3,11},{11,3},{4,12},{12,4},... | collective-permute-start | bytes 3145736 | tf_op jit(solution)/shard_map/ppermute | solution.py:368
  194.4 22.9 %collective-permute-start.28 = (bf16[512,512]{1,0:T(8,128)(2,1)}, bf16[512,512]{1,0:T(8,128)(2,1)}, u32[]{:S(2)}, u32[]{:S(2)}) collective-permute-start(bf16[512,512]{1,0:T(8,128)(2,1)} %collective-permute-done.27), channel_id=1, source_target_pairs={{0,8},{8,0},{1,9},{9,1},{2,10},{10,2},{3,11},{11,3},{4,12},{12,4},... | collective-permute-start | bytes 1572872 | tf_op jit(solution)/shard_map/ppermute | solution.py:368
  194.9 27.0 %collective-permute-start.30 = (bf16[512,512]{1,0:T(8,128)(2,1)}, bf16[512,512]{1,0:T(8,128)(2,1)}, u32[]{:S(2)}, u32[]{:S(2)}) collective-permute-start(bf16[512,512]{1,0:T(8,128)(2,1)} %collective-permute-done.29), channel_id=1, source_target_pairs={{0,8},{8,0},{1,9},{9,1},{2,10},{10,2},{3,11},{11,3},{4,12},{12,4},... | collective-permute-start | bytes 1572872 | tf_op jit(solution)/shard_map/ppermute | solution.py:368
  217.3 33.9 %collective-permute-start.19 = (bf16[512,512]{1,0:T(8,128)(2,1)}, bf16[512,512]{1,0:T(8,128)(2,1)}, u32[]{:S(2)}, u32[]{:S(2)}) collective-permute-start(bf16[512,512]{1,0:T(8,128)(2,1)} %get-tuple-element.105), channel_id=1, source_target_pairs={{0,6},{1,7},{2,4},{3,5},{4,2},{5,3},{6,0},{7,1},{8,14},{9,15},{10,... | collective-permute-start | bytes 1572872 | tf_op jit(solution)/shard_map/ppermute | solution.py:373
  221.9 29.5 %collective-permute-start.21 = (bf16[512,512]{1,0:T(8,128)(2,1)}, bf16[512,512]{1,0:T(8,128)(2,1)}, u32[]{:S(2)}, u32[]{:S(2)}) collective-permute-start(bf16[512,512]{1,0:T(8,128)(2,1)} %get-tuple-element.106), channel_id=1, source_target_pairs={{0,7},{1,6},{2,5},{3,4},{4,3},{5,2},{6,1},{7,0},{8,15},{9,14},{10,... | collective-permute-start | bytes 1572872 | tf_op jit(solution)/shard_map/ppermute | solution.py:373
  221.9 29.6 %collective-permute-start.10 = (bf16[4,128,512]{2,1,0:T(8,128)(2,1)}, bf16[4,128,512]{2,1,0:T(8,128)(2,1)}, u32[]{:S(2)}, u32[]{:S(2)}) collective-permute-start(bf16[4,128,512]{2,1,0:T(8,128)(2,1)} %get-tuple-element.91), channel_id=1, source_target_pairs={{0,1},{1,0},{2,3},{3,2},{4,5},{5,4},{6,7},{7,6},{8,9},{9,8},{10,11... | collective-permute-start | bytes 1572872 | tf_op jit(solution)/shard_map/ppermute | solution.py:373
  222.1 31.9 %collective-permute-start.11 = (bf16[4,128,512]{2,1,0:T(8,128)(2,1)}, bf16[4,128,512]{2,1,0:T(8,128)(2,1)}, u32[]{:S(2)}, u32[]{:S(2)}) collective-permute-start(bf16[4,128,512]{2,1,0:T(8,128)(2,1)} %get-tuple-element.92), channel_id=1, source_target_pairs={{0,6},{1,7},{2,4},{3,5},{4,2},{5,3},{6,0},{7,1},{8,14},{9,15},{10,... | collective-permute-start | bytes 1572872 | tf_op jit(solution)/shard_map/ppermute | solution.py:373
  224.9 39.2 %collective-permute-start.12 = (bf16[4,128,512]{2,1,0:T(8,128)(2,1)}, bf16[4,128,512]{2,1,0:T(8,128)(2,1)}, u32[]{:S(2)}, u32[]{:S(2)}) collective-permute-start(bf16[4,128,512]{2,1,0:T(8,128)(2,1)} %get-tuple-element.95), channel_id=1, source_target_pairs={{0,4},{1,5},{2,6},{3,7},{4,0},{5,1},{6,2},{7,3},{8,12},{9,13},{10,... | collective-permute-start | bytes 1572872 | tf_op jit(solution)/shard_map/ppermute | solution.py:373
  251.3 55.8 %collective-permute-start.23 = (bf16[512,1024]{1,0:T(8,128)(2,1)}, bf16[512,1024]{1,0:T(8,128)(2,1)}, u32[]{:S(2)}, u32[]{:S(2)}) collective-permute-start(bf16[512,1024]{1,0:T(8,128)(2,1)} %get-tuple-element.108), channel_id=1, source_target_pairs={{0,1},{1,0},{2,3},{3,2},{4,5},{5,4},{6,7},{7,6},{8,9},{9,8},{10,11... | collective-permute-start | bytes 3145736 | tf_op jit(solution)/shard_map/ppermute | solution.py:373
  251.3 22.8 %collective-permute-start.13 = (bf16[4,128,512]{2,1,0:T(8,128)(2,1)}, bf16[4,128,512]{2,1,0:T(8,128)(2,1)}, u32[]{:S(2)}, u32[]{:S(2)}) collective-permute-start(bf16[4,128,512]{2,1,0:T(8,128)(2,1)} %get-tuple-element.96), channel_id=1, source_target_pairs={{0,2},{1,3},{2,0},{3,1},{4,6},{5,7},{6,4},{7,5},{8,10},{9,11},{10,... | collective-permute-start | bytes 1572872 | tf_op jit(solution)/shard_map/ppermute | solution.py:373
  251.4 26.2 %collective-permute-start.14 = (bf16[4,128,512]{2,1,0:T(8,128)(2,1)}, bf16[4,128,512]{2,1,0:T(8,128)(2,1)}, u32[]{:S(2)}, u32[]{:S(2)}) collective-permute-start(bf16[4,128,512]{2,1,0:T(8,128)(2,1)} %get-tuple-element.97), channel_id=1, source_target_pairs={{0,7},{1,6},{2,5},{3,4},{4,3},{5,2},{6,1},{7,0},{8,15},{9,14},{10,... | collective-permute-start | bytes 1572872 | tf_op jit(solution)/shard_map/ppermute | solution.py:373
  254.0 32.4 %collective-permute-start.15 = (bf16[4,128,512]{2,1,0:T(8,128)(2,1)}, bf16[4,128,512]{2,1,0:T(8,128)(2,1)}, u32[]{:S(2)}, u32[]{:S(2)}) collective-permute-start(bf16[4,128,512]{2,1,0:T(8,128)(2,1)} %get-tuple-element.98), channel_id=1, source_target_pairs={{0,5},{1,4},{2,7},{3,6},{4,1},{5,0},{6,3},{7,2},{8,13},{9,12},{10,... | collective-permute-start | bytes 1572872 | tf_op jit(solution)/shard_map/ppermute | solution.py:373
  264.1 23.9 %collective-permute-start.16 = (bf16[4,128,512]{2,1,0:T(8,128)(2,1)}, bf16[4,128,512]{2,1,0:T(8,128)(2,1)}, u32[]{:S(2)}, u32[]{:S(2)}) collective-permute-start(bf16[4,128,512]{2,1,0:T(8,128)(2,1)} %get-tuple-element.99), channel_id=1, source_target_pairs={{0,3},{1,2},{2,1},{3,0},{4,7},{5,6},{6,5},{7,4},{8,11},{9,10},{10,... | collective-permute-start | bytes 1572872 | tf_op jit(solution)/shard_map/ppermute | solution.py:373
  274.2 30.9 %collective-permute-start.20 = (bf16[512,512]{1,0:T(8,128)(2,1)}, bf16[512,512]{1,0:T(8,128)(2,1)}, u32[]{:S(2)}, u32[]{:S(2)}) collective-permute-start(bf16[512,512]{1,0:T(8,128)(2,1)} %collective-permute-done.19), channel_id=1, source_target_pairs={{0,8},{8,0},{1,9},{9,1},{2,10},{10,2},{3,11},{11,3},{4,12},{12,4},... | collective-permute-start | bytes 1572872 | tf_op jit(solution)/shard_map/ppermute | solution.py:368
  277.6 29.4 %collective-permute-start.22 = (bf16[512,512]{1,0:T(8,128)(2,1)}, bf16[512,512]{1,0:T(8,128)(2,1)}, u32[]{:S(2)}, u32[]{:S(2)}) collective-permute-start(bf16[512,512]{1,0:T(8,128)(2,1)} %collective-permute-done.21), channel_id=1, source_target_pairs={{0,8},{8,0},{1,9},{9,1},{2,10},{10,2},{3,11},{11,3},{4,12},{12,4},... | collective-permute-start | bytes 1572872 | tf_op jit(solution)/shard_map/ppermute | solution.py:368
  286.4 36.6 %collective-permute-start.39 = (bf16[4,128,256]{2,1,0:T(8,128)(2,1)}, bf16[4,128,256]{2,1,0:T(8,128)(2,1)}, u32[]{:S(2)}, u32[]{:S(2)}) collective-permute-start(bf16[4,128,256]{2,1,0:T(8,128)(2,1)} %get-tuple-element.131), channel_id=1, source_target_pairs={{0,2},{1,3},{2,0},{3,1},{4,6},{5,7},{6,4},{7,5},{8,10},{9,11},{10,... | collective-permute-start | bytes 786440 | tf_op jit(solution)/shard_map/ppermute | solution.py:373
  288.0 35.0 %collective-permute-start.40 = (bf16[4,128,256]{2,1,0:T(8,128)(2,1)}, bf16[4,128,256]{2,1,0:T(8,128)(2,1)}, u32[]{:S(2)}, u32[]{:S(2)}) collective-permute-start(bf16[4,128,256]{2,1,0:T(8,128)(2,1)} %get-tuple-element.132), channel_id=1, source_target_pairs={{0,3},{1,2},{2,1},{3,0},{4,7},{5,6},{6,5},{7,4},{8,11},{9,10},{10,... | collective-permute-start | bytes 786440 | tf_op jit(solution)/shard_map/ppermute | solution.py:373
  305.0 20.8 %collective-permute-start.41 = (bf16[4,128,256]{2,1,0:T(8,128)(2,1)}, bf16[4,128,256]{2,1,0:T(8,128)(2,1)}, u32[]{:S(2)}, u32[]{:S(2)}) collective-permute-start(bf16[4,128,256]{2,1,0:T(8,128)(2,1)} %get-tuple-element.133), channel_id=1, source_target_pairs={{0,4},{1,5},{2,6},{3,7},{4,0},{5,1},{6,2},{7,3},{8,12},{9,13},{10,... | collective-permute-start | bytes 786440 | tf_op jit(solution)/shard_map/ppermute | solution.py:373
  307.0 19.2 %collective-permute-start.42 = (bf16[4,128,256]{2,1,0:T(8,128)(2,1)}, bf16[4,128,256]{2,1,0:T(8,128)(2,1)}, u32[]{:S(2)}, u32[]{:S(2)}) collective-permute-start(bf16[4,128,256]{2,1,0:T(8,128)(2,1)} %get-tuple-element.134), channel_id=1, source_target_pairs={{0,5},{1,4},{2,7},{3,6},{4,1},{5,0},{6,3},{7,2},{8,13},{9,12},{10,... | collective-permute-start | bytes 786440 | tf_op jit(solution)/shard_map/ppermute | solution.py:373
  307.0 85.5 %collective-permute-start.17 = (bf16[2048,512]{1,0:T(8,128)(2,1)}, bf16[2048,512]{1,0:T(8,128)(2,1)}, u32[]{:S(2)}, u32[]{:S(2)}) collective-permute-start(bf16[2048,512]{1,0:T(8,128)(2,1)} %get-tuple-element.101), channel_id=1, source_target_pairs={{0,8},{8,0},{1,9},{9,1},{2,10},{10,2},{3,11},{11,3},{4,12},{12,4},... | collective-permute-start | bytes 6291464 | tf_op jit(solution)/shard_map/ppermute | solution.py:368
  322.9 3.6 collective-permute-start.38
  323.0 10.5 %collective-permute-start.43 = (bf16[4,128,256]{2,1,0:T(8,128)(2,1)}, bf16[4,128,256]{2,1,0:T(8,128)(2,1)}, u32[]{:S(2)}, u32[]{:S(2)}) collective-permute-start(bf16[4,128,256]{2,1,0:T(8,128)(2,1)} %get-tuple-element.135), channel_id=1, source_target_pairs={{0,6},{1,7},{2,4},{3,5},{4,2},{5,3},{6,0},{7,1},{8,14},{9,15},{10,... | collective-permute-start | bytes 786440 | tf_op jit(solution)/shard_map/ppermute | solution.py:373
  325.8 35.9 %collective-permute-start.33 = (bf16[4,128,512]{2,1,0:T(8,128)(2,1)}, bf16[4,128,512]{2,1,0:T(8,128)(2,1)}, u32[]{:S(2)}, u32[]{:S(2)}) collective-permute-start(bf16[4,128,512]{2,1,0:T(8,128)(2,1)} %get-tuple-element.122), channel_id=1, source_target_pairs={{0,2},{1,3},{2,0},{3,1},{4,6},{5,7},{6,4},{7,5},{8,10},{9,11},{10,... | collective-permute-start | bytes 1572872 | tf_op jit(solution)/shard_map/ppermute | solution.py:373
  326.3 36.4 %collective-permute-start.34 = (bf16[4,128,512]{2,1,0:T(8,128)(2,1)}, bf16[4,128,512]{2,1,0:T(8,128)(2,1)}, u32[]{:S(2)}, u32[]{:S(2)}) collective-permute-start(bf16[4,128,512]{2,1,0:T(8,128)(2,1)} %get-tuple-element.123), channel_id=1, source_target_pairs={{0,4},{1,5},{2,6},{3,7},{4,0},{5,1},{6,2},{7,3},{8,12},{9,13},{10,... | collective-permute-start | bytes 1572872 | tf_op jit(solution)/shard_map/ppermute | solution.py:373
  326.5 36.5 %collective-permute-start.25 = (bf16[4,128,512]{2,1,0:T(8,128)(2,1)}, bf16[4,128,512]{2,1,0:T(8,128)(2,1)}, u32[]{:S(2)}, u32[]{:S(2)}) collective-permute-start(bf16[4,128,512]{2,1,0:T(8,128)(2,1)} %get-tuple-element.114), channel_id=1, source_target_pairs={{0,1},{1,0},{2,3},{3,2},{4,5},{5,4},{6,7},{7,6},{8,9},{9,8},{10,11... | collective-permute-start | bytes 1572872 | tf_op jit(solution)/shard_map/ppermute | solution.py:373
  333.5 15.8 %collective-permute-start.44 = (bf16[4,128,256]{2,1,0:T(8,128)(2,1)}, bf16[4,128,256]{2,1,0:T(8,128)(2,1)}, u32[]{:S(2)}, u32[]{:S(2)}) collective-permute-start(bf16[4,128,256]{2,1,0:T(8,128)(2,1)} %get-tuple-element.136), channel_id=1, source_target_pairs={{0,7},{1,6},{2,5},{3,4},{4,3},{5,2},{6,1},{7,0},{8,15},{9,14},{10,... | collective-permute-start | bytes 786440 | tf_op jit(solution)/shard_map/ppermute | solution.py:373
  349.3 7.2 %collective-permute-start.18 = (f32[8,2048]{1,0:T(8,128)}, f32[8,2048]{1,0:T(8,128)}, u32[]{:S(2)}, u32[]{:S(2)}) collective-permute-start(f32[8,2048]{1,0:T(8,128)} %get-tuple-element.103.refs_0_), channel_id=1, source_target_pairs={{0,8},{8,0},{1,9},{9,1},{2,10},{10,2},{3,11},{11,3},{4,12},{12,4},... | collective-permute-start | bytes 196616 | tf_op jit(solution)/shard_map/ppermute | solution.py:368
  356.5 17.2 %collective-permute-start.26 = (bf16[4,128,512]{2,1,0:T(8,128)(2,1)}, bf16[4,128,512]{2,1,0:T(8,128)(2,1)}, u32[]{:S(2)}, u32[]{:S(2)}) collective-permute-start(bf16[4,128,512]{2,1,0:T(8,128)(2,1)} %get-tuple-element.115), channel_id=1, source_target_pairs={{0,6},{1,7},{2,4},{3,5},{4,2},{5,3},{6,0},{7,1},{8,14},{9,15},{10,... | collective-permute-start | bytes 1572872 | tf_op jit(solution)/shard_map/ppermute | solution.py:373
  361.7 12.3 %collective-permute-start.46 = (f32[32,512]{1,0:T(8,128)}, f32[32,512]{1,0:T(8,128)}, u32[]{:S(2)}, u32[]{:S(2)}) collective-permute-start(f32[32,512]{1,0:T(8,128)} %get-tuple-element.143.refs_26_), channel_id=1, source_target_pairs={{0,2},{1,3},{2,0},{3,1},{4,6},{5,7},{6,4},{7,5},{8,10},{9,11},{10,... | collective-permute-start | bytes 196616 | tf_op jit(solution)/shard_map/ppermute | solution.py:373
  362.7 12.4 %collective-permute-start.47 = (f32[32,512]{1,0:T(8,128)}, f32[32,512]{1,0:T(8,128)}, u32[]{:S(2)}, u32[]{:S(2)}) collective-permute-start(f32[32,512]{1,0:T(8,128)} %get-tuple-element.143.refs_26_), channel_id=1, source_target_pairs={{0,4},{1,5},{2,6},{3,7},{4,0},{5,1},{6,2},{7,3},{8,12},{9,13},{10,... | collective-permute-start | bytes 196616 | tf_op jit(solution)/shard_map/ppermute | solution.py:373
  363.0 13.4 %collective-permute-start.48 = (f32[32,512]{1,0:T(8,128)}, f32[32,512]{1,0:T(8,128)}, u32[]{:S(2)}, u32[]{:S(2)}) collective-permute-start(f32[32,512]{1,0:T(8,128)} %get-tuple-element.143.refs_26_), channel_id=1, source_target_pairs={{0,6},{1,7},{2,4},{3,5},{4,2},{5,3},{6,0},{7,1},{8,14},{9,15},{10,... | collective-permute-start | bytes 196616 | tf_op jit(solution)/shard_map/ppermute | solution.py:373
  373.6 18.1 %collective-permute-start.35 = (bf16[4,128,512]{2,1,0:T(8,128)(2,1)}, bf16[4,128,512]{2,1,0:T(8,128)(2,1)}, u32[]{:S(2)}, u32[]{:S(2)}) collective-permute-start(bf16[4,128,512]{2,1,0:T(8,128)(2,1)} %get-tuple-element.126), channel_id=1, source_target_pairs={{0,3},{1,2},{2,1},{3,0},{4,7},{5,6},{6,5},{7,4},{8,11},{9,10},{10,... | collective-permute-start | bytes 1572872 | tf_op jit(solution)/shard_map/ppermute | solution.py:373
  374.1 18.0 %collective-permute-start.36 = (bf16[4,128,512]{2,1,0:T(8,128)(2,1)}, bf16[4,128,512]{2,1,0:T(8,128)(2,1)}, u32[]{:S(2)}, u32[]{:S(2)}) collective-permute-start(bf16[4,128,512]{2,1,0:T(8,128)(2,1)} %get-tuple-element.127), channel_id=1, source_target_pairs={{0,5},{1,4},{2,7},{3,6},{4,1},{5,0},{6,3},{7,2},{8,13},{9,12},{10,... | collective-permute-start | bytes 1572872 | tf_op jit(solution)/shard_map/ppermute | solution.py:373
  375.1 37.4 %collective-permute-start.37 = (bf16[4,128,512]{2,1,0:T(8,128)(2,1)}, bf16[4,128,512]{2,1,0:T(8,128)(2,1)}, u32[]{:S(2)}, u32[]{:S(2)}) collective-permute-start(bf16[4,128,512]{2,1,0:T(8,128)(2,1)} %get-tuple-element.128), channel_id=1, source_target_pairs={{0,7},{1,6},{2,5},{3,4},{4,3},{5,2},{6,1},{7,0},{8,15},{9,14},{10,... | collective-permute-start | bytes 1572872 | tf_op jit(solution)/shard_map/ppermute | solution.py:373
  376.4 36.1 %collective-permute-start.45 = (bf16[2048,256]{1,0:T(8,128)(2,1)}, bf16[2048,256]{1,0:T(8,128)(2,1)}, u32[]{:S(2)}, u32[]{:S(2)}) collective-permute-start(bf16[2048,256]{1,0:T(8,128)(2,1)} %shard_map.142.refs_3_), channel_id=1, source_target_pairs={{0,8},{8,0},{1,9},{9,1},{2,10},{10,2},{3,11},{11,3},{4,12},{12,4},... | collective-permute-start | bytes 3145736 | tf_op jit(solution)/shard_map/ppermute | solution.py:368
  391.7 20.8 %collective-permute-start.49 = (f32[32,512]{1,0:T(8,128)}, f32[32,512]{1,0:T(8,128)}, u32[]{:S(2)}, u32[]{:S(2)}) collective-permute-start(f32[32,512]{1,0:T(8,128)} %get-tuple-element.144.refs_5_), channel_id=1, source_target_pairs={{0,1},{1,0},{2,3},{3,2},{4,5},{5,4},{6,7},{7,6},{8,9},{9,8},{10,11... | collective-permute-start | bytes 196616 | tf_op jit(solution)/shard_map/ppermute | solution.py:373
  392.0 20.5 %collective-permute-start.50 = (f32[32,512]{1,0:T(8,128)}, f32[32,512]{1,0:T(8,128)}, u32[]{:S(2)}, u32[]{:S(2)}) collective-permute-start(f32[32,512]{1,0:T(8,128)} %get-tuple-element.144.refs_5_), channel_id=1, source_target_pairs={{0,8},{8,0},{1,9},{9,1},{2,10},{10,2},{3,11},{11,3},{4,12},{12,4},... | collective-permute-start | bytes 196616 | tf_op jit(solution)/shard_map/ppermute | solution.py:368
  392.5 20.0 %collective-permute-start.51 = (f32[32,512]{1,0:T(8,128)}, f32[32,512]{1,0:T(8,128)}, u32[]{:S(2)}, u32[]{:S(2)}) collective-permute-start(f32[32,512]{1,0:T(8,128)} %get-tuple-element.144.refs_5_), channel_id=1, source_target_pairs={{0,9},{1,8},{2,11},{3,10},{4,13},{5,12},{6,15},{7,14},{8,1},{9,0},... | collective-permute-start | bytes 196616 | tf_op jit(solution)/shard_map/ppermute | solution.py:541
